TPU v7x, 256 devices: a 8x8x2 block of a 8x8x16 slice. The times are simulated.
256 devices in a mesh: groups: 2 (over z), expert: 64 (over x, y), replica: 2 (over core).
Axes of the slice: x: 8, y: 8, z: 2, core: 2. Of those that a mesh axis runs over, the one named last changes fastest.
The devices are a block of a 8x8x16 slice.
Arguments:
- queries: bfloat16 [1024, 8192], P(('groups', 'expert', 'replica')), parts along dimension 0, may hold values from -250 to 250
- token_keys: bfloat16 [1024, 512], P(('groups', 'expert', 'replica')), parts along dimension 0, may hold values from -6 to 6
- token_values: bfloat16 [1024, 512], P(('groups', 'expert', 'replica')), parts along dimension 0, may hold values from -6 to 6
- stored_keys: bfloat16 [1024, 256, 512], P(('groups', 'expert', 'replica')), parts along dimension 0, may hold values from -7 to 7
- stored_values: bfloat16 [1024, 256, 512], P(('groups', 'expert', 'replica')), parts along dimension 0, may hold values from -6 to 6
- kv_len: int32 [1024], P(('groups', 'expert', 'replica')), parts along dimension 0, may hold values from 2 to 256, as said below
- residual: bfloat16 [1024, 4096], P(('groups', 'expert', 'replica')), parts along dimension 0, may hold values from -6 to 6
- out_weight: bfloat16 [8192, 4096], P(('expert', 'replica')), may hold values from -0.1875 to 0.1875
- norm_gain: bfloat16 [4096], replicated, may hold values from 0.25 to 1.75
- expert_ids: int32 [1024, 8], P(('groups', 'expert')), parts along dimension 0, may hold values from 0 to 63, all different within a row; in each aligned block of 8 rows (0 to 7, 8 to 15, ...) at most 2 rows name the same one
- route_weight: float32 [1024, 8], P(('groups', 'expert')), parts along dimension 0, may hold values from 0.05 to 1
- w_gate: bfloat16 [64, 4096, 768], P('expert', None, 'replica'), may hold values from -0.09375 to 0.09375
- w_up: bfloat16 [64, 4096, 768], P('expert', None, 'replica'), may hold values from -0.09375 to 0.09375
- w_down: bfloat16 [64, 768, 4096], P('expert', 'replica'), may hold values from -0.4375 to 0.4375
Outputs:
- updated: bfloat16 [1024, 4096], P(('groups', 'expert', 'replica')), parts along dimension 0
There are 2 independent parts, one for each index of `groups`. A program takes and returns all parts, laid end to end along the dimension named above; an argument that names none is the same for every part. Nothing has to cross between parts.
Inputs may be any that keep to these rules, and one draw needn't show every extreme that they name: `kv_len`: at least 2; some sequence uses all 256 positions. `expert_ids`: each token names 8 different experts; in each aligned block of 8 tokens no expert is named by more than 2 tokens, and some block reaches it.
All inputs are finite; a program needn't handle non-finite values.
Results may differ from a plain program's by a relative error of at most 0.01.
Values may be sent and summed in bfloat16 or wider, within the bound.
No kernel may reach another device: no remote copies, remote signals or barrier semaphores. Data moves between devices by JAX's collectives and lax.ppermute only.
A program may use at most 64 MiB of HBM per device.

v0:
```python
import math

import jax
import jax.numpy as jnp
from jax import lax
from jax.sharding import PartitionSpec as P

HEAD_WIDTH = 128


def shifted(block, axis, distance):
    devices = range(lax.axis_size(axis))
    route = [(i - distance, i) for i in devices if i - distance in devices]
    return lax.ppermute(block, axis, route)


def sent_to_all(x, axis):
    copies = jnp.broadcast_to(x, (lax.axis_size(axis), *x.shape))
    return lax.all_to_all(copies, axis, split_axis=0, concat_axis=0, tiled=True)


def laid_out(parts, dim):
    shape = list(parts.shape[1:])
    shape[dim] *= parts.shape[0]
    return jnp.moveaxis(parts, 0, dim).reshape(shape)


def gathered_copies(x, axis, dim):
    parts = sent_to_all(x, axis)
    return laid_out(parts, dim)


def split_up(x, dim, size):
    shape = x.shape
    parts = x.reshape(*shape[:dim], size, shape[dim] // size, *shape[dim + 1 :])
    return jnp.moveaxis(parts, dim, 0)


def sent_and_summed(x, axis, dim):
    size = lax.axis_size(axis)
    parts = lax.all_to_all(split_up(x, dim, size), axis, 0, 0, tiled=True)
    return jnp.sum(parts.astype(jnp.float32), axis=0)


def attend_local(queries, token_keys, token_values, stored_keys, stored_values, kv_len):
    seq_count = queries.shape[0]
    cache_len = stored_keys.shape[1]
    kv_count = token_keys.shape[1] // HEAD_WIDTH
    query_group_width = queries.shape[1] // HEAD_WIDTH // kv_count
    query_head_rows = queries.reshape(seq_count, kv_count, query_group_width, HEAD_WIDTH)
    keys_from_cache = stored_keys.reshape(seq_count, cache_len, kv_count, HEAD_WIDTH)
    values_from_cache = stored_values.reshape(seq_count, cache_len, kv_count, HEAD_WIDTH)
    keys_latest = token_keys.reshape(seq_count, kv_count, HEAD_WIDTH)
    values_latest = token_values.astype(jnp.float32).reshape(seq_count, kv_count, HEAD_WIDTH)
    inv_root = 1.0 / math.sqrt(HEAD_WIDTH)
    cached_scores = (
        jnp.einsum(
            "bgqd,bpgd->bgqp", query_head_rows, keys_from_cache, preferred_element_type=jnp.float32
        )
        * inv_root
    )
    positions = lax.broadcasted_iota(jnp.int32, (seq_count, cache_len), 1)
    visible = positions < kv_len[:, None]
    cached_scores = jnp.where(visible[:, None, None, :], cached_scores, -jnp.inf)
    fresh_score = (
        jnp.einsum(
            "bgqd,bgd->bgq", query_head_rows, keys_latest, preferred_element_type=jnp.float32
        )
        * inv_root
    )
    highest = jnp.maximum(jnp.max(cached_scores, axis=-1), fresh_score)
    cached_exp = jnp.exp(cached_scores - highest[..., None])
    fresh_exp = jnp.exp(fresh_score - highest)
    totals = jnp.sum(cached_exp, axis=-1) + fresh_exp
    cached_prob = (cached_exp / totals[..., None]).astype(jnp.bfloat16)
    fresh_prob = lax.optimization_barrier((fresh_exp / totals).astype(jnp.bfloat16)).astype(
        jnp.float32
    )
    mixed = jnp.einsum(
        "bgqp,bpgd->bgqd", cached_prob, values_from_cache, preferred_element_type=jnp.float32
    )
    mixed = mixed + fresh_prob[..., None] * values_latest[:, :, None, :]
    return mixed.reshape(seq_count, -1).astype(jnp.bfloat16)


def on_device(
    queries,
    token_keys,
    token_values,
    stored_keys,
    stored_values,
    kv_len,
    residual,
    out_weight,
    norm_gain,
    expert_ids,
    route_weight,
    w_gate,
    w_up,
    w_down,
):
    attended = attend_local(queries, token_keys, token_values, stored_keys, stored_values, kv_len)
    column_groups = 8
    device_count = lax.axis_size(("expert", "replica"))
    seq_count, feature_total = attended.shape
    row_count, model_width = out_weight.shape
    feature_groups = device_count // column_groups
    feature_block = feature_total // feature_groups
    col_width = model_width // column_groups
    device_rank = lax.axis_index(("expert", "replica"))
    block_place = device_rank % column_groups
    slot_ids = jnp.arange(column_groups, dtype=jnp.int32)
    own_piece = lax.dynamic_slice_in_dim(out_weight, block_place * col_width, col_width, 1)
    empty_block = jnp.zeros((column_groups, row_count, col_width), out_weight.dtype)
    stacked = jnp.where((slot_ids == block_place)[:, None, None], own_piece[None], empty_block)
    for offset in range(1 - column_groups, column_groups):
        if offset != 0:
            target_place = (device_rank + offset) % column_groups
            sent_piece = lax.dynamic_slice_in_dim(
                out_weight, target_place * col_width, col_width, 1
            )
            arrived_piece = shifted(sent_piece, ("expert", "replica"), offset)
            stacked = jnp.where(
                (slot_ids == block_place - offset)[:, None, None], arrived_piece[None], stacked
            )
    weight_block = stacked.reshape(column_groups * row_count, col_width)
    repeated = jnp.repeat(
        attended.reshape(seq_count, feature_groups, feature_block), column_groups, axis=1
    )
    all_tokens = lax.all_to_all(
        repeated, ("expert", "replica"), split_axis=1, concat_axis=0, tiled=True
    )
    all_tokens = all_tokens.reshape(-1, feature_block)
    partial_cols = jnp.dot(all_tokens, weight_block, preferred_element_type=jnp.float32)
    partial_cols = partial_cols.reshape(-1, 1, col_width)
    came_back = lax.all_to_all(
        partial_cols.astype(jnp.bfloat16),
        ("expert", "replica"),
        split_axis=0,
        concat_axis=1,
        tiled=True,
    ).astype(partial_cols.dtype)
    projected = jnp.sum(
        came_back.reshape(seq_count, feature_groups, column_groups, col_width), axis=1
    ).reshape(seq_count, model_width)
    hidden_state = residual.astype(jnp.float32) + projected
    mean_square = jnp.mean(hidden_state * hidden_state, axis=-1, keepdims=True)
    normed = (hidden_state * lax.rsqrt(mean_square + 1e-06) * norm_gain.astype(jnp.float32)).astype(
        jnp.bfloat16
    )
    pair_tokens = gathered_copies(normed, "replica", 0)
    token_count, topk_count = expert_ids.shape
    expert_count = lax.axis_size("expert")
    capacity = max(2, -(-(token_count * topk_count) // expert_count))
    flat_ids = expert_ids.reshape(-1)
    row_total = flat_ids.shape[0]
    same_expert = flat_ids[:, None] == flat_ids[None, :]
    row_iota = lax.broadcasted_iota(jnp.int32, (row_total, row_total), 0)
    col_iota = lax.broadcasted_iota(jnp.int32, (row_total, row_total), 1)
    slot_ranks = jnp.sum(jnp.where(same_expert & (col_iota < row_iota), 1, 0), axis=1).astype(
        jnp.int32
    )
    slot_of = (flat_ids * capacity + slot_ranks).reshape(token_count, topk_count)
    slot_total = expert_count * capacity
    slot_iota = jnp.arange(slot_total, dtype=jnp.int32)
    slot_hits = slot_of[None, :, :] == slot_iota[:, None, None]
    pick_table = jnp.sum(slot_hits.astype(jnp.float32), axis=2).astype(jnp.bfloat16)
    outgoing = jnp.dot(pick_table, pair_tokens, preferred_element_type=jnp.float32).astype(
        jnp.bfloat16
    )
    outgoing = outgoing.reshape(expert_count, capacity, -1)
    mixing = route_weight / jnp.sum(route_weight, axis=1, keepdims=True)
    combine_rows = jnp.sum(jnp.where(slot_hits, mixing[None, :, :], 0.0), axis=2).T
    incoming = lax.all_to_all(outgoing, "expert", split_axis=0, concat_axis=0, tiled=True)
    model_width = incoming.shape[-1]
    lead_shape = incoming.shape[:2]
    slot_rows = incoming.reshape(-1, model_width)
    gate_act = jnp.dot(slot_rows, w_gate[0], preferred_element_type=jnp.float32)
    up_act = jnp.dot(slot_rows, w_up[0], preferred_element_type=jnp.float32)
    hidden_act = (jax.nn.silu(gate_act) * up_act).astype(jnp.bfloat16)
    partial_value = jnp.dot(hidden_act, w_down[0], preferred_element_type=jnp.float32).reshape(
        lead_shape + (model_width,)
    )
    arrived = lax.all_to_all(
        partial_value.astype(jnp.bfloat16), "expert", split_axis=0, concat_axis=0, tiled=True
    ).astype(partial_value.dtype)
    returned = arrived
    returned = returned.reshape(slot_total, -1)
    pair_moe = jnp.dot(combine_rows, returned, preferred_element_type=jnp.float32)
    moe_out = sent_and_summed(pair_moe.astype(jnp.bfloat16), "replica", 0)
    return (hidden_state + moe_out).astype(jnp.bfloat16)


def solution(mesh):
    in_specs = (
        P(("groups", "expert", "replica"), None),
        P(("groups", "expert", "replica"), None),
        P(("groups", "expert", "replica"), None),
        P(("groups", "expert", "replica"), None, None),
        P(("groups", "expert", "replica"), None, None),
        P(("groups", "expert", "replica")),
        P(("groups", "expert", "replica"), None),
        P(("expert", "replica"), None),
        P(),
        P(("groups", "expert"), None),
        P(("groups", "expert"), None),
        P("expert", None, "replica"),
        P("expert", None, "replica"),
        P("expert", "replica", None),
    )
    out_specs = P(("groups", "expert", "replica"), None)
    return jax.shard_map(
        on_device, mesh=mesh, in_specs=in_specs, out_specs=out_specs, check_vma=False
    )
```

profile of v0, /device:TPU:513, one launch (start us, length us, event | category | flops | bytes accessed | tf_op | source)
XLA Modules:
  0.0 251.0 jit_solution(15461882330532982091)
XLA Ops:
  0.0 0.9 iota_compare_fusion.2
  0.9 0.8 reshape.609
  1.7 0.7 reshape.602
  2.4 0.8 copy.40
  3.2 0.1 fusion.26
  3.3 1.7 fusion.25
  5.1 0.2 fusion.18
  5.3 1.5 fusion.13
  6.9 0.1 convert_element_type.79
  6.9 0.1 copy.31
  7.0 0.9 broadcast_in_dim.239
  7.9 28.1 %all-to-all-start = ((bf16[4,128,512]{2,0,1:T(4,128)(2,1)}), bf16[4,128,512]{2,0,1:T(4,128)(2,1)}, u32[]{:S(2)}, u32[]{:S(2)}) async-start(bf16[4,128,512]{2,0,1:T(4,128)(2,1)} %bitcast.68), calls=%async_computation | async-start | bytes 1048576 | tf_op jit(solution)/shard_map/all_to_all | solution.py:130
  36.3 2.2 constant_dynamic-slice_fusion.14
  38.5 7.6 %collective-permute-start = (bf16[64,512]{1,0:T(8,128)(2,1)}, bf16[64,512]{1,0:T(8,128)(2,1)S(1)}, u32[]{:S(2)}, u32[]{:S(2)}) collective-permute-start(bf16[64,512]{1,0:T(8,128)(2,1)} %get-tuple-element.7), channel_id=1, source_target_pairs={{0,7},{1,8},{2,9},{3,10},{4,11},{5,12},{6,13},{7,14},{8,15},{9,16}... | collective-permute-start | bytes 196616 | tf_op jit(solution)/shard_map/ppermute | solution.py:14
  46.1 1.3 collective-permute-start.12
  47.4 1.3 collective-permute-start.11
  48.7 1.3 collective-permute-start.10
  50.0 1.3 collective-permute-start.9
  51.5 1.3 collective-permute-start.8
  52.8 9.0 %collective-permute-done.12 = bf16[64,512]{1,0:T(8,128)(2,1)} collective-permute-done((bf16[64,512]{1,0:T(8,128)(2,1)}, bf16[64,512]{1,0:T(8,128)(2,1)}, u32[]{:S(2)}, u32[]{:S(2)}) %collective-permute-start.12) | collective-permute-done | bytes 65568 | tf_op jit(solution)/shard_map/ppermute | solution.py:14
  61.8 1.9 collective-permute-start.7
  63.7 3.7 %collective-permute-start.6 = (bf16[64,512]{1,0:T(8,128)(2,1)}, bf16[64,512]{1,0:T(8,128)(2,1)S(1)}, u32[]{:S(2)}, u32[]{:S(2)}) collective-permute-start(bf16[64,512]{1,0:T(8,128)(2,1)} %get-tuple-element.14), channel_id=1, source_target_pairs={{0,1},{1,2},{2,3},{3,4},{4,5},{5,6},{6,7},{7,8},{8,9},{9,10},{10,1... | collective-permute-start | bytes 196616 | tf_op jit(solution)/shard_map/ppermute | solution.py:14
  67.4 1.3 collective-permute-start.5
  68.8 2.7 %collective-permute-start.4 = (bf16[64,512]{1,0:T(8,128)(2,1)}, bf16[64,512]{1,0:T(8,128)(2,1)S(1)}, u32[]{:S(2)}, u32[]{:S(2)}) collective-permute-start(bf16[64,512]{1,0:T(8,128)(2,1)} %get-tuple-element.16), channel_id=1, source_target_pairs={{0,3},{1,4},{2,5},{3,6},{4,7},{5,8},{6,9},{7,10},{8,11},{9,12},{10... | collective-permute-start | bytes 196616 | tf_op jit(solution)/shard_map/ppermute | solution.py:14
  71.5 2.4 collective-permute-start.3
  74.0 8.8 %collective-permute-start.2 = (bf16[64,512]{1,0:T(8,128)(2,1)S(1)}, bf16[64,512]{1,0:T(8,128)(2,1)S(1)}, u32[]{:S(2)}, u32[]{:S(2)}) collective-permute-start(bf16[64,512]{1,0:T(8,128)(2,1)S(1)} %get-tuple-element.18), channel_id=1, source_target_pairs={{0,5},{1,6},{2,7},{3,8},{4,9},{5,10},{6,11},{7,12},{8,13},{9,14},{... | collective-permute-start | bytes 196616 | tf_op jit(solution)/shard_map/ppermute | solution.py:14
  82.8 4.9 %collective-permute-start.1 = (bf16[64,512]{1,0:T(8,128)(2,1)S(1)}, bf16[64,512]{1,0:T(8,128)(2,1)S(1)}, u32[]{:S(2)}, u32[]{:S(2)}) collective-permute-start(bf16[64,512]{1,0:T(8,128)(2,1)S(1)} %get-tuple-element.19), channel_id=1, source_target_pairs={{0,6},{1,7},{2,8},{3,9},{4,10},{5,11},{6,12},{7,13},{8,14},{9,15},... | collective-permute-start | bytes 196616 | tf_op jit(solution)/shard_map/ppermute | solution.py:14
  87.7 1.3 collective-permute-start.13
  89.1 8.8 %collective-permute-done.13 = bf16[64,512]{1,0:T(8,128)(2,1)S(1)} collective-permute-done((bf16[64,512]{1,0:T(8,128)(2,1)S(1)}, bf16[64,512]{1,0:T(8,128)(2,1)S(1)}, u32[]{:S(2)}, u32[]{:S(2)}) %collective-permute-start.13) | collective-permute-done | bytes 65568 | tf_op jit(solution)/shard_map/ppermute | solution.py:14
  97.8 2.5 select_select_fusion
  100.3 2.0 reshape.595
  102.3 2.4 fusion.5
  104.7 0.5 broadcast.557
  105.2 2.7 %reduce = bf16[512,512]{1,0:T(8,128)(2,1)} reduce(bf16[512,1,512]{2,0,1:T(8,128)(2,1)} %fusion.5, bf16[]{:T(256)} %broadcast.557), dimensions={1}, to_apply=%copy.32.reduce_sub_computation | reduce | bytes 1048578 | tf_op jit(solution)/shard_map/convert_element_type | solution.py:137
  108.0 2.2 reshape.610
  110.1 16.1 %all-to-all-start.1 = ((bf16[128,2,1024]{2,1,0:T(2,128)(2,1)}), bf16[128,2,1024]{2,1,0:T(2,128)(2,1)}, u32[]{:S(2)}, u32[]{:S(2)}) async-start(bf16[128,2,1024]{2,1,0:T(2,128)(2,1)} %reshape.610), calls=%async_computation.1 | async-start | bytes 1048576 | tf_op jit(solution)/shard_map/all_to_all | solution.py:136
  126.3 0.1 eq.224
  126.4 0.2 select_reduce_fusion.1
  126.5 0.1 reduce_sum.77
  126.7 0.1 reduce_sum.78
  126.8 0.1 broadcast_divide_fusion
  126.9 0.1 convert_reduce_fusion.1
  127.0 18.4 %all-to-all-done.1 = bf16[128,2,1024]{2,1,0:T(2,128)(2,1)} async-done(((bf16[128,2,1024]{2,1,0:T(2,128)(2,1)}), bf16[128,2,1024]{2,1,0:T(2,128)(2,1)}, u32[]{:S(2)}, u32[]{:S(2)}) %all-to-all-start.1) | async-done | bytes 524320 | tf_op jit(solution)/shard_map/all_to_all | solution.py:136
  145.4 4.3 %reshape.611 = bf16[512,1,512]{2,1,0:T(2,128)(2,1)} reshape(bf16[128,2,1024]{2,1,0:T(2,128)(2,1)} %all-to-all-done.1) | data formatting | bytes 1048576
  149.8 2.3 convert_bitcast_fusion
  152.1 0.3 copy.37
  152.3 0.1 bitcast_reduce_fusion
  152.5 0.1 multiply_reduce_fusion
  152.6 0.1 multiply_convert_fusion
  152.8 4.6 %all_to_all.44 = bf16[2,4,4096]{2,1,0:T(4,128)(2,1)S(1)} all-to-all(bf16[2,4,4096]{2,1,0:T(4,128)(2,1)S(1)} %broadcast_in_dim.275), channel_id=1, replica_groups=mesh['groups'=2,'expert'=64,'replica'=2] {'replica'}, dimensions={0} | all-to-all | bytes 131072 | tf_op jit(solution)/shard_map/all_to_all | solution.py:19
  157.4 1.5 convolution_convert_fusion.1
  158.9 2.5 %reshape.598 = bf16[64,2,4096]{2,1,0:T(2,128)(2,1)} reshape(bf16[128,4096]{1,0:T(8,128)(2,1)} %convolution_convert_fusion.1) | data formatting | bytes 2097152 | tf_op jit(solution)/shard_map/reshape | solution.py:171
  161.4 33.8 %all_to_all.45 = bf16[64,2,4096]{2,1,0:T(2,128)(2,1)} all-to-all(bf16[64,2,4096]{2,1,0:T(2,128)(2,1)} %reshape.598), channel_id=1, replica_groups=mesh['groups'=2,'expert'=64,'replica'=2] {'expert'}, dimensions={0} | all-to-all | bytes 2097152 | tf_op jit(solution)/shard_map/all_to_all | solution.py:174
  195.2 2.2 reshape.599
  197.5 3.1 %fusion.3 = f32[128,384]{1,0:T(8,128)S(1)} fusion(bf16[128,4096]{1,0:T(8,128)(2,1)} %reshape.599, bf16[1,4096,384]{2,1,0:T(8,128)(2,1)} %param.25), kind=kOutput, calls=%fused_computation.6 | convolution fusion | flops 402653184 | bytes 4390912 | tf_op jit(solution)/shard_map/dot_general | solution.py:178
  200.5 0.4 copy-done.6
  200.9 0.7 fusion.10
  201.7 0.7 convolution_convert_fusion
  202.4 1.1 copy.34
  203.5 35.5 %all_to_all.46 = bf16[64,2,4096]{2,1,0:T(2,128)(2,1)} all-to-all(bf16[64,2,4096]{2,1,0:T(2,128)(2,1)S(1)} %copy.34), channel_id=1, replica_groups=mesh['groups'=2,'expert'=64,'replica'=2] {'expert'}, dimensions={0} | all-to-all | bytes 2097152 | tf_op jit(solution)/shard_map/all_to_all | solution.py:184
  239.0 2.3 reshape.600
  241.3 1.5 fusion.27
  242.8 7.6 %all_to_all.47 = bf16[2,4,4096]{2,1,0:T(4,128)(2,1)S(1)} all-to-all(bf16[2,4,4096]{2,1,0:T(4,128)(2,1)S(1)} %reshape.601), channel_id=1, replica_groups=mesh['groups'=2,'expert'=64,'replica'=2] {'replica'}, dimensions={0} | all-to-all | bytes 131072 | tf_op jit(solution)/shard_map/all_to_all | solution.py:41
  250.4 0.6 add_convert_fusion
  (45 shorter events, 0.3 us)
Async XLA Ops:
  0.0 201.7 %copy-start = (bf16[1,384,4096]{2,1,0:T(8,128)(2,1)S(1)}, bf16[1,384,4096]{2,1,0:T(8,128)(2,1)}, u32[]{:S(2)}) copy-start(bf16[1,384,4096]{2,1,0:T(8,128)(2,1)} %param.27) | copy-start | bytes 9437188
  7.9 92.4 %all-to-all-start = ((bf16[4,128,512]{2,0,1:T(4,128)(2,1)}), bf16[4,128,512]{2,0,1:T(4,128)(2,1)}, u32[]{:S(2)}, u32[]{:S(2)}) async-start(bf16[4,128,512]{2,0,1:T(4,128)(2,1)} %bitcast.68), calls=%async_computation | async-start | bytes 1048576 | tf_op jit(solution)/shard_map/all_to_all | solution.py:130
  38.5 13.0 %collective-permute-start = (bf16[64,512]{1,0:T(8,128)(2,1)}, bf16[64,512]{1,0:T(8,128)(2,1)S(1)}, u32[]{:S(2)}, u32[]{:S(2)}) collective-permute-start(bf16[64,512]{1,0:T(8,128)(2,1)} %get-tuple-element.7), channel_id=1, source_target_pairs={{0,7},{1,8},{2,9},{3,10},{4,11},{5,12},{6,13},{7,14},{8,15},{9,16}... | collective-permute-start | bytes 196616 | tf_op jit(solution)/shard_map/ppermute | solution.py:14
  46.1 15.7 %collective-permute-start.12 = (bf16[64,512]{1,0:T(8,128)(2,1)}, bf16[64,512]{1,0:T(8,128)(2,1)}, u32[]{:S(2)}, u32[]{:S(2)}) collective-permute-start(bf16[64,512]{1,0:T(8,128)(2,1)} %get-tuple-element.8), channel_id=1, source_target_pairs={{6,0},{7,1},{8,2},{9,3},{10,4},{11,5},{12,6},{13,7},{14,8},{15,9},... | collective-permute-start | bytes 196616 | tf_op jit(solution)/shard_map/ppermute | solution.py:14
  47.4 16.3 %collective-permute-start.11 = (bf16[64,512]{1,0:T(8,128)(2,1)}, bf16[64,512]{1,0:T(8,128)(2,1)}, u32[]{:S(2)}, u32[]{:S(2)}) collective-permute-start(bf16[64,512]{1,0:T(8,128)(2,1)} %get-tuple-element.9), channel_id=1, source_target_pairs={{5,0},{6,1},{7,2},{8,3},{9,4},{10,5},{11,6},{12,7},{13,8},{14,9},{... | collective-permute-start | bytes 196616 | tf_op jit(solution)/shard_map/ppermute | solution.py:14
  48.7 18.7 %collective-permute-start.10 = (bf16[64,512]{1,0:T(8,128)(2,1)}, bf16[64,512]{1,0:T(8,128)(2,1)}, u32[]{:S(2)}, u32[]{:S(2)}) collective-permute-start(bf16[64,512]{1,0:T(8,128)(2,1)} %get-tuple-element.10), channel_id=1, source_target_pairs={{4,0},{5,1},{6,2},{7,3},{8,4},{9,5},{10,6},{11,7},{12,8},{13,9},{1... | collective-permute-start | bytes 196616 | tf_op jit(solution)/shard_map/ppermute | solution.py:14
  50.0 18.7 %collective-permute-start.9 = (bf16[64,512]{1,0:T(8,128)(2,1)}, bf16[64,512]{1,0:T(8,128)(2,1)}, u32[]{:S(2)}, u32[]{:S(2)}) collective-permute-start(bf16[64,512]{1,0:T(8,128)(2,1)} %get-tuple-element.11), channel_id=1, source_target_pairs={{3,0},{4,1},{5,2},{6,3},{7,4},{8,5},{9,6},{10,7},{11,8},{12,9},{13... | collective-permute-start | bytes 196616 | tf_op jit(solution)/shard_map/ppermute | solution.py:14
  51.5 20.0 %collective-permute-start.8 = (bf16[64,512]{1,0:T(8,128)(2,1)}, bf16[64,512]{1,0:T(8,128)(2,1)S(1)}, u32[]{:S(2)}, u32[]{:S(2)}) collective-permute-start(bf16[64,512]{1,0:T(8,128)(2,1)} %get-tuple-element.12), channel_id=1, source_target_pairs={{2,0},{3,1},{4,2},{5,3},{6,4},{7,5},{8,6},{9,7},{10,8},{11,9},{12,... | collective-permute-start | bytes 196616 | tf_op jit(solution)/shard_map/ppermute | solution.py:14
  61.8 12.2 %collective-permute-start.7 = (bf16[64,512]{1,0:T(8,128)(2,1)}, bf16[64,512]{1,0:T(8,128)(2,1)S(1)}, u32[]{:S(2)}, u32[]{:S(2)}) collective-permute-start(bf16[64,512]{1,0:T(8,128)(2,1)} %get-tuple-element.13), channel_id=1, source_target_pairs={{1,0},{2,1},{3,2},{4,3},{5,4},{6,5},{7,6},{8,7},{9,8},{10,9},{11,1... | collective-permute-start | bytes 196616 | tf_op jit(solution)/shard_map/ppermute | solution.py:14
  63.7 19.0 %collective-permute-start.6 = (bf16[64,512]{1,0:T(8,128)(2,1)}, bf16[64,512]{1,0:T(8,128)(2,1)S(1)}, u32[]{:S(2)}, u32[]{:S(2)}) collective-permute-start(bf16[64,512]{1,0:T(8,128)(2,1)} %get-tuple-element.14), channel_id=1, source_target_pairs={{0,1},{1,2},{2,3},{3,4},{4,5},{5,6},{6,7},{7,8},{8,9},{9,10},{10,1... | collective-permute-start | bytes 196616 | tf_op jit(solution)/shard_map/ppermute | solution.py:14
  67.4 20.2 %collective-permute-start.5 = (bf16[64,512]{1,0:T(8,128)(2,1)}, bf16[64,512]{1,0:T(8,128)(2,1)S(1)}, u32[]{:S(2)}, u32[]{:S(2)}) collective-permute-start(bf16[64,512]{1,0:T(8,128)(2,1)} %get-tuple-element.15), channel_id=1, source_target_pairs={{0,2},{1,3},{2,4},{3,5},{4,6},{5,7},{6,8},{7,9},{8,10},{9,11},{10,... | collective-permute-start | bytes 196616 | tf_op jit(solution)/shard_map/ppermute | solution.py:14
  68.8 20.2 %collective-permute-start.4 = (bf16[64,512]{1,0:T(8,128)(2,1)}, bf16[64,512]{1,0:T(8,128)(2,1)S(1)}, u32[]{:S(2)}, u32[]{:S(2)}) collective-permute-start(bf16[64,512]{1,0:T(8,128)(2,1)} %get-tuple-element.16), channel_id=1, source_target_pairs={{0,3},{1,4},{2,5},{3,6},{4,7},{5,8},{6,9},{7,10},{8,11},{9,12},{10... | collective-permute-start | bytes 196616 | tf_op jit(solution)/shard_map/ppermute | solution.py:14
  71.5 17.5 %collective-permute-start.3 = (bf16[64,512]{1,0:T(8,128)(2,1)S(1)}, bf16[64,512]{1,0:T(8,128)(2,1)S(1)}, u32[]{:S(2)}, u32[]{:S(2)}) collective-permute-start(bf16[64,512]{1,0:T(8,128)(2,1)S(1)} %get-tuple-element.17), channel_id=1, source_target_pairs={{0,4},{1,5},{2,6},{3,7},{4,8},{5,9},{6,10},{7,11},{8,12},{9,13},{1... | collective-permute-start | bytes 196616 | tf_op jit(solution)/shard_map/ppermute | solution.py:14
  74.0 15.1 %collective-permute-start.2 = (bf16[64,512]{1,0:T(8,128)(2,1)S(1)}, bf16[64,512]{1,0:T(8,128)(2,1)S(1)}, u32[]{:S(2)}, u32[]{:S(2)}) collective-permute-start(bf16[64,512]{1,0:T(8,128)(2,1)S(1)} %get-tuple-element.18), channel_id=1, source_target_pairs={{0,5},{1,6},{2,7},{3,8},{4,9},{5,10},{6,11},{7,12},{8,13},{9,14},{... | collective-permute-start | bytes 196616 | tf_op jit(solution)/shard_map/ppermute | solution.py:14
  82.8 6.3 %collective-permute-start.1 = (bf16[64,512]{1,0:T(8,128)(2,1)S(1)}, bf16[64,512]{1,0:T(8,128)(2,1)S(1)}, u32[]{:S(2)}, u32[]{:S(2)}) collective-permute-start(bf16[64,512]{1,0:T(8,128)(2,1)S(1)} %get-tuple-element.19), channel_id=1, source_target_pairs={{0,6},{1,7},{2,8},{3,9},{4,10},{5,11},{6,12},{7,13},{8,14},{9,15},... | collective-permute-start | bytes 196616 | tf_op jit(solution)/shard_map/ppermute | solution.py:14
  87.7 10.2 %collective-permute-start.13 = (bf16[64,512]{1,0:T(8,128)(2,1)S(1)}, bf16[64,512]{1,0:T(8,128)(2,1)S(1)}, u32[]{:S(2)}, u32[]{:S(2)}) collective-permute-start(bf16[64,512]{1,0:T(8,128)(2,1)S(1)} %get-tuple-element.21), channel_id=1, source_target_pairs={{7,0},{8,1},{9,2},{10,3},{11,4},{12,5},{13,6},{14,7},{15,8},{16,9}... | collective-permute-start | bytes 196616 | tf_op jit(solution)/shard_map/ppermute | solution.py:14
  100.3 26.0 %copy-start.3 = (s32[8,8]{1,0:T(8,128)S(1)}, s32[8,8]{1,0:T(8,128)}, u32[]{:S(2)}) copy-start(s32[8,8]{1,0:T(8,128)} %param.23) | copy-start | bytes 772
  100.3 26.3 %copy-start.5 = (bf16[4096]{0:T(1024)(128)(2,1)S(1)}, bf16[4096]{0:T(1024)(128)(2,1)}, u32[]{:S(2)}) copy-start(bf16[4096]{0:T(1024)(128)(2,1)} %param.22) | copy-start | bytes 24580
  100.3 26.4 %copy-start.4 = (f32[8,8]{1,0:T(8,128)S(1)}, f32[8,8]{1,0:T(8,128)}, u32[]{:S(2)}) copy-start(f32[8,8]{1,0:T(8,128)} %param.24) | copy-start | bytes 772
  110.1 35.3 %all-to-all-start.1 = ((bf16[128,2,1024]{2,1,0:T(2,128)(2,1)}), bf16[128,2,1024]{2,1,0:T(2,128)(2,1)}, u32[]{:S(2)}, u32[]{:S(2)}) async-start(bf16[128,2,1024]{2,1,0:T(2,128)(2,1)} %reshape.610), calls=%async_computation.1 | async-start | bytes 1048576 | tf_op jit(solution)/shard_map/all_to_all | solution.py:136
  127.0 25.5 %copy-start.2 = (bf16[4,4096]{1,0:T(4,128)(2,1)S(1)}, bf16[4,4096]{1,0:T(4,128)(2,1)}, u32[]{:S(2)}) copy-start(bf16[4,4096]{1,0:T(4,128)(2,1)} %param.20) | copy-start | bytes 98308
  197.5 3.1 %copy-start.1 = (bf16[128,4096]{1,0:T(8,128)(2,1)S(1)}, bf16[128,4096]{1,0:T(8,128)(2,1)}, u32[]{:S(2)}) copy-start(bf16[128,4096]{1,0:T(8,128)(2,1)} %reshape.599) | copy-start | bytes 3145732
  197.5 3.5 %copy-start.6 = (bf16[1,4096,384]{2,1,0:T(8,128)(2,1)S(1)}, bf16[1,4096,384]{2,1,0:T(8,128)(2,1)}, u32[]{:S(2)}) copy-start(bf16[1,4096,384]{2,1,0:T(8,128)(2,1)} %param.26) | copy-start | bytes 9437188
where the time goes:
time: 253 us; the launch traced here: 251 us
  starting transfers between devices  85.4 us (34%)
  blocking collectives  81.4 us (32%)
  waiting for transfers between devices  36.3 us (14%)
  local copies, waits for them, and re-layouts  23.7 us (9%)
  matrix products  13.3 us (5%)
  other arithmetic  10.2 us (4%)
    ppermute x14, starting transfers between devices, shifted(): return lax.ppermute(block, axis, route)  41.2 us
    all_to_all x1, blocking collectives, on_device(): lax.all_to_all(partial_value.astype(jnp.bfloat16), 'expert', split_axis=0...  35.5 us
    all_to_all x1, blocking collectives, on_device(): lax.all_to_all(outgoing, 'expert', split_axis=0, concat_axis=0, tiled=True)  33.8 us
    all_to_all x1, starting transfers between devices, on_device(): lax.all_to_all(repeated, ('expert', 'replica'), split_axis=1, concat_axis...  28.1 us
    all_to_all x1, waiting for transfers between devices, on_device(): lax.all_to_all(partial_cols.astype(jnp.bfloat16), ('expert', 'replica'),...  18.4 us
    ppermute x14, waiting for transfers between devices, shifted(): return lax.ppermute(block, axis, route)  17.8 us
    all_to_all x1, starting transfers between devices, on_device(): lax.all_to_all(partial_cols.astype(jnp.bfloat16), ('expert', 'replica'),...  16.1 us
    unnamed x18, local copies, waits for them, and re-layouts  8.05 us
  transfers between devices with their start and end apart: 16, of which 3 were waited for; matrix products, arithmetic and copies ran while one was open for 2% of the time, Pallas kernels for 0%

commit v1 on v0

v1 whole, which is shorter than its diff:
```python
import math

import jax
import jax.numpy as jnp
from jax import lax
from jax.sharding import PartitionSpec as P

HEAD_WIDTH = 128
CHIPS, CORES = "expert", "replica"


def swapped(x):
    return lax.ppermute(x, CORES, [(0, 1), (1, 0)])


def by_core(core, own, other, axis):
    return jnp.where(
        core == 0,
        jnp.concatenate([own, other], axis=axis),
        jnp.concatenate([other, own], axis=axis),
    )


def attend_local(queries, token_keys, token_values, stored_keys, stored_values, kv_len):
    seq_count = queries.shape[0]
    cache_len = stored_keys.shape[1]
    kv_count = token_keys.shape[1] // HEAD_WIDTH
    query_group_width = queries.shape[1] // HEAD_WIDTH // kv_count
    query_head_rows = queries.reshape(seq_count, kv_count, query_group_width, HEAD_WIDTH)
    keys_from_cache = stored_keys.reshape(seq_count, cache_len, kv_count, HEAD_WIDTH)
    values_from_cache = stored_values.reshape(seq_count, cache_len, kv_count, HEAD_WIDTH)
    keys_latest = token_keys.reshape(seq_count, kv_count, HEAD_WIDTH)
    values_latest = token_values.astype(jnp.float32).reshape(seq_count, kv_count, HEAD_WIDTH)
    inv_root = 1.0 / math.sqrt(HEAD_WIDTH)
    cached_scores = (
        jnp.einsum(
            "bgqd,bpgd->bgqp", query_head_rows, keys_from_cache, preferred_element_type=jnp.float32
        )
        * inv_root
    )
    positions = lax.broadcasted_iota(jnp.int32, (seq_count, cache_len), 1)
    visible = positions < kv_len[:, None]
    cached_scores = jnp.where(visible[:, None, None, :], cached_scores, -jnp.inf)
    fresh_score = (
        jnp.einsum(
            "bgqd,bgd->bgq", query_head_rows, keys_latest, preferred_element_type=jnp.float32
        )
        * inv_root
    )
    highest = jnp.maximum(jnp.max(cached_scores, axis=-1), fresh_score)
    cached_exp = jnp.exp(cached_scores - highest[..., None])
    fresh_exp = jnp.exp(fresh_score - highest)
    totals = jnp.sum(cached_exp, axis=-1) + fresh_exp
    cached_prob = (cached_exp / totals[..., None]).astype(jnp.bfloat16)
    fresh_prob = lax.optimization_barrier((fresh_exp / totals).astype(jnp.bfloat16)).astype(
        jnp.float32
    )
    mixed = jnp.einsum(
        "bgqp,bpgd->bgqd", cached_prob, values_from_cache, preferred_element_type=jnp.float32
    )
    mixed = mixed + fresh_prob[..., None] * values_latest[:, :, None, :]
    return mixed.reshape(seq_count, -1).astype(jnp.bfloat16)


def quad_step(side, dx, dy):
    return [
        (x * side + y, (x ^ dx) * side + (y ^ dy)) for x in range(side) for y in range(side)
    ]


def on_device(
    queries,
    token_keys,
    token_values,
    stored_keys,
    stored_values,
    kv_len,
    residual,
    out_weight,
    norm_gain,
    expert_ids,
    route_weight,
    w_gate,
    w_up,
    w_down,
):
    chips = lax.axis_size(CHIPS)
    side = math.isqrt(chips)
    chip = lax.axis_index(CHIPS)
    core = lax.axis_index(CORES)
    place = (chip // side) % 2 * 2 + chip % 2
    row_count, model_width = out_weight.shape
    seq_count, feature_total = queries.shape
    col_width = model_width // 4
    half_width = model_width // 2
    pieces = []
    for d in range(4):
        piece = lax.dynamic_slice_in_dim(out_weight, (place ^ d) * col_width, col_width, 1)
        pieces.append(lax.ppermute(piece, CHIPS, quad_step(side, d // 2, d % 2)) if d else piece)
    weight_own = jnp.stack(pieces)
    weight_other = swapped(weight_own)

    attended = attend_local(queries, token_keys, token_values, stored_keys, stored_values, kv_len)
    attended = attended.reshape(seq_count, chips, 2, row_count)
    attended = jnp.where(core == 0, attended, attended[:, :, ::-1])
    squares = attended.reshape(seq_count, side // 2, 2, side // 2, 2, 2, row_count)
    squares = squares.transpose(1, 3, 0, 5, 2, 4, 6)
    by_place = jnp.stack(
        [
            jnp.stack(
                [squares[:, :, :, :, (p ^ d) // 2, (p ^ d) % 2] for d in range(4)], axis=4
            )
            for p in range(4)
        ]
    )
    by_place = by_place.reshape(2, 2, side // 2, side // 2, seq_count, -1)
    outgoing = by_place.transpose(2, 0, 3, 1, 4, 5).reshape(chips, seq_count, -1)
    tokens = lax.all_to_all(outgoing, CHIPS, 0, 0, tiled=True)
    weight = jnp.concatenate(
        [weight_own.reshape(-1, col_width), weight_other.reshape(-1, col_width)]
    )
    partial_cols = jnp.dot(
        tokens.reshape(chips * seq_count, -1), weight, preferred_element_type=jnp.float32
    ).astype(jnp.bfloat16)
    came_back = lax.all_to_all(
        partial_cols.reshape(chips, seq_count, col_width), CHIPS, 0, 0, tiled=True
    )
    came_back = came_back.reshape(side // 2, 2, side // 2, 2, seq_count, col_width)
    projected = jnp.sum(came_back.astype(jnp.float32), axis=(0, 2))
    projected = projected.transpose(2, 0, 1, 3).reshape(seq_count, model_width)
    hidden_state = residual.astype(jnp.float32) + projected
    mean_square = jnp.mean(hidden_state * hidden_state, axis=-1, keepdims=True)
    normed = (hidden_state * lax.rsqrt(mean_square + 1e-06) * norm_gain.astype(jnp.float32)).astype(
        jnp.bfloat16
    )

    token_count, topk_count = expert_ids.shape
    capacity = 2
    flat_ids = expert_ids.reshape(-1)
    row_total = flat_ids.shape[0]
    same_expert = flat_ids[:, None] == flat_ids[None, :]
    row_iota = lax.broadcasted_iota(jnp.int32, (row_total, row_total), 0)
    col_iota = lax.broadcasted_iota(jnp.int32, (row_total, row_total), 1)
    slot_ranks = jnp.sum(jnp.where(same_expert & (col_iota < row_iota), 1, 0), axis=1).astype(
        jnp.int32
    )
    slot_of = (flat_ids * capacity + slot_ranks).reshape(token_count, topk_count)
    mixing = route_weight / jnp.sum(route_weight, axis=1, keepdims=True)
    slot_of = jnp.where(core == 0, slot_of, jnp.roll(slot_of, -seq_count, axis=0))
    mixing = jnp.where(core == 0, mixing, jnp.roll(mixing, -seq_count, axis=0))
    slot_total = chips * capacity
    slot_iota = jnp.arange(slot_total, dtype=jnp.int32)
    slot_hits = slot_of[None, :, :] == slot_iota[:, None, None]
    pick_table = jnp.sum(slot_hits.astype(jnp.float32), axis=2).astype(jnp.bfloat16)
    combine_rows = jnp.sum(jnp.where(slot_hits, mixing[None, :, :], 0.0), axis=2).T

    normed_halves = normed.reshape(seq_count, 2, half_width)
    kept = jnp.where(core == 0, normed_halves[:, 0], normed_halves[:, 1])
    given = jnp.where(core == 0, normed_halves[:, 1], normed_halves[:, 0])
    pair_tokens = jnp.concatenate([kept, swapped(given)])
    dispatched = jnp.dot(pick_table, pair_tokens, preferred_element_type=jnp.float32).astype(
        jnp.bfloat16
    )
    incoming = lax.all_to_all(
        dispatched.reshape(chips, capacity, half_width), CHIPS, 0, 0, tiled=True
    )
    incoming = incoming.reshape(slot_total, half_width)
    slot_rows = by_core(core, incoming, swapped(incoming), 1)
    gate_act = jnp.dot(slot_rows, w_gate[0], preferred_element_type=jnp.float32)
    up_act = jnp.dot(slot_rows, w_up[0], preferred_element_type=jnp.float32)
    hidden_act = (jax.nn.silu(gate_act) * up_act).astype(jnp.bfloat16)
    partial_out = jnp.dot(hidden_act, w_down[0], preferred_element_type=jnp.float32)
    out_halves = partial_out.reshape(slot_total, 2, half_width)
    out_kept = jnp.where(core == 0, out_halves[:, 0], out_halves[:, 1])
    out_given = jnp.where(core == 0, out_halves[:, 1], out_halves[:, 0]).astype(jnp.bfloat16)
    expert_out = (out_kept + swapped(out_given).astype(jnp.float32)).astype(jnp.bfloat16)
    returned = lax.all_to_all(
        expert_out.reshape(chips, capacity, half_width), CHIPS, 0, 0, tiled=True
    ).reshape(slot_total, half_width)
    pair_moe = jnp.dot(
        combine_rows, returned.astype(jnp.float32), preferred_element_type=jnp.float32
    )
    moe_out = by_core(core, pair_moe[:seq_count], swapped(pair_moe[seq_count:]), 1)
    return (hidden_state + moe_out).astype(jnp.bfloat16)


def solution(mesh):
    in_specs = (
        P(("groups", "expert", "replica"), None),
        P(("groups", "expert", "replica"), None),
        P(("groups", "expert", "replica"), None),
        P(("groups", "expert", "replica"), None, None),
        P(("groups", "expert", "replica"), None, None),
        P(("groups", "expert", "replica")),
        P(("groups", "expert", "replica"), None),
        P(("expert", "replica"), None),
        P(),
        P(("groups", "expert"), None),
        P(("groups", "expert"), None),
        P("expert", None, "replica"),
        P("expert", None, "replica"),
        P("expert", "replica", None),
    )
    out_specs = P(("groups", "expert", "replica"), None)
    return jax.shard_map(
        on_device, mesh=mesh, in_specs=in_specs, out_specs=out_specs, check_vma=False
    )
```

time: 253 us -> 179 us (0.71)
  starting transfers between devices: 85.4 us -> 47.5 us
  blocking collectives: 81.4 us -> 46.5 us
  waiting for transfers between devices: 36.3 us -> 29.3 us
  matrix products: 13.3 us -> 17.8 us
    all_to_all x4 -> x2, blocking collectives: 81.4 us -> 46.5 us  [the longest x1 23.3 us: on_device(): lax.all_to_all(expert_out.reshape(chips, capacity, half_width), CHIPS, 0,...]
    all_to_all x2, starting transfers between devices: 44.2 us -> 13.6 us  [the longest x1 7.11 us: on_device(): lax.all_to_all(partial_cols.reshape(chips, seq_count, col_width), CHIPS,...]
    ppermute x14 -> x8, waiting for transfers between devices: 17.8 us -> 3.5 us  [the longest x5 3.49 us: swapped(): return lax.ppermute(x, CORES, [(0, 1), (1, 0)])]
    all_to_all x2, waiting for transfers between devices: 18.4 us -> 25.8 us  [the longest x1 14.1 us: on_device(): lax.all_to_all(partial_cols.reshape(chips, seq_count, col_width), CHIPS,...]
    ppermute x14 -> x8, starting transfers between devices: 41.2 us -> 33.9 us  [the longest x5 29.3 us: swapped(): return lax.ppermute(x, CORES, [(0, 1), (1, 0)])]
    unnamed x18 -> x11, local copies, waits for them, and re-layouts: 8.05 us -> 0.87 us
    dot_general x1, matrix products: 0.71 us -> 5.64 us  [on_device(): jnp.dot(hidden_act, w_down[0], preferred_element_type=jnp.float32)]
    dot_general x1, local copies, waits for them, and re-layouts: 0.04 us -> 4.65 us  [on_device(): jnp.dot(hidden_act, w_down[0], preferred_element_type=jnp.float32)]
  transfers between devices with their start and end apart: 16 -> 10, of which waited for: 3 -> 5; matrix products, arithmetic and copies ran while one was open for 2% -> 11% of each run, Pallas kernels for 0% -> 0%
where the time goes in v1:
time: 179 us; the launch traced here: 178 us
  starting transfers between devices  47.5 us (27%)
  blocking collectives  46.5 us (26%)
  waiting for transfers between devices  29.3 us (16%)
  local copies, waits for them, and re-layouts  25.2 us (14%)
  matrix products  17.8 us (10%)
  other arithmetic  11.4 us (6%)
    ppermute x5, starting transfers between devices, swapped(): return lax.ppermute(x, CORES, [(0, 1), (1, 0)])  29.3 us
    all_to_all x1, blocking collectives, on_device(): lax.all_to_all(expert_out.reshape(chips, capacity, half_width), CHIPS, 0,...  23.3 us
    all_to_all x1, blocking collectives, on_device(): lax.all_to_all(dispatched.reshape(chips, capacity, half_width), CHIPS, 0,...  23.2 us
    all_to_all x1, waiting for transfers between devices, on_device(): lax.all_to_all(partial_cols.reshape(chips, seq_count, col_width), CHIPS,...  14.1 us
    all_to_all x1, waiting for transfers between devices, on_device(): tokens = lax.all_to_all(outgoing, CHIPS, 0, 0, tiled=True)  11.7 us
    all_to_all x1, starting transfers between devices, on_device(): lax.all_to_all(partial_cols.reshape(chips, seq_count, col_width), CHIPS,...  7.11 us
    all_to_all x1, starting transfers between devices, on_device(): tokens = lax.all_to_all(outgoing, CHIPS, 0, 0, tiled=True)  6.47 us
    dot_general x1, matrix products, on_device(): jnp.dot(hidden_act, w_down[0], preferred_element_type=jnp.float32)  5.64 us
  transfers between devices with their start and end apart: 10, of which 5 were waited for; matrix products, arithmetic and copies ran while one was open for 11% of the time, Pallas kernels for 0%

profile of v1, /device:TPU:513, one launch (start us, length us, event | category | flops | bytes accessed | tf_op | source)
XLA Modules:
  0.0 178.0 jit_solution(6365688490689803709)
XLA Ops:
  0.0 2.0 %dynamic-slice_bitcast_fusion = (bf16[1,64,1024]{2,1,0:T(8,128)(2,1)S(1)}, bf16[64,1024]{1,0:T(8,128)(2,1)}, bf16[64,1024]{1,0:T(8,128)(2,1)}, bf16[64,1024]{1,0:T(8,128)(2,1)S(1)}) fusion(bf16[64,4096]{1,0:T(8,128)(2,1)} %param.21, s32[]{:T(128)S(6)} %select_n.117, s32[]{:T(128)S(6)} %select_n.118, s32[]{:T(128)S(6)} %select_n.120, s32[]{:T(128)S(6)} %select_n.119), kind=kLoop, calls=%fused_computation.36 | loop fusion | bytes 1048592 | tf_op jit(solution)/shard_map/stack | solution.py:100
  2.0 3.3 %collective-permute-start = (bf16[64,1024]{1,0:T(8,128)(2,1)}, bf16[64,1024]{1,0:T(8,128)(2,1)}, u32[]{:S(2)}, u32[]{:S(2)}) collective-permute-start(bf16[64,1024]{1,0:T(8,128)(2,1)} %get-tuple-element.8), channel_id=1, source_target_pairs={{0,2},{2,0},{4,6},{6,4},{8,10},{10,8},{12,14},{14,12},{16,18},{18,... | collective-permute-start | bytes 393224 | tf_op jit(solution)/shard_map/ppermute | solution.py:99
  5.3 1.1 collective-permute-start.2
  6.4 0.3 collective-permute-start.1
  6.7 0.7 iota_compare_fusion.2
  7.4 0.7 reshape.134
  8.1 0.7 reshape.128
  8.8 0.8 copy.75
  9.6 0.1 fusion.46
  9.8 1.7 fusion.45
  11.5 0.2 fusion.15
  11.7 2.2 %fusion.5 = bf16[4,4,16,128]{3,2,1,0:T(8,128)(2,1)} fusion(f32[4,4,16,256]{3,2,1,0:T(8,128)S(1)} %get-tuple-element.30, f32[4,4,16]{2,1,0:T(4,128)S(1)} %get-tuple-element.24, f32[4,4,16]{2,1,0:T(4,128)S(1)} %multiply_maximum_fusion, f32[4,4,128]{2,1,0:T(4,128)S(1)} %reshape.128, f32[4,4,16]{2,1,0:T(4,128)S(1)} %convert_element_type.66, ...), kind=kOutput, calls=%fused_computation.9 | convolution fusion | flops 17072128 | bytes 1387520 | tf_op jit(solution)/shard_map/bgqp,bpgd->bgqd/dot_general | solution.py:58
  13.9 0.9 convert_element_type.68
  14.9 0.2 fusion.41
  15.1 0.1 copy_bitcast_fusion
  15.2 0.1 copy_bitcast_fusion.2
  15.3 0.6 maximum_bitcast_fusion
  15.9 0.0 collective-permute-done
  15.9 0.0 collective-permute-done.1
  15.9 1.9 %pad_maximum_fusion.1 = bf16[4,64,1024]{2,1,0:T(8,128)(2,1)} fusion(bf16[1,64,1024]{2,1,0:T(8,128)(2,1)} %bitcast.18, bf16[1,64,1024]{2,1,0:T(8,128)(2,1)} %bitcast.17, bf16[1,64,1024]{2,1,0:T(8,128)(2,1)} %bitcast.16, bf16[1,64,1024]{2,1,0:T(8,128)(2,1)S(1)} %get-tuple-element.7), kind=kLoop, calls=%fused_computation.24 | loop fusion | flops 786432 | bytes 1048576 | tf_op jit(solution)/shard_map/stack | solution.py:100
  17.8 19.2 %collective-permute-start.3 = (bf16[4,64,1024]{2,1,0:T(8,128)(2,1)}, bf16[4,64,1024]{2,1,0:T(8,128)(2,1)}, u32[]{:S(2)}, u32[]{:S(2)}) collective-permute-start(bf16[4,64,1024]{2,1,0:T(8,128)(2,1)} %pad_maximum_fusion.1), channel_id=1, source_target_pairs={{0,1},{1,0},{2,3},{3,2},{4,5},{5,4},{6,7},{7,6},{8,9},{9,8},{10,11... | collective-permute-start | bytes 1572872 | tf_op jit(solution)/shard_map/ppermute | solution.py:13
  37.0 1.1 pad_maximum_fusion
  38.1 1.5 copy.65
  39.6 1.4 reshape.116
  40.9 0.8 copy.66
  41.7 6.5 %all-to-all-start = ((bf16[64,4,512]{2,1,0:T(4,128)(2,1)}), bf16[64,4,512]{2,1,0:T(4,128)(2,1)S(1)}, u32[]{:S(2)}, u32[]{:S(2)}) async-start(bf16[64,4,512]{2,1,0:T(4,128)(2,1)} %bitcast.103), calls=%async_computation | async-start | bytes 524288 | tf_op jit(solution)/shard_map/all_to_all | solution.py:118
  48.2 0.1 eq.20
  48.3 0.2 select_reduce_fusion.1
  48.5 0.1 reduce_sum.68
  48.6 0.1 reduce_sum.69
  48.7 0.1 broadcast_divide_fusion
  48.8 11.7 %all-to-all-done = bf16[64,4,512]{2,1,0:T(4,128)(2,1)S(1)} async-done(((bf16[64,4,512]{2,1,0:T(4,128)(2,1)}), bf16[64,4,512]{2,1,0:T(4,128)(2,1)S(1)}, u32[]{:S(2)}, u32[]{:S(2)}) %all-to-all-start) | async-done | bytes 262176 | tf_op jit(solution)/shard_map/all_to_all | solution.py:118
  60.5 0.8 reshape.118
  61.3 0.0 collective-permute-done.3
  61.3 2.5 %convolution_convert_fusion.1 = bf16[256,1024]{1,0:T(8,128)(2,1)} fusion(bf16[256,512]{1,0:T(8,128)(2,1)} %reshape.118, bf16[256,1024]{1,0:T(8,128)(2,1)} %bitcast.20, bf16[256,1024]{1,0:T(8,128)(2,1)} %bitcast.19), kind=kOutput, calls=%fused_computation.5 | convolution fusion | flops 270794752 | bytes 1835008 | tf_op jit(solution)/shard_map/dot_general | solution.py:122
  63.8 2.0 %reshape.121 = bf16[64,4,1024]{2,1,0:T(4,128)(2,1)} reshape(bf16[256,1024]{1,0:T(8,128)(2,1)} %convolution_convert_fusion.1) | data formatting | bytes 1048576 | tf_op jit(solution)/shard_map/reshape | solution.py:126
  65.8 7.1 %all-to-all-start.1 = ((bf16[64,4,1024]{2,1,0:T(4,128)(2,1)}), bf16[64,4,1024]{2,1,0:T(4,128)(2,1)}, u32[]{:S(2)}, u32[]{:S(2)}) async-start(bf16[64,4,1024]{2,1,0:T(4,128)(2,1)} %reshape.121), calls=%async_computation.1 | async-start | bytes 1048576 | tf_op jit(solution)/shard_map/all_to_all | solution.py:125
  73.0 0.1 maximum_select_fusion.10
  73.1 14.1 %all-to-all-done.1 = bf16[64,4,1024]{2,1,0:T(4,128)(2,1)} async-done(((bf16[64,4,1024]{2,1,0:T(4,128)(2,1)}), bf16[64,4,1024]{2,1,0:T(4,128)(2,1)}, u32[]{:S(2)}, u32[]{:S(2)}) %all-to-all-start.1) | async-done | bytes 524320 | tf_op jit(solution)/shard_map/all_to_all | solution.py:125
  87.1 1.3 convert_reduce_fusion
  88.4 0.1 multiply_reduce_fusion
  88.6 0.1 multiply_convert_fusion.1
  88.7 5.0 %collective-permute-start.4 = (bf16[4,2048]{1,0:T(4,128)(2,1)S(1)}, bf16[4,2048]{1,0:T(4,128)(2,1)S(1)}, u32[]{:S(2)}, u32[]{:S(2)}) collective-permute-start(bf16[4,2048]{1,0:T(4,128)(2,1)S(1)} %get-tuple-element.22), channel_id=1, source_target_pairs={{0,1},{1,0},{2,3},{3,2},{4,5},{5,4},{6,7},{7,6},{8,9},{9,8},{10,11... | collective-permute-start | bytes 49160 | tf_op jit(solution)/shard_map/ppermute | solution.py:13
  93.7 0.1 convert_reduce_fusion.1
  93.8 0.7 collective-permute-done.4
  94.6 1.1 convolution_convert_fusion
  95.7 2.2 %reshape.124 = bf16[64,2,2048]{2,1,0:T(2,128)(2,1)} reshape(bf16[128,2048]{1,0:T(8,128)(2,1)} %convolution_convert_fusion) | data formatting | bytes 1048576 | tf_op jit(solution)/shard_map/reshape | solution.py:165
  97.9 23.2 %all_to_all.20 = bf16[64,2,2048]{2,1,0:T(2,128)(2,1)} all-to-all(bf16[64,2,2048]{2,1,0:T(2,128)(2,1)} %reshape.124), channel_id=1, replica_groups=mesh['groups'=2,'expert'=64,'replica'=2] {'expert'}, dimensions={0} | all-to-all | bytes 1048576 | tf_op jit(solution)/shard_map/all_to_all | solution.py:164
  121.1 2.0 %reshape.125 = bf16[128,2048]{1,0:T(8,128)(2,1)} reshape(bf16[64,2,2048]{2,1,0:T(2,128)(2,1)} %all_to_all.20) | data formatting | bytes 1048576 | tf_op jit(solution)/shard_map/reshape | solution.py:167
  123.1 2.3 %collective-permute-start.5 = (bf16[128,2048]{1,0:T(8,128)(2,1)}, bf16[128,2048]{1,0:T(8,128)(2,1)}, u32[]{:S(2)}, u32[]{:S(2)}) collective-permute-start(bf16[128,2048]{1,0:T(8,128)(2,1)} %reshape.125), channel_id=1, source_target_pairs={{0,1},{1,0},{2,3},{3,2},{4,5},{5,4},{6,7},{7,6},{8,9},{9,8},{10,11... | collective-permute-start | bytes 1572872 | tf_op jit(solution)/shard_map/ppermute | solution.py:13
  125.4 4.7 %copy.72 = bf16[4096,384]{1,0:T(8,128)(2,1)} copy(bf16[4096,384]{0,1:T(8,128)(2,1)} %bitcast.96) | data formatting | bytes 6291456 | tf_op jit(solution)/shard_map/dot_general | solution.py:172
  130.0 3.3 %fusion.2 = f32[128,384]{1,0:T(8,128)S(1)} fusion(bf16[1,4096,384]{2,1,0:T(8,128)(2,1)} %param.25, bf16[128,2048]{1,0:T(8,128)(2,1)} %collective-permute-done.5, bf16[128,2048]{1,0:T(8,128)(2,1)} %reshape.125, pred[]{:T(512)S(6)} %eq.19), kind=kOutput, calls=%fused_computation.2 | convolution fusion | flops 407371776 | bytes 4390913 | tf_op jit(solution)/shard_map/dot_general | solution.py:169
  133.3 5.6 %fusion.22 = f32[128,2,2048]{2,0,1:T(8,128)} fusion(bf16[2,2048,384]{2,1,0:T(8,128)(2,1)} %bitcast.97, bf16[1,4096,384]{2,1,0:T(8,128)(2,1)S(1)} %copy-done, bf16[128,2048]{1,0:T(8,128)(2,1)} %collective-permute-done.5, bf16[128,2048]{1,0:T(8,128)(2,1)} %reshape.125, pred[]{:T(512)S(6)} %eq.19, f32[128,384]{1,0:T(8,128)S(1)} %fusion.2), kind=kOutput, calls=%fused_computation.31 | convolution fusion | flops 810319872 | bytes 9633793 | tf_op jit(solution)/shard_map/dot_general | solution.py:172
  138.9 1.6 fusion.14
  140.6 0.1 collective-permute-start.6
  140.7 1.9 %collective-permute-done.6 = bf16[128,2048]{1,0:T(8,128)(2,1)S(1)} collective-permute-done((bf16[128,2048]{1,0:T(8,128)(2,1)S(1)}, bf16[128,2048]{1,0:T(8,128)(2,1)S(1)}, u32[]{:S(2)}, u32[]{:S(2)}) %collective-permute-start.6) | collective-permute-done | bytes 524320 | tf_op jit(solution)/shard_map/ppermute | solution.py:13
  142.6 2.5 %fusion.13 = bf16[128,2048]{1,0:T(8,128)(2,1)} fusion(bf16[128,2048]{1,0:T(8,128)(2,1)S(1)} %collective-permute-done.6, f32[128,2,2048]{2,0,1:T(8,128)} %fusion.22, pred[]{:T(512)S(6)} %eq.19), kind=kLoop, calls=%fused_computation.20 | loop fusion | flops 1048576 | bytes 3145729 | tf_op jit(solution)/shard_map/convert_element_type | solution.py:176
  145.1 2.2 %reshape.126 = bf16[64,2,2048]{2,1,0:T(2,128)(2,1)} reshape(bf16[128,2048]{1,0:T(8,128)(2,1)} %fusion.13) | data formatting | bytes 1048576 | tf_op jit(solution)/shard_map/reshape | solution.py:178
  147.3 23.3 %all_to_all.21 = bf16[64,2,2048]{2,1,0:T(2,128)(2,1)} all-to-all(bf16[64,2,2048]{2,1,0:T(2,128)(2,1)} %reshape.126), channel_id=1, replica_groups=mesh['groups'=2,'expert'=64,'replica'=2] {'expert'}, dimensions={0} | all-to-all | bytes 1048576 | tf_op jit(solution)/shard_map/all_to_all | solution.py:177
  170.6 2.0 %reshape.127 = bf16[128,2048]{1,0:T(8,128)(2,1)} reshape(bf16[64,2,2048]{2,1,0:T(2,128)(2,1)} %all_to_all.21) | data formatting | bytes 1048576 | tf_op jit(solution)/shard_map/reshape | solution.py:179
  172.6 1.2 fusion.47
  173.9 2.6 %collective-permute-start.7 = (f32[4,2048]{1,0:T(4,128)S(1)}, f32[4,2048]{1,0:T(4,128)S(1)}, u32[]{:S(2)}, u32[]{:S(2)}) collective-permute-start(f32[4,2048]{1,0:T(4,128)S(1)} %get-tuple-element.20), channel_id=1, source_target_pairs={{0,1},{1,0},{2,3},{3,2},{4,5},{5,4},{6,7},{7,6},{8,9},{9,8},{10,11... | collective-permute-start | bytes 98312 | tf_op jit(solution)/shard_map/ppermute | solution.py:13
  176.5 0.9 collective-permute-done.7
  177.3 0.6 fusion.28
  (25 shorter events, 0.2 us)
Async XLA Ops:
  0.0 133.3 %copy-start = (bf16[1,4096,384]{2,1,0:T(8,128)(2,1)S(1)}, bf16[1,4096,384]{2,1,0:T(8,128)(2,1)}, u32[]{:S(2)}) copy-start(bf16[1,4096,384]{2,1,0:T(8,128)(2,1)} %param.26) | copy-start | bytes 9437188
  2.0 13.9 %collective-permute-start = (bf16[64,1024]{1,0:T(8,128)(2,1)}, bf16[64,1024]{1,0:T(8,128)(2,1)}, u32[]{:S(2)}, u32[]{:S(2)}) collective-permute-start(bf16[64,1024]{1,0:T(8,128)(2,1)} %get-tuple-element.8), channel_id=1, source_target_pairs={{0,2},{2,0},{4,6},{6,4},{8,10},{10,8},{12,14},{14,12},{16,18},{18,... | collective-permute-start | bytes 393224 | tf_op jit(solution)/shard_map/ppermute | solution.py:99
  5.3 10.6 %collective-permute-start.2 = (bf16[64,1024]{1,0:T(8,128)(2,1)}, bf16[64,1024]{1,0:T(8,128)(2,1)}, u32[]{:S(2)}, u32[]{:S(2)}) collective-permute-start(bf16[64,1024]{1,0:T(8,128)(2,1)} %get-tuple-element.9), channel_id=1, source_target_pairs={{0,18},{2,16},{4,22},{6,20},{8,26},{10,24},{12,30},{14,28},{16,2},... | collective-permute-start | bytes 393224 | tf_op jit(solution)/shard_map/ppermute | solution.py:99
  6.4 9.5 %collective-permute-start.1 = (bf16[64,1024]{1,0:T(8,128)(2,1)S(1)}, bf16[64,1024]{1,0:T(8,128)(2,1)}, u32[]{:S(2)}, u32[]{:S(2)}) collective-permute-start(bf16[64,1024]{1,0:T(8,128)(2,1)S(1)} %get-tuple-element.10), channel_id=1, source_target_pairs={{0,16},{2,18},{4,20},{6,22},{8,24},{10,26},{12,28},{14,30},{16,0},... | collective-permute-start | bytes 393224 | tf_op jit(solution)/shard_map/ppermute | solution.py:99
  17.8 30.4 %copy-start.3 = (s32[8,8]{1,0:T(8,128)S(1)}, s32[8,8]{1,0:T(8,128)}, u32[]{:S(2)}) copy-start(s32[8,8]{1,0:T(8,128)} %param.23) | copy-start | bytes 772
  17.8 30.8 %copy-start.4 = (bf16[4096]{0:T(1024)(128)(2,1)S(1)}, bf16[4096]{0:T(1024)(128)(2,1)}, u32[]{:S(2)}) copy-start(bf16[4096]{0:T(1024)(128)(2,1)} %param.22) | copy-start | bytes 24580
  17.8 30.8 %copy-start.2 = (f32[8,8]{1,0:T(8,128)S(1)}, f32[8,8]{1,0:T(8,128)}, u32[]{:S(2)}) copy-start(f32[8,8]{1,0:T(8,128)} %param.24) | copy-start | bytes 772
  17.8 43.5 %collective-permute-start.3 = (bf16[4,64,1024]{2,1,0:T(8,128)(2,1)}, bf16[4,64,1024]{2,1,0:T(8,128)(2,1)}, u32[]{:S(2)}, u32[]{:S(2)}) collective-permute-start(bf16[4,64,1024]{2,1,0:T(8,128)(2,1)} %pad_maximum_fusion.1), channel_id=1, source_target_pairs={{0,1},{1,0},{2,3},{3,2},{4,5},{5,4},{6,7},{7,6},{8,9},{9,8},{10,11... | collective-permute-start | bytes 1572872 | tf_op jit(solution)/shard_map/ppermute | solution.py:13
  41.7 18.8 %all-to-all-start = ((bf16[64,4,512]{2,1,0:T(4,128)(2,1)}), bf16[64,4,512]{2,1,0:T(4,128)(2,1)S(1)}, u32[]{:S(2)}, u32[]{:S(2)}) async-start(bf16[64,4,512]{2,1,0:T(4,128)(2,1)} %bitcast.103), calls=%async_computation | async-start | bytes 524288 | tf_op jit(solution)/shard_map/all_to_all | solution.py:118
  61.3 27.1 %copy-start.1 = (bf16[4,4096]{1,0:T(4,128)(2,1)S(1)}, bf16[4,4096]{1,0:T(4,128)(2,1)}, u32[]{:S(2)}) copy-start(bf16[4,4096]{1,0:T(4,128)(2,1)} %param.20) | copy-start | bytes 98308
  65.8 21.3 %all-to-all-start.1 = ((bf16[64,4,1024]{2,1,0:T(4,128)(2,1)}), bf16[64,4,1024]{2,1,0:T(4,128)(2,1)}, u32[]{:S(2)}, u32[]{:S(2)}) async-start(bf16[64,4,1024]{2,1,0:T(4,128)(2,1)} %reshape.121), calls=%async_computation.1 | async-start | bytes 1048576 | tf_op jit(solution)/shard_map/all_to_all | solution.py:125
  88.7 5.9 %collective-permute-start.4 = (bf16[4,2048]{1,0:T(4,128)(2,1)S(1)}, bf16[4,2048]{1,0:T(4,128)(2,1)S(1)}, u32[]{:S(2)}, u32[]{:S(2)}) collective-permute-start(bf16[4,2048]{1,0:T(4,128)(2,1)S(1)} %get-tuple-element.22), channel_id=1, source_target_pairs={{0,1},{1,0},{2,3},{3,2},{4,5},{5,4},{6,7},{7,6},{8,9},{9,8},{10,11... | collective-permute-start | bytes 49160 | tf_op jit(solution)/shard_map/ppermute | solution.py:13
  123.1 6.9 %collective-permute-start.5 = (bf16[128,2048]{1,0:T(8,128)(2,1)}, bf16[128,2048]{1,0:T(8,128)(2,1)}, u32[]{:S(2)}, u32[]{:S(2)}) collective-permute-start(bf16[128,2048]{1,0:T(8,128)(2,1)} %reshape.125), channel_id=1, source_target_pairs={{0,1},{1,0},{2,3},{3,2},{4,5},{5,4},{6,7},{7,6},{8,9},{9,8},{10,11... | collective-permute-start | bytes 1572872 | tf_op jit(solution)/shard_map/ppermute | solution.py:13
  140.6 2.0 %collective-permute-start.6 = (bf16[128,2048]{1,0:T(8,128)(2,1)S(1)}, bf16[128,2048]{1,0:T(8,128)(2,1)S(1)}, u32[]{:S(2)}, u32[]{:S(2)}) collective-permute-start(bf16[128,2048]{1,0:T(8,128)(2,1)S(1)} %fusion.14), channel_id=1, source_target_pairs={{0,1},{1,0},{2,3},{3,2},{4,5},{5,4},{6,7},{7,6},{8,9},{9,8},{10,11... | collective-permute-start | bytes 1572872 | tf_op jit(solution)/shard_map/ppermute | solution.py:13
  173.9 3.5 %collective-permute-start.7 = (f32[4,2048]{1,0:T(4,128)S(1)}, f32[4,2048]{1,0:T(4,128)S(1)}, u32[]{:S(2)}, u32[]{:S(2)}) collective-permute-start(f32[4,2048]{1,0:T(4,128)S(1)} %get-tuple-element.20), channel_id=1, source_target_pairs={{0,1},{1,0},{2,3},{3,2},{4,5},{5,4},{6,7},{7,6},{8,9},{9,8},{10,11... | collective-permute-start | bytes 98312 | tf_op jit(solution)/shard_map/ppermute | solution.py:13

commit v2 on v1

v2 whole, which is shorter than its diff:
```python
import math

import jax
import jax.numpy as jnp
from jax import lax
from jax.experimental import pallas as pl
from jax.experimental.pallas import tpu as pltpu
from jax.sharding import PartitionSpec as P

HEAD_WIDTH = 128
CHIPS, CORES = "expert", "replica"
F32, BF16 = jnp.float32, jnp.bfloat16
IN_VMEM = pl.BlockSpec(memory_space=pltpu.VMEM)
IN_SMEM = pl.BlockSpec(memory_space=pltpu.SMEM)
IN_HBM = pl.BlockSpec(memory_space=pltpu.HBM)


def swapped(x):
    return lax.ppermute(x, CORES, [(0, 1), (1, 0)])


def quad_step(side, dx, dy):
    return [
        (x * side + y, (x ^ dx) * side + (y ^ dy)) for x in range(side) for y in range(side)
    ]


MIB = 1 << 20


def in_hbm(x):
    return pltpu.with_memory_space_constraint(x, pltpu.HBM)


def in_vmem(x):
    return pltpu.with_memory_space_constraint(x, pltpu.VMEM)


def kernel_call(body, name, outs, in_specs, limit, scratch=()):
    return pl.pallas_call(
        body,
        name=name,
        out_shape=outs,
        in_specs=in_specs,
        out_specs=jax.tree.map(lambda _: IN_VMEM, outs),
        scratch_shapes=list(scratch),
        compiler_params=pltpu.CompilerParams(vmem_limit_bytes=limit * MIB),
    )


def shape(*dims, dtype=BF16):
    return jax.ShapeDtypeStruct(dims, dtype)


def attend_body(
    q_ref, tk_ref, tv_ref, len_ref, keys_hbm, values_hbm, out_ref, keys, values, rows, mixed, sems
):
    core = lax.axis_index(CORES)
    seq_count, cache_len, kv_width = keys_hbm.shape
    kv_count = kv_width // HEAD_WIDTH
    head_count = q_ref.shape[1] // HEAD_WIDTH
    group = head_count // kv_count
    side = group // 2
    copies = []
    for b in range(seq_count):
        pair = []
        for j, (source, target) in enumerate(((keys_hbm, keys), (values_hbm, values))):
            copy = pltpu.make_async_copy(source.at[b], target.at[b], sems.at[j, b])
            copy.start()
            pair.append(copy)
        copies.append(pair)
    for h in range(head_count):
        piece = q_ref[:, h * HEAD_WIDTH : (h + 1) * HEAD_WIDTH].astype(F32)
        rows[pl.ds(h, seq_count, stride=head_count), :] = piece
    inv_root = 1.0 / math.sqrt(HEAD_WIDTH)
    positions = lax.broadcasted_iota(jnp.int32, (group, cache_len), 1)
    for b in range(seq_count):
        for copy in copies[b]:
            copy.wait()
        visible = positions < len_ref[b]
        for g in range(kv_count):
            lanes = slice(g * HEAD_WIDTH, (g + 1) * HEAD_WIDTH)
            first = b * head_count + g * group
            query = rows[first : first + group, :]
            scores = lax.dot_general(
                query.astype(BF16),
                keys[b, :, lanes],
                (((1,), (1,)), ((), ())),
                preferred_element_type=F32,
            )
            scores = jnp.where(visible, scores * inv_root, -jnp.inf)
            fresh = jnp.sum(query * tk_ref[b : b + 1, lanes].astype(F32), axis=1, keepdims=True)
            fresh = fresh * inv_root
            highest = jnp.maximum(jnp.max(scores, axis=1, keepdims=True), fresh)
            cached_exp = jnp.exp(scores - highest)
            fresh_exp = jnp.exp(fresh - highest)
            totals = jnp.sum(cached_exp, axis=1, keepdims=True) + fresh_exp
            prob = (cached_exp / totals).astype(BF16)
            fresh_prob = (fresh_exp / totals).astype(BF16).astype(F32)
            out = jnp.dot(prob, values[b, :, lanes], preferred_element_type=F32)
            out = out + fresh_prob * tv_ref[b : b + 1, lanes].astype(F32)
            out = pltpu.roll(out, core * (HEAD_WIDTH // 2), 1)
            for a in range(2):
                start = g * group * seq_count + a * seq_count + b
                mixed[pl.ds(start, side, stride=2 * seq_count), :] = out[a * side : (a + 1) * side]
    tile = 2 * seq_count
    for g in range(kv_count):
        for y in range(side):
            for part, source in enumerate((y, y ^ 1)):
                at = (g * side + source) * tile
                near = mixed[at : at + tile, :]
                far = pltpu.roll(near, seq_count, 0)
                lanes = slice(part * HEAD_WIDTH, (part + 1) * HEAD_WIDTH)
                out_ref[2 * g * side + y, :, lanes] = near.astype(BF16)
                out_ref[(2 * g + 1) * side + y, :, lanes] = far.astype(BF16)


def attend(queries, token_keys, token_values, kv_len, stored_keys, stored_values):
    seq_count, feature_total = queries.shape
    heads = feature_total // HEAD_WIDTH
    return kernel_call(
        attend_body,
        "attend",
        shape(heads, 2 * seq_count, 2 * HEAD_WIDTH),
        [IN_VMEM, IN_VMEM, IN_VMEM, IN_SMEM, IN_HBM, IN_HBM],
        8,
        [
            pltpu.VMEM(stored_keys.shape, BF16),
            pltpu.VMEM(stored_values.shape, BF16),
            pltpu.VMEM((seq_count * heads, HEAD_WIDTH), F32),
            pltpu.VMEM((seq_count * heads, HEAD_WIDTH), F32),
            pltpu.SemaphoreType.DMA((2, seq_count)),
        ],
    )(
        in_hbm(queries),
        in_hbm(token_keys),
        in_hbm(token_values),
        kv_len,
        in_hbm(stored_keys),
        in_hbm(stored_values),
    )


def project_body(x_ref, *refs):
    own, other, out_ref = refs[:4], refs[4:8], refs[8]
    chips, tile, width = x_ref.shape
    cols = own[0].shape[1]
    half = cols // 2
    weights = [
        jnp.concatenate([own[d][...], other[d][...], own[d + 1][...], other[d + 1][...]])
        for d in (0, 2)
    ]
    step = 16
    low = lax.broadcasted_iota(jnp.int32, (step, tile, half), 1) < tile // 2
    for at in range(0, chips, step):
        x = x_ref[at : at + step].reshape(step * tile, width)
        near = jnp.dot(x, weights[0], preferred_element_type=F32).reshape(step, tile, cols)
        far = jnp.dot(x, weights[1], preferred_element_type=F32).reshape(step, tile, cols)
        kept = jnp.where(low, near[:, :, :half], far[:, :, half:])
        moved = jnp.where(low, near[:, :, half:], far[:, :, :half])
        moved = pltpu.roll(moved, tile // 2, 1)
        out_ref[at : at + step] = (kept + moved).astype(BF16)


def project(x, own, other):
    cols = own[0].shape[1]
    return kernel_call(
        project_body, "project", shape(x.shape[0], x.shape[1], cols // 2), [IN_VMEM] * 9, 12
    )(x, *map(in_hbm, own), *map(in_hbm, other))


def settle_body(x_ref, residual_ref, gain_ref, hidden_ref, kept_ref, given_ref, normed):
    core = lax.axis_index(CORES)
    chips, tile, half = x_ref.shape
    side = math.isqrt(chips)
    blocks = 4
    seq_count = tile // 2
    width = residual_ref.shape[1]

    def rows_of(ref, k):
        low, high = (ref[:, (2 * k + q) * half : (2 * k + q + 1) * half].astype(F32) for q in (0, 1))
        low, high = (jnp.broadcast_to(v, (seq_count, half)) for v in (low, high))
        return jnp.concatenate([low, high])

    square = jnp.zeros((tile, 1), F32)
    for k in range(blocks):
        total = rows_of(residual_ref, k)
        for x in range(k // 2, side, 2):
            for y in range(k % 2, side, 2):
                total = total + x_ref[x * side + y].astype(F32)
        hidden_ref[k] = total
        square = square + jnp.sum(total * total, axis=1, keepdims=True)
    square = jnp.broadcast_to(square, (tile, HEAD_WIDTH))
    square = square + pltpu.roll(square, seq_count, 0)
    scale = lax.rsqrt(square[:, :1] / width + 1e-06)
    for k in range(blocks):
        normed[k] = (hidden_ref[k] * scale * rows_of(gain_ref, k)).astype(BF16)
    kept_ref[...] = normed[pl.ds(core * 2, 2)]
    given_ref[...] = normed[pl.ds(2 - core * 2, 2)]


def settle(x, residual, gain):
    tile, half = x.shape[1:]
    return kernel_call(
        settle_body,
        "settle",
        (shape(4, tile, half, dtype=F32), shape(2, tile, half), shape(2, tile, half)),
        [IN_VMEM] * 3,
        6,
        [pltpu.VMEM((4, tile, half), BF16)],
    )(x, residual, gain)


def route_body(ids_ref, weight_ref, pick_ref, mix_ref):
    core = lax.axis_index(CORES)
    tokens, topk = ids_ref.shape
    seq_count = tokens // 2
    lanes = pick_ref.shape[1]
    lane = lax.broadcasted_iota(jnp.int32, (tokens, lanes), 1)
    row = lax.broadcasted_iota(jnp.int32, (tokens, lanes), 0)
    weight = weight_ref[...]
    mixing = weight / jnp.sum(weight, axis=1, keepdims=True)
    ids = ids_ref[...]
    hit = jnp.zeros((tokens, lanes), F32)
    share = jnp.zeros((tokens, lanes), F32)
    for k in range(topk):
        same = ids[:, k : k + 1] == lane // 8
        hit = jnp.where(same, 1.0, hit)
        share = jnp.where(same, mixing[:, k : k + 1], share)
    rank = jnp.zeros((tokens, lanes), F32)
    for t in range(tokens - 1):
        rank = rank + jnp.where(row > t, jnp.broadcast_to(hit[t : t + 1], (tokens, lanes)), 0.0)
    taken = jnp.where(rank == (lane % 2).astype(F32), hit, 0.0)
    share = share * taken
    own_low = (row < seq_count) == (core == 0)
    quarter = lane // 2 % 4
    for src in range(2):
        low = own_low if src == 0 else jnp.logical_not(own_low)
        chosen = jnp.where(low, taken, pltpu.roll(taken, seq_count, 0))
        shares = jnp.where(low, share, pltpu.roll(share, seq_count, 0))
        for kk in range(2):
            at = (src * 2 + kk) * tokens
            mine = quarter == kk * 2 + row // seq_count
            pick_ref[at : at + tokens, :] = jnp.where(mine, chosen, 0.0).astype(BF16)
            value = jnp.where(mine, shares, 0.0)
            coarse = value.astype(BF16)
            mix_ref[at : at + tokens, :] = coarse
            mix_ref[4 * tokens + at : 5 * tokens + at, :] = (value - coarse.astype(F32)).astype(BF16)


def route(expert_ids, route_weight, chips):
    tokens = expert_ids.shape[0]
    return kernel_call(
        route_body,
        "route",
        (shape(4 * tokens, 8 * chips), shape(8 * tokens, 8 * chips)),
        [IN_VMEM] * 2,
        4,
    )(expert_ids, route_weight)


def dispatch_body(kept_ref, other_ref, pick_ref, out_ref):
    pieces = [r[...].reshape(-1, r.shape[2]) for r in (kept_ref, other_ref)]
    rows = lax.dot_general(
        pick_ref[...],
        jnp.concatenate(pieces),
        (((0,), (0,)), ((), ())),
        preferred_element_type=F32,
    )
    out_ref[...] = rows.astype(BF16).reshape(out_ref.shape)


def dispatch(kept, other, pick):
    tile, half = kept.shape[1:]
    return kernel_call(
        dispatch_body, "dispatch", shape(pick.shape[1] // tile, tile, half), [IN_VMEM] * 3, 6
    )(kept, other, pick)


def slot_order(size, back=False):
    sorted_row = lax.broadcasted_iota(jnp.int32, (size, size), 1 if back else 0)
    row = lax.broadcasted_iota(jnp.int32, (size, size), 0 if back else 1)
    slot = sorted_row % (size // 4)
    quarter = sorted_row // (size // 4)
    return jnp.where(row == slot // 2 * 8 + quarter * 2 + slot % 2, 1.0, 0.0).astype(BF16)


def gate_body(own_ref, other_ref, gate_ref, up_ref, out_ref):
    core = lax.axis_index(CORES)
    chips, tile, part = own_ref.shape
    size = 256
    groups = chips * tile // size
    order = slot_order(size)
    slots = size // 4
    gate = up = None
    for half, ref in ((core, own_ref), (1 - core, other_ref)):
        sorted_rows = []
        for g in range(groups):
            rows = ref[g * size // tile : (g + 1) * size // tile].reshape(size, part)
            sorted_rows.append(jnp.dot(order, rows, preferred_element_type=F32).astype(BF16))
        for p in range(4):
            x = jnp.concatenate([r[p * slots : (p + 1) * slots] for r in sorted_rows])
            at = pl.multiple_of(half * (4 * part) + p * part, part)
            gate_part = jnp.dot(x, gate_ref[0, pl.ds(at, part), :], preferred_element_type=F32)
            up_part = jnp.dot(x, up_ref[0, pl.ds(at, part), :], preferred_element_type=F32)
            gate = gate_part if gate is None else gate + gate_part
            up = up_part if up is None else up + up_part
    out_ref[...] = (gate / (1.0 + jnp.exp(-gate)) * up).astype(BF16)


def gate_up(own, other, w_gate, w_up):
    chips, tile, _ = own.shape
    return kernel_call(
        gate_body, "gate_up", shape(chips * tile // 4, w_gate.shape[2]), [IN_VMEM] * 4, 16
    )(own, other, in_hbm(w_gate), in_hbm(w_up))


def down_body(own_ref, other_ref, down_ref, moved_ref, out_ref):
    core = lax.axis_index(CORES)
    chips, tile, part = out_ref.shape
    size = 256
    groups = chips * tile // size
    order = slot_order(size, back=True)
    slots = size // 4
    own, other = own_ref[...], other_ref[...]
    quarters = []
    for p in range(4):
        at = pl.multiple_of(core * (4 * part) + p * part, part)
        value = jnp.dot(own, down_ref[0, :, pl.ds(at, part)], preferred_element_type=F32)
        value = value + jnp.dot(
            other, moved_ref[:, p * part : (p + 1) * part], preferred_element_type=F32
        )
        quarters.append(value.astype(BF16))
    for g in range(groups):
        rows = jnp.concatenate([v[g * slots : (g + 1) * slots] for v in quarters])
        rows = jnp.dot(order, rows, preferred_element_type=F32).astype(BF16)
        out_ref[g * size // tile : (g + 1) * size // tile] = rows.reshape(size // tile, tile, part)


def down(own, other, w_down, moved_down, tile):
    slots = own.shape[0]
    part = moved_down.shape[1] // 4
    return kernel_call(
        down_body, "down", shape(slots * 4 // tile, tile, part), [IN_VMEM] * 4, 14
    )(own, other, w_down, moved_down)


def combine_body(x_ref, mix_ref, own_ref, other_ref):
    x = x_ref[...].reshape(-1, x_ref.shape[2])
    rows = jnp.dot(mix_ref[...], x, preferred_element_type=F32)
    count = rows.shape[0] // 2
    rows = rows[:count] + rows[count:]
    own_ref[...] = rows[: count // 2].reshape(own_ref.shape)
    other_ref[...] = rows[count // 2 :].reshape(other_ref.shape)


def combine(x, mix):
    out = shape(2, x.shape[1], x.shape[2], dtype=F32)
    return kernel_call(combine_body, "combine", (out, out), [IN_VMEM] * 2, 4)(x, mix)


def finish_body(hidden_ref, own_ref, other_ref, out_ref, total):
    core = lax.axis_index(CORES)
    blocks, tile, half = hidden_ref.shape
    total[pl.ds(core * 2, 2)] = own_ref[...]
    total[pl.ds(2 - core * 2, 2)] = other_ref[...]
    for k in range(blocks):
        value = (hidden_ref[k] + total[k]).astype(BF16)
        for q in range(2):
            at = (2 * k + q) * half
            out_ref[:, at : at + half] = value[q * tile // 2 : (q + 1) * tile // 2]


def finish(hidden, own, other):
    blocks, tile, half = hidden.shape
    return kernel_call(
        finish_body,
        "finish",
        shape(tile // 2, 2 * blocks * half),
        [IN_VMEM] * 3,
        2,
        [pltpu.VMEM(hidden.shape, F32)],
    )(hidden, own, other)


def on_device(
    queries,
    token_keys,
    token_values,
    stored_keys,
    stored_values,
    kv_len,
    residual,
    out_weight,
    norm_gain,
    expert_ids,
    route_weight,
    w_gate,
    w_up,
    w_down,
):
    chips = lax.axis_size(CHIPS)
    side = math.isqrt(chips)
    chip = lax.axis_index(CHIPS)
    core = lax.axis_index(CORES)
    place = chip // side % 2 * 2 + chip % 2
    model_width = out_weight.shape[1]
    col_width = model_width // 4
    half_width = model_width // 2

    outgoing = attend(queries, token_keys, token_values, kv_len, stored_keys, stored_values)
    tokens = lax.all_to_all(outgoing, CHIPS, 0, 0, tiled=True)
    own = []
    for d in range(4):
        piece = lax.dynamic_slice_in_dim(out_weight, (place ^ d) * col_width, col_width, 1)
        own.append(lax.ppermute(piece, CHIPS, quad_step(side, d // 2, d % 2)) if d else piece)
    other = [swapped(piece) for piece in own]
    given_down = lax.dynamic_slice_in_dim(w_down[0], (1 - core) * half_width, half_width, 1)
    moved_down = swapped(given_down)
    pick, mix = route(expert_ids, route_weight, chips)

    came_back = lax.all_to_all(project(tokens, own, other), CHIPS, 0, 0, tiled=True)
    hidden, kept, given = settle(came_back, residual, norm_gain[None])
    incoming = lax.all_to_all(dispatch(kept, swapped(given), pick), CHIPS, 0, 0, tiled=True)
    act = gate_up(incoming, swapped(incoming), w_gate, w_up)
    expert_out = down(act, swapped(act), w_down, moved_down, incoming.shape[1])
    returned = lax.all_to_all(expert_out, CHIPS, 0, 0, tiled=True)
    moe_own, moe_given = combine(returned, mix)
    return finish(hidden, moe_own, swapped(moe_given))


def solution(mesh):
    in_specs = (
        P(("groups", "expert", "replica"), None),
        P(("groups", "expert", "replica"), None),
        P(("groups", "expert", "replica"), None),
        P(("groups", "expert", "replica"), None, None),
        P(("groups", "expert", "replica"), None, None),
        P(("groups", "expert", "replica")),
        P(("groups", "expert", "replica"), None),
        P(("expert", "replica"), None),
        P(),
        P(("groups", "expert"), None),
        P(("groups", "expert"), None),
        P("expert", None, "replica"),
        P("expert", None, "replica"),
        P("expert", "replica", None),
    )
    out_specs = P(("groups", "expert", "replica"), None)
    return jax.shard_map(
        on_device, mesh=mesh, in_specs=in_specs, out_specs=out_specs, check_vma=False
    )
```

time: 179 us -> 149 us (0.83)
  blocking collectives: 46.5 us -> 22.5 us
  Pallas kernels: 0 us -> 20.3 us
  local copies, waits for them, and re-layouts: 25.2 us -> 5.62 us
  matrix products: 17.8 us -> 0 us
  starting transfers between devices: 47.5 us -> 65 us
  other arithmetic: 11.4 us -> 0 us
  waiting for transfers between devices: 29.3 us -> 34.4 us
    all_to_all x2 -> x1, blocking collectives: 46.5 us -> 22.5 us  [on_device(): returned = lax.all_to_all(expert_out, CHIPS, 0, 0, tiled=True)]
    pallas_call x0 -> x9, Pallas kernels: none -> 20.3 us  [the longest x1 8.58 us: attend(): kernel_call(attend_body, 'attend', shape(heads, 2 * seq_count, 2 * HEAD_W...]
    dot_general x8 -> x0, matrix products: 17.8 us -> none  [the longest x1 5.64 us: on_device(): jnp.dot(hidden_act, w_down[0], preferred_element_type=jnp.float32)]
    all_to_all x1, starting transfers between devices: 6.47 us -> 21.8 us  [on_device(): tokens = lax.all_to_all(outgoing, CHIPS, 0, 0, tiled=True)]
    all_to_all x1 -> x2, waiting for transfers between devices: 14.1 us -> 29.3 us  [the longest x1 15.5 us: on_device(): lax.all_to_all(project(tokens, own, other), CHIPS, 0, 0, tiled=True)]
    reshape x8 -> x0, local copies, waits for them, and re-layouts: 13.3 us -> none  [the longest x1 2.17 us: on_device(): expert_out.reshape(chips, capacity, half_width)]
    all_to_all x1 -> x2, starting transfers between devices: 7.11 us -> 19.5 us  [the longest x1 12.2 us: on_device(): lax.all_to_all(project(tokens, own, other), CHIPS, 0, 0, tiled=True)]
    all_to_all x1, waiting for transfers between devices: 11.7 us -> 0.01 us  [on_device(): tokens = lax.all_to_all(outgoing, CHIPS, 0, 0, tiled=True)]
  transfers between devices with their start and end apart: 10 -> 15, of which waited for: 5 -> 7; matrix products, arithmetic and copies ran while one was open for 11% -> 2% of each run, Pallas kernels for 0% -> 3%
where the time goes in v2:
time: 149 us; the launch traced here: 148 us
  starting transfers between devices  65 us (44%)
  waiting for transfers between devices  34.4 us (23%)
  blocking collectives  22.5 us (15%)
  Pallas kernels  20.3 us (14%)
  local copies, waits for them, and re-layouts  5.62 us (4%)
    all_to_all x1, blocking collectives, on_device(): returned = lax.all_to_all(expert_out, CHIPS, 0, 0, tiled=True)  22.5 us
    all_to_all x1, starting transfers between devices, on_device(): tokens = lax.all_to_all(outgoing, CHIPS, 0, 0, tiled=True)  21.8 us
    ppermute x9, starting transfers between devices, swapped(): return lax.ppermute(x, CORES, [(0, 1), (1, 0)])  20.9 us
    all_to_all x1, waiting for transfers between devices, on_device(): lax.all_to_all(project(tokens, own, other), CHIPS, 0, 0, tiled=True)  15.5 us
    all_to_all x1, waiting for transfers between devices, on_device(): lax.all_to_all(dispatch(kept, swapped(given), pick), CHIPS, 0, 0, tiled=T...  13.9 us
    all_to_all x1, starting transfers between devices, on_device(): lax.all_to_all(project(tokens, own, other), CHIPS, 0, 0, tiled=True)  12.2 us
    pallas_call x1, Pallas kernels, attend(): kernel_call(attend_body, 'attend', shape(heads, 2 * seq_count, 2 * HEAD_W...  8.58 us
    all_to_all x1, starting transfers between devices, on_device(): lax.all_to_all(dispatch(kept, swapped(given), pick), CHIPS, 0, 0, tiled=T...  7.29 us
  transfers between devices with their start and end apart: 15, of which 7 were waited for; matrix products, arithmetic and copies ran while one was open for 2% of the time, Pallas kernels for 3%

profile of v2, /device:TPU:513, one launch (start us, length us, event | category | flops | bytes accessed | tf_op | source)
XLA Modules:
  0.0 148.0 jit_solution(15249862129654259431)
XLA Ops:
  0.0 0.7 copy-done.6
  0.7 8.6 %attend.1 = bf16[64,8,256]{2,1,0:T(8,128)(2,1)} custom-call(bf16[4,8192]{1,0:T(4,128)(2,1)} %q_ref.1, bf16[4,512]{1,0:T(4,128)(2,1)} %tk_ref.1, bf16[4,512]{1,0:T(4,128)(2,1)} %tv_ref.1, s32[4]{0:T(128)S(1)} %copy-done.6, bf16[4,256,512]{2,1,0:T(8,128)(2,1)} %keys_hbm.1, bf16[4,256,512]{2,1,0:T(8,128)(2,1)} %values_hbm.1), custom_call_target="tpu_custom_call" | custom-call | tf_op jit(solution)/shard_map/attend/pallas_call | solution.py:121
  9.3 0.0 copy-start.4
  9.3 0.0 copy-start.5
  9.3 21.8 %all-to-all-start = ((bf16[64,8,256]{2,1,0:T(8,128)(2,1)}), bf16[64,8,256]{2,1,0:T(8,128)(2,1)S(1)}, u32[]{:S(2)}, u32[]{:S(2)}) async-start(bf16[64,8,256]{2,1,0:T(8,128)(2,1)} %attend.1), calls=%async_computation | async-start | bytes 524288 | tf_op jit(solution)/shard_map/all_to_all | solution.py:412
  31.1 0.0 copy-start
  31.2 1.3 constant_dynamic-slice_fusion
  32.5 0.0 copy-start.7
  32.5 1.2 collective-permute-start.2
  33.6 0.3 collective-permute-start
  33.9 1.3 collective-permute-start.1
  35.2 5.9 %collective-permute-start.3 = (bf16[64,1024]{1,0:T(8,128)(2,1)S(1)}, bf16[64,1024]{1,0:T(8,128)(2,1)S(1)}, u32[]{:S(2)}, u32[]{:S(2)}) collective-permute-start(bf16[64,1024]{1,0:T(8,128)(2,1)S(1)} %get-tuple-element.21.refs_0_), channel_id=1, source_target_pairs={{0,1},{1,0},{2,3},{3,2},{4,5},{5,4},{6,7},{7,6},{8,9},{9,8},{10,11... | collective-permute-start | bytes 393224 | tf_op jit(solution)/shard_map/ppermute | solution.py:19
  41.2 0.0 collective-permute-done.2.refs_3_
  41.2 3.1 %collective-permute-start.6 = (bf16[64,1024]{1,0:T(8,128)(2,1)S(1)}, bf16[64,1024]{1,0:T(8,128)(2,1)S(1)}, u32[]{:S(2)}, u32[]{:S(2)}) collective-permute-start(bf16[64,1024]{1,0:T(8,128)(2,1)S(1)} %collective-permute-done.2.refs_3_), channel_id=1, source_target_pairs={{0,1},{1,0},{2,3},{3,2},{4,5},{5,4},{6,7},{7,6},{8,9},{9,8},{10,11... | collective-permute-start | bytes 393224 | tf_op jit(solution)/shard_map/ppermute | solution.py:19
  44.3 0.0 collective-permute-done.refs_1_
  44.3 1.7 %collective-permute-start.4 = (bf16[64,1024]{1,0:T(8,128)(2,1)S(1)}, bf16[64,1024]{1,0:T(8,128)(2,1)S(1)}, u32[]{:S(2)}, u32[]{:S(2)}) collective-permute-start(bf16[64,1024]{1,0:T(8,128)(2,1)S(1)} %collective-permute-done.refs_1_), channel_id=1, source_target_pairs={{0,1},{1,0},{2,3},{3,2},{4,5},{5,4},{6,7},{7,6},{8,9},{9,8},{10,11... | collective-permute-start | bytes 393224 | tf_op jit(solution)/shard_map/ppermute | solution.py:19
  46.1 0.0 collective-permute-done.1.refs_2_
  46.1 0.1 collective-permute-start.5
  46.2 0.0 collective-permute-done.3.refs_4_
  46.2 0.0 collective-permute-done.6.refs_7_
  46.2 0.0 copy-start.12
  46.2 0.8 collective-permute-done.4.refs_5_
  47.1 0.0 copy-done.7
  47.1 0.0 copy-done.8
  47.1 0.0 copy-done.9
  47.1 0.0 copy-done.10
  47.1 0.0 copy-done.11
  47.1 0.0 copy-done.12
  47.1 0.0 copy-start.13
  47.1 0.6 copy-done.13
  47.7 0.0 collective-permute-done.5.refs_6_
  47.7 0.0 all-to-all-done.x_ref
  47.7 2.0 %project.1 = bf16[64,8,512]{2,1,0:T(8,128)(2,1)S(1)} custom-call(bf16[64,8,256]{2,1,0:T(8,128)(2,1)S(1)} %all-to-all-done.x_ref, bf16[64,1024]{1,0:T(8,128)(2,1)} %copy-done.7, bf16[64,1024]{1,0:T(8,128)(2,1)} %copy-done.9, bf16[64,1024]{1,0:T(8,128)(2,1)} %copy-done.10, bf16[64,1024]{1,0:T(8,128)(2,1)} %copy-done.8, bf16[64,1024]{1,0:T(8,128)(2,1)} %copy-done.11, ...), custom_call_target="tpu_custom_call" | custom-call | tf_op jit(solution)/shard_map/project/pallas_call | solution.py:167
  49.8 0.0 copy-start.1
  49.8 0.8 copy-done.1
  50.6 12.2 %all-to-all-start.1 = ((bf16[64,8,512]{2,1,0:T(8,128)(2,1)}), bf16[64,8,512]{2,1,0:T(8,128)(2,1)}, u32[]{:S(2)}, u32[]{:S(2)}) async-start(bf16[64,8,512]{2,1,0:T(8,128)(2,1)} %copy-done.1), calls=%async_computation.1 | async-start | bytes 1048576 | tf_op jit(solution)/shard_map/all_to_all | solution.py:422
  62.8 0.0 copy-done.14
  62.8 15.5 %all-to-all-done.1.x_ref = bf16[64,8,512]{2,1,0:T(8,128)(2,1)} async-done(((bf16[64,8,512]{2,1,0:T(8,128)(2,1)}), bf16[64,8,512]{2,1,0:T(8,128)(2,1)}, u32[]{:S(2)}, u32[]{:S(2)}) %all-to-all-start.1) | async-done | bytes 524320 | tf_op jit(solution)/shard_map/all_to_all | solution.py:422
  78.3 0.0 copy-done.3
  78.3 1.3 settle.1
  79.6 3.2 %collective-permute-start.7 = (bf16[2,8,512]{2,1,0:T(8,128)(2,1)S(1)}, bf16[2,8,512]{2,1,0:T(8,128)(2,1)S(1)}, u32[]{:S(2)}, u32[]{:S(2)}) collective-permute-start(bf16[2,8,512]{2,1,0:T(8,128)(2,1)S(1)} %get-tuple-element.14), channel_id=1, source_target_pairs={{0,1},{1,0},{2,3},{3,2},{4,5},{5,4},{6,7},{7,6},{8,9},{9,8},{10,11... | collective-permute-start | bytes 49160 | tf_op jit(solution)/shard_map/ppermute | solution.py:19
  82.8 0.0 copy-done.4
  82.8 0.0 copy-done.5
  82.8 0.2 route.1
  83.0 0.6 collective-permute-done.7.other_ref
  83.6 0.3 dispatch.1
  83.9 0.0 copy-start.2
  83.9 0.8 copy-done.2
  84.7 7.3 %all-to-all-start.2 = ((bf16[64,8,512]{2,1,0:T(8,128)(2,1)}), bf16[64,8,512]{2,1,0:T(8,128)(2,1)}, u32[]{:S(2)}, u32[]{:S(2)}) async-start(bf16[64,8,512]{2,1,0:T(8,128)(2,1)} %copy-done.2), calls=%async_computation.2 | async-start | bytes 1048576 | tf_op jit(solution)/shard_map/all_to_all | solution.py:424
  92.1 1.4 dynamic-slice_bitcast_fusion
  93.4 0.6 collective-permute-start.10
  94.0 13.9 %all-to-all-done.2.own_ref = bf16[64,8,512]{2,1,0:T(8,128)(2,1)} async-done(((bf16[64,8,512]{2,1,0:T(8,128)(2,1)}), bf16[64,8,512]{2,1,0:T(8,128)(2,1)}, u32[]{:S(2)}, u32[]{:S(2)}) %all-to-all-start.2) | async-done | bytes 524320 | tf_op jit(solution)/shard_map/all_to_all | solution.py:424
  107.8 2.8 %collective-permute-start.8 = (bf16[64,8,512]{2,1,0:T(8,128)(2,1)}, bf16[64,8,512]{2,1,0:T(8,128)(2,1)S(1)}, u32[]{:S(2)}, u32[]{:S(2)}) collective-permute-start(bf16[64,8,512]{2,1,0:T(8,128)(2,1)} %all-to-all-done.2.own_ref), channel_id=1, source_target_pairs={{0,1},{1,0},{2,3},{3,2},{4,5},{5,4},{6,7},{7,6},{8,9},{9,8},{10,11... | collective-permute-start | bytes 1572872 | tf_op jit(solution)/shard_map/ppermute | solution.py:19
  110.6 1.7 %collective-permute-done.8.other_ref = bf16[64,8,512]{2,1,0:T(8,128)(2,1)S(1)} collective-permute-done((bf16[64,8,512]{2,1,0:T(8,128)(2,1)}, bf16[64,8,512]{2,1,0:T(8,128)(2,1)S(1)}, u32[]{:S(2)}, u32[]{:S(2)}) %collective-permute-start.8) | collective-permute-done | bytes 524320 | tf_op jit(solution)/shard_map/ppermute | solution.py:19
  112.3 4.7 %gate_up.1.own_ref = bf16[128,384]{1,0:T(8,128)(2,1)S(1)} custom-call(bf16[64,8,512]{2,1,0:T(8,128)(2,1)} %all-to-all-done.2.own_ref, bf16[64,8,512]{2,1,0:T(8,128)(2,1)S(1)} %collective-permute-done.8.other_ref, bf16[1,4096,384]{2,1,0:T(8,128)(2,1)} %gate_ref.1, bf16[1,4096,384]{2,1,0:T(8,128)(2,1)} %up_ref.1), custom_call_target="tpu_custom_call" | custom-call | tf_op jit(solution)/shard_map/gate_up/pallas_call | solution.py:313
  117.1 0.5 collective-permute-start.9
  117.5 0.0 collective-permute-done.10.moved_ref
  117.6 0.9 collective-permute-done.9.other_ref
  118.5 2.4 %down.1 = bf16[64,8,512]{2,1,0:T(8,128)(2,1)S(1)} custom-call(bf16[128,384]{1,0:T(8,128)(2,1)S(1)} %gate_up.1.own_ref, bf16[128,384]{1,0:T(8,128)(2,1)S(1)} %collective-permute-done.9.other_ref, bf16[1,384,4096]{2,1,0:T(8,128)(2,1)S(1)} %copy-done, bf16[384,2048]{1,0:T(8,128)(2,1)} %collective-permute-done.10.moved_ref), custom_call_target="tpu_custom_call" | custom-call | tf_op jit(solution)/shard_map/down/pallas_call | solution.py:343
  120.9 22.5 %all_to_all.20.x_ref = bf16[64,8,512]{2,1,0:T(8,128)(2,1)S(1)} all-to-all(bf16[64,8,512]{2,1,0:T(8,128)(2,1)S(1)} %down.1), channel_id=1, replica_groups=mesh['groups'=2,'expert'=64,'replica'=2] {'expert'}, dimensions={0} | all-to-all | bytes 1048576 | tf_op jit(solution)/shard_map/all_to_all | solution.py:427
  143.3 0.2 combine.1
  143.5 3.0 %collective-permute-start.11 = (f32[2,8,512]{2,1,0:T(8,128)S(1)}, f32[2,8,512]{2,1,0:T(8,128)S(1)}, u32[]{:S(2)}, u32[]{:S(2)}) collective-permute-start(f32[2,8,512]{2,1,0:T(8,128)S(1)} %get-tuple-element.18), channel_id=1, source_target_pairs={{0,1},{1,0},{2,3},{3,2},{4,5},{5,4},{6,7},{7,6},{8,9},{9,8},{10,11... | collective-permute-start | bytes 98312 | tf_op jit(solution)/shard_map/ppermute | solution.py:19
  146.5 0.9 collective-permute-done.11.other_ref
  147.4 0.6 finish.1
  (9 shorter events, 0.0 us)
Async XLA Ops:
  0.0 78.3 %copy-start.3 = (bf16[4,4096]{1,0:T(4,128)(2,1)S(1)}, bf16[4,4096]{1,0:T(4,128)(2,1)}, u32[]{:S(2)}) copy-start(bf16[4,4096]{1,0:T(4,128)(2,1)} %residual_ref.1) | copy-start | bytes 98308
  0.0 0.7 copy-start.6
  0.7 62.1 %copy-start.14 = (bf16[4096]{0:T(1024)(128)(2,1)S(1)}, bf16[4096]{0:T(1024)(128)(2,1)}, u32[]{:S(2)}) copy-start(bf16[4096]{0:T(1024)(128)(2,1)} %param.22) | copy-start | bytes 24580
  9.3 73.5 %copy-start.4 = (s32[8,8]{1,0:T(8,128)S(1)}, s32[8,8]{1,0:T(8,128)}, u32[]{:S(2)}) copy-start(s32[8,8]{1,0:T(8,128)} %ids_ref.1) | copy-start | bytes 772
  9.3 73.5 %copy-start.5 = (f32[8,8]{1,0:T(8,128)S(1)}, f32[8,8]{1,0:T(8,128)}, u32[]{:S(2)}) copy-start(f32[8,8]{1,0:T(8,128)} %weight_ref.1) | copy-start | bytes 772
  9.3 38.5 %all-to-all-start = ((bf16[64,8,256]{2,1,0:T(8,128)(2,1)}), bf16[64,8,256]{2,1,0:T(8,128)(2,1)S(1)}, u32[]{:S(2)}, u32[]{:S(2)}) async-start(bf16[64,8,256]{2,1,0:T(8,128)(2,1)} %attend.1), calls=%async_computation | async-start | bytes 524288 | tf_op jit(solution)/shard_map/all_to_all | solution.py:412
  31.1 60.9 %copy-start = (bf16[1,384,4096]{2,1,0:T(8,128)(2,1)S(1)}, bf16[1,384,4096]{2,1,0:T(8,128)(2,1)}, u32[]{:S(2)}) copy-start(bf16[1,384,4096]{2,1,0:T(8,128)(2,1)} %down_ref.1) | copy-start | bytes 9437188
  32.5 14.6 %copy-start.7 = (bf16[64,1024]{1,0:T(8,128)(2,1)}, bf16[64,1024]{1,0:T(8,128)(2,1)S(1)}, u32[]{:S(2)}) copy-start(bf16[64,1024]{1,0:T(8,128)(2,1)S(1)} %get-tuple-element.21.refs_0_) | copy-start | bytes 393220
  32.5 8.7 %collective-permute-start.2 = (bf16[64,1024]{1,0:T(8,128)(2,1)S(1)}, bf16[64,1024]{1,0:T(8,128)(2,1)S(1)}, u32[]{:S(2)}, u32[]{:S(2)}) collective-permute-start(bf16[64,1024]{1,0:T(8,128)(2,1)S(1)} %get-tuple-element.19), channel_id=1, source_target_pairs={{0,18},{2,16},{4,22},{6,20},{8,26},{10,24},{12,30},{14,28},{16,2},... | collective-permute-start | bytes 393224 | tf_op jit(solution)/shard_map/ppermute | solution.py:416
  33.6 10.7 %collective-permute-start = (bf16[64,1024]{1,0:T(8,128)(2,1)S(1)}, bf16[64,1024]{1,0:T(8,128)(2,1)S(1)}, u32[]{:S(2)}, u32[]{:S(2)}) collective-permute-start(bf16[64,1024]{1,0:T(8,128)(2,1)S(1)} %get-tuple-element.20), channel_id=1, source_target_pairs={{0,2},{2,0},{4,6},{6,4},{8,10},{10,8},{12,14},{14,12},{16,18},{18,... | collective-permute-start | bytes 393224 | tf_op jit(solution)/shard_map/ppermute | solution.py:416
  33.9 12.1 %collective-permute-start.1 = (bf16[64,1024]{1,0:T(8,128)(2,1)S(1)}, bf16[64,1024]{1,0:T(8,128)(2,1)S(1)}, u32[]{:S(2)}, u32[]{:S(2)}) collective-permute-start(bf16[64,1024]{1,0:T(8,128)(2,1)S(1)} %get-tuple-element.22), channel_id=1, source_target_pairs={{0,16},{2,18},{4,20},{6,22},{8,24},{10,26},{12,28},{14,30},{16,0},... | collective-permute-start | bytes 393224 | tf_op jit(solution)/shard_map/ppermute | solution.py:416
  35.2 11.0 %collective-permute-start.3 = (bf16[64,1024]{1,0:T(8,128)(2,1)S(1)}, bf16[64,1024]{1,0:T(8,128)(2,1)S(1)}, u32[]{:S(2)}, u32[]{:S(2)}) collective-permute-start(bf16[64,1024]{1,0:T(8,128)(2,1)S(1)} %get-tuple-element.21.refs_0_), channel_id=1, source_target_pairs={{0,1},{1,0},{2,3},{3,2},{4,5},{5,4},{6,7},{7,6},{8,9},{9,8},{10,11... | collective-permute-start | bytes 393224 | tf_op jit(solution)/shard_map/ppermute | solution.py:19
  41.2 5.9 %copy-start.8 = (bf16[64,1024]{1,0:T(8,128)(2,1)}, bf16[64,1024]{1,0:T(8,128)(2,1)S(1)}, u32[]{:S(2)}) copy-start(bf16[64,1024]{1,0:T(8,128)(2,1)S(1)} %collective-permute-done.2.refs_3_) | copy-start | bytes 393220
  41.2 5.0 %collective-permute-start.6 = (bf16[64,1024]{1,0:T(8,128)(2,1)S(1)}, bf16[64,1024]{1,0:T(8,128)(2,1)S(1)}, u32[]{:S(2)}, u32[]{:S(2)}) collective-permute-start(bf16[64,1024]{1,0:T(8,128)(2,1)S(1)} %collective-permute-done.2.refs_3_), channel_id=1, source_target_pairs={{0,1},{1,0},{2,3},{3,2},{4,5},{5,4},{6,7},{7,6},{8,9},{9,8},{10,11... | collective-permute-start | bytes 393224 | tf_op jit(solution)/shard_map/ppermute | solution.py:19
  44.3 2.7 %copy-start.9 = (bf16[64,1024]{1,0:T(8,128)(2,1)}, bf16[64,1024]{1,0:T(8,128)(2,1)S(1)}, u32[]{:S(2)}) copy-start(bf16[64,1024]{1,0:T(8,128)(2,1)S(1)} %collective-permute-done.refs_1_) | copy-start | bytes 393220
  44.3 2.7 %collective-permute-start.4 = (bf16[64,1024]{1,0:T(8,128)(2,1)S(1)}, bf16[64,1024]{1,0:T(8,128)(2,1)S(1)}, u32[]{:S(2)}, u32[]{:S(2)}) collective-permute-start(bf16[64,1024]{1,0:T(8,128)(2,1)S(1)} %collective-permute-done.refs_1_), channel_id=1, source_target_pairs={{0,1},{1,0},{2,3},{3,2},{4,5},{5,4},{6,7},{7,6},{8,9},{9,8},{10,11... | collective-permute-start | bytes 393224 | tf_op jit(solution)/shard_map/ppermute | solution.py:19
  46.1 1.0 copy-start.10
  46.1 1.7 %collective-permute-start.5 = (bf16[64,1024]{1,0:T(8,128)(2,1)S(1)}, bf16[64,1024]{1,0:T(8,128)(2,1)}, u32[]{:S(2)}, u32[]{:S(2)}) collective-permute-start(bf16[64,1024]{1,0:T(8,128)(2,1)S(1)} %collective-permute-done.1.refs_2_), channel_id=1, source_target_pairs={{0,1},{1,0},{2,3},{3,2},{4,5},{5,4},{6,7},{7,6},{8,9},{9,8},{10,11... | collective-permute-start | bytes 393224 | tf_op jit(solution)/shard_map/ppermute | solution.py:19
  46.2 0.9 copy-start.11
  46.2 0.9 copy-start.12
  47.1 0.6 copy-start.13
  49.8 0.8 copy-start.1
  50.6 27.7 %all-to-all-start.1 = ((bf16[64,8,512]{2,1,0:T(8,128)(2,1)}), bf16[64,8,512]{2,1,0:T(8,128)(2,1)}, u32[]{:S(2)}, u32[]{:S(2)}) async-start(bf16[64,8,512]{2,1,0:T(8,128)(2,1)} %copy-done.1), calls=%async_computation.1 | async-start | bytes 1048576 | tf_op jit(solution)/shard_map/all_to_all | solution.py:422
  79.6 4.0 %collective-permute-start.7 = (bf16[2,8,512]{2,1,0:T(8,128)(2,1)S(1)}, bf16[2,8,512]{2,1,0:T(8,128)(2,1)S(1)}, u32[]{:S(2)}, u32[]{:S(2)}) collective-permute-start(bf16[2,8,512]{2,1,0:T(8,128)(2,1)S(1)} %get-tuple-element.14), channel_id=1, source_target_pairs={{0,1},{1,0},{2,3},{3,2},{4,5},{5,4},{6,7},{7,6},{8,9},{9,8},{10,11... | collective-permute-start | bytes 49160 | tf_op jit(solution)/shard_map/ppermute | solution.py:19
  83.9 0.8 copy-start.2
  84.7 23.1 %all-to-all-start.2 = ((bf16[64,8,512]{2,1,0:T(8,128)(2,1)}), bf16[64,8,512]{2,1,0:T(8,128)(2,1)}, u32[]{:S(2)}, u32[]{:S(2)}) async-start(bf16[64,8,512]{2,1,0:T(8,128)(2,1)} %copy-done.2), calls=%async_computation.2 | async-start | bytes 1048576 | tf_op jit(solution)/shard_map/all_to_all | solution.py:424
  93.4 24.1 %collective-permute-start.10 = (bf16[384,2048]{1,0:T(8,128)(2,1)}, bf16[384,2048]{1,0:T(8,128)(2,1)}, u32[]{:S(2)}, u32[]{:S(2)}) collective-permute-start(bf16[384,2048]{1,0:T(8,128)(2,1)} %dynamic-slice_bitcast_fusion), channel_id=1, source_target_pairs={{0,1},{1,0},{2,3},{3,2},{4,5},{5,4},{6,7},{7,6},{8,9},{9,8},{10,11... | collective-permute-start | bytes 4718600 | tf_op jit(solution)/shard_map/ppermute | solution.py:19
  107.8 4.5 %collective-permute-start.8 = (bf16[64,8,512]{2,1,0:T(8,128)(2,1)}, bf16[64,8,512]{2,1,0:T(8,128)(2,1)S(1)}, u32[]{:S(2)}, u32[]{:S(2)}) collective-permute-start(bf16[64,8,512]{2,1,0:T(8,128)(2,1)} %all-to-all-done.2.own_ref), channel_id=1, source_target_pairs={{0,1},{1,0},{2,3},{3,2},{4,5},{5,4},{6,7},{7,6},{8,9},{9,8},{10,11... | collective-permute-start | bytes 1572872 | tf_op jit(solution)/shard_map/ppermute | solution.py:19
  117.1 1.4 collective-permute-start.9
  143.5 3.8 %collective-permute-start.11 = (f32[2,8,512]{2,1,0:T(8,128)S(1)}, f32[2,8,512]{2,1,0:T(8,128)S(1)}, u32[]{:S(2)}, u32[]{:S(2)}) collective-permute-start(f32[2,8,512]{2,1,0:T(8,128)S(1)} %get-tuple-element.18), channel_id=1, source_target_pairs={{0,1},{1,0},{2,3},{3,2},{4,5},{5,4},{6,7},{7,6},{8,9},{9,8},{10,11... | collective-permute-start | bytes 98312 | tf_op jit(solution)/shard_map/ppermute | solution.py:19

commit v3 on v2

v3 whole, which is shorter than its diff:
```python
import math

import jax
import jax.numpy as jnp
from jax import lax
from jax.experimental import pallas as pl
from jax.experimental.pallas import tpu as pltpu
from jax.sharding import PartitionSpec as P

HEAD_WIDTH = 128
CHIPS, CORES = "expert", "replica"
F32, BF16 = jnp.float32, jnp.bfloat16
IN_VMEM = pl.BlockSpec(memory_space=pltpu.VMEM)
IN_SMEM = pl.BlockSpec(memory_space=pltpu.SMEM)
IN_HBM = pl.BlockSpec(memory_space=pltpu.HBM)


def swapped(x):
    return lax.ppermute(x, CORES, [(0, 1), (1, 0)])


def quad_step(side, dx, dy):
    return [
        (x * side + y, (x ^ dx) * side + (y ^ dy)) for x in range(side) for y in range(side)
    ]


MIB = 1 << 20


def in_hbm(x):
    return pltpu.with_memory_space_constraint(x, pltpu.HBM)


def in_vmem(x):
    return pltpu.with_memory_space_constraint(x, pltpu.VMEM)


def kernel_call(body, outs, in_specs, limit, scratch=()):
    return pl.pallas_call(
        body,
        out_shape=outs,
        in_specs=in_specs,
        out_specs=jax.tree.map(lambda _: IN_VMEM, outs),
        scratch_shapes=list(scratch),
        compiler_params=pltpu.CompilerParams(vmem_limit_bytes=limit * MIB),
    )


def shape(*dims, dtype=BF16):
    return jax.ShapeDtypeStruct(dims, dtype)


def attend_body(
    q_hbm,
    tk_hbm,
    tv_hbm,
    len_hbm,
    keys_hbm,
    values_hbm,
    weight_hbm,
    out_ref,
    piece0,
    piece1,
    piece2,
    piece3,
    q_ref,
    tk_ref,
    tv_ref,
    len_ref,
    keys,
    values,
    rows,
    mixed,
    sems,
    few,
):
    core = lax.axis_index(CORES)
    seq_count, cache_len, kv_width = keys_hbm.shape
    kv_count = kv_width // HEAD_WIDTH
    head_count = q_hbm.shape[1] // HEAD_WIDTH
    group = head_count // kv_count
    side = group // 2
    small = [
        pltpu.make_async_copy(source, target, few.at[j])
        for j, (source, target) in enumerate(
            ((q_hbm, q_ref), (tk_hbm, tk_ref), (tv_hbm, tv_ref), (len_hbm, len_ref))
        )
    ]
    for copy in small:
        copy.start()
    copies = []
    for b in range(seq_count):
        pair = []
        for j, (source, target) in enumerate(((keys_hbm, keys), (values_hbm, values))):
            copy = pltpu.make_async_copy(source.at[b], target.at[b], sems.at[j, b])
            copy.start()
            pair.append(copy)
        copies.append(pair)
    chip = lax.axis_index(CHIPS)
    place = chip // side % 2 * 2 + chip % 2
    sliced = []
    for d, piece in enumerate((piece0, piece1, piece2, piece3)):
        cols = piece.shape[1]
        at = pl.multiple_of((place ^ d) * cols, cols)
        sliced.append(
            pltpu.make_async_copy(weight_hbm.at[:, pl.ds(at, cols)], piece, few.at[len(small) + d])
        )
        sliced[-1].start()
    for copy in small:
        copy.wait()
    for h in range(head_count):
        piece = q_ref[:, h * HEAD_WIDTH : (h + 1) * HEAD_WIDTH].astype(F32)
        rows[pl.ds(h, seq_count, stride=head_count), :] = piece
    inv_root = 1.0 / math.sqrt(HEAD_WIDTH)
    positions = lax.broadcasted_iota(jnp.int32, (head_count, cache_len), 1)
    lanes = [slice(g * HEAD_WIDTH, (g + 1) * HEAD_WIDTH) for g in range(kv_count)]
    for b in range(seq_count):
        query = rows[b * head_count : (b + 1) * head_count, :]
        latest = [tk_ref[b : b + 1, lanes[g]].astype(F32) for g in range(kv_count)]
        latest = jnp.concatenate([jnp.broadcast_to(v, (group, HEAD_WIDTH)) for v in latest])
        fresh = jnp.sum(query * latest, axis=1, keepdims=True) * inv_root
        query = query.astype(BF16)
        copies[b][0].wait()
        scores = [
            lax.dot_general(
                query[g * group : (g + 1) * group],
                keys[b, :, lanes[g]],
                (((1,), (1,)), ((), ())),
                preferred_element_type=F32,
            )
            for g in range(kv_count)
        ]
        scores = jnp.where(positions < len_ref[b], jnp.concatenate(scores) * inv_root, -jnp.inf)
        highest = jnp.maximum(jnp.max(scores, axis=1, keepdims=True), fresh)
        cached_exp = jnp.exp(scores - highest)
        fresh_exp = jnp.exp(fresh - highest)
        totals = jnp.sum(cached_exp, axis=1, keepdims=True) + fresh_exp
        prob = (cached_exp / totals).astype(BF16)
        fresh_prob = (fresh_exp / totals).astype(BF16).astype(F32)
        copies[b][1].wait()
        for g in range(kv_count):
            heads = slice(g * group, (g + 1) * group)
            out = jnp.dot(prob[heads], values[b, :, lanes[g]], preferred_element_type=F32)
            out = out + fresh_prob[heads] * tv_ref[b : b + 1, lanes[g]].astype(F32)
            out = pltpu.roll(out, core * (HEAD_WIDTH // 2), 1)
            for a in range(2):
                start = g * group * seq_count + a * seq_count + b
                mixed[pl.ds(start, side, stride=2 * seq_count), :] = out[a * side : (a + 1) * side]
    tile = 2 * seq_count
    for g in range(kv_count):
        for y in range(side):
            for part, source in enumerate((y, y ^ 1)):
                at = (g * side + source) * tile
                near = mixed[at : at + tile, :]
                far = pltpu.roll(near, seq_count, 0)
                out_ref[2 * g * side + y, :, lanes[part]] = near.astype(BF16)
                out_ref[(2 * g + 1) * side + y, :, lanes[part]] = far.astype(BF16)
    for copy in sliced:
        copy.wait()


def attend(queries, token_keys, token_values, kv_len, stored_keys, stored_values, out_weight):
    seq_count, feature_total = queries.shape
    heads = feature_total // HEAD_WIDTH
    rows, cols = out_weight.shape
    return pl.pallas_call(
        attend_body,
        name="attend",
        out_shape=[pltpu.HBM((heads, 2 * seq_count, 2 * HEAD_WIDTH), BF16)]
        + [pltpu.HBM((rows, cols // 4), BF16)] * 4,
        in_specs=[IN_HBM] * 7,
        out_specs=[IN_VMEM] + [IN_HBM] * 4,
        scratch_shapes=[
            pltpu.VMEM(queries.shape, BF16),
            pltpu.VMEM(token_keys.shape, BF16),
            pltpu.VMEM(token_values.shape, BF16),
            pltpu.SMEM(kv_len.shape, jnp.int32),
            pltpu.VMEM(stored_keys.shape, BF16),
            pltpu.VMEM(stored_values.shape, BF16),
            pltpu.VMEM((seq_count * heads, HEAD_WIDTH), F32),
            pltpu.VMEM((seq_count * heads, HEAD_WIDTH), F32),
            pltpu.SemaphoreType.DMA((2, seq_count)),
            pltpu.SemaphoreType.DMA((8,)),
        ],
        compiler_params=pltpu.CompilerParams(vmem_limit_bytes=8 * MIB),
    )(
        *map(
            in_hbm,
            (queries, token_keys, token_values, kv_len, stored_keys, stored_values, out_weight),
        )
    )


def copy_all(pairs, sems):
    copies = [pltpu.make_async_copy(*pair, sems.at[j]) for j, pair in enumerate(pairs)]
    for copy in copies:
        copy.start()
    for copy in copies:
        copy.wait()


def stack_body(*refs):
    own, other, out_ref, sems = refs[:4], refs[4:8], refs[8], refs[9]
    rows = own[0].shape[0]
    pairs = []
    for d in range(4):
        for half, source in enumerate((own[d], other[d])):
            at = (d % 2 * 2 + half) * rows
            pairs.append((source, out_ref.at[d // 2, at : at + rows]))
    copy_all(pairs, sems)


def stack(own, other):
    rows, cols = own[0].shape
    return pl.pallas_call(
        stack_body,
        name="stack",
        out_shape=pltpu.VMEM((2, 4 * rows, cols), BF16),
        in_specs=[IN_HBM] * 8,
        out_specs=IN_VMEM,
        scratch_shapes=[pltpu.SemaphoreType.DMA((8,))],
        compiler_params=pltpu.CompilerParams(vmem_limit_bytes=2 * MIB),
    )(*map(in_hbm, own), *map(in_hbm, other))


def halves_body(gate_hbm, up_hbm, down_hbm, kept_ref, *refs):
    outs, sems = refs[:3], refs[3]
    core = lax.axis_index(CORES)
    half = kept_ref.shape[0]
    kept, given = (pl.ds(pl.multiple_of(j * half, half), half) for j in (core, 1 - core))
    copy_all(
        (
            (gate_hbm.at[0, kept, :], kept_ref),
            (gate_hbm.at[0, given, :], outs[0]),
            (up_hbm.at[0, given, :], outs[1]),
            (down_hbm.at[0, :, given], outs[2]),
        ),
        sems,
    )


def halves(w_gate, w_up, w_down):
    _, width, units = w_gate.shape
    tall, wide = (width // 2, units), (units, width // 2)
    return pl.pallas_call(
        halves_body,
        name="halves",
        out_shape=[pltpu.VMEM(tall, BF16)] + [pltpu.HBM(dims, BF16) for dims in (tall, tall, wide)],
        in_specs=[IN_HBM] * 3,
        out_specs=[IN_VMEM] + [IN_HBM] * 3,
        scratch_shapes=[pltpu.SemaphoreType.DMA((4,))],
        compiler_params=pltpu.CompilerParams(vmem_limit_bytes=2 * MIB),
    )(*map(in_hbm, (w_gate, w_up, w_down)))


def project_body(x_ref, weight_ref, out_ref):
    chips, tile, width = x_ref.shape
    cols = weight_ref.shape[2]
    half = cols // 2
    step = 16
    low = lax.broadcasted_iota(jnp.int32, (step, tile, half), 1) < tile // 2
    for at in range(0, chips, step):
        x = x_ref[at : at + step].reshape(step * tile, width)
        near, far = (
            jnp.dot(x, weight_ref[j], preferred_element_type=F32).reshape(step, tile, cols)
            for j in range(2)
        )
        kept = jnp.where(low, near[:, :, :half], far[:, :, half:])
        moved = jnp.where(low, near[:, :, half:], far[:, :, :half])
        moved = pltpu.roll(moved, tile // 2, 1)
        out_ref[at : at + step] = (kept + moved).astype(BF16)


def project(x, weight):
    cols = weight.shape[2]
    return kernel_call(
        project_body, pltpu.HBM((x.shape[0], x.shape[1], cols // 2), BF16), [IN_VMEM] * 2, 12
    )(x, in_vmem(weight))


def settle_body(x_ref, residual_ref, gain_ref, hidden_ref, kept_ref, given_ref, normed):
    core = lax.axis_index(CORES)
    chips, tile, half = x_ref.shape
    side = math.isqrt(chips)
    blocks = 4
    seq_count = tile // 2
    width = residual_ref.shape[1]

    def rows_of(ref, k):
        low, high = (ref[:, (2 * k + q) * half : (2 * k + q + 1) * half].astype(F32) for q in (0, 1))
        low, high = (jnp.broadcast_to(v, (seq_count, half)) for v in (low, high))
        return jnp.concatenate([low, high])

    square = jnp.zeros((tile, 1), F32)
    for k in range(blocks):
        total = rows_of(residual_ref, k)
        for x in range(k // 2, side, 2):
            for y in range(k % 2, side, 2):
                total = total + x_ref[x * side + y].astype(F32)
        hidden_ref[k] = total
        square = square + jnp.sum(total * total, axis=1, keepdims=True)
    square = jnp.broadcast_to(square, (tile, HEAD_WIDTH))
    square = square + pltpu.roll(square, seq_count, 0)
    scale = lax.rsqrt(square[:, :1] / width + 1e-06)
    for k in range(blocks):
        normed[k] = (hidden_ref[k] * scale * rows_of(gain_ref, k)).astype(BF16)
    kept_ref[...] = normed[pl.ds(core * 2, 2)]
    given_ref[...] = normed[pl.ds(2 - core * 2, 2)]


def settle(x, residual, gain):
    tile, half = x.shape[1:]
    return kernel_call(
        settle_body,
        (shape(4, tile, half, dtype=F32), shape(2, tile, half), shape(2, tile, half)),
        [IN_VMEM] * 3,
        6,
        [pltpu.VMEM((4, tile, half), BF16)],
    )(x, residual, gain)


def route_body(ids_ref, weight_ref, pick_ref, mix_ref):
    core = lax.axis_index(CORES)
    tokens, topk = ids_ref.shape
    seq_count = tokens // 2
    lanes = pick_ref.shape[1]
    lane = lax.broadcasted_iota(jnp.int32, (tokens, lanes), 1)
    row = lax.broadcasted_iota(jnp.int32, (tokens, lanes), 0)
    weight = weight_ref[...]
    mixing = weight / jnp.sum(weight, axis=1, keepdims=True)
    ids = ids_ref[...]
    hit = jnp.zeros((tokens, lanes), F32)
    share = jnp.zeros((tokens, lanes), F32)
    for k in range(topk):
        same = ids[:, k : k + 1] == lane // 8
        hit = jnp.where(same, 1.0, hit)
        share = jnp.where(same, mixing[:, k : k + 1], share)
    rank = jnp.zeros((tokens, lanes), F32)
    for t in range(tokens - 1):
        rank = rank + jnp.where(row > t, jnp.broadcast_to(hit[t : t + 1], (tokens, lanes)), 0.0)
    taken = jnp.where(rank == (lane % 2).astype(F32), hit, 0.0)
    share = share * taken
    own_low = (row < seq_count) == (core == 0)
    quarter = lane // 2 % 4
    for src in range(2):
        low = own_low if src == 0 else jnp.logical_not(own_low)
        chosen = jnp.where(low, taken, pltpu.roll(taken, seq_count, 0))
        shares = jnp.where(low, share, pltpu.roll(share, seq_count, 0))
        for kk in range(2):
            at = (src * 2 + kk) * tokens
            mine = quarter == kk * 2 + row // seq_count
            pick_ref[at : at + tokens, :] = jnp.where(mine, chosen, 0.0).astype(BF16)
            value = jnp.where(mine, shares, 0.0)
            coarse = value.astype(BF16)
            mix_ref[at : at + tokens, :] = coarse
            mix_ref[4 * tokens + at : 5 * tokens + at, :] = (value - coarse.astype(F32)).astype(BF16)


def route(expert_ids, route_weight, chips):
    tokens = expert_ids.shape[0]
    return kernel_call(
        route_body, (shape(4 * tokens, 8 * chips), shape(8 * tokens, 8 * chips)), [IN_VMEM] * 2, 4
    )(expert_ids, route_weight)


def dispatch_body(kept_ref, other_ref, pick_ref, out_ref):
    pieces = [r[...].reshape(-1, r.shape[2]) for r in (kept_ref, other_ref)]
    rows = lax.dot_general(
        pick_ref[...],
        jnp.concatenate(pieces),
        (((0,), (0,)), ((), ())),
        preferred_element_type=F32,
    )
    out_ref[...] = rows.astype(BF16).reshape(out_ref.shape)


def dispatch(kept, other, pick):
    tile, half = kept.shape[1:]
    return kernel_call(
        dispatch_body, pltpu.HBM((pick.shape[1] // tile, tile, half), BF16), [IN_VMEM] * 3, 6
    )(kept, other, pick)


def slot_order(size, back=False):
    sorted_row = lax.broadcasted_iota(jnp.int32, (size, size), 1 if back else 0)
    row = lax.broadcasted_iota(jnp.int32, (size, size), 0 if back else 1)
    slot = sorted_row % (size // 4)
    quarter = sorted_row // (size // 4)
    return jnp.where(row == slot // 2 * 8 + quarter * 2 + slot % 2, 1.0, 0.0).astype(BF16)


def gate_body(
    x_ref,
    gate_ref,
    up_hbm,
    down_hbm,
    gate_moved,
    up_moved,
    down_moved,
    part_ref,
    sent_ref,
    down_ref,
    buffers,
    sems,
):
    core = lax.axis_index(CORES)
    chips, tile, part = x_ref.shape
    half, units = gate_ref.shape
    kept = pl.ds(pl.multiple_of(core * half, half), half)
    pairs = (
        (up_hbm.at[0, kept, :], buffers.at[0]),
        (gate_moved, buffers.at[1]),
        (up_moved, buffers.at[2]),
        (down_hbm.at[0, :, kept], down_ref.at[:units]),
        (down_moved, down_ref.at[units:]),
    )
    copies = [pltpu.make_async_copy(*pair, sems.at[j]) for j, pair in enumerate(pairs)]
    for copy in copies:
        copy.start()
    size = 256
    groups = chips * tile // size
    order = slot_order(size)
    slots = size // 4
    sorted_rows = []
    for g in range(groups):
        rows = x_ref[g * size // tile : (g + 1) * size // tile].reshape(size, part)
        sorted_rows.append(jnp.dot(order, rows, preferred_element_type=F32).astype(BF16))
    quarters = [
        jnp.concatenate([r[p * slots : (p + 1) * slots] for r in sorted_rows]) for p in range(4)
    ]
    x = jnp.concatenate(quarters, axis=1)
    for j in range(4):
        if j:
            copies[j - 1].wait()
        weight = buffers[j - 1] if j else gate_ref[...]
        value = jnp.dot(x, weight, preferred_element_type=F32)
        part_ref[:, j * units : (j + 1) * units] = value
        at = (j + 2) % 4 * units
        sent_ref[:, at : at + units] = value.astype(BF16)
    for copy in copies[3:]:
        copy.wait()


def gate_up(x, gate_own, w_up, w_down, moved):
    chips, tile, _ = x.shape
    half, units = gate_own.shape
    dims = chips * tile // 4, 4 * units
    return pl.pallas_call(
        gate_body,
        name="gate_up",
        out_shape=[
            pltpu.VMEM(dims, F32),
            pltpu.VMEM(dims, BF16),
            pltpu.VMEM((2 * units, half), BF16),
        ],
        in_specs=[IN_VMEM] * 2 + [IN_HBM] * 5,
        out_specs=[IN_VMEM] * 3,
        scratch_shapes=[pltpu.VMEM((3, half, units), BF16), pltpu.SemaphoreType.DMA((5,))],
        compiler_params=pltpu.CompilerParams(vmem_limit_bytes=16 * MIB),
    )(x, in_vmem(gate_own), *map(in_hbm, (w_up, w_down, *moved)))


def down_body(part_ref, arrived_ref, down_ref, out_ref):
    chips, tile, part = out_ref.shape
    size = 256
    groups = chips * tile // size
    order = slot_order(size, back=True)
    slots = size // 4
    units = down_ref.shape[0] // 2

    def act(at):
        gate, up = (
            part_ref[:, j : j + units] + arrived_ref[:, j : j + units].astype(F32)
            for j in (at, at + units)
        )
        return (gate / (1.0 + jnp.exp(-gate)) * up).astype(BF16)

    hidden = jnp.concatenate([act(0), act(2 * units)], axis=1)
    quarters = []
    for p in range(4):
        lanes = slice(p * part, (p + 1) * part)
        value = jnp.dot(hidden, down_ref[:, lanes], preferred_element_type=F32)
        quarters.append(value.astype(BF16))
    for g in range(groups):
        rows = jnp.concatenate([v[g * slots : (g + 1) * slots] for v in quarters])
        rows = jnp.dot(order, rows, preferred_element_type=F32).astype(BF16)
        out_ref[g * size // tile : (g + 1) * size // tile] = rows.reshape(size // tile, tile, part)


def down(part, arrived, weight, tile):
    slots = part.shape[0]
    width = weight.shape[1] // 4
    return kernel_call(
        down_body, pltpu.HBM((slots * 4 // tile, tile, width), BF16), [IN_VMEM] * 3, 8
    )(part, arrived, in_vmem(weight))


def combine_body(x_ref, mix_ref, own_ref, other_ref):
    x = x_ref[...].reshape(-1, x_ref.shape[2])
    rows = jnp.dot(mix_ref[...], x, preferred_element_type=F32)
    count = rows.shape[0] // 2
    rows = rows[:count] + rows[count:]
    own_ref[...] = rows[: count // 2].reshape(own_ref.shape)
    other_ref[...] = rows[count // 2 :].reshape(other_ref.shape)


def combine(x, mix):
    out = shape(2, x.shape[1], x.shape[2], dtype=F32)
    return kernel_call(combine_body, (out, out), [IN_VMEM] * 2, 4)(x, mix)


def finish_body(hidden_ref, own_ref, other_ref, out_ref, total):
    core = lax.axis_index(CORES)
    blocks, tile, half = hidden_ref.shape
    total[pl.ds(core * 2, 2)] = own_ref[...]
    total[pl.ds(2 - core * 2, 2)] = other_ref[...]
    for k in range(blocks):
        value = (hidden_ref[k] + total[k]).astype(BF16)
        for q in range(2):
            at = (2 * k + q) * half
            out_ref[:, at : at + half] = value[q * tile // 2 : (q + 1) * tile // 2]


def finish(hidden, own, other):
    blocks, tile, half = hidden.shape
    return kernel_call(
        finish_body, shape(tile // 2, 2 * blocks * half), [IN_VMEM] * 3, 2, [pltpu.VMEM(hidden.shape, F32)]
    )(hidden, own, other)


def on_device(
    queries,
    token_keys,
    token_values,
    stored_keys,
    stored_values,
    kv_len,
    residual,
    out_weight,
    norm_gain,
    expert_ids,
    route_weight,
    w_gate,
    w_up,
    w_down,
):
    chips = lax.axis_size(CHIPS)
    side = math.isqrt(chips)
    outgoing, *pieces = attend(
        queries, token_keys, token_values, kv_len, stored_keys, stored_values, out_weight
    )
    own = [pieces[0]] + [
        lax.ppermute(pieces[d], CHIPS, quad_step(side, d // 2, d % 2)) for d in (1, 2, 3)
    ]
    tokens = lax.all_to_all(outgoing, CHIPS, 0, 0, tiled=True)
    other = [swapped(piece) for piece in own]
    weight = stack(own, other)
    gate_own, *given_halves = halves(w_gate, w_up, w_down)
    moved = [swapped(x) for x in given_halves]
    pick, mix = route(expert_ids, route_weight, chips)

    sums = project(tokens, weight)
    came_back = lax.all_to_all(sums, CHIPS, 0, 0, tiled=True)
    hidden, normed, normed_given = settle(came_back, residual, norm_gain[None])
    outgoing = dispatch(normed, swapped(normed_given), pick)
    incoming = lax.all_to_all(outgoing, CHIPS, 0, 0, tiled=True)
    part, sent, down_weight = gate_up(incoming, gate_own, w_up, w_down, moved)
    expert_out = down(part, swapped(sent), down_weight, incoming.shape[1])
    returned = lax.all_to_all(expert_out, CHIPS, 0, 0, tiled=True)
    moe_own, moe_given = combine(returned, mix)
    return finish(hidden, moe_own, swapped(moe_given))


def solution(mesh):
    in_specs = (
        P(("groups", "expert", "replica"), None),
        P(("groups", "expert", "replica"), None),
        P(("groups", "expert", "replica"), None),
        P(("groups", "expert", "replica"), None, None),
        P(("groups", "expert", "replica"), None, None),
        P(("groups", "expert", "replica")),
        P(("groups", "expert", "replica"), None),
        P(("expert", "replica"), None),
        P(),
        P(("groups", "expert"), None),
        P(("groups", "expert"), None),
        P("expert", None, "replica"),
        P("expert", None, "replica"),
        P("expert", "replica", None),
    )
    out_specs = P(("groups", "expert", "replica"), None)
    return jax.shard_map(
        on_device, mesh=mesh, in_specs=in_specs, out_specs=out_specs, check_vma=False
    )
```

time: 149 us -> 292 us (1.96)
  Pallas kernels: 20.3 us -> 173 us
  waiting for transfers between devices: 34.4 us -> 24.9 us
  starting transfers between devices: 65 us -> 70 us
  local copies, waits for them, and re-layouts: 5.62 us -> 0.71 us
    pallas_call x9 -> x11, Pallas kernels: 20.3 us -> 173 us  [the longest x1 144 us: halves(): pl.pallas_call(halves_body, name='halves', out_shape=[pltpu.VMEM(tall, BF...]
    all_to_all x2, waiting for transfers between devices: 29.3 us -> 15.3 us  [the longest x1 15.3 us: on_device(): incoming = lax.all_to_all(outgoing, CHIPS, 0, 0, tiled=True)]
    all_to_all x2, starting transfers between devices: 19.5 us -> 26.1 us  [the longest x1 13.4 us: on_device(): incoming = lax.all_to_all(outgoing, CHIPS, 0, 0, tiled=True)]
    ppermute x9 -> x10, waiting for transfers between devices: 5.01 us -> 9.58 us  [swapped(): return lax.ppermute(x, CORES, [(0, 1), (1, 0)])]
    ppermute x9 -> x10, starting transfers between devices: 20.9 us -> 19.3 us  [swapped(): return lax.ppermute(x, CORES, [(0, 1), (1, 0)])]
  transfers between devices with their start and end apart: 15 -> 16, of which waited for: 7 -> 5; matrix products, arithmetic and copies ran while one was open for 2% -> 0% of each run, Pallas kernels for 3% -> 50%
where the time goes in v3:
time: 292 us; the launch traced here: 291 us
  Pallas kernels  173 us (59%)
  starting transfers between devices  70 us (24%)
  waiting for transfers between devices  24.9 us (9%)
  blocking collectives  22.6 us (8%)
    pallas_call x1, Pallas kernels, halves(): pl.pallas_call(halves_body, name='halves', out_shape=[pltpu.VMEM(tall, BF...  144 us
    all_to_all x1, blocking collectives, on_device(): returned = lax.all_to_all(expert_out, CHIPS, 0, 0, tiled=True)  22.6 us
    all_to_all x1, starting transfers between devices, on_device(): tokens = lax.all_to_all(outgoing, CHIPS, 0, 0, tiled=True)  21.8 us
    ppermute x10, starting transfers between devices, swapped(): return lax.ppermute(x, CORES, [(0, 1), (1, 0)])  19.3 us
    pallas_call x1, Pallas kernels, attend(): pl.pallas_call(attend_body, name='attend', out_shape=[pltpu.HBM((heads, 2...  17.8 us
    all_to_all x1, waiting for transfers between devices, on_device(): incoming = lax.all_to_all(outgoing, CHIPS, 0, 0, tiled=True)  15.3 us
    all_to_all x1, starting transfers between devices, on_device(): incoming = lax.all_to_all(outgoing, CHIPS, 0, 0, tiled=True)  13.4 us
    all_to_all x1, starting transfers between devices, on_device(): came_back = lax.all_to_all(sums, CHIPS, 0, 0, tiled=True)  12.7 us
  transfers between devices with their start and end apart: 16, of which 5 were waited for; matrix products, arithmetic and copies ran while one was open for 0% of the time, Pallas kernels for 50%

profile of v3, /device:TPU:513, one launch (start us, length us, event | category | flops | bytes accessed | tf_op | source)
XLA Modules:
  0.0 291.1 jit_solution(16338926180058162206)
XLA Ops:
  0.0 17.8 %attend.1 = (bf16[64,8,256]{2,1,0:T(8,128)(2,1)}, bf16[64,1024]{1,0:T(8,128)(2,1)}, bf16[64,1024]{1,0:T(8,128)(2,1)}, bf16[64,1024]{1,0:T(8,128)(2,1)}, bf16[64,1024]{1,0:T(8,128)(2,1)}) custom-call(bf16[4,8192]{1,0:T(4,128)(2,1)} %q_hbm.1, bf16[4,512]{1,0:T(4,128)(2,1)} %tk_hbm.1, bf16[4,512]{1,0:T(4,128)(2,1)} %tv_hbm.1, s32[4]{0:T(128)} %len_hbm.1, ...), custom_call_target="tpu_custom_call" | custom-call | tf_op jit(solution)/shard_map/attend/pallas_call | solution.py:167
  17.8 21.8 %all-to-all-start = ((bf16[64,8,256]{2,1,0:T(8,128)(2,1)}), bf16[64,8,256]{2,1,0:T(8,128)(2,1)S(1)}, u32[]{:S(2)}, u32[]{:S(2)}) async-start(bf16[64,8,256]{2,1,0:T(8,128)(2,1)} %get-tuple-element.24), calls=%async_computation | async-start | bytes 524288 | tf_op jit(solution)/shard_map/all_to_all | solution.py:556
  39.7 0.3 collective-permute-start
  39.9 1.2 collective-permute-start.1
  41.1 1.3 collective-permute-start.2
  42.4 5.9 %collective-permute-start.3 = (bf16[64,1024]{1,0:T(8,128)(2,1)}, bf16[64,1024]{1,0:T(8,128)(2,1)S(1)}, u32[]{:S(2)}, u32[]{:S(2)}) collective-permute-start(bf16[64,1024]{1,0:T(8,128)(2,1)} %get-tuple-element.25.refs_0_), channel_id=1, source_target_pairs={{0,1},{1,0},{2,3},{3,2},{4,5},{5,4},{6,7},{7,6},{8,9},{9,8},{10,11... | collective-permute-start | bytes 393224 | tf_op jit(solution)/shard_map/ppermute | solution.py:19
  48.4 0.0 collective-permute-done.refs_1_
  48.4 3.5 %collective-permute-start.4 = (bf16[64,1024]{1,0:T(8,128)(2,1)S(1)}, bf16[64,1024]{1,0:T(8,128)(2,1)S(1)}, u32[]{:S(2)}, u32[]{:S(2)}) collective-permute-start(bf16[64,1024]{1,0:T(8,128)(2,1)S(1)} %collective-permute-done.refs_1_), channel_id=1, source_target_pairs={{0,1},{1,0},{2,3},{3,2},{4,5},{5,4},{6,7},{7,6},{8,9},{9,8},{10,11... | collective-permute-start | bytes 393224 | tf_op jit(solution)/shard_map/ppermute | solution.py:19
  51.8 0.0 collective-permute-done.1.refs_2_
  51.8 0.0 copy-start.4
  51.8 0.1 collective-permute-start.5
  52.0 0.0 collective-permute-done.2.refs_3_
  52.0 0.0 copy-start.5
  52.0 1.7 collective-permute-start.6
  53.7 0.0 collective-permute-done.3.refs_4_
  53.7 0.0 collective-permute-done.4.refs_5_
  53.7 0.0 copy-start.7
  53.7 0.0 collective-permute-done.5.refs_6_
  53.7 0.0 copy-start.8
  53.7 0.9 collective-permute-done.6.refs_7_
  54.7 0.0 copy-done.3
  54.7 0.0 copy-done.4
  54.7 0.0 copy-done.5
  54.7 0.0 copy-done.6
  54.7 0.0 copy-done.7
  54.7 0.0 copy-done.8
  54.7 0.0 copy-start.9
  54.7 0.7 copy-done.9
  55.3 1.3 stack.1.weight_ref
  56.7 0.0 all-to-all-done.x_ref
  56.7 1.6 shard_map.136
  58.3 12.7 %all-to-all-start.1 = ((bf16[64,8,512]{2,1,0:T(8,128)(2,1)}), bf16[64,8,512]{2,1,0:T(8,128)(2,1)S(1)}, u32[]{:S(2)}, u32[]{:S(2)}) async-start(bf16[64,8,512]{2,1,0:T(8,128)(2,1)} %shard_map.136), calls=%async_computation.1 | async-start | bytes 1048576 | tf_op jit(solution)/shard_map/all_to_all | solution.py:564
  70.9 0.0 copy-start.10
  70.9 0.0 copy-start
  71.0 0.0 copy-start.1
  71.0 0.0 copy-start.2
  71.0 144.1 %halves.1 = (bf16[2048,384]{1,0:T(8,128)(2,1)S(1)}, bf16[2048,384]{1,0:T(8,128)(2,1)}, bf16[2048,384]{1,0:T(8,128)(2,1)}, bf16[384,2048]{1,0:T(8,128)(2,1)}) custom-call(bf16[1,4096,384]{2,1,0:T(8,128)(2,1)} %gate_hbm.1, bf16[1,4096,384]{2,1,0:T(8,128)(2,1)} %up_hbm.3, bf16[1,384,4096]{2,1,0:T(8,128)(2,1)} %down_hbm.3), custom_call_target="tpu_custom_call" | custom-call | tf_op jit(solution)/shard_map/halves/pallas_call | solution.py:246
  215.1 0.8 collective-permute-start.8
  215.9 0.1 collective-permute-start.9
  216.0 0.4 collective-permute-start.10
  216.4 0.0 copy-done.10
  216.4 0.0 all-to-all-done.1.x_ref
  216.4 0.0 copy-done
  216.4 0.2 shard_map.137
  216.7 0.5 collective-permute-start.7
  217.1 0.0 copy-done.1
  217.1 0.0 copy-done.2
  217.1 0.2 shard_map.138
  217.3 6.4 %collective-permute-done.7.other_ref = bf16[2,8,512]{2,1,0:T(8,128)(2,1)S(1)} collective-permute-done((bf16[2,8,512]{2,1,0:T(8,128)(2,1)S(1)}, bf16[2,8,512]{2,1,0:T(8,128)(2,1)S(1)}, u32[]{:S(2)}, u32[]{:S(2)}) %collective-permute-start.7) | collective-permute-done | bytes 16416 | tf_op jit(solution)/shard_map/ppermute | solution.py:19
  223.7 1.1 shard_map.139
  224.8 13.4 %all-to-all-start.2 = ((bf16[64,8,512]{2,1,0:T(8,128)(2,1)}), bf16[64,8,512]{2,1,0:T(8,128)(2,1)S(1)}, u32[]{:S(2)}, u32[]{:S(2)}) async-start(bf16[64,8,512]{2,1,0:T(8,128)(2,1)} %shard_map.139), calls=%async_computation.2 | async-start | bytes 1048576 | tf_op jit(solution)/shard_map/all_to_all | solution.py:567
  238.3 0.0 collective-permute-done.8.gate_moved
  238.3 0.0 collective-permute-done.9.up_moved
  238.3 0.0 collective-permute-done.10.down_moved
  238.3 15.3 %all-to-all-done.2.x_ref = bf16[64,8,512]{2,1,0:T(8,128)(2,1)S(1)} async-done(((bf16[64,8,512]{2,1,0:T(8,128)(2,1)}), bf16[64,8,512]{2,1,0:T(8,128)(2,1)S(1)}, u32[]{:S(2)}, u32[]{:S(2)}) %all-to-all-start.2) | async-done | bytes 524320 | tf_op jit(solution)/shard_map/all_to_all | solution.py:567
  253.6 3.8 %gate_up.1 = (f32[128,1536]{1,0:T(8,128)S(1)}, bf16[128,1536]{1,0:T(8,128)(2,1)S(1)}, bf16[768,2048]{1,0:T(8,128)(2,1)S(1)}) custom-call(bf16[64,8,512]{2,1,0:T(8,128)(2,1)S(1)} %all-to-all-done.2.x_ref, bf16[2048,384]{1,0:T(8,128)(2,1)S(1)} %get-tuple-element.33.gate_ref, bf16[1,4096,384]{2,1,0:T(8,128)(2,1)} %up_hbm.3, bf16[1,384,4096]{2,1,0:T(8,128)(2,1)} %down_hbm.3, ...), custom_call_target="tpu_custom_call" | custom-call | tf_op jit(solution)/shard_map/gate_up/pallas_call | solution.py:449
  257.4 3.3 %collective-permute-start.11 = (bf16[128,1536]{1,0:T(8,128)(2,1)S(1)}, bf16[128,1536]{1,0:T(8,128)(2,1)S(1)}, u32[]{:S(2)}, u32[]{:S(2)}) collective-permute-start(bf16[128,1536]{1,0:T(8,128)(2,1)S(1)} %get-tuple-element.38), channel_id=1, source_target_pairs={{0,1},{1,0},{2,3},{3,2},{4,5},{5,4},{6,7},{7,6},{8,9},{9,8},{10,11... | collective-permute-start | bytes 1179656 | tf_op jit(solution)/shard_map/ppermute | solution.py:19
  260.7 1.3 collective-permute-done.11.arrived_ref
  262.1 1.7 shard_map.140
  263.8 22.6 %all_to_all.20.x_ref = bf16[64,8,512]{2,1,0:T(8,128)(2,1)S(1)} all-to-all(bf16[64,8,512]{2,1,0:T(8,128)(2,1)} %shard_map.140), channel_id=1, replica_groups=mesh['groups'=2,'expert'=64,'replica'=2] {'expert'}, dimensions={0} | all-to-all | bytes 1048576 | tf_op jit(solution)/shard_map/all_to_all | solution.py:570
  286.4 0.2 shard_map.141
  286.6 3.1 %collective-permute-start.12 = (f32[2,8,512]{2,1,0:T(8,128)S(1)}, f32[2,8,512]{2,1,0:T(8,128)S(1)}, u32[]{:S(2)}, u32[]{:S(2)}) collective-permute-start(f32[2,8,512]{2,1,0:T(8,128)S(1)} %get-tuple-element.42), channel_id=1, source_target_pairs={{0,1},{1,0},{2,3},{3,2},{4,5},{5,4},{6,7},{7,6},{8,9},{9,8},{10,11... | collective-permute-start | bytes 98312 | tf_op jit(solution)/shard_map/ppermute | solution.py:19
  289.6 0.9 collective-permute-done.12.other_ref
  290.5 0.6 shard_map.142
  (3 shorter events, 0.0 us)
Async XLA Ops:
  17.8 38.9 %all-to-all-start = ((bf16[64,8,256]{2,1,0:T(8,128)(2,1)}), bf16[64,8,256]{2,1,0:T(8,128)(2,1)S(1)}, u32[]{:S(2)}, u32[]{:S(2)}) async-start(bf16[64,8,256]{2,1,0:T(8,128)(2,1)} %get-tuple-element.24), calls=%async_computation | async-start | bytes 524288 | tf_op jit(solution)/shard_map/all_to_all | solution.py:556
  39.7 8.7 %collective-permute-start = (bf16[64,1024]{1,0:T(8,128)(2,1)}, bf16[64,1024]{1,0:T(8,128)(2,1)S(1)}, u32[]{:S(2)}, u32[]{:S(2)}) collective-permute-start(bf16[64,1024]{1,0:T(8,128)(2,1)} %get-tuple-element.26), channel_id=1, source_target_pairs={{0,2},{2,0},{4,6},{6,4},{8,10},{10,8},{12,14},{14,12},{16,18},{18,... | collective-permute-start | bytes 393224 | tf_op jit(solution)/shard_map/ppermute | solution.py:554
  39.9 11.9 %collective-permute-start.1 = (bf16[64,1024]{1,0:T(8,128)(2,1)}, bf16[64,1024]{1,0:T(8,128)(2,1)S(1)}, u32[]{:S(2)}, u32[]{:S(2)}) collective-permute-start(bf16[64,1024]{1,0:T(8,128)(2,1)} %get-tuple-element.27), channel_id=1, source_target_pairs={{0,16},{2,18},{4,20},{6,22},{8,24},{10,26},{12,28},{14,30},{16,0},... | collective-permute-start | bytes 393224 | tf_op jit(solution)/shard_map/ppermute | solution.py:554
  41.1 10.8 %collective-permute-start.2 = (bf16[64,1024]{1,0:T(8,128)(2,1)}, bf16[64,1024]{1,0:T(8,128)(2,1)S(1)}, u32[]{:S(2)}, u32[]{:S(2)}) collective-permute-start(bf16[64,1024]{1,0:T(8,128)(2,1)} %get-tuple-element.28), channel_id=1, source_target_pairs={{0,18},{2,16},{4,22},{6,20},{8,26},{10,24},{12,30},{14,28},{16,2},... | collective-permute-start | bytes 393224 | tf_op jit(solution)/shard_map/ppermute | solution.py:554
  42.4 11.2 %collective-permute-start.3 = (bf16[64,1024]{1,0:T(8,128)(2,1)}, bf16[64,1024]{1,0:T(8,128)(2,1)S(1)}, u32[]{:S(2)}, u32[]{:S(2)}) collective-permute-start(bf16[64,1024]{1,0:T(8,128)(2,1)} %get-tuple-element.25.refs_0_), channel_id=1, source_target_pairs={{0,1},{1,0},{2,3},{3,2},{4,5},{5,4},{6,7},{7,6},{8,9},{9,8},{10,11... | collective-permute-start | bytes 393224 | tf_op jit(solution)/shard_map/ppermute | solution.py:19
  48.4 6.3 %copy-start.3 = (bf16[64,1024]{1,0:T(8,128)(2,1)}, bf16[64,1024]{1,0:T(8,128)(2,1)S(1)}, u32[]{:S(2)}) copy-start(bf16[64,1024]{1,0:T(8,128)(2,1)S(1)} %collective-permute-done.refs_1_) | copy-start | bytes 393220
  48.4 5.3 %collective-permute-start.4 = (bf16[64,1024]{1,0:T(8,128)(2,1)S(1)}, bf16[64,1024]{1,0:T(8,128)(2,1)S(1)}, u32[]{:S(2)}, u32[]{:S(2)}) collective-permute-start(bf16[64,1024]{1,0:T(8,128)(2,1)S(1)} %collective-permute-done.refs_1_), channel_id=1, source_target_pairs={{0,1},{1,0},{2,3},{3,2},{4,5},{5,4},{6,7},{7,6},{8,9},{9,8},{10,11... | collective-permute-start | bytes 393224 | tf_op jit(solution)/shard_map/ppermute | solution.py:19
  51.8 2.8 copy-start.4
  51.8 1.9 collective-permute-start.5
  52.0 2.7 copy-start.5
  52.0 2.7 collective-permute-start.6
  53.7 1.0 copy-start.6
  53.7 1.0 copy-start.7
  53.7 1.0 copy-start.8
  54.7 0.7 copy-start.9
  58.3 158.1 %all-to-all-start.1 = ((bf16[64,8,512]{2,1,0:T(8,128)(2,1)}), bf16[64,8,512]{2,1,0:T(8,128)(2,1)S(1)}, u32[]{:S(2)}, u32[]{:S(2)}) async-start(bf16[64,8,512]{2,1,0:T(8,128)(2,1)} %shard_map.136), calls=%async_computation.1 | async-start | bytes 1048576 | tf_op jit(solution)/shard_map/all_to_all | solution.py:564
  70.9 145.4 %copy-start.10 = (bf16[4096]{0:T(1024)(128)(2,1)S(1)}, bf16[4096]{0:T(1024)(128)(2,1)}, u32[]{:S(2)}) copy-start(bf16[4096]{0:T(1024)(128)(2,1)} %param.22) | copy-start | bytes 24580
  70.9 145.4 %copy-start = (bf16[4,4096]{1,0:T(4,128)(2,1)S(1)}, bf16[4,4096]{1,0:T(4,128)(2,1)}, u32[]{:S(2)}) copy-start(bf16[4,4096]{1,0:T(4,128)(2,1)} %residual_ref.1) | copy-start | bytes 98308
  71.0 146.1 %copy-start.1 = (s32[8,8]{1,0:T(8,128)S(1)}, s32[8,8]{1,0:T(8,128)}, u32[]{:S(2)}) copy-start(s32[8,8]{1,0:T(8,128)} %ids_ref.1) | copy-start | bytes 772
  71.0 146.1 %copy-start.2 = (f32[8,8]{1,0:T(8,128)S(1)}, f32[8,8]{1,0:T(8,128)}, u32[]{:S(2)}) copy-start(f32[8,8]{1,0:T(8,128)} %weight_ref.1) | copy-start | bytes 772
  215.1 23.2 %collective-permute-start.8 = (bf16[2048,384]{1,0:T(8,128)(2,1)}, bf16[2048,384]{1,0:T(8,128)(2,1)}, u32[]{:S(2)}, u32[]{:S(2)}) collective-permute-start(bf16[2048,384]{1,0:T(8,128)(2,1)} %get-tuple-element.34), channel_id=1, source_target_pairs={{0,1},{1,0},{2,3},{3,2},{4,5},{5,4},{6,7},{7,6},{8,9},{9,8},{10,11... | collective-permute-start | bytes 4718600 | tf_op jit(solution)/shard_map/ppermute | solution.py:19
  215.9 22.4 %collective-permute-start.9 = (bf16[2048,384]{1,0:T(8,128)(2,1)}, bf16[2048,384]{1,0:T(8,128)(2,1)}, u32[]{:S(2)}, u32[]{:S(2)}) collective-permute-start(bf16[2048,384]{1,0:T(8,128)(2,1)} %get-tuple-element.35), channel_id=1, source_target_pairs={{0,1},{1,0},{2,3},{3,2},{4,5},{5,4},{6,7},{7,6},{8,9},{9,8},{10,11... | collective-permute-start | bytes 4718600 | tf_op jit(solution)/shard_map/ppermute | solution.py:19
  216.0 22.3 %collective-permute-start.10 = (bf16[384,2048]{1,0:T(8,128)(2,1)}, bf16[384,2048]{1,0:T(8,128)(2,1)}, u32[]{:S(2)}, u32[]{:S(2)}) collective-permute-start(bf16[384,2048]{1,0:T(8,128)(2,1)} %get-tuple-element.36), channel_id=1, source_target_pairs={{0,1},{1,0},{2,3},{3,2},{4,5},{5,4},{6,7},{7,6},{8,9},{9,8},{10,11... | collective-permute-start | bytes 4718600 | tf_op jit(solution)/shard_map/ppermute | solution.py:19
  216.7 7.1 %collective-permute-start.7 = (bf16[2,8,512]{2,1,0:T(8,128)(2,1)S(1)}, bf16[2,8,512]{2,1,0:T(8,128)(2,1)S(1)}, u32[]{:S(2)}, u32[]{:S(2)}) collective-permute-start(bf16[2,8,512]{2,1,0:T(8,128)(2,1)S(1)} %get-tuple-element.31), channel_id=1, source_target_pairs={{0,1},{1,0},{2,3},{3,2},{4,5},{5,4},{6,7},{7,6},{8,9},{9,8},{10,11... | collective-permute-start | bytes 49160 | tf_op jit(solution)/shard_map/ppermute | solution.py:19
  224.8 28.8 %all-to-all-start.2 = ((bf16[64,8,512]{2,1,0:T(8,128)(2,1)}), bf16[64,8,512]{2,1,0:T(8,128)(2,1)S(1)}, u32[]{:S(2)}, u32[]{:S(2)}) async-start(bf16[64,8,512]{2,1,0:T(8,128)(2,1)} %shard_map.139), calls=%async_computation.2 | async-start | bytes 1048576 | tf_op jit(solution)/shard_map/all_to_all | solution.py:567
  257.4 4.7 %collective-permute-start.11 = (bf16[128,1536]{1,0:T(8,128)(2,1)S(1)}, bf16[128,1536]{1,0:T(8,128)(2,1)S(1)}, u32[]{:S(2)}, u32[]{:S(2)}) collective-permute-start(bf16[128,1536]{1,0:T(8,128)(2,1)S(1)} %get-tuple-element.38), channel_id=1, source_target_pairs={{0,1},{1,0},{2,3},{3,2},{4,5},{5,4},{6,7},{7,6},{8,9},{9,8},{10,11... | collective-permute-start | bytes 1179656 | tf_op jit(solution)/shard_map/ppermute | solution.py:19
  286.6 3.9 %collective-permute-start.12 = (f32[2,8,512]{2,1,0:T(8,128)S(1)}, f32[2,8,512]{2,1,0:T(8,128)S(1)}, u32[]{:S(2)}, u32[]{:S(2)}) collective-permute-start(f32[2,8,512]{2,1,0:T(8,128)S(1)} %get-tuple-element.42), channel_id=1, source_target_pairs={{0,1},{1,0},{2,3},{3,2},{4,5},{5,4},{6,7},{7,6},{8,9},{9,8},{10,11... | collective-permute-start | bytes 98312 | tf_op jit(solution)/shard_map/ppermute | solution.py:19

commit v4 on v3

--- a/solution.py
+++ b/solution.py
@@ -70,6 +70,7 @@
     len_ref,
     keys,
     values,
+    pieces,
     rows,
     mixed,
     sems,
@@ -99,13 +100,13 @@
         copies.append(pair)
     chip = lax.axis_index(CHIPS)
     place = chip // side % 2 * 2 + chip % 2
-    sliced = []
+    sliced, stored = [], []
     for d, piece in enumerate((piece0, piece1, piece2, piece3)):
         cols = piece.shape[1]
         at = pl.multiple_of((place ^ d) * cols, cols)
-        sliced.append(
-            pltpu.make_async_copy(weight_hbm.at[:, pl.ds(at, cols)], piece, few.at[len(small) + d])
-        )
+        source = weight_hbm.at[:, pl.ds(at, cols)]
+        sliced.append(pltpu.make_async_copy(source, pieces.at[d], few.at[len(small) + d]))
+        stored.append(pltpu.make_async_copy(pieces.at[d], piece, few.at[len(small) + 4 + d]))
         sliced[-1].start()
     for copy in small:
         copy.wait()
@@ -147,6 +148,10 @@
             for a in range(2):
                 start = g * group * seq_count + a * seq_count + b
                 mixed[pl.ds(start, side, stride=2 * seq_count), :] = out[a * side : (a + 1) * side]
+        if b == seq_count // 2:
+            for d in range(4):
+                sliced[d].wait()
+                stored[d].start()
     tile = 2 * seq_count
     for g in range(kv_count):
         for y in range(side):
@@ -156,7 +161,7 @@
                 far = pltpu.roll(near, seq_count, 0)
                 out_ref[2 * g * side + y, :, lanes[part]] = near.astype(BF16)
                 out_ref[(2 * g + 1) * side + y, :, lanes[part]] = far.astype(BF16)
-    for copy in sliced:
+    for copy in stored:
         copy.wait()
 
 
@@ -178,10 +183,11 @@
             pltpu.SMEM(kv_len.shape, jnp.int32),
             pltpu.VMEM(stored_keys.shape, BF16),
             pltpu.VMEM(stored_values.shape, BF16),
+            pltpu.VMEM((4, rows, cols // 4), BF16),
             pltpu.VMEM((seq_count * heads, HEAD_WIDTH), F32),
             pltpu.VMEM((seq_count * heads, HEAD_WIDTH), F32),
             pltpu.SemaphoreType.DMA((2, seq_count)),
-            pltpu.SemaphoreType.DMA((8,)),
+            pltpu.SemaphoreType.DMA((12,)),
         ],
         compiler_params=pltpu.CompilerParams(vmem_limit_bytes=8 * MIB),
     )(
@@ -225,19 +231,24 @@
 
 
 def halves_body(gate_hbm, up_hbm, down_hbm, kept_ref, *refs):
-    outs, sems = refs[:3], refs[3]
+    outs, (tall, wide, sems) = refs[:3], refs[3:]
     core = lax.axis_index(CORES)
     half = kept_ref.shape[0]
     kept, given = (pl.ds(pl.multiple_of(j * half, half), half) for j in (core, 1 - core))
-    copy_all(
-        (
-            (gate_hbm.at[0, kept, :], kept_ref),
-            (gate_hbm.at[0, given, :], outs[0]),
-            (up_hbm.at[0, given, :], outs[1]),
-            (down_hbm.at[0, :, given], outs[2]),
-        ),
-        sems,
-    )
+    held = (tall.at[0], tall.at[1], wide)
+    sources = (gate_hbm.at[0, given, :], up_hbm.at[0, given, :], down_hbm.at[0, :, given])
+    loads = [pltpu.make_async_copy(sources[j], held[j], sems.at[j]) for j in range(3)]
+    stores = [pltpu.make_async_copy(held[j], outs[j], sems.at[3 + j]) for j in range(3)]
+    own = pltpu.make_async_copy(gate_hbm.at[0, kept, :], kept_ref, sems.at[6])
+    for load in loads:
+        load.start()
+    own.start()
+    for load, store in zip(loads, stores, strict=True):
+        load.wait()
+        store.start()
+    own.wait()
+    for store in stores:
+        store.wait()
 
 
 def halves(w_gate, w_up, w_down):
@@ -249,8 +260,12 @@
         out_shape=[pltpu.VMEM(tall, BF16)] + [pltpu.HBM(dims, BF16) for dims in (tall, tall, wide)],
         in_specs=[IN_HBM] * 3,
         out_specs=[IN_VMEM] + [IN_HBM] * 3,
-        scratch_shapes=[pltpu.SemaphoreType.DMA((4,))],
-        compiler_params=pltpu.CompilerParams(vmem_limit_bytes=2 * MIB),
+        scratch_shapes=[
+            pltpu.VMEM((2, *tall), BF16),
+            pltpu.VMEM(wide, BF16),
+            pltpu.SemaphoreType.DMA((7,)),
+        ],
+        compiler_params=pltpu.CompilerParams(vmem_limit_bytes=6 * MIB),
     )(*map(in_hbm, (w_gate, w_up, w_down)))
 
 

time: 292 us -> 139 us (0.48)
  Pallas kernels: 173 us -> 19.3 us
  waiting for transfers between devices: 24.9 us -> 29.3 us
  starting transfers between devices: 70 us -> 66.4 us
    pallas_call x1, Pallas kernels: 144 us -> 4.03 us  [halves(): pl.pallas_call(halves_body, name='halves', out_shape=[pltpu.VMEM(tall, BF...]
    pallas_call x1, Pallas kernels: 17.8 us -> 4.49 us  [attend(): pl.pallas_call(attend_body, name='attend', out_shape=[pltpu.HBM((heads, 2...]
    all_to_all x1, waiting for transfers between devices: 0.01 us -> 10 us  [on_device(): came_back = lax.all_to_all(sums, CHIPS, 0, 0, tiled=True)]
    all_to_all x1, starting transfers between devices: 13.4 us -> 7.19 us  [on_device(): incoming = lax.all_to_all(outgoing, CHIPS, 0, 0, tiled=True)]
    ppermute x10, waiting for transfers between devices: 9.58 us -> 3.8 us  [swapped(): return lax.ppermute(x, CORES, [(0, 1), (1, 0)])]
  transfers between devices with their start and end apart: 16 -> 16, of which waited for: 5 -> 6; matrix products, arithmetic and copies ran while one was open for 0% -> 0% of each run, Pallas kernels for 50% -> 5%
where the time goes in v4:
time: 139 us
  starting transfers between devices  66.4 us (48%)
  waiting for transfers between devices  29.3 us (21%)
  blocking collectives  22.7 us (16%)
  Pallas kernels  19.3 us (14%)
    all_to_all x1, blocking collectives, on_device(): returned = lax.all_to_all(expert_out, CHIPS, 0, 0, tiled=True)  22.7 us
    ppermute x10, starting transfers between devices, swapped(): return lax.ppermute(x, CORES, [(0, 1), (1, 0)])  22 us
    all_to_all x1, starting transfers between devices, on_device(): tokens = lax.all_to_all(outgoing, CHIPS, 0, 0, tiled=True)  21.8 us
    all_to_all x1, waiting for transfers between devices, on_device(): incoming = lax.all_to_all(outgoing, CHIPS, 0, 0, tiled=True)  15.5 us
    all_to_all x1, starting transfers between devices, on_device(): came_back = lax.all_to_all(sums, CHIPS, 0, 0, tiled=True)  12.7 us
    all_to_all x1, waiting for transfers between devices, on_device(): came_back = lax.all_to_all(sums, CHIPS, 0, 0, tiled=True)  10 us
    all_to_all x1, starting transfers between devices, on_device(): incoming = lax.all_to_all(outgoing, CHIPS, 0, 0, tiled=True)  7.19 us
    pallas_call x1, Pallas kernels, attend(): pl.pallas_call(attend_body, name='attend', out_shape=[pltpu.HBM((heads, 2...  4.49 us
  transfers between devices with their start and end apart: 16, of which 6 were waited for; matrix products, arithmetic and copies ran while one was open for 0% of the time, Pallas kernels for 5%

profile of v4, /device:TPU:513, one launch (start us, length us, event | category | flops | bytes accessed | tf_op | source)
XLA Modules:
  0.0 138.7 jit_solution(7926428976440422944)
XLA Ops:
  0.0 4.5 %attend.1 = (bf16[64,8,256]{2,1,0:T(8,128)(2,1)}, bf16[64,1024]{1,0:T(8,128)(2,1)}, bf16[64,1024]{1,0:T(8,128)(2,1)}, bf16[64,1024]{1,0:T(8,128)(2,1)}, bf16[64,1024]{1,0:T(8,128)(2,1)}) custom-call(bf16[4,8192]{1,0:T(4,128)(2,1)} %q_hbm.1, bf16[4,512]{1,0:T(4,128)(2,1)} %tk_hbm.1, bf16[4,512]{1,0:T(4,128)(2,1)} %tv_hbm.1, s32[4]{0:T(128)} %len_hbm.1, ...), custom_call_target="tpu_custom_call" | custom-call | tf_op jit(solution)/shard_map/attend/pallas_call | solution.py:172
  4.5 21.8 %all-to-all-start = ((bf16[64,8,256]{2,1,0:T(8,128)(2,1)}), bf16[64,8,256]{2,1,0:T(8,128)(2,1)S(1)}, u32[]{:S(2)}, u32[]{:S(2)}) async-start(bf16[64,8,256]{2,1,0:T(8,128)(2,1)} %get-tuple-element.24), calls=%async_computation | async-start | bytes 524288 | tf_op jit(solution)/shard_map/all_to_all | solution.py:571
  26.3 0.3 collective-permute-start
  26.6 1.2 collective-permute-start.1
  27.8 1.3 collective-permute-start.2
  29.1 5.9 %collective-permute-start.3 = (bf16[64,1024]{1,0:T(8,128)(2,1)}, bf16[64,1024]{1,0:T(8,128)(2,1)S(1)}, u32[]{:S(2)}, u32[]{:S(2)}) collective-permute-start(bf16[64,1024]{1,0:T(8,128)(2,1)} %get-tuple-element.25.refs_0_), channel_id=1, source_target_pairs={{0,1},{1,0},{2,3},{3,2},{4,5},{5,4},{6,7},{7,6},{8,9},{9,8},{10,11... | collective-permute-start | bytes 393224 | tf_op jit(solution)/shard_map/ppermute | solution.py:19
  35.0 0.0 collective-permute-done.refs_1_
  35.0 0.0 copy-start.3
  35.0 3.5 %collective-permute-start.4 = (bf16[64,1024]{1,0:T(8,128)(2,1)S(1)}, bf16[64,1024]{1,0:T(8,128)(2,1)S(1)}, u32[]{:S(2)}, u32[]{:S(2)}) collective-permute-start(bf16[64,1024]{1,0:T(8,128)(2,1)S(1)} %collective-permute-done.refs_1_), channel_id=1, source_target_pairs={{0,1},{1,0},{2,3},{3,2},{4,5},{5,4},{6,7},{7,6},{8,9},{9,8},{10,11... | collective-permute-start | bytes 393224 | tf_op jit(solution)/shard_map/ppermute | solution.py:19
  38.5 0.0 collective-permute-done.1.refs_2_
  38.5 0.0 copy-start.4
  38.5 0.1 collective-permute-start.5
  38.6 0.0 collective-permute-done.2.refs_3_
  38.6 1.7 %collective-permute-start.6 = (bf16[64,1024]{1,0:T(8,128)(2,1)S(1)}, bf16[64,1024]{1,0:T(8,128)(2,1)S(1)}, u32[]{:S(2)}, u32[]{:S(2)}) collective-permute-start(bf16[64,1024]{1,0:T(8,128)(2,1)S(1)} %collective-permute-done.2.refs_3_), channel_id=1, source_target_pairs={{0,1},{1,0},{2,3},{3,2},{4,5},{5,4},{6,7},{7,6},{8,9},{9,8},{10,11... | collective-permute-start | bytes 393224 | tf_op jit(solution)/shard_map/ppermute | solution.py:19
  40.3 0.0 collective-permute-done.3.refs_4_
  40.3 0.0 collective-permute-done.4.refs_5_
  40.3 0.0 copy-start.7
  40.4 0.0 collective-permute-done.5.refs_6_
  40.4 0.0 copy-start.8
  40.4 0.9 collective-permute-done.6.refs_7_
  41.3 0.0 copy-done.3
  41.3 0.0 copy-done.4
  41.3 0.0 copy-done.5
  41.3 0.0 copy-done.6
  41.3 0.0 copy-done.7
  41.3 0.0 copy-done.8
  41.4 0.0 copy-start.9
  41.4 0.7 copy-done.9
  42.0 1.3 stack.1.weight_ref
  43.4 0.0 all-to-all-done.x_ref
  43.4 1.5 %shard_map.136 = bf16[64,8,512]{2,1,0:T(8,128)(2,1)} custom-call(bf16[64,8,256]{2,1,0:T(8,128)(2,1)S(1)} %all-to-all-done.x_ref, bf16[2,256,1024]{2,1,0:T(8,128)(2,1)S(1)} %stack.1.weight_ref), custom_call_target="tpu_custom_call" | custom-call | tf_op jit(solution)/shard_map/pallas_call | solution.py:292
  44.9 12.7 %all-to-all-start.1 = ((bf16[64,8,512]{2,1,0:T(8,128)(2,1)}), bf16[64,8,512]{2,1,0:T(8,128)(2,1)S(1)}, u32[]{:S(2)}, u32[]{:S(2)}) async-start(bf16[64,8,512]{2,1,0:T(8,128)(2,1)} %shard_map.136), calls=%async_computation.1 | async-start | bytes 1048576 | tf_op jit(solution)/shard_map/all_to_all | solution.py:579
  57.6 0.0 copy-start.10
  57.6 0.0 copy-start
  57.6 0.0 copy-start.1
  57.6 0.0 copy-start.2
  57.7 4.0 %halves.1 = (bf16[2048,384]{1,0:T(8,128)(2,1)S(1)}, bf16[2048,384]{1,0:T(8,128)(2,1)}, bf16[2048,384]{1,0:T(8,128)(2,1)}, bf16[384,2048]{1,0:T(8,128)(2,1)}) custom-call(bf16[1,4096,384]{2,1,0:T(8,128)(2,1)} %gate_hbm.1, bf16[1,4096,384]{2,1,0:T(8,128)(2,1)} %up_hbm.3, bf16[1,384,4096]{2,1,0:T(8,128)(2,1)} %down_hbm.3), custom_call_target="tpu_custom_call" | custom-call | tf_op jit(solution)/shard_map/halves/pallas_call | solution.py:257
  61.7 0.8 collective-permute-start.8
  62.5 0.1 collective-permute-start.9
  62.6 0.4 collective-permute-start.10
  63.0 0.0 copy-done.10
  63.0 10.0 %all-to-all-done.1.x_ref = bf16[64,8,512]{2,1,0:T(8,128)(2,1)S(1)} async-done(((bf16[64,8,512]{2,1,0:T(8,128)(2,1)}), bf16[64,8,512]{2,1,0:T(8,128)(2,1)S(1)}, u32[]{:S(2)}, u32[]{:S(2)}) %all-to-all-start.1) | async-done | bytes 524320 | tf_op jit(solution)/shard_map/all_to_all | solution.py:579
  73.0 0.0 copy-done
  73.0 0.2 shard_map.137
  73.3 3.4 %collective-permute-start.7 = (bf16[2,8,512]{2,1,0:T(8,128)(2,1)S(1)}, bf16[2,8,512]{2,1,0:T(8,128)(2,1)S(1)}, u32[]{:S(2)}, u32[]{:S(2)}) collective-permute-start(bf16[2,8,512]{2,1,0:T(8,128)(2,1)S(1)} %get-tuple-element.31), channel_id=1, source_target_pairs={{0,1},{1,0},{2,3},{3,2},{4,5},{5,4},{6,7},{7,6},{8,9},{9,8},{10,11... | collective-permute-start | bytes 49160 | tf_op jit(solution)/shard_map/ppermute | solution.py:19
  76.7 0.0 copy-done.1
  76.7 0.0 copy-done.2
  76.7 0.2 shard_map.138
  76.9 0.6 collective-permute-done.7.other_ref
  77.5 1.1 shard_map.139
  78.6 7.2 %all-to-all-start.2 = ((bf16[64,8,512]{2,1,0:T(8,128)(2,1)}), bf16[64,8,512]{2,1,0:T(8,128)(2,1)S(1)}, u32[]{:S(2)}, u32[]{:S(2)}) async-start(bf16[64,8,512]{2,1,0:T(8,128)(2,1)} %shard_map.139), calls=%async_computation.2 | async-start | bytes 1048576 | tf_op jit(solution)/shard_map/all_to_all | solution.py:582
  85.8 0.0 collective-permute-done.8.gate_moved
  85.8 0.0 collective-permute-done.9.up_moved
  85.8 0.0 collective-permute-done.10.down_moved
  85.8 15.5 %all-to-all-done.2.x_ref = bf16[64,8,512]{2,1,0:T(8,128)(2,1)S(1)} async-done(((bf16[64,8,512]{2,1,0:T(8,128)(2,1)}), bf16[64,8,512]{2,1,0:T(8,128)(2,1)S(1)}, u32[]{:S(2)}, u32[]{:S(2)}) %all-to-all-start.2) | async-done | bytes 524320 | tf_op jit(solution)/shard_map/all_to_all | solution.py:582
  101.3 3.8 %gate_up.1 = (f32[128,1536]{1,0:T(8,128)S(1)}, bf16[128,1536]{1,0:T(8,128)(2,1)S(1)}, bf16[768,2048]{1,0:T(8,128)(2,1)S(1)}) custom-call(bf16[64,8,512]{2,1,0:T(8,128)(2,1)S(1)} %all-to-all-done.2.x_ref, bf16[2048,384]{1,0:T(8,128)(2,1)S(1)} %get-tuple-element.33.gate_ref, bf16[1,4096,384]{2,1,0:T(8,128)(2,1)} %up_hbm.3, bf16[1,384,4096]{2,1,0:T(8,128)(2,1)} %down_hbm.3, ...), custom_call_target="tpu_custom_call" | custom-call | tf_op jit(solution)/shard_map/gate_up/pallas_call | solution.py:464
  105.2 3.0 %collective-permute-start.11 = (bf16[128,1536]{1,0:T(8,128)(2,1)S(1)}, bf16[128,1536]{1,0:T(8,128)(2,1)S(1)}, u32[]{:S(2)}, u32[]{:S(2)}) collective-permute-start(bf16[128,1536]{1,0:T(8,128)(2,1)S(1)} %get-tuple-element.38), channel_id=1, source_target_pairs={{0,1},{1,0},{2,3},{3,2},{4,5},{5,4},{6,7},{7,6},{8,9},{9,8},{10,11... | collective-permute-start | bytes 1179656 | tf_op jit(solution)/shard_map/ppermute | solution.py:19
  108.2 1.3 collective-permute-done.11.arrived_ref
  109.5 1.7 %shard_map.140 = bf16[64,8,512]{2,1,0:T(8,128)(2,1)} custom-call(f32[128,1536]{1,0:T(8,128)S(1)} %get-tuple-element.37.part_ref, bf16[128,1536]{1,0:T(8,128)(2,1)S(1)} %collective-permute-done.11.arrived_ref, bf16[768,2048]{1,0:T(8,128)(2,1)S(1)} %get-tuple-element.39.down_ref), custom_call_target="tpu_custom_call" | custom-call | tf_op jit(solution)/shard_map/pallas_call | solution.py:509
  111.2 22.7 %all_to_all.20.x_ref = bf16[64,8,512]{2,1,0:T(8,128)(2,1)S(1)} all-to-all(bf16[64,8,512]{2,1,0:T(8,128)(2,1)} %shard_map.140), channel_id=1, replica_groups=mesh['groups'=2,'expert'=64,'replica'=2] {'expert'}, dimensions={0} | all-to-all | bytes 1048576 | tf_op jit(solution)/shard_map/all_to_all | solution.py:585
  133.9 0.2 shard_map.141
  134.1 3.1 %collective-permute-start.12 = (f32[2,8,512]{2,1,0:T(8,128)S(1)}, f32[2,8,512]{2,1,0:T(8,128)S(1)}, u32[]{:S(2)}, u32[]{:S(2)}) collective-permute-start(f32[2,8,512]{2,1,0:T(8,128)S(1)} %get-tuple-element.42), channel_id=1, source_target_pairs={{0,1},{1,0},{2,3},{3,2},{4,5},{5,4},{6,7},{7,6},{8,9},{9,8},{10,11... | collective-permute-start | bytes 98312 | tf_op jit(solution)/shard_map/ppermute | solution.py:19
  137.2 0.9 collective-permute-done.12.other_ref
  138.1 0.6 shard_map.142
  (3 shorter events, 0.0 us)
Async XLA Ops:
  4.5 38.9 %all-to-all-start = ((bf16[64,8,256]{2,1,0:T(8,128)(2,1)}), bf16[64,8,256]{2,1,0:T(8,128)(2,1)S(1)}, u32[]{:S(2)}, u32[]{:S(2)}) async-start(bf16[64,8,256]{2,1,0:T(8,128)(2,1)} %get-tuple-element.24), calls=%async_computation | async-start | bytes 524288 | tf_op jit(solution)/shard_map/all_to_all | solution.py:571
  26.3 8.7 %collective-permute-start = (bf16[64,1024]{1,0:T(8,128)(2,1)}, bf16[64,1024]{1,0:T(8,128)(2,1)S(1)}, u32[]{:S(2)}, u32[]{:S(2)}) collective-permute-start(bf16[64,1024]{1,0:T(8,128)(2,1)} %get-tuple-element.26), channel_id=1, source_target_pairs={{0,2},{2,0},{4,6},{6,4},{8,10},{10,8},{12,14},{14,12},{16,18},{18,... | collective-permute-start | bytes 393224 | tf_op jit(solution)/shard_map/ppermute | solution.py:569
  26.6 11.9 %collective-permute-start.1 = (bf16[64,1024]{1,0:T(8,128)(2,1)}, bf16[64,1024]{1,0:T(8,128)(2,1)S(1)}, u32[]{:S(2)}, u32[]{:S(2)}) collective-permute-start(bf16[64,1024]{1,0:T(8,128)(2,1)} %get-tuple-element.27), channel_id=1, source_target_pairs={{0,16},{2,18},{4,20},{6,22},{8,24},{10,26},{12,28},{14,30},{16,0},... | collective-permute-start | bytes 393224 | tf_op jit(solution)/shard_map/ppermute | solution.py:569
  27.8 10.9 %collective-permute-start.2 = (bf16[64,1024]{1,0:T(8,128)(2,1)}, bf16[64,1024]{1,0:T(8,128)(2,1)S(1)}, u32[]{:S(2)}, u32[]{:S(2)}) collective-permute-start(bf16[64,1024]{1,0:T(8,128)(2,1)} %get-tuple-element.28), channel_id=1, source_target_pairs={{0,18},{2,16},{4,22},{6,20},{8,26},{10,24},{12,30},{14,28},{16,2},... | collective-permute-start | bytes 393224 | tf_op jit(solution)/shard_map/ppermute | solution.py:569
  29.1 11.2 %collective-permute-start.3 = (bf16[64,1024]{1,0:T(8,128)(2,1)}, bf16[64,1024]{1,0:T(8,128)(2,1)S(1)}, u32[]{:S(2)}, u32[]{:S(2)}) collective-permute-start(bf16[64,1024]{1,0:T(8,128)(2,1)} %get-tuple-element.25.refs_0_), channel_id=1, source_target_pairs={{0,1},{1,0},{2,3},{3,2},{4,5},{5,4},{6,7},{7,6},{8,9},{9,8},{10,11... | collective-permute-start | bytes 393224 | tf_op jit(solution)/shard_map/ppermute | solution.py:19
  35.0 6.3 %copy-start.3 = (bf16[64,1024]{1,0:T(8,128)(2,1)}, bf16[64,1024]{1,0:T(8,128)(2,1)S(1)}, u32[]{:S(2)}) copy-start(bf16[64,1024]{1,0:T(8,128)(2,1)S(1)} %collective-permute-done.refs_1_) | copy-start | bytes 393220
  35.0 5.3 %collective-permute-start.4 = (bf16[64,1024]{1,0:T(8,128)(2,1)S(1)}, bf16[64,1024]{1,0:T(8,128)(2,1)S(1)}, u32[]{:S(2)}, u32[]{:S(2)}) collective-permute-start(bf16[64,1024]{1,0:T(8,128)(2,1)S(1)} %collective-permute-done.refs_1_), channel_id=1, source_target_pairs={{0,1},{1,0},{2,3},{3,2},{4,5},{5,4},{6,7},{7,6},{8,9},{9,8},{10,11... | collective-permute-start | bytes 393224 | tf_op jit(solution)/shard_map/ppermute | solution.py:19
  38.5 2.8 %copy-start.4 = (bf16[64,1024]{1,0:T(8,128)(2,1)}, bf16[64,1024]{1,0:T(8,128)(2,1)S(1)}, u32[]{:S(2)}) copy-start(bf16[64,1024]{1,0:T(8,128)(2,1)S(1)} %collective-permute-done.1.refs_2_) | copy-start | bytes 393220
  38.5 1.9 %collective-permute-start.5 = (bf16[64,1024]{1,0:T(8,128)(2,1)S(1)}, bf16[64,1024]{1,0:T(8,128)(2,1)S(1)}, u32[]{:S(2)}, u32[]{:S(2)}) collective-permute-start(bf16[64,1024]{1,0:T(8,128)(2,1)S(1)} %collective-permute-done.1.refs_2_), channel_id=1, source_target_pairs={{0,1},{1,0},{2,3},{3,2},{4,5},{5,4},{6,7},{7,6},{8,9},{9,8},{10,11... | collective-permute-start | bytes 393224 | tf_op jit(solution)/shard_map/ppermute | solution.py:19
  38.6 2.7 %copy-start.5 = (bf16[64,1024]{1,0:T(8,128)(2,1)}, bf16[64,1024]{1,0:T(8,128)(2,1)S(1)}, u32[]{:S(2)}) copy-start(bf16[64,1024]{1,0:T(8,128)(2,1)S(1)} %collective-permute-done.2.refs_3_) | copy-start | bytes 393220
  38.6 2.7 %collective-permute-start.6 = (bf16[64,1024]{1,0:T(8,128)(2,1)S(1)}, bf16[64,1024]{1,0:T(8,128)(2,1)S(1)}, u32[]{:S(2)}, u32[]{:S(2)}) collective-permute-start(bf16[64,1024]{1,0:T(8,128)(2,1)S(1)} %collective-permute-done.2.refs_3_), channel_id=1, source_target_pairs={{0,1},{1,0},{2,3},{3,2},{4,5},{5,4},{6,7},{7,6},{8,9},{9,8},{10,11... | collective-permute-start | bytes 393224 | tf_op jit(solution)/shard_map/ppermute | solution.py:19
  40.3 1.0 copy-start.6
  40.3 1.0 copy-start.7
  40.4 1.0 copy-start.8
  41.4 0.7 copy-start.9
  44.9 28.1 %all-to-all-start.1 = ((bf16[64,8,512]{2,1,0:T(8,128)(2,1)}), bf16[64,8,512]{2,1,0:T(8,128)(2,1)S(1)}, u32[]{:S(2)}, u32[]{:S(2)}) async-start(bf16[64,8,512]{2,1,0:T(8,128)(2,1)} %shard_map.136), calls=%async_computation.1 | async-start | bytes 1048576 | tf_op jit(solution)/shard_map/all_to_all | solution.py:579
  57.6 5.4 %copy-start.10 = (bf16[4096]{0:T(1024)(128)(2,1)S(1)}, bf16[4096]{0:T(1024)(128)(2,1)}, u32[]{:S(2)}) copy-start(bf16[4096]{0:T(1024)(128)(2,1)} %param.22) | copy-start | bytes 24580
  57.6 15.4 %copy-start = (bf16[4,4096]{1,0:T(4,128)(2,1)S(1)}, bf16[4,4096]{1,0:T(4,128)(2,1)}, u32[]{:S(2)}) copy-start(bf16[4,4096]{1,0:T(4,128)(2,1)} %residual_ref.1) | copy-start | bytes 98308
  57.6 19.0 %copy-start.1 = (s32[8,8]{1,0:T(8,128)S(1)}, s32[8,8]{1,0:T(8,128)}, u32[]{:S(2)}) copy-start(s32[8,8]{1,0:T(8,128)} %ids_ref.1) | copy-start | bytes 772
  57.6 19.0 %copy-start.2 = (f32[8,8]{1,0:T(8,128)S(1)}, f32[8,8]{1,0:T(8,128)}, u32[]{:S(2)}) copy-start(f32[8,8]{1,0:T(8,128)} %weight_ref.1) | copy-start | bytes 772
  61.7 24.1 %collective-permute-start.8 = (bf16[2048,384]{1,0:T(8,128)(2,1)}, bf16[2048,384]{1,0:T(8,128)(2,1)}, u32[]{:S(2)}, u32[]{:S(2)}) collective-permute-start(bf16[2048,384]{1,0:T(8,128)(2,1)} %get-tuple-element.34), channel_id=1, source_target_pairs={{0,1},{1,0},{2,3},{3,2},{4,5},{5,4},{6,7},{7,6},{8,9},{9,8},{10,11... | collective-permute-start | bytes 4718600 | tf_op jit(solution)/shard_map/ppermute | solution.py:19
  62.5 23.3 %collective-permute-start.9 = (bf16[2048,384]{1,0:T(8,128)(2,1)}, bf16[2048,384]{1,0:T(8,128)(2,1)}, u32[]{:S(2)}, u32[]{:S(2)}) collective-permute-start(bf16[2048,384]{1,0:T(8,128)(2,1)} %get-tuple-element.35), channel_id=1, source_target_pairs={{0,1},{1,0},{2,3},{3,2},{4,5},{5,4},{6,7},{7,6},{8,9},{9,8},{10,11... | collective-permute-start | bytes 4718600 | tf_op jit(solution)/shard_map/ppermute | solution.py:19
  62.6 23.2 %collective-permute-start.10 = (bf16[384,2048]{1,0:T(8,128)(2,1)}, bf16[384,2048]{1,0:T(8,128)(2,1)}, u32[]{:S(2)}, u32[]{:S(2)}) collective-permute-start(bf16[384,2048]{1,0:T(8,128)(2,1)} %get-tuple-element.36), channel_id=1, source_target_pairs={{0,1},{1,0},{2,3},{3,2},{4,5},{5,4},{6,7},{7,6},{8,9},{9,8},{10,11... | collective-permute-start | bytes 4718600 | tf_op jit(solution)/shard_map/ppermute | solution.py:19
  73.3 4.2 %collective-permute-start.7 = (bf16[2,8,512]{2,1,0:T(8,128)(2,1)S(1)}, bf16[2,8,512]{2,1,0:T(8,128)(2,1)S(1)}, u32[]{:S(2)}, u32[]{:S(2)}) collective-permute-start(bf16[2,8,512]{2,1,0:T(8,128)(2,1)S(1)} %get-tuple-element.31), channel_id=1, source_target_pairs={{0,1},{1,0},{2,3},{3,2},{4,5},{5,4},{6,7},{7,6},{8,9},{9,8},{10,11... | collective-permute-start | bytes 49160 | tf_op jit(solution)/shard_map/ppermute | solution.py:19
  78.6 22.7 %all-to-all-start.2 = ((bf16[64,8,512]{2,1,0:T(8,128)(2,1)}), bf16[64,8,512]{2,1,0:T(8,128)(2,1)S(1)}, u32[]{:S(2)}, u32[]{:S(2)}) async-start(bf16[64,8,512]{2,1,0:T(8,128)(2,1)} %shard_map.139), calls=%async_computation.2 | async-start | bytes 1048576 | tf_op jit(solution)/shard_map/all_to_all | solution.py:582
  105.2 4.4 %collective-permute-start.11 = (bf16[128,1536]{1,0:T(8,128)(2,1)S(1)}, bf16[128,1536]{1,0:T(8,128)(2,1)S(1)}, u32[]{:S(2)}, u32[]{:S(2)}) collective-permute-start(bf16[128,1536]{1,0:T(8,128)(2,1)S(1)} %get-tuple-element.38), channel_id=1, source_target_pairs={{0,1},{1,0},{2,3},{3,2},{4,5},{5,4},{6,7},{7,6},{8,9},{9,8},{10,11... | collective-permute-start | bytes 1179656 | tf_op jit(solution)/shard_map/ppermute | solution.py:19
  134.1 3.9 %collective-permute-start.12 = (f32[2,8,512]{2,1,0:T(8,128)S(1)}, f32[2,8,512]{2,1,0:T(8,128)S(1)}, u32[]{:S(2)}, u32[]{:S(2)}) collective-permute-start(f32[2,8,512]{2,1,0:T(8,128)S(1)} %get-tuple-element.42), channel_id=1, source_target_pairs={{0,1},{1,0},{2,3},{3,2},{4,5},{5,4},{6,7},{7,6},{8,9},{9,8},{10,11... | collective-permute-start | bytes 98312 | tf_op jit(solution)/shard_map/ppermute | solution.py:19

commit v5 on v4

--- a/solution.py
+++ b/solution.py
@@ -59,7 +59,7 @@
     keys_hbm,
     values_hbm,
     weight_hbm,
-    out_ref,
+    out_hbm,
     piece0,
     piece1,
     piece2,
@@ -73,6 +73,8 @@
     pieces,
     rows,
     mixed,
+    scored,
+    out_ref,
     sems,
     few,
 ):
@@ -90,14 +92,12 @@
     ]
     for copy in small:
         copy.start()
-    copies = []
-    for b in range(seq_count):
-        pair = []
-        for j, (source, target) in enumerate(((keys_hbm, keys), (values_hbm, values))):
-            copy = pltpu.make_async_copy(source.at[b], target.at[b], sems.at[j, b])
-            copy.start()
-            pair.append(copy)
-        copies.append(pair)
+    copies = [
+        [pltpu.make_async_copy(source.at[b], target.at[b], sems.at[j, b]) for b in range(seq_count)]
+        for j, (source, target) in enumerate(((keys_hbm, keys), (values_hbm, values)))
+    ]
+    for copy in copies[0] + copies[1]:
+        copy.start()
     chip = lax.axis_index(CHIPS)
     place = chip // side % 2 * 2 + chip % 2
     sliced, stored = [], []
@@ -116,42 +116,46 @@
     inv_root = 1.0 / math.sqrt(HEAD_WIDTH)
     positions = lax.broadcasted_iota(jnp.int32, (head_count, cache_len), 1)
     lanes = [slice(g * HEAD_WIDTH, (g + 1) * HEAD_WIDTH) for g in range(kv_count)]
+    fresh = []
+    for copy in copies[0]:
+        copy.wait()
     for b in range(seq_count):
         query = rows[b * head_count : (b + 1) * head_count, :]
         latest = [tk_ref[b : b + 1, lanes[g]].astype(F32) for g in range(kv_count)]
         latest = jnp.concatenate([jnp.broadcast_to(v, (group, HEAD_WIDTH)) for v in latest])
-        fresh = jnp.sum(query * latest, axis=1, keepdims=True) * inv_root
+        fresh.append(jnp.sum(query * latest, axis=1, keepdims=True) * inv_root)
         query = query.astype(BF16)
-        copies[b][0].wait()
-        scores = [
-            lax.dot_general(
+        for g in range(kv_count):
+            at = b * head_count + g * group
+            scored[at : at + group, :] = lax.dot_general(
                 query[g * group : (g + 1) * group],
                 keys[b, :, lanes[g]],
                 (((1,), (1,)), ((), ())),
                 preferred_element_type=F32,
             )
-            for g in range(kv_count)
-        ]
-        scores = jnp.where(positions < len_ref[b], jnp.concatenate(scores) * inv_root, -jnp.inf)
-        highest = jnp.maximum(jnp.max(scores, axis=1, keepdims=True), fresh)
+    for copy in copies[1] + sliced:
+        copy.wait()
+    for copy in stored:
+        copy.start()
+    probs, fresh_probs = [], []
+    for b in range(seq_count):
+        scores = scored[b * head_count : (b + 1) * head_count, :]
+        scores = jnp.where(positions < len_ref[b], scores * inv_root, -jnp.inf)
+        highest = jnp.maximum(jnp.max(scores, axis=1, keepdims=True), fresh[b])
         cached_exp = jnp.exp(scores - highest)
-        fresh_exp = jnp.exp(fresh - highest)
-        totals = jnp.sum(cached_exp, axis=1, keepdims=True) + fresh_exp
-        prob = (cached_exp / totals).astype(BF16)
-        fresh_prob = (fresh_exp / totals).astype(BF16).astype(F32)
-        copies[b][1].wait()
+        fresh_exp = jnp.exp(fresh[b] - highest)
+        share = 1.0 / (jnp.sum(cached_exp, axis=1, keepdims=True) + fresh_exp)
+        probs.append((cached_exp * share).astype(BF16))
+        fresh_probs.append((fresh_exp * share).astype(BF16).astype(F32))
+    for b in range(seq_count):
         for g in range(kv_count):
             heads = slice(g * group, (g + 1) * group)
-            out = jnp.dot(prob[heads], values[b, :, lanes[g]], preferred_element_type=F32)
-            out = out + fresh_prob[heads] * tv_ref[b : b + 1, lanes[g]].astype(F32)
+            out = jnp.dot(probs[b][heads], values[b, :, lanes[g]], preferred_element_type=F32)
+            out = out + fresh_probs[b][heads] * tv_ref[b : b + 1, lanes[g]].astype(F32)
             out = pltpu.roll(out, core * (HEAD_WIDTH // 2), 1)
             for a in range(2):
                 start = g * group * seq_count + a * seq_count + b
                 mixed[pl.ds(start, side, stride=2 * seq_count), :] = out[a * side : (a + 1) * side]
-        if b == seq_count // 2:
-            for d in range(4):
-                sliced[d].wait()
-                stored[d].start()
     tile = 2 * seq_count
     for g in range(kv_count):
         for y in range(side):
@@ -161,6 +165,11 @@
                 far = pltpu.roll(near, seq_count, 0)
                 out_ref[2 * g * side + y, :, lanes[part]] = near.astype(BF16)
                 out_ref[(2 * g + 1) * side + y, :, lanes[part]] = far.astype(BF16)
+        sent = pl.ds(2 * g * side, 2 * side)
+        stored.append(
+            pltpu.make_async_copy(out_ref.at[sent], out_hbm.at[sent], few.at[len(small) + 8 + g])
+        )
+        stored[-1].start()
     for copy in stored:
         copy.wait()
 
@@ -175,7 +184,7 @@
         out_shape=[pltpu.HBM((heads, 2 * seq_count, 2 * HEAD_WIDTH), BF16)]
         + [pltpu.HBM((rows, cols // 4), BF16)] * 4,
         in_specs=[IN_HBM] * 7,
-        out_specs=[IN_VMEM] + [IN_HBM] * 4,
+        out_specs=[IN_HBM] * 5,
         scratch_shapes=[
             pltpu.VMEM(queries.shape, BF16),
             pltpu.VMEM(token_keys.shape, BF16),
@@ -186,8 +195,10 @@
             pltpu.VMEM((4, rows, cols // 4), BF16),
             pltpu.VMEM((seq_count * heads, HEAD_WIDTH), F32),
             pltpu.VMEM((seq_count * heads, HEAD_WIDTH), F32),
+            pltpu.VMEM((seq_count * heads, stored_keys.shape[1]), F32),
+            pltpu.VMEM((heads, 2 * seq_count, 2 * HEAD_WIDTH), BF16),
             pltpu.SemaphoreType.DMA((2, seq_count)),
-            pltpu.SemaphoreType.DMA((12,)),
+            pltpu.SemaphoreType.DMA((16,)),
         ],
         compiler_params=pltpu.CompilerParams(vmem_limit_bytes=8 * MIB),
     )(
@@ -231,42 +242,97 @@
 
 
 def halves_body(gate_hbm, up_hbm, down_hbm, kept_ref, *refs):
-    outs, (tall, wide, sems) = refs[:3], refs[3:]
+    outs, (tall, wide, sems) = refs[:2], refs[2:]
     core = lax.axis_index(CORES)
-    half = kept_ref.shape[0]
-    kept, given = (pl.ds(pl.multiple_of(j * half, half), half) for j in (core, 1 - core))
-    held = (tall.at[0], tall.at[1], wide)
-    sources = (gate_hbm.at[0, given, :], up_hbm.at[0, given, :], down_hbm.at[0, :, given])
-    loads = [pltpu.make_async_copy(sources[j], held[j], sems.at[j]) for j in range(3)]
-    stores = [pltpu.make_async_copy(held[j], outs[j], sems.at[3 + j]) for j in range(3)]
-    own = pltpu.make_async_copy(gate_hbm.at[0, kept, :], kept_ref, sems.at[6])
-    for load in loads:
-        load.start()
-    own.start()
-    for load, store in zip(loads, stores, strict=True):
-        load.wait()
-        store.start()
-    own.wait()
-    for store in stores:
-        store.wait()
-
-
-def halves(w_gate, w_up, w_down):
+    count = kept_ref.shape[0]
+    half, both = tall.shape
+    units = both // 2
+    given = pl.ds(pl.multiple_of((1 - core) * half, half), half)
+    kept = pl.ds(pl.multiple_of(core * half, half), count)
+    left, right = slice(0, units), slice(units, both)
+    pairs = (
+        (gate_hbm.at[0, given, :], tall.at[:, left]),
+        (up_hbm.at[0, given, :], tall.at[:, right]),
+        (down_hbm.at[0, :, given], wide),
+        (gate_hbm.at[0, kept, :], kept_ref.at[:, left]),
+        (up_hbm.at[0, kept, :], kept_ref.at[:, right]),
+        (tall, outs[0]),
+        (wide, outs[1]),
+    )
+    copies = [pltpu.make_async_copy(*pair, sems.at[j]) for j, pair in enumerate(pairs)]
+    for copy in copies[:5]:
+        copy.start()
+    for copy in copies[:2]:
+        copy.wait()
+    copies[5].start()
+    copies[2].wait()
+    copies[6].start()
+    for copy in copies[3:]:
+        copy.wait()
+
+
+def halves(w_gate, w_up, w_down, kept_share):
     _, width, units = w_gate.shape
-    tall, wide = (width // 2, units), (units, width // 2)
+    tall, wide = (width // 2, 2 * units), (units, width // 2)
     return pl.pallas_call(
         halves_body,
         name="halves",
-        out_shape=[pltpu.VMEM(tall, BF16)] + [pltpu.HBM(dims, BF16) for dims in (tall, tall, wide)],
+        out_shape=[
+            pltpu.VMEM((int(width // 2 * kept_share), 2 * units), BF16),
+            pltpu.HBM(tall, BF16),
+            pltpu.HBM(wide, BF16),
+        ],
         in_specs=[IN_HBM] * 3,
-        out_specs=[IN_VMEM] + [IN_HBM] * 3,
+        out_specs=[IN_VMEM] + [IN_HBM] * 2,
         scratch_shapes=[
-            pltpu.VMEM((2, *tall), BF16),
+            pltpu.VMEM(tall, BF16),
             pltpu.VMEM(wide, BF16),
             pltpu.SemaphoreType.DMA((7,)),
         ],
         compiler_params=pltpu.CompilerParams(vmem_limit_bytes=6 * MIB),
     )(*map(in_hbm, (w_gate, w_up, w_down)))
+
+
+def project_body(x_ref, weight_ref, out_hbm, held, sems):
+    chips, tile, width = x_ref.shape
+    cols = weight_ref.shape[2]
+    half = cols // 2
+    step = 16
+    low = lax.broadcasted_iota(jnp.int32, (step, tile, half), 1) < tile // 2
+    copies = []
+    for j, at in enumerate(range(0, chips, step)):
+        rows = slice(at, at + step)
+        x = x_ref[rows].reshape(step * tile, width)
+        near, far = (
+            jnp.dot(x, weight_ref[j], preferred_element_type=F32).reshape(step, tile, cols)
+            for j in range(2)
+        )
+        kept = jnp.where(low, near[:, :, :half], far[:, :, half:])
+        moved = jnp.where(low, near[:, :, half:], far[:, :, :half])
+        moved = pltpu.roll(moved, tile // 2, 1)
+        held[rows] = (kept + moved).astype(BF16)
+        copies.append(pltpu.make_async_copy(held.at[rows], out_hbm.at[rows], sems.at[j]))
+        copies[-1].start()
+    for copy in copies:
+        copy.wait()
+
+
+def sending_call(body, dims, in_specs, limit, chunks):
+    return pl.pallas_call(
+        body,
+        out_shape=pltpu.HBM(dims, BF16),
+        in_specs=in_specs,
+        out_specs=IN_HBM,
+        scratch_shapes=[pltpu.VMEM(dims, BF16), pltpu.SemaphoreType.DMA((chunks,))],
+        compiler_params=pltpu.CompilerParams(vmem_limit_bytes=limit * MIB),
+    )
+
+
+def project(x, weight):
+    dims = x.shape[0], x.shape[1], weight.shape[2] // 2
+    return sending_call(project_body, dims, [IN_VMEM] * 2, 12, x.shape[0] // 16)(
+        x, in_vmem(weight)
+    )
 
 
 def project_body(x_ref, weight_ref, out_ref):
@@ -379,22 +445,31 @@
     )(expert_ids, route_weight)
 
 
-def dispatch_body(kept_ref, other_ref, pick_ref, out_ref):
+def dispatch_body(kept_ref, other_ref, pick_ref, out_hbm, held, sems):
     pieces = [r[...].reshape(-1, r.shape[2]) for r in (kept_ref, other_ref)]
-    rows = lax.dot_general(
-        pick_ref[...],
-        jnp.concatenate(pieces),
-        (((0,), (0,)), ((), ())),
-        preferred_element_type=F32,
-    )
-    out_ref[...] = rows.astype(BF16).reshape(out_ref.shape)
+    tokens = jnp.concatenate(pieces)
+    chips, tile, half = held.shape
+    step = chips // 2
+    copies = []
+    for j in range(2):
+        rows = lax.dot_general(
+            pick_ref[:, j * step * tile : (j + 1) * step * tile],
+            tokens,
+            (((0,), (0,)), ((), ())),
+            preferred_element_type=F32,
+        )
+        sent = slice(j * step, (j + 1) * step)
+        held[sent] = rows.astype(BF16).reshape(step, tile, half)
+        copies.append(pltpu.make_async_copy(held.at[sent], out_hbm.at[sent], sems.at[j]))
+        copies[-1].start()
+    for copy in copies:
+        copy.wait()
 
 
 def dispatch(kept, other, pick):
     tile, half = kept.shape[1:]
-    return kernel_call(
-        dispatch_body, pltpu.HBM((pick.shape[1] // tile, tile, half), BF16), [IN_VMEM] * 3, 6
-    )(kept, other, pick)
+    dims = pick.shape[1] // tile, tile, half
+    return sending_call(dispatch_body, dims, [IN_VMEM] * 3, 6, 2)(kept, other, pick)
 
 
 def slot_order(size, back=False):
@@ -405,31 +480,18 @@
     return jnp.where(row == slot // 2 * 8 + quarter * 2 + slot % 2, 1.0, 0.0).astype(BF16)
 
 
-def gate_body(
-    x_ref,
-    gate_ref,
-    up_hbm,
-    down_hbm,
-    gate_moved,
-    up_moved,
-    down_moved,
-    part_ref,
-    sent_ref,
-    down_ref,
-    buffers,
-    sems,
-):
+def gate_body(x_ref, kept_ref, gate_hbm, up_hbm, moved_hbm, part_ref, sent_ref, rest, moved, sems):
     core = lax.axis_index(CORES)
     chips, tile, part = x_ref.shape
-    half, units = gate_ref.shape
-    kept = pl.ds(pl.multiple_of(core * half, half), half)
-    pairs = (
-        (up_hbm.at[0, kept, :], buffers.at[0]),
-        (gate_moved, buffers.at[1]),
-        (up_moved, buffers.at[2]),
-        (down_hbm.at[0, :, kept], down_ref.at[:units]),
-        (down_moved, down_ref.at[units:]),
-    )
+    half, both = moved.shape
+    units = both // 2
+    count = kept_ref.shape[0]
+    late = pl.ds(pl.multiple_of(core * half + count, part), half - count)
+    pairs = [(gate_hbm.at[0, late, :], rest.at[:, :units]), (up_hbm.at[0, late, :], rest.at[:, units:])]
+    step = half // 2
+    for j in range(2):
+        rows = slice(j * step, (j + 1) * step)
+        pairs.append((moved_hbm.at[rows], moved.at[rows]))
     copies = [pltpu.make_async_copy(*pair, sems.at[j]) for j, pair in enumerate(pairs)]
     for copy in copies:
         copy.start()
@@ -445,39 +507,69 @@
         jnp.concatenate([r[p * slots : (p + 1) * slots] for r in sorted_rows]) for p in range(4)
     ]
     x = jnp.concatenate(quarters, axis=1)
-    for j in range(4):
-        if j:
-            copies[j - 1].wait()
-        weight = buffers[j - 1] if j else gate_ref[...]
-        value = jnp.dot(x, weight, preferred_element_type=F32)
-        part_ref[:, j * units : (j + 1) * units] = value
-        at = (j + 2) % 4 * units
-        sent_ref[:, at : at + units] = value.astype(BF16)
-    for copy in copies[3:]:
-        copy.wait()
-
-
-def gate_up(x, gate_own, w_up, w_down, moved):
+    own = jnp.dot(x[:, :count], kept_ref[...], preferred_element_type=F32)
+    for copy in copies[:2]:
+        copy.wait()
+    own = own + jnp.dot(x[:, count:], rest[...], preferred_element_type=F32)
+    part_ref[:, :both] = own
+    sent_ref[:, both:] = own.astype(BF16)
+    copies[2].wait()
+    other = jnp.dot(x[:, :step], moved[:step], preferred_element_type=F32)
+    copies[3].wait()
+    other = other + jnp.dot(x[:, step:], moved[step:], preferred_element_type=F32)
+    part_ref[:, both:] = other
+    sent_ref[:, :both] = other.astype(BF16)
+
+
+def gate_up(x, kept, w_gate, w_up, moved):
     chips, tile, _ = x.shape
-    half, units = gate_own.shape
-    dims = chips * tile // 4, 4 * units
+    half, both = moved.shape
+    dims = chips * tile // 4, 2 * both
     return pl.pallas_call(
         gate_body,
         name="gate_up",
-        out_shape=[
-            pltpu.VMEM(dims, F32),
-            pltpu.VMEM(dims, BF16),
-            pltpu.VMEM((2 * units, half), BF16),
+        out_shape=[pltpu.VMEM(dims, F32), pltpu.VMEM(dims, BF16)],
+        in_specs=[IN_VMEM] * 2 + [IN_HBM] * 3,
+        out_specs=[IN_VMEM] * 2,
+        scratch_shapes=[
+            pltpu.VMEM((half - kept.shape[0], both), BF16),
+            pltpu.VMEM((half, both), BF16),
+            pltpu.SemaphoreType.DMA((4,)),
         ],
-        in_specs=[IN_VMEM] * 2 + [IN_HBM] * 5,
-        out_specs=[IN_VMEM] * 3,
-        scratch_shapes=[pltpu.VMEM((3, half, units), BF16), pltpu.SemaphoreType.DMA((5,))],
-        compiler_params=pltpu.CompilerParams(vmem_limit_bytes=16 * MIB),
-    )(x, in_vmem(gate_own), *map(in_hbm, (w_up, w_down, *moved)))
-
-
-def down_body(part_ref, arrived_ref, down_ref, out_ref):
-    chips, tile, part = out_ref.shape
+        compiler_params=pltpu.CompilerParams(vmem_limit_bytes=14 * MIB),
+    )(x, in_vmem(kept), *map(in_hbm, (w_gate, w_up, moved)))
+
+
+def fetch_body(down_hbm, moved_hbm, after_ref, out_ref, sems):
+    del after_ref
+    core = lax.axis_index(CORES)
+    units, half = moved_hbm.shape
+    kept = pl.ds(pl.multiple_of(core * half, half), half)
+    copies = [
+        pltpu.make_async_copy(down_hbm.at[0, :, kept], out_ref.at[:units], sems.at[0]),
+        pltpu.make_async_copy(moved_hbm, out_ref.at[units:], sems.at[1]),
+    ]
+    for copy in copies:
+        copy.start()
+    for copy in copies:
+        copy.wait()
+
+
+def fetch_down(w_down, moved, after):
+    units, half = moved.shape
+    return pl.pallas_call(
+        fetch_body,
+        name="fetch_down",
+        out_shape=pltpu.VMEM((2 * units, half), BF16),
+        in_specs=[IN_HBM] * 3,
+        out_specs=IN_VMEM,
+        scratch_shapes=[pltpu.SemaphoreType.DMA((2,))],
+        compiler_params=pltpu.CompilerParams(vmem_limit_bytes=MIB),
+    )(in_hbm(w_down), in_hbm(moved), after)
+
+
+def down_body(part_ref, arrived_ref, down_ref, out_hbm, held, sems):
+    chips, tile, part = held.shape
     size = 256
     groups = chips * tile // size
     order = slot_order(size, back=True)
@@ -497,18 +589,23 @@
         lanes = slice(p * part, (p + 1) * part)
         value = jnp.dot(hidden, down_ref[:, lanes], preferred_element_type=F32)
         quarters.append(value.astype(BF16))
+    copies = []
     for g in range(groups):
         rows = jnp.concatenate([v[g * slots : (g + 1) * slots] for v in quarters])
         rows = jnp.dot(order, rows, preferred_element_type=F32).astype(BF16)
-        out_ref[g * size // tile : (g + 1) * size // tile] = rows.reshape(size // tile, tile, part)
+        sent = slice(g * size // tile, (g + 1) * size // tile)
+        held[sent] = rows.reshape(size // tile, tile, part)
+        copies.append(pltpu.make_async_copy(held.at[sent], out_hbm.at[sent], sems.at[g]))
+        copies[-1].start()
+    for copy in copies:
+        copy.wait()
 
 
 def down(part, arrived, weight, tile):
-    slots = part.shape[0]
-    width = weight.shape[1] // 4
-    return kernel_call(
-        down_body, pltpu.HBM((slots * 4 // tile, tile, width), BF16), [IN_VMEM] * 3, 8
-    )(part, arrived, in_vmem(weight))
+    dims = part.shape[0] * 4 // tile, tile, weight.shape[1] // 4
+    return sending_call(down_body, dims, [IN_VMEM] * 3, 8, 2)(
+        part, arrived, in_vmem(weight)
+    )
 
 
 def combine_body(x_ref, mix_ref, own_ref, other_ref):
@@ -571,8 +668,8 @@
     tokens = lax.all_to_all(outgoing, CHIPS, 0, 0, tiled=True)
     other = [swapped(piece) for piece in own]
     weight = stack(own, other)
-    gate_own, *given_halves = halves(w_gate, w_up, w_down)
-    moved = [swapped(x) for x in given_halves]
+    kept, *given_halves = halves(w_gate, w_up, w_down, 0.75)
+    gate_moved, down_moved = (swapped(x) for x in given_halves)
     pick, mix = route(expert_ids, route_weight, chips)
 
     sums = project(tokens, weight)
@@ -580,7 +677,8 @@
     hidden, normed, normed_given = settle(came_back, residual, norm_gain[None])
     outgoing = dispatch(normed, swapped(normed_given), pick)
     incoming = lax.all_to_all(outgoing, CHIPS, 0, 0, tiled=True)
-    part, sent, down_weight = gate_up(incoming, gate_own, w_up, w_down, moved)
+    part, sent = gate_up(incoming, kept, w_gate, w_up, gate_moved)
+    down_weight = fetch_down(w_down, down_moved, part)
     expert_out = down(part, swapped(sent), down_weight, incoming.shape[1])
     returned = lax.all_to_all(expert_out, CHIPS, 0, 0, tiled=True)
     moe_own, moe_given = combine(returned, mix)

time: 139 us -> 147 us (1.058)
  blocking collectives: 22.7 us -> 46.1 us
  starting transfers between devices: 66.4 us -> 52.3 us
  waiting for transfers between devices: 29.3 us -> 26.9 us
    all_to_all x0 -> x1, blocking collectives: none -> 22.8 us  [on_device(): incoming = lax.all_to_all(outgoing, CHIPS, 0, 0, tiled=True)]
    all_to_all x1 -> x0, waiting for transfers between devices: 15.5 us -> none  [on_device(): incoming = lax.all_to_all(outgoing, CHIPS, 0, 0, tiled=True)]
    all_to_all x1, starting transfers between devices: 21.8 us -> 7.24 us  [on_device(): tokens = lax.all_to_all(outgoing, CHIPS, 0, 0, tiled=True)]
    ppermute x3, waiting for transfers between devices: 0.01 us -> 9.69 us  [on_device(): lax.ppermute(pieces[d], CHIPS, quad_step(side, d // 2, d % 2))]
    ppermute x10 -> x9, starting transfers between devices: 22 us -> 31.5 us  [swapped(): return lax.ppermute(x, CORES, [(0, 1), (1, 0)])]
    all_to_all x1 -> x0, starting transfers between devices: 7.19 us -> none  [on_device(): incoming = lax.all_to_all(outgoing, CHIPS, 0, 0, tiled=True)]
    all_to_all x1, waiting for transfers between devices: 10 us -> 14.7 us  [on_device(): came_back = lax.all_to_all(sums, CHIPS, 0, 0, tiled=True)]
    pallas_call x3 -> x4, Pallas kernels: 6.81 us -> 8.67 us  [the longest x1 4.06 us: halves(): pl.pallas_call(halves_body, name='halves', out_shape=[pltpu.VMEM((int(wid...]
  transfers between devices with their start and end apart: 16 -> 14, of which waited for: 6 -> 7; matrix products, arithmetic and copies ran while one was open for 0% -> 0% of each run, Pallas kernels for 5% -> 9%
where the time goes in v5:
time: 147 us
  starting transfers between devices  52.3 us (36%)
  blocking collectives  46.1 us (31%)
  waiting for transfers between devices  26.9 us (18%)
  Pallas kernels  20 us (14%)
    ppermute x9, starting transfers between devices, swapped(): return lax.ppermute(x, CORES, [(0, 1), (1, 0)])  31.5 us
    all_to_all x1, blocking collectives, on_device(): returned = lax.all_to_all(expert_out, CHIPS, 0, 0, tiled=True)  23.3 us
    all_to_all x1, blocking collectives, on_device(): incoming = lax.all_to_all(outgoing, CHIPS, 0, 0, tiled=True)  22.8 us
    all_to_all x1, waiting for transfers between devices, on_device(): came_back = lax.all_to_all(sums, CHIPS, 0, 0, tiled=True)  14.7 us
    all_to_all x1, starting transfers between devices, on_device(): came_back = lax.all_to_all(sums, CHIPS, 0, 0, tiled=True)  10.8 us
    ppermute x3, waiting for transfers between devices, on_device(): lax.ppermute(pieces[d], CHIPS, quad_step(side, d // 2, d % 2))  9.69 us
    all_to_all x1, starting transfers between devices, on_device(): tokens = lax.all_to_all(outgoing, CHIPS, 0, 0, tiled=True)  7.24 us
    pallas_call x1, Pallas kernels, halves(): pl.pallas_call(halves_body, name='halves', out_shape=[pltpu.VMEM((int(wid...  4.06 us
  transfers between devices with their start and end apart: 14, of which 7 were waited for; matrix products, arithmetic and copies ran while one was open for 0% of the time, Pallas kernels for 9%

profile of v5, /device:TPU:513, one launch (start us, length us, event | category | flops | bytes accessed | tf_op | source)
XLA Modules:
  0.0 146.7 jit_solution(13875633432072165257)
XLA Ops:
  0.0 4.1 %halves.1 = (bf16[1536,768]{1,0:T(8,128)(2,1)S(1)}, bf16[2048,768]{1,0:T(8,128)(2,1)}, bf16[384,2048]{1,0:T(8,128)(2,1)}) custom-call(bf16[1,4096,384]{2,1,0:T(8,128)(2,1)} %gate_hbm.3, bf16[1,4096,384]{2,1,0:T(8,128)(2,1)} %up_hbm.3, bf16[1,384,4096]{2,1,0:T(8,128)(2,1)} %down_hbm.3), custom_call_target="tpu_custom_call" | custom-call | tf_op jit(solution)/shard_map/halves/pallas_call | solution.py:277
  4.1 20.5 %collective-permute-start.8 = (bf16[2048,768]{1,0:T(8,128)(2,1)}, bf16[2048,768]{1,0:T(8,128)(2,1)}, u32[]{:S(2)}, u32[]{:S(2)}) collective-permute-start(bf16[2048,768]{1,0:T(8,128)(2,1)} %get-tuple-element.32), channel_id=1, source_target_pairs={{0,1},{1,0},{2,3},{3,2},{4,5},{5,4},{6,7},{7,6},{8,9},{9,8},{10,11... | collective-permute-start | bytes 9437192 | tf_op jit(solution)/shard_map/ppermute | solution.py:19
  24.6 3.2 %attend.1 = (bf16[64,8,256]{2,1,0:T(8,128)(2,1)}, bf16[64,1024]{1,0:T(8,128)(2,1)}, bf16[64,1024]{1,0:T(8,128)(2,1)}, bf16[64,1024]{1,0:T(8,128)(2,1)}, bf16[64,1024]{1,0:T(8,128)(2,1)}) custom-call(bf16[4,8192]{1,0:T(4,128)(2,1)} %q_hbm.1, bf16[4,512]{1,0:T(4,128)(2,1)} %tk_hbm.1, bf16[4,512]{1,0:T(4,128)(2,1)} %tv_hbm.1, s32[4]{0:T(128)} %len_hbm.1, ...), custom_call_target="tpu_custom_call" | custom-call | tf_op jit(solution)/shard_map/attend/pallas_call | solution.py:181
  27.8 0.0 copy-start.10
  27.8 0.0 copy-start
  27.8 0.0 copy-start.1
  27.9 0.0 copy-start.2
  27.9 7.2 %all-to-all-start = ((bf16[64,8,256]{2,1,0:T(8,128)(2,1)}), bf16[64,8,256]{2,1,0:T(8,128)(2,1)}, u32[]{:S(2)}, u32[]{:S(2)}) async-start(bf16[64,8,256]{2,1,0:T(8,128)(2,1)} %get-tuple-element.22), calls=%async_computation | async-start | bytes 524288 | tf_op jit(solution)/shard_map/all_to_all | solution.py:668
  35.1 0.1 collective-permute-start
  35.3 1.1 collective-permute-start.1
  36.4 1.5 %collective-permute-start.2 = (bf16[64,1024]{1,0:T(8,128)(2,1)}, bf16[64,1024]{1,0:T(8,128)(2,1)S(1)}, u32[]{:S(2)}, u32[]{:S(2)}) collective-permute-start(bf16[64,1024]{1,0:T(8,128)(2,1)} %get-tuple-element.26), channel_id=1, source_target_pairs={{0,18},{2,16},{4,22},{6,20},{8,26},{10,24},{12,30},{14,28},{16,2},... | collective-permute-start | bytes 393224 | tf_op jit(solution)/shard_map/ppermute | solution.py:666
  37.9 0.9 collective-permute-start.3
  38.8 9.7 %collective-permute-done.refs_1_ = bf16[64,1024]{1,0:T(8,128)(2,1)S(1)} collective-permute-done((bf16[64,1024]{1,0:T(8,128)(2,1)}, bf16[64,1024]{1,0:T(8,128)(2,1)S(1)}, u32[]{:S(2)}, u32[]{:S(2)}) %collective-permute-start) | collective-permute-done | bytes 131104 | tf_op jit(solution)/shard_map/ppermute | solution.py:666
  48.4 0.0 copy-start.3
  48.4 0.4 collective-permute-start.4
  48.8 0.0 collective-permute-done.1.refs_2_
  48.8 0.0 copy-start.4
  48.8 0.1 collective-permute-start.5
  49.0 0.0 collective-permute-done.2.refs_3_
  49.0 0.0 copy-start.5
  49.0 0.4 collective-permute-start.6
  49.3 0.0 collective-permute-done.3.refs_4_
  49.3 0.0 copy-start.6
  49.3 0.5 collective-permute-done.4.refs_5_
  49.8 0.0 copy-start.7
  49.8 0.4 collective-permute-done.5.refs_6_
  50.2 0.0 copy-start.8
  50.2 0.2 collective-permute-done.6.refs_7_
  50.4 0.0 copy-done.3
  50.4 0.0 copy-done.4
  50.4 0.0 copy-done.5
  50.4 0.0 copy-done.6
  50.4 0.1 copy-done.7
  50.5 0.4 copy-done.8
  50.8 0.0 copy-start.9
  50.8 0.7 copy-done.9
  51.5 1.3 stack.1.weight_ref
  52.9 0.0 all-to-all-done.x_ref
  52.9 2.6 %shard_map.136 = bf16[64,8,512]{2,1,0:T(8,128)(2,1)} custom-call(bf16[64,8,256]{2,1,0:T(8,128)(2,1)} %all-to-all-done.x_ref, bf16[2,256,1024]{2,1,0:T(8,128)(2,1)S(1)} %stack.1.weight_ref), custom_call_target="tpu_custom_call" | custom-call | tf_op jit(solution)/shard_map/pallas_call | solution.py:358
  55.4 10.8 %all-to-all-start.1 = ((bf16[64,8,512]{2,1,0:T(8,128)(2,1)}), bf16[64,8,512]{2,1,0:T(8,128)(2,1)S(1)}, u32[]{:S(2)}, u32[]{:S(2)}) async-start(bf16[64,8,512]{2,1,0:T(8,128)(2,1)} %shard_map.136), calls=%async_computation.1 | async-start | bytes 1048576 | tf_op jit(solution)/shard_map/all_to_all | solution.py:676
  66.3 0.7 collective-permute-start.10
  67.0 0.0 copy-done.10
  67.0 14.7 %all-to-all-done.1.x_ref = bf16[64,8,512]{2,1,0:T(8,128)(2,1)S(1)} async-done(((bf16[64,8,512]{2,1,0:T(8,128)(2,1)}), bf16[64,8,512]{2,1,0:T(8,128)(2,1)S(1)}, u32[]{:S(2)}, u32[]{:S(2)}) %all-to-all-start.1) | async-done | bytes 524320 | tf_op jit(solution)/shard_map/all_to_all | solution.py:676
  81.8 0.0 copy-done
  81.8 0.2 shard_map.137
  82.0 3.0 %collective-permute-start.7 = (bf16[2,8,512]{2,1,0:T(8,128)(2,1)S(1)}, bf16[2,8,512]{2,1,0:T(8,128)(2,1)S(1)}, u32[]{:S(2)}, u32[]{:S(2)}) collective-permute-start(bf16[2,8,512]{2,1,0:T(8,128)(2,1)S(1)} %get-tuple-element.29), channel_id=1, source_target_pairs={{0,1},{1,0},{2,3},{3,2},{4,5},{5,4},{6,7},{7,6},{8,9},{9,8},{10,11... | collective-permute-start | bytes 49160 | tf_op jit(solution)/shard_map/ppermute | solution.py:19
  85.1 0.0 copy-done.1
  85.1 0.0 copy-done.2
  85.1 0.2 shard_map.138
  85.3 0.6 collective-permute-done.7.other_ref
  85.9 1.0 shard_map.139
  87.0 22.8 %all_to_all.20.x_ref = bf16[64,8,512]{2,1,0:T(8,128)(2,1)S(1)} all-to-all(bf16[64,8,512]{2,1,0:T(8,128)(2,1)} %shard_map.139), channel_id=1, replica_groups=mesh['groups'=2,'expert'=64,'replica'=2] {'expert'}, dimensions={0} | all-to-all | bytes 1048576 | tf_op jit(solution)/shard_map/all_to_all | solution.py:679
  109.8 0.0 collective-permute-done.8.moved_hbm
  109.8 3.0 %gate_up.1 = (f32[128,1536]{1,0:T(8,128)S(1)}, bf16[128,1536]{1,0:T(8,128)(2,1)S(1)}) custom-call(bf16[64,8,512]{2,1,0:T(8,128)(2,1)S(1)} %all_to_all.20.x_ref, bf16[1536,768]{1,0:T(8,128)(2,1)S(1)} %get-tuple-element.31.kept_ref, bf16[1,4096,384]{2,1,0:T(8,128)(2,1)} %gate_hbm.3, bf16[1,4096,384]{2,1,0:T(8,128)(2,1)} %up_hbm.3, ...), custom_call_target="tpu_custom_call" | custom-call | tf_op jit(solution)/shard_map/gate_up/pallas_call | solution.py:528
  112.7 3.0 %collective-permute-start.9 = (bf16[128,1536]{1,0:T(8,128)(2,1)S(1)}, bf16[128,1536]{1,0:T(8,128)(2,1)S(1)}, u32[]{:S(2)}, u32[]{:S(2)}) collective-permute-start(bf16[128,1536]{1,0:T(8,128)(2,1)S(1)} %get-tuple-element.34), channel_id=1, source_target_pairs={{0,1},{1,0},{2,3},{3,2},{4,5},{5,4},{6,7},{7,6},{8,9},{9,8},{10,11... | collective-permute-start | bytes 1179656 | tf_op jit(solution)/shard_map/ppermute | solution.py:19
  115.8 0.0 collective-permute-done.10.moved_hbm
  115.8 1.9 %fetch_down.1.down_ref = bf16[768,2048]{1,0:T(8,128)(2,1)S(1)} custom-call(bf16[1,384,4096]{2,1,0:T(8,128)(2,1)} %down_hbm.3, bf16[384,2048]{1,0:T(8,128)(2,1)} %collective-permute-done.10.moved_hbm, f32[128,1536]{1,0:T(8,128)S(1)} %get-tuple-element.33.after_ref.part_ref), custom_call_target="tpu_custom_call" | custom-call | tf_op jit(solution)/shard_map/fetch_down/pallas_call | solution.py:560
  117.7 0.0 collective-permute-done.9.arrived_ref
  117.7 1.7 %shard_map.140 = bf16[64,8,512]{2,1,0:T(8,128)(2,1)} custom-call(f32[128,1536]{1,0:T(8,128)S(1)} %get-tuple-element.33.after_ref.part_ref, bf16[128,1536]{1,0:T(8,128)(2,1)S(1)} %collective-permute-done.9.arrived_ref, bf16[768,2048]{1,0:T(8,128)(2,1)S(1)} %fetch_down.1.down_ref), custom_call_target="tpu_custom_call" | custom-call | tf_op jit(solution)/shard_map/pallas_call | solution.py:606
  119.3 23.3 %all_to_all.21.x_ref = bf16[64,8,512]{2,1,0:T(8,128)(2,1)S(1)} all-to-all(bf16[64,8,512]{2,1,0:T(8,128)(2,1)} %shard_map.140), channel_id=1, replica_groups=mesh['groups'=2,'expert'=64,'replica'=2] {'expert'}, dimensions={0} | all-to-all | bytes 1048576 | tf_op jit(solution)/shard_map/all_to_all | solution.py:683
  142.6 0.2 shard_map.141
  142.8 2.4 %collective-permute-start.11 = (f32[2,8,512]{2,1,0:T(8,128)S(1)}, f32[2,8,512]{2,1,0:T(8,128)S(1)}, u32[]{:S(2)}, u32[]{:S(2)}) collective-permute-start(f32[2,8,512]{2,1,0:T(8,128)S(1)} %get-tuple-element.38), channel_id=1, source_target_pairs={{0,1},{1,0},{2,3},{3,2},{4,5},{5,4},{6,7},{7,6},{8,9},{9,8},{10,11... | collective-permute-start | bytes 98312 | tf_op jit(solution)/shard_map/ppermute | solution.py:19
  145.2 0.9 collective-permute-done.11.other_ref
  146.0 0.6 shard_map.142
  (1 shorter events, 0.0 us)
Async XLA Ops:
  4.1 105.7 %collective-permute-start.8 = (bf16[2048,768]{1,0:T(8,128)(2,1)}, bf16[2048,768]{1,0:T(8,128)(2,1)}, u32[]{:S(2)}, u32[]{:S(2)}) collective-permute-start(bf16[2048,768]{1,0:T(8,128)(2,1)} %get-tuple-element.32), channel_id=1, source_target_pairs={{0,1},{1,0},{2,3},{3,2},{4,5},{5,4},{6,7},{7,6},{8,9},{9,8},{10,11... | collective-permute-start | bytes 9437192 | tf_op jit(solution)/shard_map/ppermute | solution.py:19
  27.8 39.2 %copy-start.10 = (bf16[4096]{0:T(1024)(128)(2,1)S(1)}, bf16[4096]{0:T(1024)(128)(2,1)}, u32[]{:S(2)}) copy-start(bf16[4096]{0:T(1024)(128)(2,1)} %param.22) | copy-start | bytes 24580
  27.8 54.0 %copy-start = (bf16[4,4096]{1,0:T(4,128)(2,1)S(1)}, bf16[4,4096]{1,0:T(4,128)(2,1)}, u32[]{:S(2)}) copy-start(bf16[4,4096]{1,0:T(4,128)(2,1)} %residual_ref.1) | copy-start | bytes 98308
  27.8 57.2 %copy-start.1 = (s32[8,8]{1,0:T(8,128)S(1)}, s32[8,8]{1,0:T(8,128)}, u32[]{:S(2)}) copy-start(s32[8,8]{1,0:T(8,128)} %ids_ref.1) | copy-start | bytes 772
  27.9 57.2 %copy-start.2 = (f32[8,8]{1,0:T(8,128)S(1)}, f32[8,8]{1,0:T(8,128)}, u32[]{:S(2)}) copy-start(f32[8,8]{1,0:T(8,128)} %weight_ref.1) | copy-start | bytes 772
  27.9 25.0 %all-to-all-start = ((bf16[64,8,256]{2,1,0:T(8,128)(2,1)}), bf16[64,8,256]{2,1,0:T(8,128)(2,1)}, u32[]{:S(2)}, u32[]{:S(2)}) async-start(bf16[64,8,256]{2,1,0:T(8,128)(2,1)} %get-tuple-element.22), calls=%async_computation | async-start | bytes 524288 | tf_op jit(solution)/shard_map/all_to_all | solution.py:668
  35.1 13.3 %collective-permute-start = (bf16[64,1024]{1,0:T(8,128)(2,1)}, bf16[64,1024]{1,0:T(8,128)(2,1)S(1)}, u32[]{:S(2)}, u32[]{:S(2)}) collective-permute-start(bf16[64,1024]{1,0:T(8,128)(2,1)} %get-tuple-element.24), channel_id=1, source_target_pairs={{0,2},{2,0},{4,6},{6,4},{8,10},{10,8},{12,14},{14,12},{16,18},{18,... | collective-permute-start | bytes 393224 | tf_op jit(solution)/shard_map/ppermute | solution.py:666
  35.3 13.6 %collective-permute-start.1 = (bf16[64,1024]{1,0:T(8,128)(2,1)}, bf16[64,1024]{1,0:T(8,128)(2,1)S(1)}, u32[]{:S(2)}, u32[]{:S(2)}) collective-permute-start(bf16[64,1024]{1,0:T(8,128)(2,1)} %get-tuple-element.25), channel_id=1, source_target_pairs={{0,16},{2,18},{4,20},{6,22},{8,24},{10,26},{12,28},{14,30},{16,0},... | collective-permute-start | bytes 393224 | tf_op jit(solution)/shard_map/ppermute | solution.py:666
  36.4 12.6 %collective-permute-start.2 = (bf16[64,1024]{1,0:T(8,128)(2,1)}, bf16[64,1024]{1,0:T(8,128)(2,1)S(1)}, u32[]{:S(2)}, u32[]{:S(2)}) collective-permute-start(bf16[64,1024]{1,0:T(8,128)(2,1)} %get-tuple-element.26), channel_id=1, source_target_pairs={{0,18},{2,16},{4,22},{6,20},{8,26},{10,24},{12,30},{14,28},{16,2},... | collective-permute-start | bytes 393224 | tf_op jit(solution)/shard_map/ppermute | solution.py:666
  37.9 11.5 %collective-permute-start.3 = (bf16[64,1024]{1,0:T(8,128)(2,1)}, bf16[64,1024]{1,0:T(8,128)(2,1)S(1)}, u32[]{:S(2)}, u32[]{:S(2)}) collective-permute-start(bf16[64,1024]{1,0:T(8,128)(2,1)} %get-tuple-element.23.refs_0_), channel_id=1, source_target_pairs={{0,1},{1,0},{2,3},{3,2},{4,5},{5,4},{6,7},{7,6},{8,9},{9,8},{10,11... | collective-permute-start | bytes 393224 | tf_op jit(solution)/shard_map/ppermute | solution.py:19
  48.4 1.9 %copy-start.3 = (bf16[64,1024]{1,0:T(8,128)(2,1)}, bf16[64,1024]{1,0:T(8,128)(2,1)S(1)}, u32[]{:S(2)}) copy-start(bf16[64,1024]{1,0:T(8,128)(2,1)S(1)} %collective-permute-done.refs_1_) | copy-start | bytes 393220
  48.4 1.4 collective-permute-start.4
  48.8 1.5 %copy-start.4 = (bf16[64,1024]{1,0:T(8,128)(2,1)}, bf16[64,1024]{1,0:T(8,128)(2,1)S(1)}, u32[]{:S(2)}) copy-start(bf16[64,1024]{1,0:T(8,128)(2,1)S(1)} %collective-permute-done.1.refs_2_) | copy-start | bytes 393220
  48.8 1.3 collective-permute-start.5
  49.0 1.4 copy-start.5
  49.0 1.4 collective-permute-start.6
  49.3 1.0 copy-start.6
  49.8 0.7 copy-start.7
  50.2 0.7 copy-start.8
  50.8 0.7 copy-start.9
  55.4 26.4 %all-to-all-start.1 = ((bf16[64,8,512]{2,1,0:T(8,128)(2,1)}), bf16[64,8,512]{2,1,0:T(8,128)(2,1)S(1)}, u32[]{:S(2)}, u32[]{:S(2)}) async-start(bf16[64,8,512]{2,1,0:T(8,128)(2,1)} %shard_map.136), calls=%async_computation.1 | async-start | bytes 1048576 | tf_op jit(solution)/shard_map/all_to_all | solution.py:676
  66.3 49.5 %collective-permute-start.10 = (bf16[384,2048]{1,0:T(8,128)(2,1)}, bf16[384,2048]{1,0:T(8,128)(2,1)}, u32[]{:S(2)}, u32[]{:S(2)}) collective-permute-start(bf16[384,2048]{1,0:T(8,128)(2,1)} %get-tuple-element.35), channel_id=1, source_target_pairs={{0,1},{1,0},{2,3},{3,2},{4,5},{5,4},{6,7},{7,6},{8,9},{9,8},{10,11... | collective-permute-start | bytes 4718600 | tf_op jit(solution)/shard_map/ppermute | solution.py:19
  82.0 3.9 %collective-permute-start.7 = (bf16[2,8,512]{2,1,0:T(8,128)(2,1)S(1)}, bf16[2,8,512]{2,1,0:T(8,128)(2,1)S(1)}, u32[]{:S(2)}, u32[]{:S(2)}) collective-permute-start(bf16[2,8,512]{2,1,0:T(8,128)(2,1)S(1)} %get-tuple-element.29), channel_id=1, source_target_pairs={{0,1},{1,0},{2,3},{3,2},{4,5},{5,4},{6,7},{7,6},{8,9},{9,8},{10,11... | collective-permute-start | bytes 49160 | tf_op jit(solution)/shard_map/ppermute | solution.py:19
  112.7 4.9 %collective-permute-start.9 = (bf16[128,1536]{1,0:T(8,128)(2,1)S(1)}, bf16[128,1536]{1,0:T(8,128)(2,1)S(1)}, u32[]{:S(2)}, u32[]{:S(2)}) collective-permute-start(bf16[128,1536]{1,0:T(8,128)(2,1)S(1)} %get-tuple-element.34), channel_id=1, source_target_pairs={{0,1},{1,0},{2,3},{3,2},{4,5},{5,4},{6,7},{7,6},{8,9},{9,8},{10,11... | collective-permute-start | bytes 1179656 | tf_op jit(solution)/shard_map/ppermute | solution.py:19
  142.8 3.2 %collective-permute-start.11 = (f32[2,8,512]{2,1,0:T(8,128)S(1)}, f32[2,8,512]{2,1,0:T(8,128)S(1)}, u32[]{:S(2)}, u32[]{:S(2)}) collective-permute-start(f32[2,8,512]{2,1,0:T(8,128)S(1)} %get-tuple-element.38), channel_id=1, source_target_pairs={{0,1},{1,0},{2,3},{3,2},{4,5},{5,4},{6,7},{7,6},{8,9},{9,8},{10,11... | collective-permute-start | bytes 98312 | tf_op jit(solution)/shard_map/ppermute | solution.py:19

commit v6 on v5

--- a/solution.py
+++ b/solution.py
@@ -662,9 +662,9 @@
     outgoing, *pieces = attend(
         queries, token_keys, token_values, kv_len, stored_keys, stored_values, out_weight
     )
-    own = [pieces[0]] + [
-        lax.ppermute(pieces[d], CHIPS, quad_step(side, d // 2, d % 2)) for d in (1, 2, 3)
-    ]
+    own = [pieces[0]]
+    for d in (1, 2, 3):
+        own.append(lax.ppermute(pieces[d], CHIPS, quad_step(side, d // 2, d % 2)))
     tokens = lax.all_to_all(outgoing, CHIPS, 0, 0, tiled=True)
     other = [swapped(piece) for piece in own]
     weight = stack(own, other)

time: 147 us -> 147 us (level)
  no operation moved by 1% of the time
where the time goes in v6:
time: 147 us
  starting transfers between devices  52.3 us (36%)
  blocking collectives  46.1 us (31%)
  waiting for transfers between devices  26.9 us (18%)
  Pallas kernels  20 us (14%)
    ppermute x9, starting transfers between devices, swapped(): return lax.ppermute(x, CORES, [(0, 1), (1, 0)])  31.5 us
    all_to_all x1, blocking collectives, on_device(): returned = lax.all_to_all(expert_out, CHIPS, 0, 0, tiled=True)  23.3 us
    all_to_all x1, blocking collectives, on_device(): incoming = lax.all_to_all(outgoing, CHIPS, 0, 0, tiled=True)  22.8 us
    all_to_all x1, waiting for transfers between devices, on_device(): came_back = lax.all_to_all(sums, CHIPS, 0, 0, tiled=True)  14.7 us
    all_to_all x1, starting transfers between devices, on_device(): came_back = lax.all_to_all(sums, CHIPS, 0, 0, tiled=True)  10.8 us
    ppermute x3, waiting for transfers between devices, on_device(): own.append(lax.ppermute(pieces[d], CHIPS, quad_step(side, d // 2, d % 2)))  9.69 us
    all_to_all x1, starting transfers between devices, on_device(): tokens = lax.all_to_all(outgoing, CHIPS, 0, 0, tiled=True)  7.24 us
    pallas_call x1, Pallas kernels, halves(): pl.pallas_call(halves_body, name='halves', out_shape=[pltpu.VMEM((int(wid...  4.06 us
  transfers between devices with their start and end apart: 14, of which 7 were waited for; matrix products, arithmetic and copies ran while one was open for 0% of the time, Pallas kernels for 9%

profile of v6, /device:TPU:513, one launch (start us, length us, event | category | flops | bytes accessed | tf_op | source)
XLA Modules:
  0.0 146.7 jit_solution(13875633432072165257)
XLA Ops:
  0.0 4.1 %halves.1 = (bf16[1536,768]{1,0:T(8,128)(2,1)S(1)}, bf16[2048,768]{1,0:T(8,128)(2,1)}, bf16[384,2048]{1,0:T(8,128)(2,1)}) custom-call(bf16[1,4096,384]{2,1,0:T(8,128)(2,1)} %gate_hbm.3, bf16[1,4096,384]{2,1,0:T(8,128)(2,1)} %up_hbm.3, bf16[1,384,4096]{2,1,0:T(8,128)(2,1)} %down_hbm.3), custom_call_target="tpu_custom_call" | custom-call | tf_op jit(solution)/shard_map/halves/pallas_call | solution.py:277
  4.1 20.5 %collective-permute-start.8 = (bf16[2048,768]{1,0:T(8,128)(2,1)}, bf16[2048,768]{1,0:T(8,128)(2,1)}, u32[]{:S(2)}, u32[]{:S(2)}) collective-permute-start(bf16[2048,768]{1,0:T(8,128)(2,1)} %get-tuple-element.32), channel_id=1, source_target_pairs={{0,1},{1,0},{2,3},{3,2},{4,5},{5,4},{6,7},{7,6},{8,9},{9,8},{10,11... | collective-permute-start | bytes 9437192 | tf_op jit(solution)/shard_map/ppermute | solution.py:19
  24.6 3.2 %attend.1 = (bf16[64,8,256]{2,1,0:T(8,128)(2,1)}, bf16[64,1024]{1,0:T(8,128)(2,1)}, bf16[64,1024]{1,0:T(8,128)(2,1)}, bf16[64,1024]{1,0:T(8,128)(2,1)}, bf16[64,1024]{1,0:T(8,128)(2,1)}) custom-call(bf16[4,8192]{1,0:T(4,128)(2,1)} %q_hbm.1, bf16[4,512]{1,0:T(4,128)(2,1)} %tk_hbm.1, bf16[4,512]{1,0:T(4,128)(2,1)} %tv_hbm.1, s32[4]{0:T(128)} %len_hbm.1, ...), custom_call_target="tpu_custom_call" | custom-call | tf_op jit(solution)/shard_map/attend/pallas_call | solution.py:181
  27.8 0.0 copy-start.10
  27.8 0.0 copy-start
  27.8 0.0 copy-start.1
  27.9 0.0 copy-start.2
  27.9 7.2 %all-to-all-start = ((bf16[64,8,256]{2,1,0:T(8,128)(2,1)}), bf16[64,8,256]{2,1,0:T(8,128)(2,1)}, u32[]{:S(2)}, u32[]{:S(2)}) async-start(bf16[64,8,256]{2,1,0:T(8,128)(2,1)} %get-tuple-element.22), calls=%async_computation | async-start | bytes 524288 | tf_op jit(solution)/shard_map/all_to_all | solution.py:668
  35.1 0.1 collective-permute-start
  35.3 1.1 collective-permute-start.1
  36.4 1.5 %collective-permute-start.2 = (bf16[64,1024]{1,0:T(8,128)(2,1)}, bf16[64,1024]{1,0:T(8,128)(2,1)S(1)}, u32[]{:S(2)}, u32[]{:S(2)}) collective-permute-start(bf16[64,1024]{1,0:T(8,128)(2,1)} %get-tuple-element.26), channel_id=1, source_target_pairs={{0,18},{2,16},{4,22},{6,20},{8,26},{10,24},{12,30},{14,28},{16,2},... | collective-permute-start | bytes 393224 | tf_op jit(solution)/shard_map/ppermute | solution.py:667
  37.9 0.9 collective-permute-start.3
  38.8 9.7 %collective-permute-done.refs_1_ = bf16[64,1024]{1,0:T(8,128)(2,1)S(1)} collective-permute-done((bf16[64,1024]{1,0:T(8,128)(2,1)}, bf16[64,1024]{1,0:T(8,128)(2,1)S(1)}, u32[]{:S(2)}, u32[]{:S(2)}) %collective-permute-start) | collective-permute-done | bytes 131104 | tf_op jit(solution)/shard_map/ppermute | solution.py:667
  48.4 0.0 copy-start.3
  48.4 0.4 collective-permute-start.4
  48.8 0.0 collective-permute-done.1.refs_2_
  48.8 0.0 copy-start.4
  48.8 0.1 collective-permute-start.5
  49.0 0.0 collective-permute-done.2.refs_3_
  49.0 0.0 copy-start.5
  49.0 0.4 collective-permute-start.6
  49.3 0.0 collective-permute-done.3.refs_4_
  49.3 0.0 copy-start.6
  49.3 0.5 collective-permute-done.4.refs_5_
  49.8 0.0 copy-start.7
  49.8 0.4 collective-permute-done.5.refs_6_
  50.2 0.0 copy-start.8
  50.2 0.2 collective-permute-done.6.refs_7_
  50.4 0.0 copy-done.3
  50.4 0.0 copy-done.4
  50.4 0.0 copy-done.5
  50.4 0.0 copy-done.6
  50.4 0.1 copy-done.7
  50.5 0.4 copy-done.8
  50.8 0.0 copy-start.9
  50.8 0.7 copy-done.9
  51.5 1.3 stack.1.weight_ref
  52.9 0.0 all-to-all-done.x_ref
  52.9 2.6 %shard_map.136 = bf16[64,8,512]{2,1,0:T(8,128)(2,1)} custom-call(bf16[64,8,256]{2,1,0:T(8,128)(2,1)} %all-to-all-done.x_ref, bf16[2,256,1024]{2,1,0:T(8,128)(2,1)S(1)} %stack.1.weight_ref), custom_call_target="tpu_custom_call" | custom-call | tf_op jit(solution)/shard_map/pallas_call | solution.py:358
  55.4 10.8 %all-to-all-start.1 = ((bf16[64,8,512]{2,1,0:T(8,128)(2,1)}), bf16[64,8,512]{2,1,0:T(8,128)(2,1)S(1)}, u32[]{:S(2)}, u32[]{:S(2)}) async-start(bf16[64,8,512]{2,1,0:T(8,128)(2,1)} %shard_map.136), calls=%async_computation.1 | async-start | bytes 1048576 | tf_op jit(solution)/shard_map/all_to_all | solution.py:676
  66.3 0.7 collective-permute-start.10
  67.0 0.0 copy-done.10
  67.0 14.7 %all-to-all-done.1.x_ref = bf16[64,8,512]{2,1,0:T(8,128)(2,1)S(1)} async-done(((bf16[64,8,512]{2,1,0:T(8,128)(2,1)}), bf16[64,8,512]{2,1,0:T(8,128)(2,1)S(1)}, u32[]{:S(2)}, u32[]{:S(2)}) %all-to-all-start.1) | async-done | bytes 524320 | tf_op jit(solution)/shard_map/all_to_all | solution.py:676
  81.8 0.0 copy-done
  81.8 0.2 shard_map.137
  82.0 3.0 %collective-permute-start.7 = (bf16[2,8,512]{2,1,0:T(8,128)(2,1)S(1)}, bf16[2,8,512]{2,1,0:T(8,128)(2,1)S(1)}, u32[]{:S(2)}, u32[]{:S(2)}) collective-permute-start(bf16[2,8,512]{2,1,0:T(8,128)(2,1)S(1)} %get-tuple-element.29), channel_id=1, source_target_pairs={{0,1},{1,0},{2,3},{3,2},{4,5},{5,4},{6,7},{7,6},{8,9},{9,8},{10,11... | collective-permute-start | bytes 49160 | tf_op jit(solution)/shard_map/ppermute | solution.py:19
  85.1 0.0 copy-done.1
  85.1 0.0 copy-done.2
  85.1 0.2 shard_map.138
  85.3 0.6 collective-permute-done.7.other_ref
  85.9 1.0 shard_map.139
  87.0 22.8 %all_to_all.20.x_ref = bf16[64,8,512]{2,1,0:T(8,128)(2,1)S(1)} all-to-all(bf16[64,8,512]{2,1,0:T(8,128)(2,1)} %shard_map.139), channel_id=1, replica_groups=mesh['groups'=2,'expert'=64,'replica'=2] {'expert'}, dimensions={0} | all-to-all | bytes 1048576 | tf_op jit(solution)/shard_map/all_to_all | solution.py:679
  109.8 0.0 collective-permute-done.8.moved_hbm
  109.8 3.0 %gate_up.1 = (f32[128,1536]{1,0:T(8,128)S(1)}, bf16[128,1536]{1,0:T(8,128)(2,1)S(1)}) custom-call(bf16[64,8,512]{2,1,0:T(8,128)(2,1)S(1)} %all_to_all.20.x_ref, bf16[1536,768]{1,0:T(8,128)(2,1)S(1)} %get-tuple-element.31.kept_ref, bf16[1,4096,384]{2,1,0:T(8,128)(2,1)} %gate_hbm.3, bf16[1,4096,384]{2,1,0:T(8,128)(2,1)} %up_hbm.3, ...), custom_call_target="tpu_custom_call" | custom-call | tf_op jit(solution)/shard_map/gate_up/pallas_call | solution.py:528
  112.7 3.0 %collective-permute-start.9 = (bf16[128,1536]{1,0:T(8,128)(2,1)S(1)}, bf16[128,1536]{1,0:T(8,128)(2,1)S(1)}, u32[]{:S(2)}, u32[]{:S(2)}) collective-permute-start(bf16[128,1536]{1,0:T(8,128)(2,1)S(1)} %get-tuple-element.34), channel_id=1, source_target_pairs={{0,1},{1,0},{2,3},{3,2},{4,5},{5,4},{6,7},{7,6},{8,9},{9,8},{10,11... | collective-permute-start | bytes 1179656 | tf_op jit(solution)/shard_map/ppermute | solution.py:19
  115.8 0.0 collective-permute-done.10.moved_hbm
  115.8 1.9 %fetch_down.1.down_ref = bf16[768,2048]{1,0:T(8,128)(2,1)S(1)} custom-call(bf16[1,384,4096]{2,1,0:T(8,128)(2,1)} %down_hbm.3, bf16[384,2048]{1,0:T(8,128)(2,1)} %collective-permute-done.10.moved_hbm, f32[128,1536]{1,0:T(8,128)S(1)} %get-tuple-element.33.after_ref.part_ref), custom_call_target="tpu_custom_call" | custom-call | tf_op jit(solution)/shard_map/fetch_down/pallas_call | solution.py:560
  117.7 0.0 collective-permute-done.9.arrived_ref
  117.7 1.7 %shard_map.140 = bf16[64,8,512]{2,1,0:T(8,128)(2,1)} custom-call(f32[128,1536]{1,0:T(8,128)S(1)} %get-tuple-element.33.after_ref.part_ref, bf16[128,1536]{1,0:T(8,128)(2,1)S(1)} %collective-permute-done.9.arrived_ref, bf16[768,2048]{1,0:T(8,128)(2,1)S(1)} %fetch_down.1.down_ref), custom_call_target="tpu_custom_call" | custom-call | tf_op jit(solution)/shard_map/pallas_call | solution.py:606
  119.3 23.3 %all_to_all.21.x_ref = bf16[64,8,512]{2,1,0:T(8,128)(2,1)S(1)} all-to-all(bf16[64,8,512]{2,1,0:T(8,128)(2,1)} %shard_map.140), channel_id=1, replica_groups=mesh['groups'=2,'expert'=64,'replica'=2] {'expert'}, dimensions={0} | all-to-all | bytes 1048576 | tf_op jit(solution)/shard_map/all_to_all | solution.py:683
  142.6 0.2 shard_map.141
  142.8 2.4 %collective-permute-start.11 = (f32[2,8,512]{2,1,0:T(8,128)S(1)}, f32[2,8,512]{2,1,0:T(8,128)S(1)}, u32[]{:S(2)}, u32[]{:S(2)}) collective-permute-start(f32[2,8,512]{2,1,0:T(8,128)S(1)} %get-tuple-element.38), channel_id=1, source_target_pairs={{0,1},{1,0},{2,3},{3,2},{4,5},{5,4},{6,7},{7,6},{8,9},{9,8},{10,11... | collective-permute-start | bytes 98312 | tf_op jit(solution)/shard_map/ppermute | solution.py:19
  145.2 0.9 collective-permute-done.11.other_ref
  146.0 0.6 shard_map.142
  (1 shorter events, 0.0 us)
Async XLA Ops:
  4.1 105.7 %collective-permute-start.8 = (bf16[2048,768]{1,0:T(8,128)(2,1)}, bf16[2048,768]{1,0:T(8,128)(2,1)}, u32[]{:S(2)}, u32[]{:S(2)}) collective-permute-start(bf16[2048,768]{1,0:T(8,128)(2,1)} %get-tuple-element.32), channel_id=1, source_target_pairs={{0,1},{1,0},{2,3},{3,2},{4,5},{5,4},{6,7},{7,6},{8,9},{9,8},{10,11... | collective-permute-start | bytes 9437192 | tf_op jit(solution)/shard_map/ppermute | solution.py:19
  27.8 39.2 %copy-start.10 = (bf16[4096]{0:T(1024)(128)(2,1)S(1)}, bf16[4096]{0:T(1024)(128)(2,1)}, u32[]{:S(2)}) copy-start(bf16[4096]{0:T(1024)(128)(2,1)} %param.22) | copy-start | bytes 24580
  27.8 54.0 %copy-start = (bf16[4,4096]{1,0:T(4,128)(2,1)S(1)}, bf16[4,4096]{1,0:T(4,128)(2,1)}, u32[]{:S(2)}) copy-start(bf16[4,4096]{1,0:T(4,128)(2,1)} %residual_ref.1) | copy-start | bytes 98308
  27.8 57.2 %copy-start.1 = (s32[8,8]{1,0:T(8,128)S(1)}, s32[8,8]{1,0:T(8,128)}, u32[]{:S(2)}) copy-start(s32[8,8]{1,0:T(8,128)} %ids_ref.1) | copy-start | bytes 772
  27.9 57.2 %copy-start.2 = (f32[8,8]{1,0:T(8,128)S(1)}, f32[8,8]{1,0:T(8,128)}, u32[]{:S(2)}) copy-start(f32[8,8]{1,0:T(8,128)} %weight_ref.1) | copy-start | bytes 772
  27.9 25.0 %all-to-all-start = ((bf16[64,8,256]{2,1,0:T(8,128)(2,1)}), bf16[64,8,256]{2,1,0:T(8,128)(2,1)}, u32[]{:S(2)}, u32[]{:S(2)}) async-start(bf16[64,8,256]{2,1,0:T(8,128)(2,1)} %get-tuple-element.22), calls=%async_computation | async-start | bytes 524288 | tf_op jit(solution)/shard_map/all_to_all | solution.py:668
  35.1 13.3 %collective-permute-start = (bf16[64,1024]{1,0:T(8,128)(2,1)}, bf16[64,1024]{1,0:T(8,128)(2,1)S(1)}, u32[]{:S(2)}, u32[]{:S(2)}) collective-permute-start(bf16[64,1024]{1,0:T(8,128)(2,1)} %get-tuple-element.24), channel_id=1, source_target_pairs={{0,2},{2,0},{4,6},{6,4},{8,10},{10,8},{12,14},{14,12},{16,18},{18,... | collective-permute-start | bytes 393224 | tf_op jit(solution)/shard_map/ppermute | solution.py:667
  35.3 13.6 %collective-permute-start.1 = (bf16[64,1024]{1,0:T(8,128)(2,1)}, bf16[64,1024]{1,0:T(8,128)(2,1)S(1)}, u32[]{:S(2)}, u32[]{:S(2)}) collective-permute-start(bf16[64,1024]{1,0:T(8,128)(2,1)} %get-tuple-element.25), channel_id=1, source_target_pairs={{0,16},{2,18},{4,20},{6,22},{8,24},{10,26},{12,28},{14,30},{16,0},... | collective-permute-start | bytes 393224 | tf_op jit(solution)/shard_map/ppermute | solution.py:667
  36.4 12.6 %collective-permute-start.2 = (bf16[64,1024]{1,0:T(8,128)(2,1)}, bf16[64,1024]{1,0:T(8,128)(2,1)S(1)}, u32[]{:S(2)}, u32[]{:S(2)}) collective-permute-start(bf16[64,1024]{1,0:T(8,128)(2,1)} %get-tuple-element.26), channel_id=1, source_target_pairs={{0,18},{2,16},{4,22},{6,20},{8,26},{10,24},{12,30},{14,28},{16,2},... | collective-permute-start | bytes 393224 | tf_op jit(solution)/shard_map/ppermute | solution.py:667
  37.9 11.5 %collective-permute-start.3 = (bf16[64,1024]{1,0:T(8,128)(2,1)}, bf16[64,1024]{1,0:T(8,128)(2,1)S(1)}, u32[]{:S(2)}, u32[]{:S(2)}) collective-permute-start(bf16[64,1024]{1,0:T(8,128)(2,1)} %get-tuple-element.23.refs_0_), channel_id=1, source_target_pairs={{0,1},{1,0},{2,3},{3,2},{4,5},{5,4},{6,7},{7,6},{8,9},{9,8},{10,11... | collective-permute-start | bytes 393224 | tf_op jit(solution)/shard_map/ppermute | solution.py:19
  48.4 1.9 %copy-start.3 = (bf16[64,1024]{1,0:T(8,128)(2,1)}, bf16[64,1024]{1,0:T(8,128)(2,1)S(1)}, u32[]{:S(2)}) copy-start(bf16[64,1024]{1,0:T(8,128)(2,1)S(1)} %collective-permute-done.refs_1_) | copy-start | bytes 393220
  48.4 1.4 collective-permute-start.4
  48.8 1.5 %copy-start.4 = (bf16[64,1024]{1,0:T(8,128)(2,1)}, bf16[64,1024]{1,0:T(8,128)(2,1)S(1)}, u32[]{:S(2)}) copy-start(bf16[64,1024]{1,0:T(8,128)(2,1)S(1)} %collective-permute-done.1.refs_2_) | copy-start | bytes 393220
  48.8 1.3 collective-permute-start.5
  49.0 1.4 copy-start.5
  49.0 1.4 collective-permute-start.6
  49.3 1.0 copy-start.6
  49.8 0.7 copy-start.7
  50.2 0.7 copy-start.8
  50.8 0.7 copy-start.9
  55.4 26.4 %all-to-all-start.1 = ((bf16[64,8,512]{2,1,0:T(8,128)(2,1)}), bf16[64,8,512]{2,1,0:T(8,128)(2,1)S(1)}, u32[]{:S(2)}, u32[]{:S(2)}) async-start(bf16[64,8,512]{2,1,0:T(8,128)(2,1)} %shard_map.136), calls=%async_computation.1 | async-start | bytes 1048576 | tf_op jit(solution)/shard_map/all_to_all | solution.py:676
  66.3 49.5 %collective-permute-start.10 = (bf16[384,2048]{1,0:T(8,128)(2,1)}, bf16[384,2048]{1,0:T(8,128)(2,1)}, u32[]{:S(2)}, u32[]{:S(2)}) collective-permute-start(bf16[384,2048]{1,0:T(8,128)(2,1)} %get-tuple-element.35), channel_id=1, source_target_pairs={{0,1},{1,0},{2,3},{3,2},{4,5},{5,4},{6,7},{7,6},{8,9},{9,8},{10,11... | collective-permute-start | bytes 4718600 | tf_op jit(solution)/shard_map/ppermute | solution.py:19
  82.0 3.9 %collective-permute-start.7 = (bf16[2,8,512]{2,1,0:T(8,128)(2,1)S(1)}, bf16[2,8,512]{2,1,0:T(8,128)(2,1)S(1)}, u32[]{:S(2)}, u32[]{:S(2)}) collective-permute-start(bf16[2,8,512]{2,1,0:T(8,128)(2,1)S(1)} %get-tuple-element.29), channel_id=1, source_target_pairs={{0,1},{1,0},{2,3},{3,2},{4,5},{5,4},{6,7},{7,6},{8,9},{9,8},{10,11... | collective-permute-start | bytes 49160 | tf_op jit(solution)/shard_map/ppermute | solution.py:19
  112.7 4.9 %collective-permute-start.9 = (bf16[128,1536]{1,0:T(8,128)(2,1)S(1)}, bf16[128,1536]{1,0:T(8,128)(2,1)S(1)}, u32[]{:S(2)}, u32[]{:S(2)}) collective-permute-start(bf16[128,1536]{1,0:T(8,128)(2,1)S(1)} %get-tuple-element.34), channel_id=1, source_target_pairs={{0,1},{1,0},{2,3},{3,2},{4,5},{5,4},{6,7},{7,6},{8,9},{9,8},{10,11... | collective-permute-start | bytes 1179656 | tf_op jit(solution)/shard_map/ppermute | solution.py:19
  142.8 3.2 %collective-permute-start.11 = (f32[2,8,512]{2,1,0:T(8,128)S(1)}, f32[2,8,512]{2,1,0:T(8,128)S(1)}, u32[]{:S(2)}, u32[]{:S(2)}) collective-permute-start(f32[2,8,512]{2,1,0:T(8,128)S(1)} %get-tuple-element.38), channel_id=1, source_target_pairs={{0,1},{1,0},{2,3},{3,2},{4,5},{5,4},{6,7},{7,6},{8,9},{9,8},{10,11... | collective-permute-start | bytes 98312 | tf_op jit(solution)/shard_map/ppermute | solution.py:19

commit v7 on v5

--- a/solution.py
+++ b/solution.py
@@ -60,10 +60,9 @@
     values_hbm,
     weight_hbm,
     out_hbm,
-    piece0,
-    piece1,
-    piece2,
-    piece3,
+    piece_own,
+    piece_near,
+    piece_diagonal,
     q_ref,
     tk_ref,
     tv_ref,
@@ -101,12 +100,14 @@
     chip = lax.axis_index(CHIPS)
     place = chip // side % 2 * 2 + chip % 2
     sliced, stored = [], []
-    for d, piece in enumerate((piece0, piece1, piece2, piece3)):
+    for j, (d, piece) in enumerate(
+        ((0, piece_own), (1 + core, piece_near), (3, piece_diagonal))
+    ):
         cols = piece.shape[1]
         at = pl.multiple_of((place ^ d) * cols, cols)
         source = weight_hbm.at[:, pl.ds(at, cols)]
-        sliced.append(pltpu.make_async_copy(source, pieces.at[d], few.at[len(small) + d]))
-        stored.append(pltpu.make_async_copy(pieces.at[d], piece, few.at[len(small) + 4 + d]))
+        sliced.append(pltpu.make_async_copy(source, pieces.at[j], few.at[len(small) + j]))
+        stored.append(pltpu.make_async_copy(pieces.at[j], piece, few.at[len(small) + 3 + j]))
         sliced[-1].start()
     for copy in small:
         copy.wait()
@@ -167,7 +168,7 @@
                 out_ref[(2 * g + 1) * side + y, :, lanes[part]] = far.astype(BF16)
         sent = pl.ds(2 * g * side, 2 * side)
         stored.append(
-            pltpu.make_async_copy(out_ref.at[sent], out_hbm.at[sent], few.at[len(small) + 8 + g])
+            pltpu.make_async_copy(out_ref.at[sent], out_hbm.at[sent], few.at[len(small) + 6 + g])
         )
         stored[-1].start()
     for copy in stored:
@@ -182,9 +183,9 @@
         attend_body,
         name="attend",
         out_shape=[pltpu.HBM((heads, 2 * seq_count, 2 * HEAD_WIDTH), BF16)]
-        + [pltpu.HBM((rows, cols // 4), BF16)] * 4,
+        + [pltpu.HBM((rows, cols // 4), BF16)] * 3,
         in_specs=[IN_HBM] * 7,
-        out_specs=[IN_HBM] * 5,
+        out_specs=[IN_HBM] * 4,
         scratch_shapes=[
             pltpu.VMEM(queries.shape, BF16),
             pltpu.VMEM(token_keys.shape, BF16),
@@ -192,13 +193,13 @@
             pltpu.SMEM(kv_len.shape, jnp.int32),
             pltpu.VMEM(stored_keys.shape, BF16),
             pltpu.VMEM(stored_values.shape, BF16),
-            pltpu.VMEM((4, rows, cols // 4), BF16),
+            pltpu.VMEM((3, rows, cols // 4), BF16),
             pltpu.VMEM((seq_count * heads, HEAD_WIDTH), F32),
             pltpu.VMEM((seq_count * heads, HEAD_WIDTH), F32),
             pltpu.VMEM((seq_count * heads, stored_keys.shape[1]), F32),
             pltpu.VMEM((heads, 2 * seq_count, 2 * HEAD_WIDTH), BF16),
             pltpu.SemaphoreType.DMA((2, seq_count)),
-            pltpu.SemaphoreType.DMA((16,)),
+            pltpu.SemaphoreType.DMA((14,)),
         ],
         compiler_params=pltpu.CompilerParams(vmem_limit_bytes=8 * MIB),
     )(
@@ -217,28 +218,37 @@
         copy.wait()
 
 
-def stack_body(*refs):
-    own, other, out_ref, sems = refs[:4], refs[4:8], refs[8], refs[9]
-    rows = own[0].shape[0]
+def stack_body(own, own_raw, near, near_raw, far, far_raw, diagonal, diagonal_far, out_ref, sems):
+    core = lax.axis_index(CORES)
+    chip = lax.axis_index(CHIPS)
+    rows, cols = own.shape
+    side = math.isqrt(lax.axis_size(CHIPS))
+    place = chip // side % 2 * 2 + chip % 2
+    block = pl.ds(pl.multiple_of(place * cols, cols), cols)
     pairs = []
-    for d in range(4):
-        for half, source in enumerate((own[d], other[d])):
-            at = (d % 2 * 2 + half) * rows
-            pairs.append((source, out_ref.at[d // 2, at : at + rows]))
+    for d, sources in (
+        (0, (own, own_raw.at[:, block])),
+        (1 + core, (near, near_raw.at[:, block])),
+        (2 - core, (far_raw.at[:, block], far)),
+        (3, (diagonal, diagonal_far)),
+    ):
+        for half, source in enumerate(sources):
+            at = pl.multiple_of((2 * d + half) * rows, rows)
+            pairs.append((source, out_ref.at[pl.ds(at, rows)]))
     copy_all(pairs, sems)
 
 
-def stack(own, other):
-    rows, cols = own[0].shape
+def stack(*pieces):
+    rows, cols = pieces[0].shape
     return pl.pallas_call(
         stack_body,
         name="stack",
-        out_shape=pltpu.VMEM((2, 4 * rows, cols), BF16),
+        out_shape=pltpu.VMEM((8 * rows, cols), BF16),
         in_specs=[IN_HBM] * 8,
         out_specs=IN_VMEM,
         scratch_shapes=[pltpu.SemaphoreType.DMA((8,))],
         compiler_params=pltpu.CompilerParams(vmem_limit_bytes=2 * MIB),
-    )(*map(in_hbm, own), *map(in_hbm, other))
+    )(*map(in_hbm, pieces))
 
 
 def halves_body(gate_hbm, up_hbm, down_hbm, kept_ref, *refs):
@@ -295,23 +305,28 @@
 
 def project_body(x_ref, weight_ref, out_hbm, held, sems):
     chips, tile, width = x_ref.shape
-    cols = weight_ref.shape[2]
+    cols = weight_ref.shape[1]
     half = cols // 2
-    step = 16
-    low = lax.broadcasted_iota(jnp.int32, (step, tile, half), 1) < tile // 2
+    step = chips // 2
+
+    def paired(first, second):
+        low = lax.broadcasted_iota(jnp.int32, first.shape, 1) < tile // 2
+        return (
+            jnp.where(low, first, pltpu.roll(second, tile // 2, 1)),
+            jnp.where(low, pltpu.roll(first, tile // 2, 1), second),
+        )
+
     copies = []
-    for j, at in enumerate(range(0, chips, step)):
-        rows = slice(at, at + step)
-        x = x_ref[rows].reshape(step * tile, width)
-        near, far = (
-            jnp.dot(x, weight_ref[j], preferred_element_type=F32).reshape(step, tile, cols)
-            for j in range(2)
-        )
-        kept = jnp.where(low, near[:, :, :half], far[:, :, half:])
-        moved = jnp.where(low, near[:, :, half:], far[:, :, :half])
-        moved = pltpu.roll(moved, tile // 2, 1)
-        held[rows] = (kept + moved).astype(BF16)
-        copies.append(pltpu.make_async_copy(held.at[rows], out_hbm.at[rows], sems.at[j]))
+    for j in range(2):
+        sent = slice(j * step, (j + 1) * step)
+        x = x_ref[sent].astype(F32).reshape(step // 2, 2, tile, width)
+        x = jnp.concatenate(paired(x[:, 0], x[:, 1]), axis=2)
+        x = x.reshape(step // 2 * tile, 2 * width).astype(BF16)
+        sums = jnp.dot(x, weight_ref[...], preferred_element_type=F32)
+        sums = sums.reshape(step // 2, tile, cols)
+        sums = jnp.stack(paired(sums[:, :, :half], sums[:, :, half:]), axis=1)
+        held[sent] = sums.reshape(step, tile, half).astype(BF16)
+        copies.append(pltpu.make_async_copy(held.at[sent], out_hbm.at[sent], sems.at[j]))
         copies[-1].start()
     for copy in copies:
         copy.wait()
@@ -329,35 +344,10 @@
 
 
 def project(x, weight):
-    dims = x.shape[0], x.shape[1], weight.shape[2] // 2
-    return sending_call(project_body, dims, [IN_VMEM] * 2, 12, x.shape[0] // 16)(
+    dims = x.shape[0], x.shape[1], weight.shape[1] // 2
+    return sending_call(project_body, dims, [IN_VMEM] * 2, 12, 2)(
         x, in_vmem(weight)
     )
-
-
-def project_body(x_ref, weight_ref, out_ref):
-    chips, tile, width = x_ref.shape
-    cols = weight_ref.shape[2]
-    half = cols // 2
-    step = 16
-    low = lax.broadcasted_iota(jnp.int32, (step, tile, half), 1) < tile // 2
-    for at in range(0, chips, step):
-        x = x_ref[at : at + step].reshape(step * tile, width)
-        near, far = (
-            jnp.dot(x, weight_ref[j], preferred_element_type=F32).reshape(step, tile, cols)
-            for j in range(2)
-        )
-        kept = jnp.where(low, near[:, :, :half], far[:, :, half:])
-        moved = jnp.where(low, near[:, :, half:], far[:, :, :half])
-        moved = pltpu.roll(moved, tile // 2, 1)
-        out_ref[at : at + step] = (kept + moved).astype(BF16)
-
-
-def project(x, weight):
-    cols = weight.shape[2]
-    return kernel_call(
-        project_body, pltpu.HBM((x.shape[0], x.shape[1], cols // 2), BF16), [IN_VMEM] * 2, 12
-    )(x, in_vmem(weight))
 
 
 def settle_body(x_ref, residual_ref, gain_ref, hidden_ref, kept_ref, given_ref, normed):
@@ -480,7 +470,9 @@
     return jnp.where(row == slot // 2 * 8 + quarter * 2 + slot % 2, 1.0, 0.0).astype(BF16)
 
 
-def gate_body(x_ref, kept_ref, gate_hbm, up_hbm, moved_hbm, part_ref, sent_ref, rest, moved, sems):
+def gate_body(
+    x_ref, kept_ref, gate_hbm, up_hbm, moved_hbm, down_hbm, part_ref, sent_ref, down_ref, rest, moved, sems
+):
     core = lax.axis_index(CORES)
     chips, tile, part = x_ref.shape
     half, both = moved.shape
@@ -492,6 +484,8 @@
     for j in range(2):
         rows = slice(j * step, (j + 1) * step)
         pairs.append((moved_hbm.at[rows], moved.at[rows]))
+    mine = pl.ds(pl.multiple_of(core * half, half), half)
+    pairs.append((down_hbm.at[0, : down_ref.shape[0], mine], down_ref))
     copies = [pltpu.make_async_copy(*pair, sems.at[j]) for j, pair in enumerate(pairs)]
     for copy in copies:
         copy.start()
@@ -519,35 +513,38 @@
     other = other + jnp.dot(x[:, step:], moved[step:], preferred_element_type=F32)
     part_ref[:, both:] = other
     sent_ref[:, :both] = other.astype(BF16)
-
-
-def gate_up(x, kept, w_gate, w_up, moved):
+    copies[4].wait()
+
+
+def gate_up(x, kept, w_gate, w_up, moved, w_down, ahead):
     chips, tile, _ = x.shape
     half, both = moved.shape
     dims = chips * tile // 4, 2 * both
     return pl.pallas_call(
         gate_body,
         name="gate_up",
-        out_shape=[pltpu.VMEM(dims, F32), pltpu.VMEM(dims, BF16)],
-        in_specs=[IN_VMEM] * 2 + [IN_HBM] * 3,
-        out_specs=[IN_VMEM] * 2,
+        out_shape=[pltpu.VMEM(dims, F32), pltpu.VMEM(dims, BF16), pltpu.VMEM((ahead, half), BF16)],
+        in_specs=[IN_VMEM] * 2 + [IN_HBM] * 4,
+        out_specs=[IN_VMEM] * 3,
         scratch_shapes=[
             pltpu.VMEM((half - kept.shape[0], both), BF16),
             pltpu.VMEM((half, both), BF16),
-            pltpu.SemaphoreType.DMA((4,)),
+            pltpu.SemaphoreType.DMA((5,)),
         ],
         compiler_params=pltpu.CompilerParams(vmem_limit_bytes=14 * MIB),
-    )(x, in_vmem(kept), *map(in_hbm, (w_gate, w_up, moved)))
+    )(x, in_vmem(kept), *map(in_hbm, (w_gate, w_up, moved, w_down)))
 
 
 def fetch_body(down_hbm, moved_hbm, after_ref, out_ref, sems):
-    del after_ref
     core = lax.axis_index(CORES)
+    ahead = after_ref.shape[0]
     units, half = moved_hbm.shape
     kept = pl.ds(pl.multiple_of(core * half, half), half)
     copies = [
-        pltpu.make_async_copy(down_hbm.at[0, :, kept], out_ref.at[:units], sems.at[0]),
-        pltpu.make_async_copy(moved_hbm, out_ref.at[units:], sems.at[1]),
+        pltpu.make_async_copy(
+            down_hbm.at[0, ahead:, kept], out_ref.at[: units - ahead], sems.at[0]
+        ),
+        pltpu.make_async_copy(moved_hbm, out_ref.at[units - ahead :], sems.at[1]),
     ]
     for copy in copies:
         copy.start()
@@ -560,7 +557,7 @@
     return pl.pallas_call(
         fetch_body,
         name="fetch_down",
-        out_shape=pltpu.VMEM((2 * units, half), BF16),
+        out_shape=pltpu.VMEM((2 * units - after.shape[0], half), BF16),
         in_specs=[IN_HBM] * 3,
         out_specs=IN_VMEM,
         scratch_shapes=[pltpu.SemaphoreType.DMA((2,))],
@@ -568,13 +565,14 @@
     )(in_hbm(w_down), in_hbm(moved), after)
 
 
-def down_body(part_ref, arrived_ref, down_ref, out_hbm, held, sems):
+def down_body(part_ref, arrived_ref, first_ref, rest_ref, out_hbm, held, sems):
     chips, tile, part = held.shape
     size = 256
     groups = chips * tile // size
     order = slot_order(size, back=True)
     slots = size // 4
-    units = down_ref.shape[0] // 2
+    ahead = first_ref.shape[0]
+    units = (ahead + rest_ref.shape[0]) // 2
 
     def act(at):
         gate, up = (
@@ -587,7 +585,8 @@
     quarters = []
     for p in range(4):
         lanes = slice(p * part, (p + 1) * part)
-        value = jnp.dot(hidden, down_ref[:, lanes], preferred_element_type=F32)
+        value = jnp.dot(hidden[:, :ahead], first_ref[:, lanes], preferred_element_type=F32)
+        value = value + jnp.dot(hidden[:, ahead:], rest_ref[:, lanes], preferred_element_type=F32)
         quarters.append(value.astype(BF16))
     copies = []
     for g in range(groups):
@@ -601,10 +600,10 @@
         copy.wait()
 
 
-def down(part, arrived, weight, tile):
-    dims = part.shape[0] * 4 // tile, tile, weight.shape[1] // 4
-    return sending_call(down_body, dims, [IN_VMEM] * 3, 8, 2)(
-        part, arrived, in_vmem(weight)
+def down(part, arrived, first, rest, tile):
+    dims = part.shape[0] * 4 // tile, tile, first.shape[1] // 4
+    return sending_call(down_body, dims, [IN_VMEM] * 4, 8, 2)(
+        part, arrived, in_vmem(first), in_vmem(rest)
     )
 
 
@@ -659,15 +658,21 @@
 ):
     chips = lax.axis_size(CHIPS)
     side = math.isqrt(chips)
-    outgoing, *pieces = attend(
+    own_raw = swapped(out_weight)
+    outgoing, own, near, diagonal = attend(
         queries, token_keys, token_values, kv_len, stored_keys, stored_values, out_weight
     )
-    own = [pieces[0]] + [
-        lax.ppermute(pieces[d], CHIPS, quad_step(side, d // 2, d % 2)) for d in (1, 2, 3)
+    step = [
+        (2 * source + j, 2 * target + j)
+        for j, way in enumerate((quad_step(side, 0, 1), quad_step(side, 1, 0)))
+        for source, target in way
     ]
+    near = lax.ppermute(near, (CHIPS, CORES), step)
+    near_raw = lax.ppermute(own_raw, (CHIPS, CORES), step)
+    diagonal = lax.ppermute(diagonal, CHIPS, quad_step(side, 1, 1))
     tokens = lax.all_to_all(outgoing, CHIPS, 0, 0, tiled=True)
-    other = [swapped(piece) for piece in own]
-    weight = stack(own, other)
+    far, far_raw, diagonal_far = (swapped(x) for x in (near, near_raw, diagonal))
+    weight = stack(own, own_raw, near, near_raw, far, far_raw, diagonal, diagonal_far)
     kept, *given_halves = halves(w_gate, w_up, w_down, 0.75)
     gate_moved, down_moved = (swapped(x) for x in given_halves)
     pick, mix = route(expert_ids, route_weight, chips)
@@ -677,9 +682,9 @@
     hidden, normed, normed_given = settle(came_back, residual, norm_gain[None])
     outgoing = dispatch(normed, swapped(normed_given), pick)
     incoming = lax.all_to_all(outgoing, CHIPS, 0, 0, tiled=True)
-    part, sent = gate_up(incoming, kept, w_gate, w_up, gate_moved)
-    down_weight = fetch_down(w_down, down_moved, part)
-    expert_out = down(part, swapped(sent), down_weight, incoming.shape[1])
+    part, sent, down_first = gate_up(incoming, kept, w_gate, w_up, gate_moved, w_down, 256)
+    down_rest = fetch_down(w_down, down_moved, down_first)
+    expert_out = down(part, swapped(sent), down_first, down_rest, incoming.shape[1])
     returned = lax.all_to_all(expert_out, CHIPS, 0, 0, tiled=True)
     moe_own, moe_given = combine(returned, mix)
     return finish(hidden, moe_own, swapped(moe_given))

time: 147 us -> 155 us (1.054)
  blocking collectives: 46.1 us -> 23.1 us
  waiting for transfers between devices: 26.9 us -> 48.7 us
  starting transfers between devices: 52.3 us -> 61.7 us
    all_to_all x1 -> x0, blocking collectives: 22.8 us -> none  [on_device(): incoming = lax.all_to_all(outgoing, CHIPS, 0, 0, tiled=True)]
    all_to_all x0 -> x1, waiting for transfers between devices: none -> 15.5 us  [on_device(): incoming = lax.all_to_all(outgoing, CHIPS, 0, 0, tiled=True)]
    all_to_all x0 -> x1, starting transfers between devices: none -> 7.42 us  [on_device(): incoming = lax.all_to_all(outgoing, CHIPS, 0, 0, tiled=True)]
    ppermute x3, waiting for transfers between devices: 9.69 us -> 15.3 us  [the longest x1 8.32 us: on_device(): near_raw = lax.ppermute(own_raw, (CHIPS, CORES), step)]
    ppermute x9, starting transfers between devices: 31.5 us -> 35.2 us  [swapped(): return lax.ppermute(x, CORES, [(0, 1), (1, 0)])]
    ppermute x3, starting transfers between devices: 2.76 us -> 1.12 us  [the longest x1 0.98 us: on_device(): diagonal = lax.ppermute(diagonal, CHIPS, quad_step(side, 1, 1))]
  transfers between devices with their start and end apart: 14 -> 15, of which waited for: 7 -> 8; matrix products, arithmetic and copies ran while one was open for 0% -> 0% of each run, Pallas kernels for 9% -> 11%
where the time goes in v7:
time: 155 us
  starting transfers between devices  61.7 us (40%)
  waiting for transfers between devices  48.7 us (31%)
  blocking collectives  23.1 us (15%)
  Pallas kernels  19.2 us (12%)
  local copies, waits for them, and re-layouts  1.72 us (1%)
    ppermute x9, starting transfers between devices, swapped(): return lax.ppermute(x, CORES, [(0, 1), (1, 0)])  35.2 us
    all_to_all x1, blocking collectives, on_device(): returned = lax.all_to_all(expert_out, CHIPS, 0, 0, tiled=True)  23.1 us
    all_to_all x1, waiting for transfers between devices, on_device(): incoming = lax.all_to_all(outgoing, CHIPS, 0, 0, tiled=True)  15.5 us
    all_to_all x1, waiting for transfers between devices, on_device(): came_back = lax.all_to_all(sums, CHIPS, 0, 0, tiled=True)  15.2 us
    all_to_all x1, starting transfers between devices, on_device(): came_back = lax.all_to_all(sums, CHIPS, 0, 0, tiled=True)  10.9 us
    ppermute x1, waiting for transfers between devices, on_device(): near_raw = lax.ppermute(own_raw, (CHIPS, CORES), step)  8.32 us
    all_to_all x1, starting transfers between devices, on_device(): incoming = lax.all_to_all(outgoing, CHIPS, 0, 0, tiled=True)  7.42 us
    all_to_all x1, starting transfers between devices, on_device(): tokens = lax.all_to_all(outgoing, CHIPS, 0, 0, tiled=True)  7.1 us
  transfers between devices with their start and end apart: 15, of which 8 were waited for; matrix products, arithmetic and copies ran while one was open for 0% of the time, Pallas kernels for 11%

profile of v7, /device:TPU:513, one launch (start us, length us, event | category | flops | bytes accessed | tf_op | source)
XLA Modules:
  0.0 154.7 jit_solution(10008439061347613105)
XLA Ops:
  0.0 20.4 %collective-permute-start = (bf16[64,4096]{1,0:T(8,128)(2,1)}, bf16[64,4096]{1,0:T(8,128)(2,1)S(1)}, u32[]{:S(2)}, u32[]{:S(2)}) collective-permute-start(bf16[64,4096]{1,0:T(8,128)(2,1)} %weight_hbm.1), channel_id=1, source_target_pairs={{0,1},{1,0},{2,3},{3,2},{4,5},{5,4},{6,7},{7,6},{8,9},{9,8},{10,11... | collective-permute-start | bytes 1572872 | tf_op jit(solution)/shard_map/ppermute | solution.py:19
  20.4 4.0 %halves.1 = (bf16[1536,768]{1,0:T(8,128)(2,1)S(1)}, bf16[2048,768]{1,0:T(8,128)(2,1)}, bf16[384,2048]{1,0:T(8,128)(2,1)}) custom-call(bf16[1,4096,384]{2,1,0:T(8,128)(2,1)} %gate_hbm.3, bf16[1,4096,384]{2,1,0:T(8,128)(2,1)} %up_hbm.3, bf16[1,384,4096]{2,1,0:T(8,128)(2,1)} %down_hbm.5), custom_call_target="tpu_custom_call" | custom-call | tf_op jit(solution)/shard_map/halves/pallas_call | solution.py:287
  24.5 0.1 collective-permute-start.8
  24.6 0.0 collective-permute-done.own_raw
  24.6 0.0 copy-start.3
  24.6 0.8 copy-done.3
  25.5 0.0 collective-permute-start.2
  25.5 8.3 %collective-permute-done.2.near_raw = bf16[64,4096]{1,0:T(8,128)(2,1)S(1)} collective-permute-done((bf16[64,4096]{1,0:T(8,128)(2,1)S(1)}, bf16[64,4096]{1,0:T(8,128)(2,1)S(1)}, u32[]{:S(2)}, u32[]{:S(2)}) %collective-permute-start.2) | collective-permute-done | bytes 524320 | tf_op jit(solution)/shard_map/ppermute | solution.py:671
  33.8 0.0 copy-start.4
  33.8 1.3 collective-permute-start.4
  35.1 3.1 %attend.1 = (bf16[64,8,256]{2,1,0:T(8,128)(2,1)}, bf16[64,1024]{1,0:T(8,128)(2,1)}, bf16[64,1024]{1,0:T(8,128)(2,1)}, bf16[64,1024]{1,0:T(8,128)(2,1)}) custom-call(bf16[4,8192]{1,0:T(4,128)(2,1)} %q_hbm.1, bf16[4,512]{1,0:T(4,128)(2,1)} %tk_hbm.1, bf16[4,512]{1,0:T(4,128)(2,1)} %tv_hbm.1, s32[4]{0:T(128)} %len_hbm.1, bf16[4,256,512]{2,1,0:T(8,128)(2,1)} %keys_hbm.1, ...), custom_call_target="tpu_custom_call" | custom-call | tf_op jit(solution)/shard_map/attend/pallas_call | solution.py:182
  38.3 7.1 %all-to-all-start = ((bf16[64,8,256]{2,1,0:T(8,128)(2,1)}), bf16[64,8,256]{2,1,0:T(8,128)(2,1)}, u32[]{:S(2)}, u32[]{:S(2)}) async-start(bf16[64,8,256]{2,1,0:T(8,128)(2,1)} %get-tuple-element.22), calls=%async_computation | async-start | bytes 524288 | tf_op jit(solution)/shard_map/all_to_all | solution.py:673
  45.4 0.0 copy-start.10
  45.4 0.0 copy-start
  45.4 0.1 collective-permute-start.1
  45.6 1.0 collective-permute-start.5
  46.5 7.0 %collective-permute-done.1.near = bf16[64,1024]{1,0:T(8,128)(2,1)S(1)} collective-permute-done((bf16[64,1024]{1,0:T(8,128)(2,1)}, bf16[64,1024]{1,0:T(8,128)(2,1)S(1)}, u32[]{:S(2)}, u32[]{:S(2)}) %collective-permute-start.1) | collective-permute-done | bytes 131104 | tf_op jit(solution)/shard_map/ppermute | solution.py:670
  53.5 0.0 copy-start.6
  53.5 4.4 %collective-permute-start.3 = (bf16[64,1024]{1,0:T(8,128)(2,1)S(1)}, bf16[64,1024]{1,0:T(8,128)(2,1)S(1)}, u32[]{:S(2)}, u32[]{:S(2)}) collective-permute-start(bf16[64,1024]{1,0:T(8,128)(2,1)S(1)} %collective-permute-done.1.near), channel_id=1, source_target_pairs={{0,1},{1,0},{2,3},{3,2},{4,5},{5,4},{6,7},{7,6},{8,9},{9,8},{10,11... | collective-permute-start | bytes 393224 | tf_op jit(solution)/shard_map/ppermute | solution.py:19
  57.9 0.0 collective-permute-done.5.diagonal
  57.9 0.0 copy-start.7
  57.9 0.1 collective-permute-start.6
  58.1 0.8 collective-permute-done.3.far
  58.9 0.0 copy-start.8
  58.9 0.4 collective-permute-done.6.diagonal_far
  59.3 0.0 collective-permute-done.4.far_raw
  59.3 0.0 copy-done.4
  59.3 0.0 copy-start.5
  59.3 0.8 copy-done.5
  60.1 0.0 copy-done.6
  60.1 0.0 copy-done.7
  60.1 0.0 copy-done.8
  60.1 0.0 copy-done.9
  60.1 0.0 copy-start.1
  60.1 0.0 copy-start.2
  60.2 1.4 stack.1.weight_ref
  61.5 0.0 all-to-all-done.x_ref
  61.5 2.1 %shard_map.136 = bf16[64,8,512]{2,1,0:T(8,128)(2,1)} custom-call(bf16[64,8,256]{2,1,0:T(8,128)(2,1)} %all-to-all-done.x_ref, bf16[512,1024]{1,0:T(8,128)(2,1)S(1)} %stack.1.weight_ref), custom_call_target="tpu_custom_call" | custom-call | tf_op jit(solution)/shard_map/pallas_call | solution.py:348
  63.7 10.9 %all-to-all-start.1 = ((bf16[64,8,512]{2,1,0:T(8,128)(2,1)}), bf16[64,8,512]{2,1,0:T(8,128)(2,1)S(1)}, u32[]{:S(2)}, u32[]{:S(2)}) async-start(bf16[64,8,512]{2,1,0:T(8,128)(2,1)} %shard_map.136), calls=%async_computation.1 | async-start | bytes 1048576 | tf_op jit(solution)/shard_map/all_to_all | solution.py:681
  74.6 0.6 collective-permute-start.10
  75.1 0.0 copy-done.10
  75.2 15.2 %all-to-all-done.1.x_ref = bf16[64,8,512]{2,1,0:T(8,128)(2,1)S(1)} async-done(((bf16[64,8,512]{2,1,0:T(8,128)(2,1)}), bf16[64,8,512]{2,1,0:T(8,128)(2,1)S(1)}, u32[]{:S(2)}, u32[]{:S(2)}) %all-to-all-start.1) | async-done | bytes 524320 | tf_op jit(solution)/shard_map/all_to_all | solution.py:681
  90.4 0.0 copy-done
  90.4 0.2 shard_map.137
  90.6 2.6 %collective-permute-start.7 = (bf16[2,8,512]{2,1,0:T(8,128)(2,1)S(1)}, bf16[2,8,512]{2,1,0:T(8,128)(2,1)S(1)}, u32[]{:S(2)}, u32[]{:S(2)}) collective-permute-start(bf16[2,8,512]{2,1,0:T(8,128)(2,1)S(1)} %get-tuple-element.28), channel_id=1, source_target_pairs={{0,1},{1,0},{2,3},{3,2},{4,5},{5,4},{6,7},{7,6},{8,9},{9,8},{10,11... | collective-permute-start | bytes 49160 | tf_op jit(solution)/shard_map/ppermute | solution.py:19
  93.3 0.0 copy-done.1
  93.3 0.0 copy-done.2
  93.3 0.2 shard_map.138
  93.5 0.6 collective-permute-done.7.other_ref
  94.1 1.0 shard_map.139
  95.1 7.4 %all-to-all-start.2 = ((bf16[64,8,512]{2,1,0:T(8,128)(2,1)}), bf16[64,8,512]{2,1,0:T(8,128)(2,1)S(1)}, u32[]{:S(2)}, u32[]{:S(2)}) async-start(bf16[64,8,512]{2,1,0:T(8,128)(2,1)} %shard_map.139), calls=%async_computation.2 | async-start | bytes 1048576 | tf_op jit(solution)/shard_map/all_to_all | solution.py:684
  102.6 0.0 collective-permute-done.8.moved_hbm
  102.6 15.5 %all-to-all-done.2.x_ref = bf16[64,8,512]{2,1,0:T(8,128)(2,1)S(1)} async-done(((bf16[64,8,512]{2,1,0:T(8,128)(2,1)}), bf16[64,8,512]{2,1,0:T(8,128)(2,1)S(1)}, u32[]{:S(2)}, u32[]{:S(2)}) %all-to-all-start.2) | async-done | bytes 524320 | tf_op jit(solution)/shard_map/all_to_all | solution.py:684
  118.1 3.0 %gate_up.1 = (f32[128,1536]{1,0:T(8,128)S(1)}, bf16[128,1536]{1,0:T(8,128)(2,1)S(1)}, bf16[256,2048]{1,0:T(8,128)(2,1)S(1)}) custom-call(bf16[64,8,512]{2,1,0:T(8,128)(2,1)S(1)} %all-to-all-done.2.x_ref, bf16[1536,768]{1,0:T(8,128)(2,1)S(1)} %get-tuple-element.30.kept_ref, bf16[1,4096,384]{2,1,0:T(8,128)(2,1)} %gate_hbm.3, bf16[1,4096,384]{2,1,0:T(8,128)(2,1)} %up_hbm.3, ...), custom_call_target="tpu_custom_call" | custom-call | tf_op jit(solution)/shard_map/gate_up/pallas_call | solution.py:523
  121.1 3.0 %collective-permute-start.9 = (bf16[128,1536]{1,0:T(8,128)(2,1)S(1)}, bf16[128,1536]{1,0:T(8,128)(2,1)S(1)}, u32[]{:S(2)}, u32[]{:S(2)}) collective-permute-start(bf16[128,1536]{1,0:T(8,128)(2,1)S(1)} %get-tuple-element.33), channel_id=1, source_target_pairs={{0,1},{1,0},{2,3},{3,2},{4,5},{5,4},{6,7},{7,6},{8,9},{9,8},{10,11... | collective-permute-start | bytes 1179656 | tf_op jit(solution)/shard_map/ppermute | solution.py:19
  124.1 0.0 collective-permute-done.10.moved_hbm
  124.1 1.6 %fetch_down.1.rest_ref = bf16[512,2048]{1,0:T(8,128)(2,1)S(1)} custom-call(bf16[1,384,4096]{2,1,0:T(8,128)(2,1)} %down_hbm.5, bf16[384,2048]{1,0:T(8,128)(2,1)} %collective-permute-done.10.moved_hbm, bf16[256,2048]{1,0:T(8,128)(2,1)S(1)} %get-tuple-element.34.after_ref.first_ref), custom_call_target="tpu_custom_call" | custom-call | tf_op jit(solution)/shard_map/fetch_down/pallas_call | solution.py:557
  125.7 0.0 collective-permute-done.9.arrived_ref
  125.7 1.7 %shard_map.140 = bf16[64,8,512]{2,1,0:T(8,128)(2,1)} custom-call(f32[128,1536]{1,0:T(8,128)S(1)} %get-tuple-element.32.part_ref, bf16[128,1536]{1,0:T(8,128)(2,1)S(1)} %collective-permute-done.9.arrived_ref, bf16[256,2048]{1,0:T(8,128)(2,1)S(1)} %get-tuple-element.34.after_ref.first_ref, bf16[512,2048]{1,0:T(8,128)(2,1)S(1)} %fetch_down.1.rest_ref), custom_call_target="tpu_custom_call" | custom-call | tf_op jit(solution)/shard_map/pallas_call | solution.py:605
  127.4 23.1 %all_to_all.20.x_ref = bf16[64,8,512]{2,1,0:T(8,128)(2,1)S(1)} all-to-all(bf16[64,8,512]{2,1,0:T(8,128)(2,1)} %shard_map.140), channel_id=1, replica_groups=mesh['groups'=2,'expert'=64,'replica'=2] {'expert'}, dimensions={0} | all-to-all | bytes 1048576 | tf_op jit(solution)/shard_map/all_to_all | solution.py:688
  150.4 0.2 shard_map.141
  150.6 2.6 %collective-permute-start.11 = (f32[2,8,512]{2,1,0:T(8,128)S(1)}, f32[2,8,512]{2,1,0:T(8,128)S(1)}, u32[]{:S(2)}, u32[]{:S(2)}) collective-permute-start(f32[2,8,512]{2,1,0:T(8,128)S(1)} %get-tuple-element.38), channel_id=1, source_target_pairs={{0,1},{1,0},{2,3},{3,2},{4,5},{5,4},{6,7},{7,6},{8,9},{9,8},{10,11... | collective-permute-start | bytes 98312 | tf_op jit(solution)/shard_map/ppermute | solution.py:19
  153.2 0.9 collective-permute-done.11.other_ref
  154.0 0.6 shard_map.142
  (2 shorter events, 0.0 us)
Async XLA Ops:
  0.0 24.6 %collective-permute-start = (bf16[64,4096]{1,0:T(8,128)(2,1)}, bf16[64,4096]{1,0:T(8,128)(2,1)S(1)}, u32[]{:S(2)}, u32[]{:S(2)}) collective-permute-start(bf16[64,4096]{1,0:T(8,128)(2,1)} %weight_hbm.1), channel_id=1, source_target_pairs={{0,1},{1,0},{2,3},{3,2},{4,5},{5,4},{6,7},{7,6},{8,9},{9,8},{10,11... | collective-permute-start | bytes 1572872 | tf_op jit(solution)/shard_map/ppermute | solution.py:19
  24.5 78.1 %collective-permute-start.8 = (bf16[2048,768]{1,0:T(8,128)(2,1)}, bf16[2048,768]{1,0:T(8,128)(2,1)}, u32[]{:S(2)}, u32[]{:S(2)}) collective-permute-start(bf16[2048,768]{1,0:T(8,128)(2,1)} %get-tuple-element.31), channel_id=1, source_target_pairs={{0,1},{1,0},{2,3},{3,2},{4,5},{5,4},{6,7},{7,6},{8,9},{9,8},{10,11... | collective-permute-start | bytes 9437192 | tf_op jit(solution)/shard_map/ppermute | solution.py:19
  24.6 0.8 copy-start.3
  25.5 8.3 %collective-permute-start.2 = (bf16[64,4096]{1,0:T(8,128)(2,1)S(1)}, bf16[64,4096]{1,0:T(8,128)(2,1)S(1)}, u32[]{:S(2)}, u32[]{:S(2)}) collective-permute-start(bf16[64,4096]{1,0:T(8,128)(2,1)S(1)} %collective-permute-done.own_raw), channel_id=1, source_target_pairs={{0,2},{2,0},{4,6},{6,4},{8,10},{10,8},{12,14},{14,12},{16,18},{18,... | collective-permute-start | bytes 1572872 | tf_op jit(solution)/shard_map/ppermute | solution.py:671
  33.8 25.5 %copy-start.4 = (bf16[64,4096]{1,0:T(8,128)(2,1)}, bf16[64,4096]{1,0:T(8,128)(2,1)S(1)}, u32[]{:S(2)}) copy-start(bf16[64,4096]{1,0:T(8,128)(2,1)S(1)} %collective-permute-done.2.near_raw) | copy-start | bytes 1572868
  33.8 25.5 %collective-permute-start.4 = (bf16[64,4096]{1,0:T(8,128)(2,1)S(1)}, bf16[64,4096]{1,0:T(8,128)(2,1)S(1)}, u32[]{:S(2)}, u32[]{:S(2)}) collective-permute-start(bf16[64,4096]{1,0:T(8,128)(2,1)S(1)} %collective-permute-done.2.near_raw), channel_id=1, source_target_pairs={{0,1},{1,0},{2,3},{3,2},{4,5},{5,4},{6,7},{7,6},{8,9},{9,8},{10,11... | collective-permute-start | bytes 1572872 | tf_op jit(solution)/shard_map/ppermute | solution.py:19
  38.3 23.3 %all-to-all-start = ((bf16[64,8,256]{2,1,0:T(8,128)(2,1)}), bf16[64,8,256]{2,1,0:T(8,128)(2,1)}, u32[]{:S(2)}, u32[]{:S(2)}) async-start(bf16[64,8,256]{2,1,0:T(8,128)(2,1)} %get-tuple-element.22), calls=%async_computation | async-start | bytes 524288 | tf_op jit(solution)/shard_map/all_to_all | solution.py:673
  45.4 29.8 %copy-start.10 = (bf16[4096]{0:T(1024)(128)(2,1)S(1)}, bf16[4096]{0:T(1024)(128)(2,1)}, u32[]{:S(2)}) copy-start(bf16[4096]{0:T(1024)(128)(2,1)} %param.22) | copy-start | bytes 24580
  45.4 45.0 %copy-start = (bf16[4,4096]{1,0:T(4,128)(2,1)S(1)}, bf16[4,4096]{1,0:T(4,128)(2,1)}, u32[]{:S(2)}) copy-start(bf16[4,4096]{1,0:T(4,128)(2,1)} %residual_ref.1) | copy-start | bytes 98308
  45.4 8.1 %collective-permute-start.1 = (bf16[64,1024]{1,0:T(8,128)(2,1)}, bf16[64,1024]{1,0:T(8,128)(2,1)S(1)}, u32[]{:S(2)}, u32[]{:S(2)}) collective-permute-start(bf16[64,1024]{1,0:T(8,128)(2,1)} %get-tuple-element.24), channel_id=1, source_target_pairs={{0,2},{2,0},{4,6},{6,4},{8,10},{10,8},{12,14},{14,12},{16,18},{18,... | collective-permute-start | bytes 393224 | tf_op jit(solution)/shard_map/ppermute | solution.py:670
  45.6 12.4 %collective-permute-start.5 = (bf16[64,1024]{1,0:T(8,128)(2,1)}, bf16[64,1024]{1,0:T(8,128)(2,1)S(1)}, u32[]{:S(2)}, u32[]{:S(2)}) collective-permute-start(bf16[64,1024]{1,0:T(8,128)(2,1)} %get-tuple-element.25), channel_id=1, source_target_pairs={{0,18},{2,16},{4,22},{6,20},{8,26},{10,24},{12,30},{14,28},{16,2},... | collective-permute-start | bytes 393224 | tf_op jit(solution)/shard_map/ppermute | solution.py:672
  53.5 6.6 %copy-start.6 = (bf16[64,1024]{1,0:T(8,128)(2,1)}, bf16[64,1024]{1,0:T(8,128)(2,1)S(1)}, u32[]{:S(2)}) copy-start(bf16[64,1024]{1,0:T(8,128)(2,1)S(1)} %collective-permute-done.1.near) | copy-start | bytes 393220
  53.5 5.4 %collective-permute-start.3 = (bf16[64,1024]{1,0:T(8,128)(2,1)S(1)}, bf16[64,1024]{1,0:T(8,128)(2,1)S(1)}, u32[]{:S(2)}, u32[]{:S(2)}) collective-permute-start(bf16[64,1024]{1,0:T(8,128)(2,1)S(1)} %collective-permute-done.1.near), channel_id=1, source_target_pairs={{0,1},{1,0},{2,3},{3,2},{4,5},{5,4},{6,7},{7,6},{8,9},{9,8},{10,11... | collective-permute-start | bytes 393224 | tf_op jit(solution)/shard_map/ppermute | solution.py:19
  57.9 2.2 %copy-start.7 = (bf16[64,1024]{1,0:T(8,128)(2,1)}, bf16[64,1024]{1,0:T(8,128)(2,1)S(1)}, u32[]{:S(2)}) copy-start(bf16[64,1024]{1,0:T(8,128)(2,1)S(1)} %collective-permute-done.5.diagonal) | copy-start | bytes 393220
  57.9 1.3 collective-permute-start.6
  58.9 1.2 copy-start.8
  59.3 0.9 copy-start.9
  59.3 0.8 copy-start.5
  60.1 33.1 %copy-start.1 = (s32[8,8]{1,0:T(8,128)S(1)}, s32[8,8]{1,0:T(8,128)}, u32[]{:S(2)}) copy-start(s32[8,8]{1,0:T(8,128)} %ids_ref.1) | copy-start | bytes 772
  60.1 33.1 %copy-start.2 = (f32[8,8]{1,0:T(8,128)S(1)}, f32[8,8]{1,0:T(8,128)}, u32[]{:S(2)}) copy-start(f32[8,8]{1,0:T(8,128)} %weight_ref.1) | copy-start | bytes 772
  63.7 26.7 %all-to-all-start.1 = ((bf16[64,8,512]{2,1,0:T(8,128)(2,1)}), bf16[64,8,512]{2,1,0:T(8,128)(2,1)S(1)}, u32[]{:S(2)}, u32[]{:S(2)}) async-start(bf16[64,8,512]{2,1,0:T(8,128)(2,1)} %shard_map.136), calls=%async_computation.1 | async-start | bytes 1048576 | tf_op jit(solution)/shard_map/all_to_all | solution.py:681
  74.6 49.5 %collective-permute-start.10 = (bf16[384,2048]{1,0:T(8,128)(2,1)}, bf16[384,2048]{1,0:T(8,128)(2,1)}, u32[]{:S(2)}, u32[]{:S(2)}) collective-permute-start(bf16[384,2048]{1,0:T(8,128)(2,1)} %get-tuple-element.35), channel_id=1, source_target_pairs={{0,1},{1,0},{2,3},{3,2},{4,5},{5,4},{6,7},{7,6},{8,9},{9,8},{10,11... | collective-permute-start | bytes 4718600 | tf_op jit(solution)/shard_map/ppermute | solution.py:19
  90.6 3.5 %collective-permute-start.7 = (bf16[2,8,512]{2,1,0:T(8,128)(2,1)S(1)}, bf16[2,8,512]{2,1,0:T(8,128)(2,1)S(1)}, u32[]{:S(2)}, u32[]{:S(2)}) collective-permute-start(bf16[2,8,512]{2,1,0:T(8,128)(2,1)S(1)} %get-tuple-element.28), channel_id=1, source_target_pairs={{0,1},{1,0},{2,3},{3,2},{4,5},{5,4},{6,7},{7,6},{8,9},{9,8},{10,11... | collective-permute-start | bytes 49160 | tf_op jit(solution)/shard_map/ppermute | solution.py:19
  95.1 22.9 %all-to-all-start.2 = ((bf16[64,8,512]{2,1,0:T(8,128)(2,1)}), bf16[64,8,512]{2,1,0:T(8,128)(2,1)S(1)}, u32[]{:S(2)}, u32[]{:S(2)}) async-start(bf16[64,8,512]{2,1,0:T(8,128)(2,1)} %shard_map.139), calls=%async_computation.2 | async-start | bytes 1048576 | tf_op jit(solution)/shard_map/all_to_all | solution.py:684
  121.1 4.6 %collective-permute-start.9 = (bf16[128,1536]{1,0:T(8,128)(2,1)S(1)}, bf16[128,1536]{1,0:T(8,128)(2,1)S(1)}, u32[]{:S(2)}, u32[]{:S(2)}) collective-permute-start(bf16[128,1536]{1,0:T(8,128)(2,1)S(1)} %get-tuple-element.33), channel_id=1, source_target_pairs={{0,1},{1,0},{2,3},{3,2},{4,5},{5,4},{6,7},{7,6},{8,9},{9,8},{10,11... | collective-permute-start | bytes 1179656 | tf_op jit(solution)/shard_map/ppermute | solution.py:19
  150.6 3.4 %collective-permute-start.11 = (f32[2,8,512]{2,1,0:T(8,128)S(1)}, f32[2,8,512]{2,1,0:T(8,128)S(1)}, u32[]{:S(2)}, u32[]{:S(2)}) collective-permute-start(f32[2,8,512]{2,1,0:T(8,128)S(1)} %get-tuple-element.38), channel_id=1, source_target_pairs={{0,1},{1,0},{2,3},{3,2},{4,5},{5,4},{6,7},{7,6},{8,9},{9,8},{10,11... | collective-permute-start | bytes 98312 | tf_op jit(solution)/shard_map/ppermute | solution.py:19

commit v8 on v7

--- a/solution.py
+++ b/solution.py
@@ -19,10 +19,19 @@
     return lax.ppermute(x, CORES, [(0, 1), (1, 0)])
 
 
-def quad_step(side, dx, dy):
-    return [
-        (x * side + y, (x ^ dx) * side + (y ^ dy)) for x in range(side) for y in range(side)
-    ]
+def square_place(chip, side):
+    x, y = chip // side % 2, chip % 2
+    return x * 2 + y, 1 + (x ^ y)
+
+
+def square_step(side, way):
+    steps = []
+    for x in range(side):
+        for y in range(side):
+            along_y = {1: (x ^ y) & 1 == 0, -1: (x ^ y) & 1 == 1}.get(way)
+            dx, dy = (1, 1) if way == 0 else ((0, 1) if along_y else (1, 0))
+            steps.append((x * side + y, (x ^ dx) * side + (y ^ dy)))
+    return steps
 
 
 MIB = 1 << 20
@@ -61,7 +70,8 @@
     weight_hbm,
     out_hbm,
     piece_own,
-    piece_near,
+    piece_next,
+    piece_last,
     piece_diagonal,
     q_ref,
     tk_ref,
@@ -98,16 +108,16 @@
     for copy in copies[0] + copies[1]:
         copy.start()
     chip = lax.axis_index(CHIPS)
-    place = chip // side % 2 * 2 + chip % 2
+    place, ahead = square_place(chip, side)
     sliced, stored = [], []
     for j, (d, piece) in enumerate(
-        ((0, piece_own), (1 + core, piece_near), (3, piece_diagonal))
+        ((0, piece_own), (ahead, piece_next), (3 - ahead, piece_last), (3, piece_diagonal))
     ):
         cols = piece.shape[1]
         at = pl.multiple_of((place ^ d) * cols, cols)
         source = weight_hbm.at[:, pl.ds(at, cols)]
         sliced.append(pltpu.make_async_copy(source, pieces.at[j], few.at[len(small) + j]))
-        stored.append(pltpu.make_async_copy(pieces.at[j], piece, few.at[len(small) + 3 + j]))
+        stored.append(pltpu.make_async_copy(pieces.at[j], piece, few.at[len(small) + 4 + j]))
         sliced[-1].start()
     for copy in small:
         copy.wait()
@@ -168,7 +178,7 @@
                 out_ref[(2 * g + 1) * side + y, :, lanes[part]] = far.astype(BF16)
         sent = pl.ds(2 * g * side, 2 * side)
         stored.append(
-            pltpu.make_async_copy(out_ref.at[sent], out_hbm.at[sent], few.at[len(small) + 6 + g])
+            pltpu.make_async_copy(out_ref.at[sent], out_hbm.at[sent], few.at[len(small) + 8 + g])
         )
         stored[-1].start()
     for copy in stored:
@@ -183,9 +193,9 @@
         attend_body,
         name="attend",
         out_shape=[pltpu.HBM((heads, 2 * seq_count, 2 * HEAD_WIDTH), BF16)]
-        + [pltpu.HBM((rows, cols // 4), BF16)] * 3,
+        + [pltpu.HBM((rows, cols // 4), BF16)] * 4,
         in_specs=[IN_HBM] * 7,
-        out_specs=[IN_HBM] * 4,
+        out_specs=[IN_HBM] * 5,
         scratch_shapes=[
             pltpu.VMEM(queries.shape, BF16),
             pltpu.VMEM(token_keys.shape, BF16),
@@ -193,13 +203,13 @@
             pltpu.SMEM(kv_len.shape, jnp.int32),
             pltpu.VMEM(stored_keys.shape, BF16),
             pltpu.VMEM(stored_values.shape, BF16),
-            pltpu.VMEM((3, rows, cols // 4), BF16),
+            pltpu.VMEM((4, rows, cols // 4), BF16),
             pltpu.VMEM((seq_count * heads, HEAD_WIDTH), F32),
             pltpu.VMEM((seq_count * heads, HEAD_WIDTH), F32),
             pltpu.VMEM((seq_count * heads, stored_keys.shape[1]), F32),
             pltpu.VMEM((heads, 2 * seq_count, 2 * HEAD_WIDTH), BF16),
             pltpu.SemaphoreType.DMA((2, seq_count)),
-            pltpu.SemaphoreType.DMA((14,)),
+            pltpu.SemaphoreType.DMA((16,)),
         ],
         compiler_params=pltpu.CompilerParams(vmem_limit_bytes=8 * MIB),
     )(
@@ -218,28 +228,21 @@
         copy.wait()
 
 
-def stack_body(own, own_raw, near, near_raw, far, far_raw, diagonal, diagonal_far, out_ref, sems):
-    core = lax.axis_index(CORES)
-    chip = lax.axis_index(CHIPS)
-    rows, cols = own.shape
+def stack_body(*refs):
+    own, other, out_ref, sems = refs[:4], refs[4:8], refs[8], refs[9]
+    rows = own[0].shape[0]
     side = math.isqrt(lax.axis_size(CHIPS))
-    place = chip // side % 2 * 2 + chip % 2
-    block = pl.ds(pl.multiple_of(place * cols, cols), cols)
+    _, ahead = square_place(lax.axis_index(CHIPS), side)
     pairs = []
-    for d, sources in (
-        (0, (own, own_raw.at[:, block])),
-        (1 + core, (near, near_raw.at[:, block])),
-        (2 - core, (far_raw.at[:, block], far)),
-        (3, (diagonal, diagonal_far)),
-    ):
-        for half, source in enumerate(sources):
+    for j, d in enumerate((0, 3 - ahead, ahead, 3)):
+        for half, source in enumerate((own[j], other[j])):
             at = pl.multiple_of((2 * d + half) * rows, rows)
             pairs.append((source, out_ref.at[pl.ds(at, rows)]))
     copy_all(pairs, sems)
 
 
-def stack(*pieces):
-    rows, cols = pieces[0].shape
+def stack(own, other):
+    rows, cols = own[0].shape
     return pl.pallas_call(
         stack_body,
         name="stack",
@@ -248,7 +251,7 @@
         out_specs=IN_VMEM,
         scratch_shapes=[pltpu.SemaphoreType.DMA((8,))],
         compiler_params=pltpu.CompilerParams(vmem_limit_bytes=2 * MIB),
-    )(*map(in_hbm, pieces))
+    )(*map(in_hbm, own), *map(in_hbm, other))
 
 
 def halves_body(gate_hbm, up_hbm, down_hbm, kept_ref, *refs):
@@ -658,21 +661,16 @@
 ):
     chips = lax.axis_size(CHIPS)
     side = math.isqrt(chips)
-    own_raw = swapped(out_weight)
-    outgoing, own, near, diagonal = attend(
+    outgoing, *pieces = attend(
         queries, token_keys, token_values, kv_len, stored_keys, stored_values, out_weight
     )
-    step = [
-        (2 * source + j, 2 * target + j)
-        for j, way in enumerate((quad_step(side, 0, 1), quad_step(side, 1, 0)))
-        for source, target in way
+    own = pieces[:1] + [
+        lax.ppermute(piece, CHIPS, square_step(side, way))
+        for piece, way in zip(pieces[1:], (1, -1, 0), strict=True)
     ]
-    near = lax.ppermute(near, (CHIPS, CORES), step)
-    near_raw = lax.ppermute(own_raw, (CHIPS, CORES), step)
-    diagonal = lax.ppermute(diagonal, CHIPS, quad_step(side, 1, 1))
     tokens = lax.all_to_all(outgoing, CHIPS, 0, 0, tiled=True)
-    far, far_raw, diagonal_far = (swapped(x) for x in (near, near_raw, diagonal))
-    weight = stack(own, own_raw, near, near_raw, far, far_raw, diagonal, diagonal_far)
+    other = [swapped(piece) for piece in own]
+    weight = stack(own, other)
     kept, *given_halves = halves(w_gate, w_up, w_down, 0.75)
     gate_moved, down_moved = (swapped(x) for x in given_halves)
     pick, mix = route(expert_ids, route_weight, chips)

time: 155 us -> 147 us (0.948)
  waiting for transfers between devices: 48.7 us -> 23.4 us
  blocking collectives: 23.1 us -> 45.9 us
  starting transfers between devices: 61.7 us -> 56.3 us
    all_to_all x0 -> x1, blocking collectives: none -> 22.9 us  [on_device(): incoming = lax.all_to_all(outgoing, CHIPS, 0, 0, tiled=True)]
    all_to_all x1 -> x0, waiting for transfers between devices: 15.5 us -> none  [on_device(): incoming = lax.all_to_all(outgoing, CHIPS, 0, 0, tiled=True)]
    ppermute x3, waiting for transfers between devices: 15.3 us -> 6.09 us  [on_device(): lax.ppermute(piece, CHIPS, square_step(side, way))]
    all_to_all x1 -> x0, starting transfers between devices: 7.42 us -> none  [on_device(): incoming = lax.all_to_all(outgoing, CHIPS, 0, 0, tiled=True)]
  transfers between devices with their start and end apart: 15 -> 14, of which waited for: 8 -> 7; matrix products, arithmetic and copies ran while one was open for 0% -> 0% of each run, Pallas kernels for 11% -> 9%
where the time goes in v8:
time: 147 us; the launch traced here: 146 us
  starting transfers between devices  56.3 us (38%)
  blocking collectives  45.9 us (31%)
  waiting for transfers between devices  23.4 us (16%)
  Pallas kernels  19.3 us (13%)
    ppermute x9, starting transfers between devices, swapped(): return lax.ppermute(x, CORES, [(0, 1), (1, 0)])  35.5 us
    all_to_all x1, blocking collectives, on_device(): returned = lax.all_to_all(expert_out, CHIPS, 0, 0, tiled=True)  23 us
    all_to_all x1, blocking collectives, on_device(): incoming = lax.all_to_all(outgoing, CHIPS, 0, 0, tiled=True)  22.9 us
    all_to_all x1, waiting for transfers between devices, on_device(): came_back = lax.all_to_all(sums, CHIPS, 0, 0, tiled=True)  14.6 us
    all_to_all x1, starting transfers between devices, on_device(): came_back = lax.all_to_all(sums, CHIPS, 0, 0, tiled=True)  11.2 us
    all_to_all x1, starting transfers between devices, on_device(): tokens = lax.all_to_all(outgoing, CHIPS, 0, 0, tiled=True)  7.24 us
    ppermute x3, waiting for transfers between devices, on_device(): lax.ppermute(piece, CHIPS, square_step(side, way))  6.09 us
    pallas_call x1, Pallas kernels, halves(): pl.pallas_call(halves_body, name='halves', out_shape=[pltpu.VMEM((int(wid...  4.06 us
  transfers between devices with their start and end apart: 14, of which 7 were waited for; matrix products, arithmetic and copies ran while one was open for 0% of the time, Pallas kernels for 9%

profile of v8, /device:TPU:513, one launch (start us, length us, event | category | flops | bytes accessed | tf_op | source)
XLA Modules:
  0.0 146.2 jit_solution(6920898664337629730)
XLA Ops:
  0.0 4.1 %halves.1 = (bf16[1536,768]{1,0:T(8,128)(2,1)S(1)}, bf16[2048,768]{1,0:T(8,128)(2,1)}, bf16[384,2048]{1,0:T(8,128)(2,1)}) custom-call(bf16[1,4096,384]{2,1,0:T(8,128)(2,1)} %gate_hbm.3, bf16[1,4096,384]{2,1,0:T(8,128)(2,1)} %up_hbm.3, bf16[1,384,4096]{2,1,0:T(8,128)(2,1)} %down_hbm.5), custom_call_target="tpu_custom_call" | custom-call | tf_op jit(solution)/shard_map/halves/pallas_call | solution.py:290
  4.1 20.5 %collective-permute-start.8 = (bf16[2048,768]{1,0:T(8,128)(2,1)}, bf16[2048,768]{1,0:T(8,128)(2,1)}, u32[]{:S(2)}, u32[]{:S(2)}) collective-permute-start(bf16[2048,768]{1,0:T(8,128)(2,1)} %get-tuple-element.33), channel_id=1, source_target_pairs={{0,1},{1,0},{2,3},{3,2},{4,5},{5,4},{6,7},{7,6},{8,9},{9,8},{10,11... | collective-permute-start | bytes 9437192 | tf_op jit(solution)/shard_map/ppermute | solution.py:19
  24.6 3.2 %attend.1 = (bf16[64,8,256]{2,1,0:T(8,128)(2,1)}, bf16[64,1024]{1,0:T(8,128)(2,1)}, bf16[64,1024]{1,0:T(8,128)(2,1)}, bf16[64,1024]{1,0:T(8,128)(2,1)}, bf16[64,1024]{1,0:T(8,128)(2,1)}) custom-call(bf16[4,8192]{1,0:T(4,128)(2,1)} %q_hbm.1, bf16[4,512]{1,0:T(4,128)(2,1)} %tk_hbm.1, bf16[4,512]{1,0:T(4,128)(2,1)} %tv_hbm.1, s32[4]{0:T(128)} %len_hbm.1, ...), custom_call_target="tpu_custom_call" | custom-call | tf_op jit(solution)/shard_map/attend/pallas_call | solution.py:192
  27.8 0.0 copy-start.10
  27.8 0.0 copy-start
  27.8 0.0 copy-start.1
  27.9 0.0 copy-start.2
  27.9 7.2 %all-to-all-start = ((bf16[64,8,256]{2,1,0:T(8,128)(2,1)}), bf16[64,8,256]{2,1,0:T(8,128)(2,1)}, u32[]{:S(2)}, u32[]{:S(2)}) async-start(bf16[64,8,256]{2,1,0:T(8,128)(2,1)} %get-tuple-element.23), calls=%async_computation | async-start | bytes 524288 | tf_op jit(solution)/shard_map/all_to_all | solution.py:671
  35.1 0.1 collective-permute-start
  35.2 1.4 collective-permute-start.1
  36.7 0.9 collective-permute-start.2
  37.5 1.2 collective-permute-start.3
  38.7 4.7 %collective-permute-done.refs_1_ = bf16[64,1024]{1,0:T(8,128)(2,1)S(1)} collective-permute-done((bf16[64,1024]{1,0:T(8,128)(2,1)}, bf16[64,1024]{1,0:T(8,128)(2,1)S(1)}, u32[]{:S(2)}, u32[]{:S(2)}) %collective-permute-start) | collective-permute-done | bytes 131104 | tf_op jit(solution)/shard_map/ppermute | solution.py:668
  43.4 0.0 copy-start.3
  43.4 3.5 %collective-permute-start.4 = (bf16[64,1024]{1,0:T(8,128)(2,1)S(1)}, bf16[64,1024]{1,0:T(8,128)(2,1)S(1)}, u32[]{:S(2)}, u32[]{:S(2)}) collective-permute-start(bf16[64,1024]{1,0:T(8,128)(2,1)S(1)} %collective-permute-done.refs_1_), channel_id=1, source_target_pairs={{0,1},{1,0},{2,3},{3,2},{4,5},{5,4},{6,7},{7,6},{8,9},{9,8},{10,11... | collective-permute-start | bytes 393224 | tf_op jit(solution)/shard_map/ppermute | solution.py:19
  46.9 1.4 collective-permute-done.1.refs_2_
  48.3 0.0 copy-start.4
  48.3 0.5 collective-permute-start.5
  48.9 0.0 collective-permute-done.2.refs_3_
  48.9 0.0 copy-start.5
  48.9 0.1 collective-permute-start.6
  49.0 0.0 collective-permute-done.3.refs_4_
  49.0 0.0 copy-start.6
  49.0 0.0 collective-permute-done.4.refs_5_
  49.0 0.0 copy-start.7
  49.0 0.8 collective-permute-done.5.refs_6_
  49.8 0.0 copy-start.8
  49.8 0.4 collective-permute-done.6.refs_7_
  50.2 0.0 copy-done.3
  50.2 0.0 copy-done.4
  50.2 0.0 copy-done.5
  50.2 0.0 copy-done.6
  50.2 0.0 copy-done.7
  50.2 0.3 copy-done.8
  50.5 0.0 copy-start.9
  50.5 0.7 copy-done.9
  51.2 1.3 stack.1.weight_ref
  52.5 0.0 all-to-all-done.x_ref
  52.5 2.2 %shard_map.136 = bf16[64,8,512]{2,1,0:T(8,128)(2,1)} custom-call(bf16[64,8,256]{2,1,0:T(8,128)(2,1)} %all-to-all-done.x_ref, bf16[512,1024]{1,0:T(8,128)(2,1)S(1)} %stack.1.weight_ref), custom_call_target="tpu_custom_call" | custom-call | tf_op jit(solution)/shard_map/pallas_call | solution.py:351
  54.7 11.2 %all-to-all-start.1 = ((bf16[64,8,512]{2,1,0:T(8,128)(2,1)}), bf16[64,8,512]{2,1,0:T(8,128)(2,1)S(1)}, u32[]{:S(2)}, u32[]{:S(2)}) async-start(bf16[64,8,512]{2,1,0:T(8,128)(2,1)} %shard_map.136), calls=%async_computation.1 | async-start | bytes 1048576 | tf_op jit(solution)/shard_map/all_to_all | solution.py:679
  65.9 0.8 collective-permute-start.10
  66.6 0.0 copy-done.10
  66.7 14.6 %all-to-all-done.1.x_ref = bf16[64,8,512]{2,1,0:T(8,128)(2,1)S(1)} async-done(((bf16[64,8,512]{2,1,0:T(8,128)(2,1)}), bf16[64,8,512]{2,1,0:T(8,128)(2,1)S(1)}, u32[]{:S(2)}, u32[]{:S(2)}) %all-to-all-start.1) | async-done | bytes 524320 | tf_op jit(solution)/shard_map/all_to_all | solution.py:679
  81.3 0.0 copy-done
  81.3 0.2 shard_map.137
  81.5 3.2 %collective-permute-start.7 = (bf16[2,8,512]{2,1,0:T(8,128)(2,1)S(1)}, bf16[2,8,512]{2,1,0:T(8,128)(2,1)S(1)}, u32[]{:S(2)}, u32[]{:S(2)}) collective-permute-start(bf16[2,8,512]{2,1,0:T(8,128)(2,1)S(1)} %get-tuple-element.30), channel_id=1, source_target_pairs={{0,1},{1,0},{2,3},{3,2},{4,5},{5,4},{6,7},{7,6},{8,9},{9,8},{10,11... | collective-permute-start | bytes 49160 | tf_op jit(solution)/shard_map/ppermute | solution.py:19
  84.8 0.0 copy-done.1
  84.8 0.0 copy-done.2
  84.8 0.2 shard_map.138
  85.0 0.6 collective-permute-done.7.other_ref
  85.6 1.1 shard_map.139
  86.7 22.9 %all_to_all.20.x_ref = bf16[64,8,512]{2,1,0:T(8,128)(2,1)S(1)} all-to-all(bf16[64,8,512]{2,1,0:T(8,128)(2,1)} %shard_map.139), channel_id=1, replica_groups=mesh['groups'=2,'expert'=64,'replica'=2] {'expert'}, dimensions={0} | all-to-all | bytes 1048576 | tf_op jit(solution)/shard_map/all_to_all | solution.py:682
  109.6 0.0 collective-permute-done.8.moved_hbm
  109.6 3.0 %gate_up.1 = (f32[128,1536]{1,0:T(8,128)S(1)}, bf16[128,1536]{1,0:T(8,128)(2,1)S(1)}, bf16[256,2048]{1,0:T(8,128)(2,1)S(1)}) custom-call(bf16[64,8,512]{2,1,0:T(8,128)(2,1)S(1)} %all_to_all.20.x_ref, bf16[1536,768]{1,0:T(8,128)(2,1)S(1)} %get-tuple-element.32.kept_ref, bf16[1,4096,384]{2,1,0:T(8,128)(2,1)} %gate_hbm.3, bf16[1,4096,384]{2,1,0:T(8,128)(2,1)} %up_hbm.3, ...), custom_call_target="tpu_custom_call" | custom-call | tf_op jit(solution)/shard_map/gate_up/pallas_call | solution.py:526
  112.5 3.0 %collective-permute-start.9 = (bf16[128,1536]{1,0:T(8,128)(2,1)S(1)}, bf16[128,1536]{1,0:T(8,128)(2,1)S(1)}, u32[]{:S(2)}, u32[]{:S(2)}) collective-permute-start(bf16[128,1536]{1,0:T(8,128)(2,1)S(1)} %get-tuple-element.35), channel_id=1, source_target_pairs={{0,1},{1,0},{2,3},{3,2},{4,5},{5,4},{6,7},{7,6},{8,9},{9,8},{10,11... | collective-permute-start | bytes 1179656 | tf_op jit(solution)/shard_map/ppermute | solution.py:19
  115.6 0.0 collective-permute-done.10.moved_hbm
  115.6 1.6 %fetch_down.1.rest_ref = bf16[512,2048]{1,0:T(8,128)(2,1)S(1)} custom-call(bf16[1,384,4096]{2,1,0:T(8,128)(2,1)} %down_hbm.5, bf16[384,2048]{1,0:T(8,128)(2,1)} %collective-permute-done.10.moved_hbm, bf16[256,2048]{1,0:T(8,128)(2,1)S(1)} %get-tuple-element.36.after_ref.first_ref), custom_call_target="tpu_custom_call" | custom-call | tf_op jit(solution)/shard_map/fetch_down/pallas_call | solution.py:560
  117.2 0.0 collective-permute-done.9.arrived_ref
  117.2 1.7 %shard_map.140 = bf16[64,8,512]{2,1,0:T(8,128)(2,1)} custom-call(f32[128,1536]{1,0:T(8,128)S(1)} %get-tuple-element.34.part_ref, bf16[128,1536]{1,0:T(8,128)(2,1)S(1)} %collective-permute-done.9.arrived_ref, bf16[256,2048]{1,0:T(8,128)(2,1)S(1)} %get-tuple-element.36.after_ref.first_ref, bf16[512,2048]{1,0:T(8,128)(2,1)S(1)} %fetch_down.1.rest_ref), custom_call_target="tpu_custom_call" | custom-call | tf_op jit(solution)/shard_map/pallas_call | solution.py:608
  118.9 23.0 %all_to_all.21.x_ref = bf16[64,8,512]{2,1,0:T(8,128)(2,1)S(1)} all-to-all(bf16[64,8,512]{2,1,0:T(8,128)(2,1)} %shard_map.140), channel_id=1, replica_groups=mesh['groups'=2,'expert'=64,'replica'=2] {'expert'}, dimensions={0} | all-to-all | bytes 1048576 | tf_op jit(solution)/shard_map/all_to_all | solution.py:686
  141.9 0.2 shard_map.141
  142.1 2.6 %collective-permute-start.11 = (f32[2,8,512]{2,1,0:T(8,128)S(1)}, f32[2,8,512]{2,1,0:T(8,128)S(1)}, u32[]{:S(2)}, u32[]{:S(2)}) collective-permute-start(f32[2,8,512]{2,1,0:T(8,128)S(1)} %get-tuple-element.40), channel_id=1, source_target_pairs={{0,1},{1,0},{2,3},{3,2},{4,5},{5,4},{6,7},{7,6},{8,9},{9,8},{10,11... | collective-permute-start | bytes 98312 | tf_op jit(solution)/shard_map/ppermute | solution.py:19
  144.7 0.9 collective-permute-done.11.other_ref
  145.5 0.6 shard_map.142
  (1 shorter events, 0.0 us)
Async XLA Ops:
  4.1 105.5 %collective-permute-start.8 = (bf16[2048,768]{1,0:T(8,128)(2,1)}, bf16[2048,768]{1,0:T(8,128)(2,1)}, u32[]{:S(2)}, u32[]{:S(2)}) collective-permute-start(bf16[2048,768]{1,0:T(8,128)(2,1)} %get-tuple-element.33), channel_id=1, source_target_pairs={{0,1},{1,0},{2,3},{3,2},{4,5},{5,4},{6,7},{7,6},{8,9},{9,8},{10,11... | collective-permute-start | bytes 9437192 | tf_op jit(solution)/shard_map/ppermute | solution.py:19
  27.8 38.8 %copy-start.10 = (bf16[4096]{0:T(1024)(128)(2,1)S(1)}, bf16[4096]{0:T(1024)(128)(2,1)}, u32[]{:S(2)}) copy-start(bf16[4096]{0:T(1024)(128)(2,1)} %param.22) | copy-start | bytes 24580
  27.8 53.4 %copy-start = (bf16[4,4096]{1,0:T(4,128)(2,1)S(1)}, bf16[4,4096]{1,0:T(4,128)(2,1)}, u32[]{:S(2)}) copy-start(bf16[4,4096]{1,0:T(4,128)(2,1)} %residual_ref.1) | copy-start | bytes 98308
  27.8 56.9 %copy-start.1 = (s32[8,8]{1,0:T(8,128)S(1)}, s32[8,8]{1,0:T(8,128)}, u32[]{:S(2)}) copy-start(s32[8,8]{1,0:T(8,128)} %ids_ref.1) | copy-start | bytes 772
  27.9 56.9 %copy-start.2 = (f32[8,8]{1,0:T(8,128)S(1)}, f32[8,8]{1,0:T(8,128)}, u32[]{:S(2)}) copy-start(f32[8,8]{1,0:T(8,128)} %weight_ref.1) | copy-start | bytes 772
  27.9 24.7 %all-to-all-start = ((bf16[64,8,256]{2,1,0:T(8,128)(2,1)}), bf16[64,8,256]{2,1,0:T(8,128)(2,1)}, u32[]{:S(2)}, u32[]{:S(2)}) async-start(bf16[64,8,256]{2,1,0:T(8,128)(2,1)} %get-tuple-element.23), calls=%async_computation | async-start | bytes 524288 | tf_op jit(solution)/shard_map/all_to_all | solution.py:671
  35.1 8.3 %collective-permute-start = (bf16[64,1024]{1,0:T(8,128)(2,1)}, bf16[64,1024]{1,0:T(8,128)(2,1)S(1)}, u32[]{:S(2)}, u32[]{:S(2)}) collective-permute-start(bf16[64,1024]{1,0:T(8,128)(2,1)} %get-tuple-element.25), channel_id=1, source_target_pairs={{0,2},{2,18},{4,6},{6,22},{8,10},{10,26},{12,14},{14,30},{16,0},{1... | collective-permute-start | bytes 393224 | tf_op jit(solution)/shard_map/ppermute | solution.py:668
  35.2 13.1 %collective-permute-start.1 = (bf16[64,1024]{1,0:T(8,128)(2,1)}, bf16[64,1024]{1,0:T(8,128)(2,1)S(1)}, u32[]{:S(2)}, u32[]{:S(2)}) collective-permute-start(bf16[64,1024]{1,0:T(8,128)(2,1)} %get-tuple-element.26), channel_id=1, source_target_pairs={{0,16},{2,0},{4,20},{6,4},{8,24},{10,8},{12,28},{14,12},{16,18},{1... | collective-permute-start | bytes 393224 | tf_op jit(solution)/shard_map/ppermute | solution.py:668
  36.7 12.2 %collective-permute-start.2 = (bf16[64,1024]{1,0:T(8,128)(2,1)}, bf16[64,1024]{1,0:T(8,128)(2,1)S(1)}, u32[]{:S(2)}, u32[]{:S(2)}) collective-permute-start(bf16[64,1024]{1,0:T(8,128)(2,1)} %get-tuple-element.27), channel_id=1, source_target_pairs={{0,18},{2,16},{4,22},{6,20},{8,26},{10,24},{12,30},{14,28},{16,2},... | collective-permute-start | bytes 393224 | tf_op jit(solution)/shard_map/ppermute | solution.py:668
  37.5 11.5 %collective-permute-start.3 = (bf16[64,1024]{1,0:T(8,128)(2,1)}, bf16[64,1024]{1,0:T(8,128)(2,1)S(1)}, u32[]{:S(2)}, u32[]{:S(2)}) collective-permute-start(bf16[64,1024]{1,0:T(8,128)(2,1)} %get-tuple-element.24.refs_0_), channel_id=1, source_target_pairs={{0,1},{1,0},{2,3},{3,2},{4,5},{5,4},{6,7},{7,6},{8,9},{9,8},{10,11... | collective-permute-start | bytes 393224 | tf_op jit(solution)/shard_map/ppermute | solution.py:19
  43.4 6.8 %copy-start.3 = (bf16[64,1024]{1,0:T(8,128)(2,1)}, bf16[64,1024]{1,0:T(8,128)(2,1)S(1)}, u32[]{:S(2)}) copy-start(bf16[64,1024]{1,0:T(8,128)(2,1)S(1)} %collective-permute-done.refs_1_) | copy-start | bytes 393220
  43.4 5.6 %collective-permute-start.4 = (bf16[64,1024]{1,0:T(8,128)(2,1)S(1)}, bf16[64,1024]{1,0:T(8,128)(2,1)S(1)}, u32[]{:S(2)}, u32[]{:S(2)}) collective-permute-start(bf16[64,1024]{1,0:T(8,128)(2,1)S(1)} %collective-permute-done.refs_1_), channel_id=1, source_target_pairs={{0,1},{1,0},{2,3},{3,2},{4,5},{5,4},{6,7},{7,6},{8,9},{9,8},{10,11... | collective-permute-start | bytes 393224 | tf_op jit(solution)/shard_map/ppermute | solution.py:19
  48.3 1.9 %copy-start.4 = (bf16[64,1024]{1,0:T(8,128)(2,1)}, bf16[64,1024]{1,0:T(8,128)(2,1)S(1)}, u32[]{:S(2)}) copy-start(bf16[64,1024]{1,0:T(8,128)(2,1)S(1)} %collective-permute-done.1.refs_2_) | copy-start | bytes 393220
  48.3 1.5 %collective-permute-start.5 = (bf16[64,1024]{1,0:T(8,128)(2,1)S(1)}, bf16[64,1024]{1,0:T(8,128)(2,1)S(1)}, u32[]{:S(2)}, u32[]{:S(2)}) collective-permute-start(bf16[64,1024]{1,0:T(8,128)(2,1)S(1)} %collective-permute-done.1.refs_2_), channel_id=1, source_target_pairs={{0,1},{1,0},{2,3},{3,2},{4,5},{5,4},{6,7},{7,6},{8,9},{9,8},{10,11... | collective-permute-start | bytes 393224 | tf_op jit(solution)/shard_map/ppermute | solution.py:19
  48.9 1.4 copy-start.5
  48.9 1.3 collective-permute-start.6
  49.0 1.2 copy-start.6
  49.0 1.2 copy-start.7
  49.8 0.7 copy-start.8
  50.5 0.7 copy-start.9
  54.7 26.6 %all-to-all-start.1 = ((bf16[64,8,512]{2,1,0:T(8,128)(2,1)}), bf16[64,8,512]{2,1,0:T(8,128)(2,1)S(1)}, u32[]{:S(2)}, u32[]{:S(2)}) async-start(bf16[64,8,512]{2,1,0:T(8,128)(2,1)} %shard_map.136), calls=%async_computation.1 | async-start | bytes 1048576 | tf_op jit(solution)/shard_map/all_to_all | solution.py:679
  65.9 49.7 %collective-permute-start.10 = (bf16[384,2048]{1,0:T(8,128)(2,1)}, bf16[384,2048]{1,0:T(8,128)(2,1)}, u32[]{:S(2)}, u32[]{:S(2)}) collective-permute-start(bf16[384,2048]{1,0:T(8,128)(2,1)} %get-tuple-element.37), channel_id=1, source_target_pairs={{0,1},{1,0},{2,3},{3,2},{4,5},{5,4},{6,7},{7,6},{8,9},{9,8},{10,11... | collective-permute-start | bytes 4718600 | tf_op jit(solution)/shard_map/ppermute | solution.py:19
  81.5 4.1 %collective-permute-start.7 = (bf16[2,8,512]{2,1,0:T(8,128)(2,1)S(1)}, bf16[2,8,512]{2,1,0:T(8,128)(2,1)S(1)}, u32[]{:S(2)}, u32[]{:S(2)}) collective-permute-start(bf16[2,8,512]{2,1,0:T(8,128)(2,1)S(1)} %get-tuple-element.30), channel_id=1, source_target_pairs={{0,1},{1,0},{2,3},{3,2},{4,5},{5,4},{6,7},{7,6},{8,9},{9,8},{10,11... | collective-permute-start | bytes 49160 | tf_op jit(solution)/shard_map/ppermute | solution.py:19
  112.5 4.6 %collective-permute-start.9 = (bf16[128,1536]{1,0:T(8,128)(2,1)S(1)}, bf16[128,1536]{1,0:T(8,128)(2,1)S(1)}, u32[]{:S(2)}, u32[]{:S(2)}) collective-permute-start(bf16[128,1536]{1,0:T(8,128)(2,1)S(1)} %get-tuple-element.35), channel_id=1, source_target_pairs={{0,1},{1,0},{2,3},{3,2},{4,5},{5,4},{6,7},{7,6},{8,9},{9,8},{10,11... | collective-permute-start | bytes 1179656 | tf_op jit(solution)/shard_map/ppermute | solution.py:19
  142.1 3.4 %collective-permute-start.11 = (f32[2,8,512]{2,1,0:T(8,128)S(1)}, f32[2,8,512]{2,1,0:T(8,128)S(1)}, u32[]{:S(2)}, u32[]{:S(2)}) collective-permute-start(f32[2,8,512]{2,1,0:T(8,128)S(1)} %get-tuple-element.40), channel_id=1, source_target_pairs={{0,1},{1,0},{2,3},{3,2},{4,5},{5,4},{6,7},{7,6},{8,9},{9,8},{10,11... | collective-permute-start | bytes 98312 | tf_op jit(solution)/shard_map/ppermute | solution.py:19

commit v9 on v8

--- a/solution.py
+++ b/solution.py
@@ -473,22 +473,17 @@
     return jnp.where(row == slot // 2 * 8 + quarter * 2 + slot % 2, 1.0, 0.0).astype(BF16)
 
 
-def gate_body(
-    x_ref, kept_ref, gate_hbm, up_hbm, moved_hbm, down_hbm, part_ref, sent_ref, down_ref, rest, moved, sems
-):
+def gate_body(x_ref, kept_ref, moved_ref, gate_hbm, up_hbm, part_ref, sent_ref, rest, sems):
     core = lax.axis_index(CORES)
     chips, tile, part = x_ref.shape
-    half, both = moved.shape
+    half, both = moved_ref.shape
     units = both // 2
     count = kept_ref.shape[0]
     late = pl.ds(pl.multiple_of(core * half + count, part), half - count)
-    pairs = [(gate_hbm.at[0, late, :], rest.at[:, :units]), (up_hbm.at[0, late, :], rest.at[:, units:])]
-    step = half // 2
-    for j in range(2):
-        rows = slice(j * step, (j + 1) * step)
-        pairs.append((moved_hbm.at[rows], moved.at[rows]))
-    mine = pl.ds(pl.multiple_of(core * half, half), half)
-    pairs.append((down_hbm.at[0, : down_ref.shape[0], mine], down_ref))
+    pairs = (
+        (gate_hbm.at[0, late, :], rest.at[:, :units]),
+        (up_hbm.at[0, late, :], rest.at[:, units:]),
+    )
     copies = [pltpu.make_async_copy(*pair, sems.at[j]) for j, pair in enumerate(pairs)]
     for copy in copies:
         copy.start()
@@ -504,68 +499,55 @@
         jnp.concatenate([r[p * slots : (p + 1) * slots] for r in sorted_rows]) for p in range(4)
     ]
     x = jnp.concatenate(quarters, axis=1)
+    other = jnp.dot(x, moved_ref[...], preferred_element_type=F32)
+    part_ref[:, both:] = other
+    sent_ref[:, :both] = other.astype(BF16)
     own = jnp.dot(x[:, :count], kept_ref[...], preferred_element_type=F32)
-    for copy in copies[:2]:
+    for copy in copies:
         copy.wait()
     own = own + jnp.dot(x[:, count:], rest[...], preferred_element_type=F32)
     part_ref[:, :both] = own
     sent_ref[:, both:] = own.astype(BF16)
-    copies[2].wait()
-    other = jnp.dot(x[:, :step], moved[:step], preferred_element_type=F32)
-    copies[3].wait()
-    other = other + jnp.dot(x[:, step:], moved[step:], preferred_element_type=F32)
-    part_ref[:, both:] = other
-    sent_ref[:, :both] = other.astype(BF16)
-    copies[4].wait()
-
-
-def gate_up(x, kept, w_gate, w_up, moved, w_down, ahead):
+
+
+def gate_up(x, kept, moved, w_gate, w_up):
     chips, tile, _ = x.shape
     half, both = moved.shape
     dims = chips * tile // 4, 2 * both
     return pl.pallas_call(
         gate_body,
         name="gate_up",
-        out_shape=[pltpu.VMEM(dims, F32), pltpu.VMEM(dims, BF16), pltpu.VMEM((ahead, half), BF16)],
-        in_specs=[IN_VMEM] * 2 + [IN_HBM] * 4,
-        out_specs=[IN_VMEM] * 3,
+        out_shape=[pltpu.VMEM(dims, F32), pltpu.VMEM(dims, BF16)],
+        in_specs=[IN_VMEM] * 3 + [IN_HBM] * 2,
+        out_specs=[IN_VMEM] * 2,
         scratch_shapes=[
             pltpu.VMEM((half - kept.shape[0], both), BF16),
-            pltpu.VMEM((half, both), BF16),
-            pltpu.SemaphoreType.DMA((5,)),
+            pltpu.SemaphoreType.DMA((2,)),
         ],
-        compiler_params=pltpu.CompilerParams(vmem_limit_bytes=14 * MIB),
-    )(x, in_vmem(kept), *map(in_hbm, (w_gate, w_up, moved, w_down)))
-
-
-def fetch_body(down_hbm, moved_hbm, after_ref, out_ref, sems):
-    core = lax.axis_index(CORES)
-    ahead = after_ref.shape[0]
-    units, half = moved_hbm.shape
-    kept = pl.ds(pl.multiple_of(core * half, half), half)
-    copies = [
-        pltpu.make_async_copy(
-            down_hbm.at[0, ahead:, kept], out_ref.at[: units - ahead], sems.at[0]
-        ),
-        pltpu.make_async_copy(moved_hbm, out_ref.at[units - ahead :], sems.at[1]),
-    ]
-    for copy in copies:
-        copy.start()
-    for copy in copies:
-        copy.wait()
-
-
-def fetch_down(w_down, moved, after):
-    units, half = moved.shape
+        compiler_params=pltpu.CompilerParams(vmem_limit_bytes=8 * MIB),
+    )(x, in_vmem(kept), in_vmem(moved), in_hbm(w_gate), in_hbm(w_up))
+
+
+def fetch_body(down_hbm, after_ref, out_ref, sem):
+    del after_ref
+    half = out_ref.shape[1]
+    kept = pl.ds(pl.multiple_of(lax.axis_index(CORES) * half, half), half)
+    copy = pltpu.make_async_copy(down_hbm.at[0, :, kept], out_ref, sem)
+    copy.start()
+    copy.wait()
+
+
+def fetch_down(w_down, after):
+    _, units, width = w_down.shape
     return pl.pallas_call(
         fetch_body,
         name="fetch_down",
-        out_shape=pltpu.VMEM((2 * units - after.shape[0], half), BF16),
-        in_specs=[IN_HBM] * 3,
+        out_shape=pltpu.VMEM((units, width // 2), BF16),
+        in_specs=[IN_HBM] * 2,
         out_specs=IN_VMEM,
-        scratch_shapes=[pltpu.SemaphoreType.DMA((2,))],
+        scratch_shapes=[pltpu.SemaphoreType.DMA],
         compiler_params=pltpu.CompilerParams(vmem_limit_bytes=MIB),
-    )(in_hbm(w_down), in_hbm(moved), after)
+    )(in_hbm(w_down), after)
 
 
 def down_body(part_ref, arrived_ref, first_ref, rest_ref, out_hbm, held, sems):
@@ -574,8 +556,7 @@
     groups = chips * tile // size
     order = slot_order(size, back=True)
     slots = size // 4
-    ahead = first_ref.shape[0]
-    units = (ahead + rest_ref.shape[0]) // 2
+    units = first_ref.shape[0]
 
     def act(at):
         gate, up = (
@@ -584,12 +565,12 @@
         )
         return (gate / (1.0 + jnp.exp(-gate)) * up).astype(BF16)
 
-    hidden = jnp.concatenate([act(0), act(2 * units)], axis=1)
+    hidden = act(0), act(2 * units)
     quarters = []
     for p in range(4):
         lanes = slice(p * part, (p + 1) * part)
-        value = jnp.dot(hidden[:, :ahead], first_ref[:, lanes], preferred_element_type=F32)
-        value = value + jnp.dot(hidden[:, ahead:], rest_ref[:, lanes], preferred_element_type=F32)
+        value = jnp.dot(hidden[0], first_ref[:, lanes], preferred_element_type=F32)
+        value = value + jnp.dot(hidden[1], rest_ref[:, lanes], preferred_element_type=F32)
         quarters.append(value.astype(BF16))
     copies = []
     for g in range(groups):
@@ -671,18 +652,19 @@
     tokens = lax.all_to_all(outgoing, CHIPS, 0, 0, tiled=True)
     other = [swapped(piece) for piece in own]
     weight = stack(own, other)
-    kept, *given_halves = halves(w_gate, w_up, w_down, 0.75)
-    gate_moved, down_moved = (swapped(x) for x in given_halves)
+    kept, gate_given, down_given = halves(w_gate, w_up, w_down, 0.75)
+    gate_moved, down_moved = swapped(gate_given), swapped(down_given)
     pick, mix = route(expert_ids, route_weight, chips)
 
     sums = project(tokens, weight)
     came_back = lax.all_to_all(sums, CHIPS, 0, 0, tiled=True)
     hidden, normed, normed_given = settle(came_back, residual, norm_gain[None])
-    outgoing = dispatch(normed, swapped(normed_given), pick)
+    normed_other = swapped(normed_given)
+    outgoing = dispatch(normed, normed_other, pick)
     incoming = lax.all_to_all(outgoing, CHIPS, 0, 0, tiled=True)
-    part, sent, down_first = gate_up(incoming, kept, w_gate, w_up, gate_moved, w_down, 256)
-    down_rest = fetch_down(w_down, down_moved, down_first)
-    expert_out = down(part, swapped(sent), down_first, down_rest, incoming.shape[1])
+    part, sent = gate_up(incoming, kept, gate_moved, w_gate, w_up)
+    down_kept = fetch_down(w_down, part)
+    expert_out = down(part, swapped(sent), down_kept, down_moved, incoming.shape[1])
     returned = lax.all_to_all(expert_out, CHIPS, 0, 0, tiled=True)
     moe_own, moe_given = combine(returned, mix)
     return finish(hidden, moe_own, swapped(moe_given))

time: 147 us -> 150 us (1.020)
  Pallas kernels: 19.3 us -> 22 us
    pallas_call x1, Pallas kernels: 1.67 us -> 3.19 us  [down(): sending_call(down_body, dims, [IN_VMEM] * 4, 8, 2)]
where the time goes in v9:
time: 150 us; the launch traced here: 149 us
  starting transfers between devices  56.5 us (38%)
  blocking collectives  45.8 us (31%)
  waiting for transfers between devices  23.4 us (16%)
  Pallas kernels  22 us (15%)
    ppermute x9, starting transfers between devices, swapped(): return lax.ppermute(x, CORES, [(0, 1), (1, 0)])  35.7 us
    all_to_all x1, blocking collectives, on_device(): returned = lax.all_to_all(expert_out, CHIPS, 0, 0, tiled=True)  22.9 us
    all_to_all x1, blocking collectives, on_device(): incoming = lax.all_to_all(outgoing, CHIPS, 0, 0, tiled=True)  22.9 us
    all_to_all x1, waiting for transfers between devices, on_device(): came_back = lax.all_to_all(sums, CHIPS, 0, 0, tiled=True)  14.6 us
    all_to_all x1, starting transfers between devices, on_device(): came_back = lax.all_to_all(sums, CHIPS, 0, 0, tiled=True)  11.2 us
    all_to_all x1, starting transfers between devices, on_device(): tokens = lax.all_to_all(outgoing, CHIPS, 0, 0, tiled=True)  7.24 us
    ppermute x3, waiting for transfers between devices, on_device(): lax.ppermute(piece, CHIPS, square_step(side, way))  6.09 us
    pallas_call x1, Pallas kernels, gate_up(): pl.pallas_call(gate_body, name='gate_up', out_shape=[pltpu.VMEM(dims, F32...  4.34 us
  transfers between devices with their start and end apart: 14, of which 7 were waited for; matrix products, arithmetic and copies ran while one was open for 0% of the time, Pallas kernels for 9%

profile of v9, /device:TPU:513, one launch (start us, length us, event | category | flops | bytes accessed | tf_op | source)
XLA Modules:
  0.0 148.9 jit_solution(16645321697427980302)
XLA Ops:
  0.0 4.1 %halves.1 = (bf16[1536,768]{1,0:T(8,128)(2,1)S(1)}, bf16[2048,768]{1,0:T(8,128)(2,1)}, bf16[384,2048]{1,0:T(8,128)(2,1)}) custom-call(bf16[1,4096,384]{2,1,0:T(8,128)(2,1)} %gate_hbm.3, bf16[1,4096,384]{2,1,0:T(8,128)(2,1)} %up_hbm.3, bf16[1,384,4096]{2,1,0:T(8,128)(2,1)} %down_hbm.3), custom_call_target="tpu_custom_call" | custom-call | tf_op jit(solution)/shard_map/halves/pallas_call | solution.py:290
  4.1 20.5 %collective-permute-start.8 = (bf16[2048,768]{1,0:T(8,128)(2,1)}, bf16[2048,768]{1,0:T(8,128)(2,1)}, u32[]{:S(2)}, u32[]{:S(2)}) collective-permute-start(bf16[2048,768]{1,0:T(8,128)(2,1)} %get-tuple-element.32), channel_id=1, source_target_pairs={{0,1},{1,0},{2,3},{3,2},{4,5},{5,4},{6,7},{7,6},{8,9},{9,8},{10,11... | collective-permute-start | bytes 9437192 | tf_op jit(solution)/shard_map/ppermute | solution.py:19
  24.6 3.2 %attend.1 = (bf16[64,8,256]{2,1,0:T(8,128)(2,1)}, bf16[64,1024]{1,0:T(8,128)(2,1)}, bf16[64,1024]{1,0:T(8,128)(2,1)}, bf16[64,1024]{1,0:T(8,128)(2,1)}, bf16[64,1024]{1,0:T(8,128)(2,1)}) custom-call(bf16[4,8192]{1,0:T(4,128)(2,1)} %q_hbm.1, bf16[4,512]{1,0:T(4,128)(2,1)} %tk_hbm.1, bf16[4,512]{1,0:T(4,128)(2,1)} %tv_hbm.1, s32[4]{0:T(128)} %len_hbm.1, ...), custom_call_target="tpu_custom_call" | custom-call | tf_op jit(solution)/shard_map/attend/pallas_call | solution.py:192
  27.8 0.0 copy-start.10
  27.8 0.0 copy-start
  27.8 0.0 copy-start.1
  27.9 0.0 copy-start.2
  27.9 7.2 %all-to-all-start = ((bf16[64,8,256]{2,1,0:T(8,128)(2,1)}), bf16[64,8,256]{2,1,0:T(8,128)(2,1)}, u32[]{:S(2)}, u32[]{:S(2)}) async-start(bf16[64,8,256]{2,1,0:T(8,128)(2,1)} %get-tuple-element.22), calls=%async_computation | async-start | bytes 524288 | tf_op jit(solution)/shard_map/all_to_all | solution.py:652
  35.1 0.1 collective-permute-start
  35.2 1.4 collective-permute-start.1
  36.7 0.9 collective-permute-start.2
  37.5 1.2 collective-permute-start.3
  38.7 4.7 %collective-permute-done.refs_1_ = bf16[64,1024]{1,0:T(8,128)(2,1)S(1)} collective-permute-done((bf16[64,1024]{1,0:T(8,128)(2,1)}, bf16[64,1024]{1,0:T(8,128)(2,1)S(1)}, u32[]{:S(2)}, u32[]{:S(2)}) %collective-permute-start) | collective-permute-done | bytes 131104 | tf_op jit(solution)/shard_map/ppermute | solution.py:649
  43.4 0.0 copy-start.3
  43.4 3.5 %collective-permute-start.4 = (bf16[64,1024]{1,0:T(8,128)(2,1)S(1)}, bf16[64,1024]{1,0:T(8,128)(2,1)S(1)}, u32[]{:S(2)}, u32[]{:S(2)}) collective-permute-start(bf16[64,1024]{1,0:T(8,128)(2,1)S(1)} %collective-permute-done.refs_1_), channel_id=1, source_target_pairs={{0,1},{1,0},{2,3},{3,2},{4,5},{5,4},{6,7},{7,6},{8,9},{9,8},{10,11... | collective-permute-start | bytes 393224 | tf_op jit(solution)/shard_map/ppermute | solution.py:19
  46.9 1.4 collective-permute-done.1.refs_2_
  48.3 0.0 copy-start.4
  48.3 0.5 collective-permute-start.5
  48.9 0.0 collective-permute-done.2.refs_3_
  48.9 0.0 copy-start.5
  48.9 0.1 collective-permute-start.6
  49.0 0.0 collective-permute-done.3.refs_4_
  49.0 0.0 copy-start.6
  49.0 0.0 collective-permute-done.4.refs_5_
  49.0 0.0 copy-start.7
  49.0 0.8 collective-permute-done.5.refs_6_
  49.8 0.0 copy-start.8
  49.8 0.4 collective-permute-done.6.refs_7_
  50.2 0.0 copy-done.3
  50.2 0.0 copy-done.4
  50.2 0.0 copy-done.5
  50.2 0.0 copy-done.6
  50.2 0.0 copy-done.7
  50.2 0.3 copy-done.8
  50.5 0.0 copy-start.9
  50.5 0.7 copy-done.9
  51.2 1.3 stack.1.weight_ref
  52.5 0.0 all-to-all-done.x_ref
  52.5 2.2 %shard_map.136 = bf16[64,8,512]{2,1,0:T(8,128)(2,1)} custom-call(bf16[64,8,256]{2,1,0:T(8,128)(2,1)} %all-to-all-done.x_ref, bf16[512,1024]{1,0:T(8,128)(2,1)S(1)} %stack.1.weight_ref), custom_call_target="tpu_custom_call" | custom-call | tf_op jit(solution)/shard_map/pallas_call | solution.py:351
  54.7 11.2 %all-to-all-start.1 = ((bf16[64,8,512]{2,1,0:T(8,128)(2,1)}), bf16[64,8,512]{2,1,0:T(8,128)(2,1)S(1)}, u32[]{:S(2)}, u32[]{:S(2)}) async-start(bf16[64,8,512]{2,1,0:T(8,128)(2,1)} %shard_map.136), calls=%async_computation.1 | async-start | bytes 1048576 | tf_op jit(solution)/shard_map/all_to_all | solution.py:660
  65.9 0.8 collective-permute-start.10
  66.6 0.0 copy-done.10
  66.7 14.6 %all-to-all-done.1.x_ref = bf16[64,8,512]{2,1,0:T(8,128)(2,1)S(1)} async-done(((bf16[64,8,512]{2,1,0:T(8,128)(2,1)}), bf16[64,8,512]{2,1,0:T(8,128)(2,1)S(1)}, u32[]{:S(2)}, u32[]{:S(2)}) %all-to-all-start.1) | async-done | bytes 524320 | tf_op jit(solution)/shard_map/all_to_all | solution.py:660
  81.3 0.0 copy-done
  81.3 0.2 shard_map.137
  81.5 3.2 %collective-permute-start.7 = (bf16[2,8,512]{2,1,0:T(8,128)(2,1)S(1)}, bf16[2,8,512]{2,1,0:T(8,128)(2,1)S(1)}, u32[]{:S(2)}, u32[]{:S(2)}) collective-permute-start(bf16[2,8,512]{2,1,0:T(8,128)(2,1)S(1)} %get-tuple-element.29), channel_id=1, source_target_pairs={{0,1},{1,0},{2,3},{3,2},{4,5},{5,4},{6,7},{7,6},{8,9},{9,8},{10,11... | collective-permute-start | bytes 49160 | tf_op jit(solution)/shard_map/ppermute | solution.py:19
  84.8 0.0 copy-done.1
  84.8 0.0 copy-done.2
  84.8 0.2 shard_map.138
  85.0 0.6 collective-permute-done.7.other_ref
  85.6 1.1 shard_map.139
  86.7 22.9 %all_to_all.20.x_ref = bf16[64,8,512]{2,1,0:T(8,128)(2,1)S(1)} all-to-all(bf16[64,8,512]{2,1,0:T(8,128)(2,1)} %shard_map.139), channel_id=1, replica_groups=mesh['groups'=2,'expert'=64,'replica'=2] {'expert'}, dimensions={0} | all-to-all | bytes 1048576 | tf_op jit(solution)/shard_map/all_to_all | solution.py:664
  109.6 0.0 collective-permute-done.8.moved_ref
  109.6 4.3 %gate_up.1 = (f32[128,1536]{1,0:T(8,128)S(1)}, bf16[128,1536]{1,0:T(8,128)(2,1)S(1)}) custom-call(bf16[64,8,512]{2,1,0:T(8,128)(2,1)S(1)} %all_to_all.20.x_ref, bf16[1536,768]{1,0:T(8,128)(2,1)S(1)} %get-tuple-element.31.kept_ref, bf16[2048,768]{1,0:T(8,128)(2,1)} %collective-permute-done.8.moved_ref, bf16[1,4096,384]{2,1,0:T(8,128)(2,1)} %gate_hbm.3, ...), custom_call_target="tpu_custom_call" | custom-call | tf_op jit(solution)/shard_map/gate_up/pallas_call | solution.py:517
  113.9 3.0 %collective-permute-start.9 = (bf16[128,1536]{1,0:T(8,128)(2,1)S(1)}, bf16[128,1536]{1,0:T(8,128)(2,1)S(1)}, u32[]{:S(2)}, u32[]{:S(2)}) collective-permute-start(bf16[128,1536]{1,0:T(8,128)(2,1)S(1)} %get-tuple-element.34), channel_id=1, source_target_pairs={{0,1},{1,0},{2,3},{3,2},{4,5},{5,4},{6,7},{7,6},{8,9},{9,8},{10,11... | collective-permute-start | bytes 1179656 | tf_op jit(solution)/shard_map/ppermute | solution.py:19
  116.9 1.4 fetch_down.1.first_ref
  118.3 0.0 collective-permute-done.10.rest_ref
  118.4 0.0 collective-permute-done.9.arrived_ref
  118.4 3.2 %shard_map.140 = bf16[64,8,512]{2,1,0:T(8,128)(2,1)} custom-call(f32[128,1536]{1,0:T(8,128)S(1)} %get-tuple-element.33.after_ref.part_ref, bf16[128,1536]{1,0:T(8,128)(2,1)S(1)} %collective-permute-done.9.arrived_ref, bf16[384,2048]{1,0:T(8,128)(2,1)S(1)} %fetch_down.1.first_ref, bf16[384,2048]{1,0:T(8,128)(2,1)} %collective-permute-done.10.rest_ref), custom_call_target="tpu_custom_call" | custom-call | tf_op jit(solution)/shard_map/pallas_call | solution.py:589
  121.6 22.9 %all_to_all.21.x_ref = bf16[64,8,512]{2,1,0:T(8,128)(2,1)S(1)} all-to-all(bf16[64,8,512]{2,1,0:T(8,128)(2,1)} %shard_map.140), channel_id=1, replica_groups=mesh['groups'=2,'expert'=64,'replica'=2] {'expert'}, dimensions={0} | all-to-all | bytes 1048576 | tf_op jit(solution)/shard_map/all_to_all | solution.py:668
  144.5 0.2 shard_map.141
  144.7 2.7 %collective-permute-start.11 = (f32[2,8,512]{2,1,0:T(8,128)S(1)}, f32[2,8,512]{2,1,0:T(8,128)S(1)}, u32[]{:S(2)}, u32[]{:S(2)}) collective-permute-start(f32[2,8,512]{2,1,0:T(8,128)S(1)} %get-tuple-element.38), channel_id=1, source_target_pairs={{0,1},{1,0},{2,3},{3,2},{4,5},{5,4},{6,7},{7,6},{8,9},{9,8},{10,11... | collective-permute-start | bytes 98312 | tf_op jit(solution)/shard_map/ppermute | solution.py:19
  147.4 0.9 collective-permute-done.11.other_ref
  148.3 0.6 shard_map.142
  (1 shorter events, 0.0 us)
Async XLA Ops:
  4.1 105.5 %collective-permute-start.8 = (bf16[2048,768]{1,0:T(8,128)(2,1)}, bf16[2048,768]{1,0:T(8,128)(2,1)}, u32[]{:S(2)}, u32[]{:S(2)}) collective-permute-start(bf16[2048,768]{1,0:T(8,128)(2,1)} %get-tuple-element.32), channel_id=1, source_target_pairs={{0,1},{1,0},{2,3},{3,2},{4,5},{5,4},{6,7},{7,6},{8,9},{9,8},{10,11... | collective-permute-start | bytes 9437192 | tf_op jit(solution)/shard_map/ppermute | solution.py:19
  27.8 38.8 %copy-start.10 = (bf16[4096]{0:T(1024)(128)(2,1)S(1)}, bf16[4096]{0:T(1024)(128)(2,1)}, u32[]{:S(2)}) copy-start(bf16[4096]{0:T(1024)(128)(2,1)} %param.22) | copy-start | bytes 24580
  27.8 53.4 %copy-start = (bf16[4,4096]{1,0:T(4,128)(2,1)S(1)}, bf16[4,4096]{1,0:T(4,128)(2,1)}, u32[]{:S(2)}) copy-start(bf16[4,4096]{1,0:T(4,128)(2,1)} %residual_ref.1) | copy-start | bytes 98308
  27.8 56.9 %copy-start.1 = (s32[8,8]{1,0:T(8,128)S(1)}, s32[8,8]{1,0:T(8,128)}, u32[]{:S(2)}) copy-start(s32[8,8]{1,0:T(8,128)} %ids_ref.1) | copy-start | bytes 772
  27.9 56.9 %copy-start.2 = (f32[8,8]{1,0:T(8,128)S(1)}, f32[8,8]{1,0:T(8,128)}, u32[]{:S(2)}) copy-start(f32[8,8]{1,0:T(8,128)} %weight_ref.1) | copy-start | bytes 772
  27.9 24.7 %all-to-all-start = ((bf16[64,8,256]{2,1,0:T(8,128)(2,1)}), bf16[64,8,256]{2,1,0:T(8,128)(2,1)}, u32[]{:S(2)}, u32[]{:S(2)}) async-start(bf16[64,8,256]{2,1,0:T(8,128)(2,1)} %get-tuple-element.22), calls=%async_computation | async-start | bytes 524288 | tf_op jit(solution)/shard_map/all_to_all | solution.py:652
  35.1 8.3 %collective-permute-start = (bf16[64,1024]{1,0:T(8,128)(2,1)}, bf16[64,1024]{1,0:T(8,128)(2,1)S(1)}, u32[]{:S(2)}, u32[]{:S(2)}) collective-permute-start(bf16[64,1024]{1,0:T(8,128)(2,1)} %get-tuple-element.24), channel_id=1, source_target_pairs={{0,2},{2,18},{4,6},{6,22},{8,10},{10,26},{12,14},{14,30},{16,0},{1... | collective-permute-start | bytes 393224 | tf_op jit(solution)/shard_map/ppermute | solution.py:649
  35.2 13.1 %collective-permute-start.1 = (bf16[64,1024]{1,0:T(8,128)(2,1)}, bf16[64,1024]{1,0:T(8,128)(2,1)S(1)}, u32[]{:S(2)}, u32[]{:S(2)}) collective-permute-start(bf16[64,1024]{1,0:T(8,128)(2,1)} %get-tuple-element.25), channel_id=1, source_target_pairs={{0,16},{2,0},{4,20},{6,4},{8,24},{10,8},{12,28},{14,12},{16,18},{1... | collective-permute-start | bytes 393224 | tf_op jit(solution)/shard_map/ppermute | solution.py:649
  36.7 12.2 %collective-permute-start.2 = (bf16[64,1024]{1,0:T(8,128)(2,1)}, bf16[64,1024]{1,0:T(8,128)(2,1)S(1)}, u32[]{:S(2)}, u32[]{:S(2)}) collective-permute-start(bf16[64,1024]{1,0:T(8,128)(2,1)} %get-tuple-element.26), channel_id=1, source_target_pairs={{0,18},{2,16},{4,22},{6,20},{8,26},{10,24},{12,30},{14,28},{16,2},... | collective-permute-start | bytes 393224 | tf_op jit(solution)/shard_map/ppermute | solution.py:649
  37.5 11.5 %collective-permute-start.3 = (bf16[64,1024]{1,0:T(8,128)(2,1)}, bf16[64,1024]{1,0:T(8,128)(2,1)S(1)}, u32[]{:S(2)}, u32[]{:S(2)}) collective-permute-start(bf16[64,1024]{1,0:T(8,128)(2,1)} %get-tuple-element.23.refs_0_), channel_id=1, source_target_pairs={{0,1},{1,0},{2,3},{3,2},{4,5},{5,4},{6,7},{7,6},{8,9},{9,8},{10,11... | collective-permute-start | bytes 393224 | tf_op jit(solution)/shard_map/ppermute | solution.py:19
  43.4 6.8 %copy-start.3 = (bf16[64,1024]{1,0:T(8,128)(2,1)}, bf16[64,1024]{1,0:T(8,128)(2,1)S(1)}, u32[]{:S(2)}) copy-start(bf16[64,1024]{1,0:T(8,128)(2,1)S(1)} %collective-permute-done.refs_1_) | copy-start | bytes 393220
  43.4 5.6 %collective-permute-start.4 = (bf16[64,1024]{1,0:T(8,128)(2,1)S(1)}, bf16[64,1024]{1,0:T(8,128)(2,1)S(1)}, u32[]{:S(2)}, u32[]{:S(2)}) collective-permute-start(bf16[64,1024]{1,0:T(8,128)(2,1)S(1)} %collective-permute-done.refs_1_), channel_id=1, source_target_pairs={{0,1},{1,0},{2,3},{3,2},{4,5},{5,4},{6,7},{7,6},{8,9},{9,8},{10,11... | collective-permute-start | bytes 393224 | tf_op jit(solution)/shard_map/ppermute | solution.py:19
  48.3 1.9 %copy-start.4 = (bf16[64,1024]{1,0:T(8,128)(2,1)}, bf16[64,1024]{1,0:T(8,128)(2,1)S(1)}, u32[]{:S(2)}) copy-start(bf16[64,1024]{1,0:T(8,128)(2,1)S(1)} %collective-permute-done.1.refs_2_) | copy-start | bytes 393220
  48.3 1.5 %collective-permute-start.5 = (bf16[64,1024]{1,0:T(8,128)(2,1)S(1)}, bf16[64,1024]{1,0:T(8,128)(2,1)S(1)}, u32[]{:S(2)}, u32[]{:S(2)}) collective-permute-start(bf16[64,1024]{1,0:T(8,128)(2,1)S(1)} %collective-permute-done.1.refs_2_), channel_id=1, source_target_pairs={{0,1},{1,0},{2,3},{3,2},{4,5},{5,4},{6,7},{7,6},{8,9},{9,8},{10,11... | collective-permute-start | bytes 393224 | tf_op jit(solution)/shard_map/ppermute | solution.py:19
  48.9 1.4 copy-start.5
  48.9 1.3 collective-permute-start.6
  49.0 1.2 copy-start.6
  49.0 1.2 copy-start.7
  49.8 0.7 copy-start.8
  50.5 0.7 copy-start.9
  54.7 26.6 %all-to-all-start.1 = ((bf16[64,8,512]{2,1,0:T(8,128)(2,1)}), bf16[64,8,512]{2,1,0:T(8,128)(2,1)S(1)}, u32[]{:S(2)}, u32[]{:S(2)}) async-start(bf16[64,8,512]{2,1,0:T(8,128)(2,1)} %shard_map.136), calls=%async_computation.1 | async-start | bytes 1048576 | tf_op jit(solution)/shard_map/all_to_all | solution.py:660
  65.9 52.5 %collective-permute-start.10 = (bf16[384,2048]{1,0:T(8,128)(2,1)}, bf16[384,2048]{1,0:T(8,128)(2,1)}, u32[]{:S(2)}, u32[]{:S(2)}) collective-permute-start(bf16[384,2048]{1,0:T(8,128)(2,1)} %get-tuple-element.35), channel_id=1, source_target_pairs={{0,1},{1,0},{2,3},{3,2},{4,5},{5,4},{6,7},{7,6},{8,9},{9,8},{10,11... | collective-permute-start | bytes 4718600 | tf_op jit(solution)/shard_map/ppermute | solution.py:19
  81.5 4.1 %collective-permute-start.7 = (bf16[2,8,512]{2,1,0:T(8,128)(2,1)S(1)}, bf16[2,8,512]{2,1,0:T(8,128)(2,1)S(1)}, u32[]{:S(2)}, u32[]{:S(2)}) collective-permute-start(bf16[2,8,512]{2,1,0:T(8,128)(2,1)S(1)} %get-tuple-element.29), channel_id=1, source_target_pairs={{0,1},{1,0},{2,3},{3,2},{4,5},{5,4},{6,7},{7,6},{8,9},{9,8},{10,11... | collective-permute-start | bytes 49160 | tf_op jit(solution)/shard_map/ppermute | solution.py:19
  113.9 4.5 %collective-permute-start.9 = (bf16[128,1536]{1,0:T(8,128)(2,1)S(1)}, bf16[128,1536]{1,0:T(8,128)(2,1)S(1)}, u32[]{:S(2)}, u32[]{:S(2)}) collective-permute-start(bf16[128,1536]{1,0:T(8,128)(2,1)S(1)} %get-tuple-element.34), channel_id=1, source_target_pairs={{0,1},{1,0},{2,3},{3,2},{4,5},{5,4},{6,7},{7,6},{8,9},{9,8},{10,11... | collective-permute-start | bytes 1179656 | tf_op jit(solution)/shard_map/ppermute | solution.py:19
  144.7 3.6 %collective-permute-start.11 = (f32[2,8,512]{2,1,0:T(8,128)S(1)}, f32[2,8,512]{2,1,0:T(8,128)S(1)}, u32[]{:S(2)}, u32[]{:S(2)}) collective-permute-start(f32[2,8,512]{2,1,0:T(8,128)S(1)} %get-tuple-element.38), channel_id=1, source_target_pairs={{0,1},{1,0},{2,3},{3,2},{4,5},{5,4},{6,7},{7,6},{8,9},{9,8},{10,11... | collective-permute-start | bytes 98312 | tf_op jit(solution)/shard_map/ppermute | solution.py:19

commit v10 on v9

--- a/solution.py
+++ b/solution.py
@@ -438,12 +438,22 @@
     )(expert_ids, route_weight)
 
 
-def dispatch_body(kept_ref, other_ref, pick_ref, out_hbm, held, sems):
+def dispatch_body(kept_ref, other_ref, pick_ref, gate_hbm, up_hbm, out_hbm, rest_ref, held, sems):
+    count, both = rest_ref.shape
+    units = both // 2
+    half = gate_hbm.shape[1] // 2
+    end = (lax.axis_index(CORES) + 1) * half
+    late = pl.ds(pl.multiple_of(end - count, count), count)
+    copies = [
+        pltpu.make_async_copy(gate_hbm.at[0, late, :], rest_ref.at[:, :units], sems.at[2]),
+        pltpu.make_async_copy(up_hbm.at[0, late, :], rest_ref.at[:, units:], sems.at[3]),
+    ]
+    for copy in copies:
+        copy.start()
     pieces = [r[...].reshape(-1, r.shape[2]) for r in (kept_ref, other_ref)]
     tokens = jnp.concatenate(pieces)
-    chips, tile, half = held.shape
+    chips, tile, part = held.shape
     step = chips // 2
-    copies = []
     for j in range(2):
         rows = lax.dot_general(
             pick_ref[:, j * step * tile : (j + 1) * step * tile],
@@ -452,17 +462,25 @@
             preferred_element_type=F32,
         )
         sent = slice(j * step, (j + 1) * step)
-        held[sent] = rows.astype(BF16).reshape(step, tile, half)
+        held[sent] = rows.astype(BF16).reshape(step, tile, part)
         copies.append(pltpu.make_async_copy(held.at[sent], out_hbm.at[sent], sems.at[j]))
         copies[-1].start()
     for copy in copies:
         copy.wait()
 
 
-def dispatch(kept, other, pick):
-    tile, half = kept.shape[1:]
-    dims = pick.shape[1] // tile, tile, half
-    return sending_call(dispatch_body, dims, [IN_VMEM] * 3, 6, 2)(kept, other, pick)
+def dispatch(kept, other, pick, w_gate, w_up, late):
+    tile, part = kept.shape[1:]
+    dims = pick.shape[1] // tile, tile, part
+    return pl.pallas_call(
+        dispatch_body,
+        name="dispatch",
+        out_shape=[pltpu.HBM(dims, BF16), pltpu.VMEM((late, 2 * w_gate.shape[2]), BF16)],
+        in_specs=[IN_VMEM] * 3 + [IN_HBM] * 2,
+        out_specs=[IN_HBM, IN_VMEM],
+        scratch_shapes=[pltpu.VMEM(dims, BF16), pltpu.SemaphoreType.DMA((4,))],
+        compiler_params=pltpu.CompilerParams(vmem_limit_bytes=6 * MIB),
+    )(kept, other, pick, in_hbm(w_gate), in_hbm(w_up))
 
 
 def slot_order(size, back=False):
@@ -473,20 +491,9 @@
     return jnp.where(row == slot // 2 * 8 + quarter * 2 + slot % 2, 1.0, 0.0).astype(BF16)
 
 
-def gate_body(x_ref, kept_ref, moved_ref, gate_hbm, up_hbm, part_ref, sent_ref, rest, sems):
-    core = lax.axis_index(CORES)
+def gate_body(x_ref, kept_ref, rest_ref, moved_ref, part_ref, sent_ref):
     chips, tile, part = x_ref.shape
-    half, both = moved_ref.shape
-    units = both // 2
-    count = kept_ref.shape[0]
-    late = pl.ds(pl.multiple_of(core * half + count, part), half - count)
-    pairs = (
-        (gate_hbm.at[0, late, :], rest.at[:, :units]),
-        (up_hbm.at[0, late, :], rest.at[:, units:]),
-    )
-    copies = [pltpu.make_async_copy(*pair, sems.at[j]) for j, pair in enumerate(pairs)]
-    for copy in copies:
-        copy.start()
+    count, both = kept_ref.shape
     size = 256
     groups = chips * tile // size
     order = slot_order(size)
@@ -499,33 +506,26 @@
         jnp.concatenate([r[p * slots : (p + 1) * slots] for r in sorted_rows]) for p in range(4)
     ]
     x = jnp.concatenate(quarters, axis=1)
+    own = jnp.dot(x[:, :count], kept_ref[...], preferred_element_type=F32)
+    own = own + jnp.dot(x[:, count:], rest_ref[...], preferred_element_type=F32)
+    part_ref[:, :both] = own
+    sent_ref[:, both:] = own.astype(BF16)
     other = jnp.dot(x, moved_ref[...], preferred_element_type=F32)
     part_ref[:, both:] = other
     sent_ref[:, :both] = other.astype(BF16)
-    own = jnp.dot(x[:, :count], kept_ref[...], preferred_element_type=F32)
-    for copy in copies:
-        copy.wait()
-    own = own + jnp.dot(x[:, count:], rest[...], preferred_element_type=F32)
-    part_ref[:, :both] = own
-    sent_ref[:, both:] = own.astype(BF16)
-
-
-def gate_up(x, kept, moved, w_gate, w_up):
+
+
+def gate_up(x, kept, rest, moved):
     chips, tile, _ = x.shape
-    half, both = moved.shape
-    dims = chips * tile // 4, 2 * both
+    dims = chips * tile // 4, 2 * kept.shape[1]
     return pl.pallas_call(
         gate_body,
         name="gate_up",
         out_shape=[pltpu.VMEM(dims, F32), pltpu.VMEM(dims, BF16)],
-        in_specs=[IN_VMEM] * 3 + [IN_HBM] * 2,
+        in_specs=[IN_VMEM] * 4,
         out_specs=[IN_VMEM] * 2,
-        scratch_shapes=[
-            pltpu.VMEM((half - kept.shape[0], both), BF16),
-            pltpu.SemaphoreType.DMA((2,)),
-        ],
-        compiler_params=pltpu.CompilerParams(vmem_limit_bytes=8 * MIB),
-    )(x, in_vmem(kept), in_vmem(moved), in_hbm(w_gate), in_hbm(w_up))
+        compiler_params=pltpu.CompilerParams(vmem_limit_bytes=6 * MIB),
+    )(x, in_vmem(kept), in_vmem(rest), in_vmem(moved))
 
 
 def fetch_body(down_hbm, after_ref, out_ref, sem):
@@ -660,9 +660,10 @@
     came_back = lax.all_to_all(sums, CHIPS, 0, 0, tiled=True)
     hidden, normed, normed_given = settle(came_back, residual, norm_gain[None])
     normed_other = swapped(normed_given)
-    outgoing = dispatch(normed, normed_other, pick)
+    late = w_gate.shape[1] // 2 - kept.shape[0]
+    outgoing, rest = dispatch(normed, normed_other, pick, w_gate, w_up, late)
     incoming = lax.all_to_all(outgoing, CHIPS, 0, 0, tiled=True)
-    part, sent = gate_up(incoming, kept, gate_moved, w_gate, w_up)
+    part, sent = gate_up(incoming, kept, rest, gate_moved)
     down_kept = fetch_down(w_down, part)
     expert_out = down(part, swapped(sent), down_kept, down_moved, incoming.shape[1])
     returned = lax.all_to_all(expert_out, CHIPS, 0, 0, tiled=True)

time: 150 us -> 148 us (0.987)
  no operation moved by 1% of the time
where the time goes in v10:
time: 148 us
  starting transfers between devices  56.5 us (38%)
  blocking collectives  45.8 us (31%)
  waiting for transfers between devices  23.4 us (16%)
  Pallas kernels  20.9 us (14%)
    ppermute x9, starting transfers between devices, swapped(): return lax.ppermute(x, CORES, [(0, 1), (1, 0)])  35.6 us
    all_to_all x1, blocking collectives, on_device(): returned = lax.all_to_all(expert_out, CHIPS, 0, 0, tiled=True)  22.9 us
    all_to_all x1, blocking collectives, on_device(): incoming = lax.all_to_all(outgoing, CHIPS, 0, 0, tiled=True)  22.9 us
    all_to_all x1, waiting for transfers between devices, on_device(): came_back = lax.all_to_all(sums, CHIPS, 0, 0, tiled=True)  14.6 us
    all_to_all x1, starting transfers between devices, on_device(): came_back = lax.all_to_all(sums, CHIPS, 0, 0, tiled=True)  11.2 us
    all_to_all x1, starting transfers between devices, on_device(): tokens = lax.all_to_all(outgoing, CHIPS, 0, 0, tiled=True)  7.24 us
    ppermute x3, waiting for transfers between devices, on_device(): lax.ppermute(piece, CHIPS, square_step(side, way))  6.09 us
    pallas_call x1, Pallas kernels, halves(): pl.pallas_call(halves_body, name='halves', out_shape=[pltpu.VMEM((int(wid...  4.05 us
  transfers between devices with their start and end apart: 14, of which 7 were waited for; matrix products, arithmetic and copies ran while one was open for 0% of the time, Pallas kernels for 9%

profile of v10, /device:TPU:513, one launch (start us, length us, event | category | flops | bytes accessed | tf_op | source)
XLA Modules:
  0.0 147.7 jit_solution(10559444610451933976)
XLA Ops:
  0.0 4.1 %halves.1 = (bf16[1536,768]{1,0:T(8,128)(2,1)S(1)}, bf16[2048,768]{1,0:T(8,128)(2,1)}, bf16[384,2048]{1,0:T(8,128)(2,1)}) custom-call(bf16[1,4096,384]{2,1,0:T(8,128)(2,1)} %gate_hbm.3, bf16[1,4096,384]{2,1,0:T(8,128)(2,1)} %up_hbm.3, bf16[1,384,4096]{2,1,0:T(8,128)(2,1)} %down_hbm.3), custom_call_target="tpu_custom_call" | custom-call | tf_op jit(solution)/shard_map/halves/pallas_call | solution.py:290
  4.1 20.5 %collective-permute-start.8 = (bf16[2048,768]{1,0:T(8,128)(2,1)}, bf16[2048,768]{1,0:T(8,128)(2,1)}, u32[]{:S(2)}, u32[]{:S(2)}) collective-permute-start(bf16[2048,768]{1,0:T(8,128)(2,1)} %get-tuple-element.36), channel_id=1, source_target_pairs={{0,1},{1,0},{2,3},{3,2},{4,5},{5,4},{6,7},{7,6},{8,9},{9,8},{10,11... | collective-permute-start | bytes 9437192 | tf_op jit(solution)/shard_map/ppermute | solution.py:19
  24.6 3.2 %attend.1 = (bf16[64,8,256]{2,1,0:T(8,128)(2,1)}, bf16[64,1024]{1,0:T(8,128)(2,1)}, bf16[64,1024]{1,0:T(8,128)(2,1)}, bf16[64,1024]{1,0:T(8,128)(2,1)}, bf16[64,1024]{1,0:T(8,128)(2,1)}) custom-call(bf16[4,8192]{1,0:T(4,128)(2,1)} %q_hbm.1, bf16[4,512]{1,0:T(4,128)(2,1)} %tk_hbm.1, bf16[4,512]{1,0:T(4,128)(2,1)} %tv_hbm.1, s32[4]{0:T(128)} %len_hbm.1, ...), custom_call_target="tpu_custom_call" | custom-call | tf_op jit(solution)/shard_map/attend/pallas_call | solution.py:192
  27.8 0.0 copy-start.10
  27.8 0.0 copy-start
  27.8 0.0 copy-start.1
  27.8 0.0 copy-start.2
  27.8 7.2 %all-to-all-start = ((bf16[64,8,256]{2,1,0:T(8,128)(2,1)}), bf16[64,8,256]{2,1,0:T(8,128)(2,1)}, u32[]{:S(2)}, u32[]{:S(2)}) async-start(bf16[64,8,256]{2,1,0:T(8,128)(2,1)} %get-tuple-element.24), calls=%async_computation | async-start | bytes 524288 | tf_op jit(solution)/shard_map/all_to_all | solution.py:652
  35.1 0.1 collective-permute-start
  35.2 1.4 collective-permute-start.1
  36.7 0.9 collective-permute-start.2
  37.5 1.2 collective-permute-start.3
  38.7 4.7 %collective-permute-done.refs_1_ = bf16[64,1024]{1,0:T(8,128)(2,1)S(1)} collective-permute-done((bf16[64,1024]{1,0:T(8,128)(2,1)}, bf16[64,1024]{1,0:T(8,128)(2,1)S(1)}, u32[]{:S(2)}, u32[]{:S(2)}) %collective-permute-start) | collective-permute-done | bytes 131104 | tf_op jit(solution)/shard_map/ppermute | solution.py:649
  43.4 0.0 copy-start.3
  43.4 3.5 %collective-permute-start.4 = (bf16[64,1024]{1,0:T(8,128)(2,1)S(1)}, bf16[64,1024]{1,0:T(8,128)(2,1)S(1)}, u32[]{:S(2)}, u32[]{:S(2)}) collective-permute-start(bf16[64,1024]{1,0:T(8,128)(2,1)S(1)} %collective-permute-done.refs_1_), channel_id=1, source_target_pairs={{0,1},{1,0},{2,3},{3,2},{4,5},{5,4},{6,7},{7,6},{8,9},{9,8},{10,11... | collective-permute-start | bytes 393224 | tf_op jit(solution)/shard_map/ppermute | solution.py:19
  46.9 1.4 collective-permute-done.1.refs_2_
  48.3 0.0 copy-start.4
  48.3 0.5 collective-permute-start.5
  48.8 0.0 collective-permute-done.2.refs_3_
  48.8 0.0 copy-start.5
  48.8 0.1 collective-permute-start.6
  49.0 0.0 collective-permute-done.3.refs_4_
  49.0 0.0 copy-start.6
  49.0 0.0 collective-permute-done.4.refs_5_
  49.0 0.0 copy-start.7
  49.0 0.8 collective-permute-done.5.refs_6_
  49.8 0.0 copy-start.8
  49.8 0.4 collective-permute-done.6.refs_7_
  50.2 0.0 copy-done.3
  50.2 0.0 copy-done.4
  50.2 0.0 copy-done.5
  50.2 0.0 copy-done.6
  50.2 0.0 copy-done.7
  50.2 0.3 copy-done.8
  50.5 0.0 copy-start.9
  50.5 0.7 copy-done.9
  51.1 1.3 stack.1.weight_ref
  52.5 0.0 all-to-all-done.x_ref
  52.5 2.1 %shard_map.136 = bf16[64,8,512]{2,1,0:T(8,128)(2,1)} custom-call(bf16[64,8,256]{2,1,0:T(8,128)(2,1)} %all-to-all-done.x_ref, bf16[512,1024]{1,0:T(8,128)(2,1)S(1)} %stack.1.weight_ref), custom_call_target="tpu_custom_call" | custom-call | tf_op jit(solution)/shard_map/pallas_call | solution.py:351
  54.7 11.2 %all-to-all-start.1 = ((bf16[64,8,512]{2,1,0:T(8,128)(2,1)}), bf16[64,8,512]{2,1,0:T(8,128)(2,1)S(1)}, u32[]{:S(2)}, u32[]{:S(2)}) async-start(bf16[64,8,512]{2,1,0:T(8,128)(2,1)} %shard_map.136), calls=%async_computation.1 | async-start | bytes 1048576 | tf_op jit(solution)/shard_map/all_to_all | solution.py:660
  65.8 0.8 collective-permute-start.10
  66.6 0.0 copy-done.10
  66.6 14.6 %all-to-all-done.1.x_ref = bf16[64,8,512]{2,1,0:T(8,128)(2,1)S(1)} async-done(((bf16[64,8,512]{2,1,0:T(8,128)(2,1)}), bf16[64,8,512]{2,1,0:T(8,128)(2,1)S(1)}, u32[]{:S(2)}, u32[]{:S(2)}) %all-to-all-start.1) | async-done | bytes 524320 | tf_op jit(solution)/shard_map/all_to_all | solution.py:660
  81.2 0.0 copy-done
  81.2 0.2 shard_map.137
  81.5 3.2 %collective-permute-start.7 = (bf16[2,8,512]{2,1,0:T(8,128)(2,1)S(1)}, bf16[2,8,512]{2,1,0:T(8,128)(2,1)S(1)}, u32[]{:S(2)}, u32[]{:S(2)}) collective-permute-start(bf16[2,8,512]{2,1,0:T(8,128)(2,1)S(1)} %get-tuple-element.31), channel_id=1, source_target_pairs={{0,1},{1,0},{2,3},{3,2},{4,5},{5,4},{6,7},{7,6},{8,9},{9,8},{10,11... | collective-permute-start | bytes 49160 | tf_op jit(solution)/shard_map/ppermute | solution.py:19
  84.7 0.0 copy-done.1
  84.7 0.0 copy-done.2
  84.7 0.2 shard_map.138
  84.9 0.6 collective-permute-done.7.other_ref
  85.6 1.2 dispatch.1
  86.7 22.9 %all_to_all.20.x_ref = bf16[64,8,512]{2,1,0:T(8,128)(2,1)S(1)} all-to-all(bf16[64,8,512]{2,1,0:T(8,128)(2,1)} %get-tuple-element.33), channel_id=1, replica_groups=mesh['groups'=2,'expert'=64,'replica'=2] {'expert'}, dimensions={0} | all-to-all | bytes 1048576 | tf_op jit(solution)/shard_map/all_to_all | solution.py:665
  109.6 0.0 collective-permute-done.8.moved_ref
  109.6 3.1 %gate_up.1 = (f32[128,1536]{1,0:T(8,128)S(1)}, bf16[128,1536]{1,0:T(8,128)(2,1)S(1)}) custom-call(bf16[64,8,512]{2,1,0:T(8,128)(2,1)S(1)} %all_to_all.20.x_ref, bf16[1536,768]{1,0:T(8,128)(2,1)S(1)} %get-tuple-element.34.kept_ref, bf16[512,768]{1,0:T(8,128)(2,1)S(1)} %get-tuple-element.35.rest_ref, bf16[2048,768]{1,0:T(8,128)(2,1)} %collective-permute-done.8.moved_ref), custom_call_target="tpu_custom_call" | custom-call | tf_op jit(solution)/shard_map/gate_up/pallas_call | solution.py:521
  112.8 3.0 %collective-permute-start.9 = (bf16[128,1536]{1,0:T(8,128)(2,1)S(1)}, bf16[128,1536]{1,0:T(8,128)(2,1)S(1)}, u32[]{:S(2)}, u32[]{:S(2)}) collective-permute-start(bf16[128,1536]{1,0:T(8,128)(2,1)S(1)} %get-tuple-element.38), channel_id=1, source_target_pairs={{0,1},{1,0},{2,3},{3,2},{4,5},{5,4},{6,7},{7,6},{8,9},{9,8},{10,11... | collective-permute-start | bytes 1179656 | tf_op jit(solution)/shard_map/ppermute | solution.py:19
  115.8 1.4 fetch_down.1.first_ref
  117.2 0.0 collective-permute-done.10.rest_ref
  117.2 0.0 collective-permute-done.9.arrived_ref
  117.2 3.2 %shard_map.139 = bf16[64,8,512]{2,1,0:T(8,128)(2,1)} custom-call(f32[128,1536]{1,0:T(8,128)S(1)} %get-tuple-element.37.after_ref.part_ref, bf16[128,1536]{1,0:T(8,128)(2,1)S(1)} %collective-permute-done.9.arrived_ref, bf16[384,2048]{1,0:T(8,128)(2,1)S(1)} %fetch_down.1.first_ref, bf16[384,2048]{1,0:T(8,128)(2,1)} %collective-permute-done.10.rest_ref), custom_call_target="tpu_custom_call" | custom-call | tf_op jit(solution)/shard_map/pallas_call | solution.py:589
  120.4 22.9 %all_to_all.21.x_ref = bf16[64,8,512]{2,1,0:T(8,128)(2,1)S(1)} all-to-all(bf16[64,8,512]{2,1,0:T(8,128)(2,1)} %shard_map.139), channel_id=1, replica_groups=mesh['groups'=2,'expert'=64,'replica'=2] {'expert'}, dimensions={0} | all-to-all | bytes 1048576 | tf_op jit(solution)/shard_map/all_to_all | solution.py:669
  143.3 0.2 shard_map.140
  143.5 2.7 %collective-permute-start.11 = (f32[2,8,512]{2,1,0:T(8,128)S(1)}, f32[2,8,512]{2,1,0:T(8,128)S(1)}, u32[]{:S(2)}, u32[]{:S(2)}) collective-permute-start(f32[2,8,512]{2,1,0:T(8,128)S(1)} %get-tuple-element.42), channel_id=1, source_target_pairs={{0,1},{1,0},{2,3},{3,2},{4,5},{5,4},{6,7},{7,6},{8,9},{9,8},{10,11... | collective-permute-start | bytes 98312 | tf_op jit(solution)/shard_map/ppermute | solution.py:19
  146.2 0.9 collective-permute-done.11.other_ref
  147.1 0.6 shard_map.141
  (1 shorter events, 0.0 us)
Async XLA Ops:
  4.1 105.6 %collective-permute-start.8 = (bf16[2048,768]{1,0:T(8,128)(2,1)}, bf16[2048,768]{1,0:T(8,128)(2,1)}, u32[]{:S(2)}, u32[]{:S(2)}) collective-permute-start(bf16[2048,768]{1,0:T(8,128)(2,1)} %get-tuple-element.36), channel_id=1, source_target_pairs={{0,1},{1,0},{2,3},{3,2},{4,5},{5,4},{6,7},{7,6},{8,9},{9,8},{10,11... | collective-permute-start | bytes 9437192 | tf_op jit(solution)/shard_map/ppermute | solution.py:19
  27.8 38.8 %copy-start.10 = (bf16[4096]{0:T(1024)(128)(2,1)S(1)}, bf16[4096]{0:T(1024)(128)(2,1)}, u32[]{:S(2)}) copy-start(bf16[4096]{0:T(1024)(128)(2,1)} %param.22) | copy-start | bytes 24580
  27.8 53.4 %copy-start = (bf16[4,4096]{1,0:T(4,128)(2,1)S(1)}, bf16[4,4096]{1,0:T(4,128)(2,1)}, u32[]{:S(2)}) copy-start(bf16[4,4096]{1,0:T(4,128)(2,1)} %residual_ref.1) | copy-start | bytes 98308
  27.8 56.9 %copy-start.1 = (s32[8,8]{1,0:T(8,128)S(1)}, s32[8,8]{1,0:T(8,128)}, u32[]{:S(2)}) copy-start(s32[8,8]{1,0:T(8,128)} %ids_ref.1) | copy-start | bytes 772
  27.8 56.9 %copy-start.2 = (f32[8,8]{1,0:T(8,128)S(1)}, f32[8,8]{1,0:T(8,128)}, u32[]{:S(2)}) copy-start(f32[8,8]{1,0:T(8,128)} %weight_ref.1) | copy-start | bytes 772
  27.8 24.7 %all-to-all-start = ((bf16[64,8,256]{2,1,0:T(8,128)(2,1)}), bf16[64,8,256]{2,1,0:T(8,128)(2,1)}, u32[]{:S(2)}, u32[]{:S(2)}) async-start(bf16[64,8,256]{2,1,0:T(8,128)(2,1)} %get-tuple-element.24), calls=%async_computation | async-start | bytes 524288 | tf_op jit(solution)/shard_map/all_to_all | solution.py:652
  35.1 8.3 %collective-permute-start = (bf16[64,1024]{1,0:T(8,128)(2,1)}, bf16[64,1024]{1,0:T(8,128)(2,1)S(1)}, u32[]{:S(2)}, u32[]{:S(2)}) collective-permute-start(bf16[64,1024]{1,0:T(8,128)(2,1)} %get-tuple-element.26), channel_id=1, source_target_pairs={{0,2},{2,18},{4,6},{6,22},{8,10},{10,26},{12,14},{14,30},{16,0},{1... | collective-permute-start | bytes 393224 | tf_op jit(solution)/shard_map/ppermute | solution.py:649
  35.2 13.1 %collective-permute-start.1 = (bf16[64,1024]{1,0:T(8,128)(2,1)}, bf16[64,1024]{1,0:T(8,128)(2,1)S(1)}, u32[]{:S(2)}, u32[]{:S(2)}) collective-permute-start(bf16[64,1024]{1,0:T(8,128)(2,1)} %get-tuple-element.27), channel_id=1, source_target_pairs={{0,16},{2,0},{4,20},{6,4},{8,24},{10,8},{12,28},{14,12},{16,18},{1... | collective-permute-start | bytes 393224 | tf_op jit(solution)/shard_map/ppermute | solution.py:649
  36.7 12.2 %collective-permute-start.2 = (bf16[64,1024]{1,0:T(8,128)(2,1)}, bf16[64,1024]{1,0:T(8,128)(2,1)S(1)}, u32[]{:S(2)}, u32[]{:S(2)}) collective-permute-start(bf16[64,1024]{1,0:T(8,128)(2,1)} %get-tuple-element.28), channel_id=1, source_target_pairs={{0,18},{2,16},{4,22},{6,20},{8,26},{10,24},{12,30},{14,28},{16,2},... | collective-permute-start | bytes 393224 | tf_op jit(solution)/shard_map/ppermute | solution.py:649
  37.5 11.5 %collective-permute-start.3 = (bf16[64,1024]{1,0:T(8,128)(2,1)}, bf16[64,1024]{1,0:T(8,128)(2,1)S(1)}, u32[]{:S(2)}, u32[]{:S(2)}) collective-permute-start(bf16[64,1024]{1,0:T(8,128)(2,1)} %get-tuple-element.25.refs_0_), channel_id=1, source_target_pairs={{0,1},{1,0},{2,3},{3,2},{4,5},{5,4},{6,7},{7,6},{8,9},{9,8},{10,11... | collective-permute-start | bytes 393224 | tf_op jit(solution)/shard_map/ppermute | solution.py:19
  43.4 6.8 %copy-start.3 = (bf16[64,1024]{1,0:T(8,128)(2,1)}, bf16[64,1024]{1,0:T(8,128)(2,1)S(1)}, u32[]{:S(2)}) copy-start(bf16[64,1024]{1,0:T(8,128)(2,1)S(1)} %collective-permute-done.refs_1_) | copy-start | bytes 393220
  43.4 5.6 %collective-permute-start.4 = (bf16[64,1024]{1,0:T(8,128)(2,1)S(1)}, bf16[64,1024]{1,0:T(8,128)(2,1)S(1)}, u32[]{:S(2)}, u32[]{:S(2)}) collective-permute-start(bf16[64,1024]{1,0:T(8,128)(2,1)S(1)} %collective-permute-done.refs_1_), channel_id=1, source_target_pairs={{0,1},{1,0},{2,3},{3,2},{4,5},{5,4},{6,7},{7,6},{8,9},{9,8},{10,11... | collective-permute-start | bytes 393224 | tf_op jit(solution)/shard_map/ppermute | solution.py:19
  48.3 1.9 %copy-start.4 = (bf16[64,1024]{1,0:T(8,128)(2,1)}, bf16[64,1024]{1,0:T(8,128)(2,1)S(1)}, u32[]{:S(2)}) copy-start(bf16[64,1024]{1,0:T(8,128)(2,1)S(1)} %collective-permute-done.1.refs_2_) | copy-start | bytes 393220
  48.3 1.5 %collective-permute-start.5 = (bf16[64,1024]{1,0:T(8,128)(2,1)S(1)}, bf16[64,1024]{1,0:T(8,128)(2,1)S(1)}, u32[]{:S(2)}, u32[]{:S(2)}) collective-permute-start(bf16[64,1024]{1,0:T(8,128)(2,1)S(1)} %collective-permute-done.1.refs_2_), channel_id=1, source_target_pairs={{0,1},{1,0},{2,3},{3,2},{4,5},{5,4},{6,7},{7,6},{8,9},{9,8},{10,11... | collective-permute-start | bytes 393224 | tf_op jit(solution)/shard_map/ppermute | solution.py:19
  48.8 1.4 copy-start.5
  48.8 1.3 collective-permute-start.6
  49.0 1.2 copy-start.6
  49.0 1.2 copy-start.7
  49.8 0.7 copy-start.8
  50.5 0.7 copy-start.9
  54.7 26.6 %all-to-all-start.1 = ((bf16[64,8,512]{2,1,0:T(8,128)(2,1)}), bf16[64,8,512]{2,1,0:T(8,128)(2,1)S(1)}, u32[]{:S(2)}, u32[]{:S(2)}) async-start(bf16[64,8,512]{2,1,0:T(8,128)(2,1)} %shard_map.136), calls=%async_computation.1 | async-start | bytes 1048576 | tf_op jit(solution)/shard_map/all_to_all | solution.py:660
  65.8 51.4 %collective-permute-start.10 = (bf16[384,2048]{1,0:T(8,128)(2,1)}, bf16[384,2048]{1,0:T(8,128)(2,1)}, u32[]{:S(2)}, u32[]{:S(2)}) collective-permute-start(bf16[384,2048]{1,0:T(8,128)(2,1)} %get-tuple-element.39), channel_id=1, source_target_pairs={{0,1},{1,0},{2,3},{3,2},{4,5},{5,4},{6,7},{7,6},{8,9},{9,8},{10,11... | collective-permute-start | bytes 4718600 | tf_op jit(solution)/shard_map/ppermute | solution.py:19
  81.5 4.1 %collective-permute-start.7 = (bf16[2,8,512]{2,1,0:T(8,128)(2,1)S(1)}, bf16[2,8,512]{2,1,0:T(8,128)(2,1)S(1)}, u32[]{:S(2)}, u32[]{:S(2)}) collective-permute-start(bf16[2,8,512]{2,1,0:T(8,128)(2,1)S(1)} %get-tuple-element.31), channel_id=1, source_target_pairs={{0,1},{1,0},{2,3},{3,2},{4,5},{5,4},{6,7},{7,6},{8,9},{9,8},{10,11... | collective-permute-start | bytes 49160 | tf_op jit(solution)/shard_map/ppermute | solution.py:19
  112.8 4.5 %collective-permute-start.9 = (bf16[128,1536]{1,0:T(8,128)(2,1)S(1)}, bf16[128,1536]{1,0:T(8,128)(2,1)S(1)}, u32[]{:S(2)}, u32[]{:S(2)}) collective-permute-start(bf16[128,1536]{1,0:T(8,128)(2,1)S(1)} %get-tuple-element.38), channel_id=1, source_target_pairs={{0,1},{1,0},{2,3},{3,2},{4,5},{5,4},{6,7},{7,6},{8,9},{9,8},{10,11... | collective-permute-start | bytes 1179656 | tf_op jit(solution)/shard_map/ppermute | solution.py:19
  143.5 3.6 %collective-permute-start.11 = (f32[2,8,512]{2,1,0:T(8,128)S(1)}, f32[2,8,512]{2,1,0:T(8,128)S(1)}, u32[]{:S(2)}, u32[]{:S(2)}) collective-permute-start(f32[2,8,512]{2,1,0:T(8,128)S(1)} %get-tuple-element.42), channel_id=1, source_target_pairs={{0,1},{1,0},{2,3},{3,2},{4,5},{5,4},{6,7},{7,6},{8,9},{9,8},{10,11... | collective-permute-start | bytes 98312 | tf_op jit(solution)/shard_map/ppermute | solution.py:19

commit v11 on v10

--- a/solution.py
+++ b/solution.py
@@ -32,6 +32,16 @@
             dx, dy = (1, 1) if way == 0 else ((0, 1) if along_y else (1, 0))
             steps.append((x * side + y, (x ^ dx) * side + (y ^ dy)))
     return steps
+
+
+def first_member(chips):
+    return chips - 2
+
+
+def exchanged(x):
+    chips = lax.axis_size(CHIPS)
+    members = [(k + first_member(chips)) % chips for k in range(chips)]
+    return lax.all_to_all(x, CHIPS, 0, 0, tiled=True, axis_index_groups=[members])
 
 
 MIB = 1 << 20
@@ -127,14 +137,13 @@
     inv_root = 1.0 / math.sqrt(HEAD_WIDTH)
     positions = lax.broadcasted_iota(jnp.int32, (head_count, cache_len), 1)
     lanes = [slice(g * HEAD_WIDTH, (g + 1) * HEAD_WIDTH) for g in range(kv_count)]
-    fresh = []
-    for copy in copies[0]:
-        copy.wait()
-    for b in range(seq_count):
+    fresh, probs, fresh_probs = {}, {}, {}
+
+    def score(b):
         query = rows[b * head_count : (b + 1) * head_count, :]
         latest = [tk_ref[b : b + 1, lanes[g]].astype(F32) for g in range(kv_count)]
         latest = jnp.concatenate([jnp.broadcast_to(v, (group, HEAD_WIDTH)) for v in latest])
-        fresh.append(jnp.sum(query * latest, axis=1, keepdims=True) * inv_root)
+        fresh[b] = jnp.sum(query * latest, axis=1, keepdims=True) * inv_root
         query = query.astype(BF16)
         for g in range(kv_count):
             at = b * head_count + g * group
@@ -144,21 +153,18 @@
                 (((1,), (1,)), ((), ())),
                 preferred_element_type=F32,
             )
-    for copy in copies[1] + sliced:
-        copy.wait()
-    for copy in stored:
-        copy.start()
-    probs, fresh_probs = [], []
-    for b in range(seq_count):
+
+    def weigh(b):
         scores = scored[b * head_count : (b + 1) * head_count, :]
         scores = jnp.where(positions < len_ref[b], scores * inv_root, -jnp.inf)
         highest = jnp.maximum(jnp.max(scores, axis=1, keepdims=True), fresh[b])
         cached_exp = jnp.exp(scores - highest)
         fresh_exp = jnp.exp(fresh[b] - highest)
         share = 1.0 / (jnp.sum(cached_exp, axis=1, keepdims=True) + fresh_exp)
-        probs.append((cached_exp * share).astype(BF16))
-        fresh_probs.append((fresh_exp * share).astype(BF16).astype(F32))
-    for b in range(seq_count):
+        probs[b] = (cached_exp * share).astype(BF16)
+        fresh_probs[b] = (fresh_exp * share).astype(BF16).astype(F32)
+
+    def mix(b):
         for g in range(kv_count):
             heads = slice(g * group, (g + 1) * group)
             out = jnp.dot(probs[b][heads], values[b, :, lanes[g]], preferred_element_type=F32)
@@ -167,6 +173,22 @@
             for a in range(2):
                 start = g * group * seq_count + a * seq_count + b
                 mixed[pl.ds(start, side, stride=2 * seq_count), :] = out[a * side : (a + 1) * side]
+
+    for copy in copies[0][:2]:
+        copy.wait()
+    score(0); score(1)
+    for copy in copies[0][2:]:
+        copy.wait()
+    score(2); score(3)
+    weigh(0); weigh(1)
+    for copy in copies[1][:2]:
+        copy.wait()
+    mix(0); mix(1); weigh(2); weigh(3)
+    for copy in copies[1][2:] + sliced:
+        copy.wait()
+    for copy in stored:
+        copy.start()
+    mix(2); mix(3)
     tile = 2 * seq_count
     for g in range(kv_count):
         for y in range(side):
@@ -320,6 +342,7 @@
         )
 
     copies = []
+    shift = chips - first_member(chips)
     for j in range(2):
         sent = slice(j * step, (j + 1) * step)
         x = x_ref[sent].astype(F32).reshape(step // 2, 2, tile, width)
@@ -329,8 +352,15 @@
         sums = sums.reshape(step // 2, tile, cols)
         sums = jnp.stack(paired(sums[:, :, :half], sums[:, :, half:]), axis=1)
         held[sent] = sums.reshape(step, tile, half).astype(BF16)
-        copies.append(pltpu.make_async_copy(held.at[sent], out_hbm.at[sent], sems.at[j]))
-        copies[-1].start()
+        last = min((j + 1) * step, chips - shift)
+        for begin, end, to in ((j * step, last, j * step + shift), (last, (j + 1) * step, 0)):
+            if end > begin:
+                copies.append(
+                    pltpu.make_async_copy(
+                        held.at[begin:end], out_hbm.at[to : to + end - begin], sems.at[len(copies)]
+                    )
+                )
+                copies[-1].start()
     for copy in copies:
         copy.wait()
 
@@ -348,7 +378,7 @@
 
 def project(x, weight):
     dims = x.shape[0], x.shape[1], weight.shape[1] // 2
-    return sending_call(project_body, dims, [IN_VMEM] * 2, 12, 2)(
+    return sending_call(project_body, dims, [IN_VMEM] * 2, 12, 3)(
         x, in_vmem(weight)
     )
 
@@ -371,7 +401,8 @@
         total = rows_of(residual_ref, k)
         for x in range(k // 2, side, 2):
             for y in range(k % 2, side, 2):
-                total = total + x_ref[x * side + y].astype(F32)
+                place = (x * side + y - first_member(chips)) % chips
+                total = total + x_ref[place].astype(F32)
         hidden_ref[k] = total
         square = square + jnp.sum(total * total, axis=1, keepdims=True)
     square = jnp.broadcast_to(square, (tile, HEAD_WIDTH))
@@ -401,13 +432,16 @@
     lanes = pick_ref.shape[1]
     lane = lax.broadcasted_iota(jnp.int32, (tokens, lanes), 1)
     row = lax.broadcasted_iota(jnp.int32, (tokens, lanes), 0)
+    chips = lanes // 8
+    expert = lane // 8 + first_member(chips)
+    expert = jnp.where(expert < chips, expert, expert - chips)
     weight = weight_ref[...]
     mixing = weight / jnp.sum(weight, axis=1, keepdims=True)
     ids = ids_ref[...]
     hit = jnp.zeros((tokens, lanes), F32)
     share = jnp.zeros((tokens, lanes), F32)
     for k in range(topk):
-        same = ids[:, k : k + 1] == lane // 8
+        same = ids[:, k : k + 1] == expert
         hit = jnp.where(same, 1.0, hit)
         share = jnp.where(same, mixing[:, k : k + 1], share)
     rank = jnp.zeros((tokens, lanes), F32)
@@ -657,16 +691,16 @@
     pick, mix = route(expert_ids, route_weight, chips)
 
     sums = project(tokens, weight)
-    came_back = lax.all_to_all(sums, CHIPS, 0, 0, tiled=True)
+    came_back = exchanged(sums)
     hidden, normed, normed_given = settle(came_back, residual, norm_gain[None])
     normed_other = swapped(normed_given)
     late = w_gate.shape[1] // 2 - kept.shape[0]
     outgoing, rest = dispatch(normed, normed_other, pick, w_gate, w_up, late)
-    incoming = lax.all_to_all(outgoing, CHIPS, 0, 0, tiled=True)
+    incoming = exchanged(outgoing)
     part, sent = gate_up(incoming, kept, rest, gate_moved)
     down_kept = fetch_down(w_down, part)
     expert_out = down(part, swapped(sent), down_kept, down_moved, incoming.shape[1])
-    returned = lax.all_to_all(expert_out, CHIPS, 0, 0, tiled=True)
+    returned = exchanged(expert_out)
     moe_own, moe_given = combine(returned, mix)
     return finish(hidden, moe_own, swapped(moe_given))
 

time: 148 us -> 146 us (0.986)
  waiting for transfers between devices: 23.4 us -> 19.9 us
    all_to_all x1, waiting for transfers between devices: 14.6 us -> 11.1 us  [exchanged(): lax.all_to_all(x, CHIPS, 0, 0, tiled=True, axis_index_groups=[members])]
where the time goes in v11:
time: 146 us; the launch traced here: 145 us
  starting transfers between devices  56.6 us (39%)
  blocking collectives  46.5 us (32%)
  Pallas kernels  20.7 us (14%)
  waiting for transfers between devices  19.9 us (14%)
    all_to_all x2, blocking collectives, exchanged(): lax.all_to_all(x, CHIPS, 0, 0, tiled=True, axis_index_groups=[members])  46.5 us
    ppermute x9, starting transfers between devices, swapped(): return lax.ppermute(x, CORES, [(0, 1), (1, 0)])  34.6 us
    all_to_all x1, starting transfers between devices, exchanged(): lax.all_to_all(x, CHIPS, 0, 0, tiled=True, axis_index_groups=[members])  12.4 us
    all_to_all x1, waiting for transfers between devices, exchanged(): lax.all_to_all(x, CHIPS, 0, 0, tiled=True, axis_index_groups=[members])  11.1 us
    all_to_all x1, starting transfers between devices, on_device(): tokens = lax.all_to_all(outgoing, CHIPS, 0, 0, tiled=True)  7.24 us
    ppermute x3, waiting for transfers between devices, on_device(): lax.ppermute(piece, CHIPS, square_step(side, way))  6.09 us
    pallas_call x1, Pallas kernels, halves(): pl.pallas_call(halves_body, name='halves', out_shape=[pltpu.VMEM((int(wid...  4.05 us
    pallas_call x1, Pallas kernels, down(): sending_call(down_body, dims, [IN_VMEM] * 4, 8, 2)  3.17 us
  transfers between devices with their start and end apart: 14, of which 7 were waited for; matrix products, arithmetic and copies ran while one was open for 0% of the time, Pallas kernels for 9%

profile of v11, /device:TPU:513, one launch (start us, length us, event | category | flops | bytes accessed | tf_op | source)
XLA Modules:
  0.0 145.0 jit_solution(225199785909301028)
XLA Ops:
  0.0 4.1 %halves.1 = (bf16[1536,768]{1,0:T(8,128)(2,1)S(1)}, bf16[2048,768]{1,0:T(8,128)(2,1)}, bf16[384,2048]{1,0:T(8,128)(2,1)}) custom-call(bf16[1,4096,384]{2,1,0:T(8,128)(2,1)} %gate_hbm.3, bf16[1,4096,384]{2,1,0:T(8,128)(2,1)} %up_hbm.3, bf16[1,384,4096]{2,1,0:T(8,128)(2,1)} %down_hbm.3), custom_call_target="tpu_custom_call" | custom-call | tf_op jit(solution)/shard_map/halves/pallas_call | solution.py:312
  4.1 20.5 %collective-permute-start.8 = (bf16[2048,768]{1,0:T(8,128)(2,1)}, bf16[2048,768]{1,0:T(8,128)(2,1)}, u32[]{:S(2)}, u32[]{:S(2)}) collective-permute-start(bf16[2048,768]{1,0:T(8,128)(2,1)} %get-tuple-element.36), channel_id=1, source_target_pairs={{0,1},{1,0},{2,3},{3,2},{4,5},{5,4},{6,7},{7,6},{8,9},{9,8},{10,11... | collective-permute-start | bytes 9437192 | tf_op jit(solution)/shard_map/ppermute | solution.py:19
  24.6 3.0 %attend.1 = (bf16[64,8,256]{2,1,0:T(8,128)(2,1)}, bf16[64,1024]{1,0:T(8,128)(2,1)}, bf16[64,1024]{1,0:T(8,128)(2,1)}, bf16[64,1024]{1,0:T(8,128)(2,1)}, bf16[64,1024]{1,0:T(8,128)(2,1)}) custom-call(bf16[4,8192]{1,0:T(4,128)(2,1)} %q_hbm.1, bf16[4,512]{1,0:T(4,128)(2,1)} %tk_hbm.1, bf16[4,512]{1,0:T(4,128)(2,1)} %tv_hbm.1, s32[4]{0:T(128)} %len_hbm.1, ...), custom_call_target="tpu_custom_call" | custom-call | tf_op jit(solution)/shard_map/attend/pallas_call | solution.py:214
  27.6 0.0 copy-start.10
  27.6 0.0 copy-start
  27.6 0.0 copy-start.1
  27.7 0.0 copy-start.2
  27.7 7.2 %all-to-all-start = ((bf16[64,8,256]{2,1,0:T(8,128)(2,1)}), bf16[64,8,256]{2,1,0:T(8,128)(2,1)}, u32[]{:S(2)}, u32[]{:S(2)}) async-start(bf16[64,8,256]{2,1,0:T(8,128)(2,1)} %get-tuple-element.24), calls=%async_computation | async-start | bytes 524288 | tf_op jit(solution)/shard_map/all_to_all | solution.py:686
  34.9 0.1 collective-permute-start
  35.1 1.4 collective-permute-start.1
  36.5 0.9 collective-permute-start.2
  37.4 1.2 collective-permute-start.3
  38.5 4.7 %collective-permute-done.refs_1_ = bf16[64,1024]{1,0:T(8,128)(2,1)S(1)} collective-permute-done((bf16[64,1024]{1,0:T(8,128)(2,1)}, bf16[64,1024]{1,0:T(8,128)(2,1)S(1)}, u32[]{:S(2)}, u32[]{:S(2)}) %collective-permute-start) | collective-permute-done | bytes 131104 | tf_op jit(solution)/shard_map/ppermute | solution.py:683
  43.2 0.0 copy-start.3
  43.2 3.5 %collective-permute-start.4 = (bf16[64,1024]{1,0:T(8,128)(2,1)S(1)}, bf16[64,1024]{1,0:T(8,128)(2,1)S(1)}, u32[]{:S(2)}, u32[]{:S(2)}) collective-permute-start(bf16[64,1024]{1,0:T(8,128)(2,1)S(1)} %collective-permute-done.refs_1_), channel_id=1, source_target_pairs={{0,1},{1,0},{2,3},{3,2},{4,5},{5,4},{6,7},{7,6},{8,9},{9,8},{10,11... | collective-permute-start | bytes 393224 | tf_op jit(solution)/shard_map/ppermute | solution.py:19
  46.7 1.4 collective-permute-done.1.refs_2_
  48.1 0.0 copy-start.4
  48.1 0.5 collective-permute-start.5
  48.7 0.0 collective-permute-done.2.refs_3_
  48.7 0.0 copy-start.5
  48.7 0.1 collective-permute-start.6
  48.8 0.0 collective-permute-done.3.refs_4_
  48.8 0.0 copy-start.6
  48.8 0.0 collective-permute-done.4.refs_5_
  48.8 0.0 copy-start.7
  48.8 0.8 collective-permute-done.5.refs_6_
  49.7 0.0 copy-start.8
  49.7 0.4 collective-permute-done.6.refs_7_
  50.0 0.0 copy-done.3
  50.0 0.0 copy-done.4
  50.0 0.0 copy-done.5
  50.0 0.0 copy-done.6
  50.0 0.0 copy-done.7
  50.1 0.3 copy-done.8
  50.3 0.0 copy-start.9
  50.3 0.7 copy-done.9
  51.0 1.3 stack.1.weight_ref
  52.3 0.0 all-to-all-done.x_ref
  52.3 2.1 %shard_map.136 = bf16[64,8,512]{2,1,0:T(8,128)(2,1)} custom-call(bf16[64,8,256]{2,1,0:T(8,128)(2,1)} %all-to-all-done.x_ref, bf16[512,1024]{1,0:T(8,128)(2,1)S(1)} %stack.1.weight_ref), custom_call_target="tpu_custom_call" | custom-call | tf_op jit(solution)/shard_map/pallas_call | solution.py:381
  54.5 12.4 %all-to-all-start.1 = ((bf16[64,8,512]{2,1,0:T(8,128)(2,1)}), bf16[64,8,512]{2,1,0:T(8,128)(2,1)S(1)}, u32[]{:S(2)}, u32[]{:S(2)}) async-start(bf16[64,8,512]{2,1,0:T(8,128)(2,1)} %shard_map.136), calls=%async_computation.1 | async-start | bytes 1048576 | tf_op jit(solution)/shard_map/all_to_all | solution.py:44
  66.9 0.9 collective-permute-start.10
  67.7 0.0 copy-done.10
  67.7 11.1 %all-to-all-done.1.x_ref = bf16[64,8,512]{2,1,0:T(8,128)(2,1)S(1)} async-done(((bf16[64,8,512]{2,1,0:T(8,128)(2,1)}), bf16[64,8,512]{2,1,0:T(8,128)(2,1)S(1)}, u32[]{:S(2)}, u32[]{:S(2)}) %all-to-all-start.1) | async-done | bytes 524320 | tf_op jit(solution)/shard_map/all_to_all | solution.py:44
  78.9 0.0 copy-done
  78.9 0.2 shard_map.137
  79.1 2.6 %collective-permute-start.7 = (bf16[2,8,512]{2,1,0:T(8,128)(2,1)S(1)}, bf16[2,8,512]{2,1,0:T(8,128)(2,1)S(1)}, u32[]{:S(2)}, u32[]{:S(2)}) collective-permute-start(bf16[2,8,512]{2,1,0:T(8,128)(2,1)S(1)} %get-tuple-element.31), channel_id=1, source_target_pairs={{0,1},{1,0},{2,3},{3,2},{4,5},{5,4},{6,7},{7,6},{8,9},{9,8},{10,11... | collective-permute-start | bytes 49160 | tf_op jit(solution)/shard_map/ppermute | solution.py:19
  81.7 0.0 copy-done.1
  81.7 0.0 copy-done.2
  81.7 0.2 shard_map.138
  81.9 0.6 collective-permute-done.7.other_ref
  82.6 1.2 dispatch.1
  83.7 23.3 %all_to_all.20.x_ref = bf16[64,8,512]{2,1,0:T(8,128)(2,1)S(1)} all-to-all(bf16[64,8,512]{2,1,0:T(8,128)(2,1)} %get-tuple-element.33), channel_id=1, replica_groups={{124,126,0,2,4,6,8,10,12,14,16,18,20,22,24,26,28,30,32,34,36,38,40,42,4..., dimensions={0} | all-to-all | bytes 1048576 | tf_op jit(solution)/shard_map/all_to_all | solution.py:44
  107.1 0.0 collective-permute-done.8.moved_ref
  107.1 3.1 %gate_up.1 = (f32[128,1536]{1,0:T(8,128)S(1)}, bf16[128,1536]{1,0:T(8,128)(2,1)S(1)}) custom-call(bf16[64,8,512]{2,1,0:T(8,128)(2,1)S(1)} %all_to_all.20.x_ref, bf16[1536,768]{1,0:T(8,128)(2,1)S(1)} %get-tuple-element.34.kept_ref, bf16[512,768]{1,0:T(8,128)(2,1)S(1)} %get-tuple-element.35.rest_ref, bf16[2048,768]{1,0:T(8,128)(2,1)} %collective-permute-done.8.moved_ref), custom_call_target="tpu_custom_call" | custom-call | tf_op jit(solution)/shard_map/gate_up/pallas_call | solution.py:555
  110.2 2.8 %collective-permute-start.9 = (bf16[128,1536]{1,0:T(8,128)(2,1)S(1)}, bf16[128,1536]{1,0:T(8,128)(2,1)S(1)}, u32[]{:S(2)}, u32[]{:S(2)}) collective-permute-start(bf16[128,1536]{1,0:T(8,128)(2,1)S(1)} %get-tuple-element.38), channel_id=1, source_target_pairs={{0,1},{1,0},{2,3},{3,2},{4,5},{5,4},{6,7},{7,6},{8,9},{9,8},{10,11... | collective-permute-start | bytes 1179656 | tf_op jit(solution)/shard_map/ppermute | solution.py:19
  113.0 1.4 fetch_down.1.first_ref
  114.4 0.0 collective-permute-done.10.rest_ref
  114.4 0.0 collective-permute-done.9.arrived_ref
  114.4 3.2 %shard_map.139 = bf16[64,8,512]{2,1,0:T(8,128)(2,1)} custom-call(f32[128,1536]{1,0:T(8,128)S(1)} %get-tuple-element.37.after_ref.part_ref, bf16[128,1536]{1,0:T(8,128)(2,1)S(1)} %collective-permute-done.9.arrived_ref, bf16[384,2048]{1,0:T(8,128)(2,1)S(1)} %fetch_down.1.first_ref, bf16[384,2048]{1,0:T(8,128)(2,1)} %collective-permute-done.10.rest_ref), custom_call_target="tpu_custom_call" | custom-call | tf_op jit(solution)/shard_map/pallas_call | solution.py:623
  117.6 23.2 %all_to_all.21.x_ref = bf16[64,8,512]{2,1,0:T(8,128)(2,1)S(1)} all-to-all(bf16[64,8,512]{2,1,0:T(8,128)(2,1)} %shard_map.139), channel_id=1, replica_groups={{124,126,0,2,4,6,8,10,12,14,16,18,20,22,24,26,28,30,32,34,36,38,40,42,4..., dimensions={0} | all-to-all | bytes 1048576 | tf_op jit(solution)/shard_map/all_to_all | solution.py:44
  140.8 0.2 shard_map.140
  141.0 2.5 %collective-permute-start.11 = (f32[2,8,512]{2,1,0:T(8,128)S(1)}, f32[2,8,512]{2,1,0:T(8,128)S(1)}, u32[]{:S(2)}, u32[]{:S(2)}) collective-permute-start(f32[2,8,512]{2,1,0:T(8,128)S(1)} %get-tuple-element.42), channel_id=1, source_target_pairs={{0,1},{1,0},{2,3},{3,2},{4,5},{5,4},{6,7},{7,6},{8,9},{9,8},{10,11... | collective-permute-start | bytes 98312 | tf_op jit(solution)/shard_map/ppermute | solution.py:19
  143.5 0.9 collective-permute-done.11.other_ref
  144.3 0.6 shard_map.141
  (1 shorter events, 0.0 us)
Async XLA Ops:
  4.1 103.0 %collective-permute-start.8 = (bf16[2048,768]{1,0:T(8,128)(2,1)}, bf16[2048,768]{1,0:T(8,128)(2,1)}, u32[]{:S(2)}, u32[]{:S(2)}) collective-permute-start(bf16[2048,768]{1,0:T(8,128)(2,1)} %get-tuple-element.36), channel_id=1, source_target_pairs={{0,1},{1,0},{2,3},{3,2},{4,5},{5,4},{6,7},{7,6},{8,9},{9,8},{10,11... | collective-permute-start | bytes 9437192 | tf_op jit(solution)/shard_map/ppermute | solution.py:19
  27.6 40.1 %copy-start.10 = (bf16[4096]{0:T(1024)(128)(2,1)S(1)}, bf16[4096]{0:T(1024)(128)(2,1)}, u32[]{:S(2)}) copy-start(bf16[4096]{0:T(1024)(128)(2,1)} %param.22) | copy-start | bytes 24580
  27.6 51.2 %copy-start = (bf16[4,4096]{1,0:T(4,128)(2,1)S(1)}, bf16[4,4096]{1,0:T(4,128)(2,1)}, u32[]{:S(2)}) copy-start(bf16[4,4096]{1,0:T(4,128)(2,1)} %residual_ref.1) | copy-start | bytes 98308
  27.6 54.1 %copy-start.1 = (s32[8,8]{1,0:T(8,128)S(1)}, s32[8,8]{1,0:T(8,128)}, u32[]{:S(2)}) copy-start(s32[8,8]{1,0:T(8,128)} %ids_ref.1) | copy-start | bytes 772
  27.7 54.1 %copy-start.2 = (f32[8,8]{1,0:T(8,128)S(1)}, f32[8,8]{1,0:T(8,128)}, u32[]{:S(2)}) copy-start(f32[8,8]{1,0:T(8,128)} %weight_ref.1) | copy-start | bytes 772
  27.7 24.7 %all-to-all-start = ((bf16[64,8,256]{2,1,0:T(8,128)(2,1)}), bf16[64,8,256]{2,1,0:T(8,128)(2,1)}, u32[]{:S(2)}, u32[]{:S(2)}) async-start(bf16[64,8,256]{2,1,0:T(8,128)(2,1)} %get-tuple-element.24), calls=%async_computation | async-start | bytes 524288 | tf_op jit(solution)/shard_map/all_to_all | solution.py:686
  34.9 8.3 %collective-permute-start = (bf16[64,1024]{1,0:T(8,128)(2,1)}, bf16[64,1024]{1,0:T(8,128)(2,1)S(1)}, u32[]{:S(2)}, u32[]{:S(2)}) collective-permute-start(bf16[64,1024]{1,0:T(8,128)(2,1)} %get-tuple-element.26), channel_id=1, source_target_pairs={{0,2},{2,18},{4,6},{6,22},{8,10},{10,26},{12,14},{14,30},{16,0},{1... | collective-permute-start | bytes 393224 | tf_op jit(solution)/shard_map/ppermute | solution.py:683
  35.1 13.1 %collective-permute-start.1 = (bf16[64,1024]{1,0:T(8,128)(2,1)}, bf16[64,1024]{1,0:T(8,128)(2,1)S(1)}, u32[]{:S(2)}, u32[]{:S(2)}) collective-permute-start(bf16[64,1024]{1,0:T(8,128)(2,1)} %get-tuple-element.27), channel_id=1, source_target_pairs={{0,16},{2,0},{4,20},{6,4},{8,24},{10,8},{12,28},{14,12},{16,18},{1... | collective-permute-start | bytes 393224 | tf_op jit(solution)/shard_map/ppermute | solution.py:683
  36.5 12.2 %collective-permute-start.2 = (bf16[64,1024]{1,0:T(8,128)(2,1)}, bf16[64,1024]{1,0:T(8,128)(2,1)S(1)}, u32[]{:S(2)}, u32[]{:S(2)}) collective-permute-start(bf16[64,1024]{1,0:T(8,128)(2,1)} %get-tuple-element.28), channel_id=1, source_target_pairs={{0,18},{2,16},{4,22},{6,20},{8,26},{10,24},{12,30},{14,28},{16,2},... | collective-permute-start | bytes 393224 | tf_op jit(solution)/shard_map/ppermute | solution.py:683
  37.4 11.5 %collective-permute-start.3 = (bf16[64,1024]{1,0:T(8,128)(2,1)}, bf16[64,1024]{1,0:T(8,128)(2,1)S(1)}, u32[]{:S(2)}, u32[]{:S(2)}) collective-permute-start(bf16[64,1024]{1,0:T(8,128)(2,1)} %get-tuple-element.25.refs_0_), channel_id=1, source_target_pairs={{0,1},{1,0},{2,3},{3,2},{4,5},{5,4},{6,7},{7,6},{8,9},{9,8},{10,11... | collective-permute-start | bytes 393224 | tf_op jit(solution)/shard_map/ppermute | solution.py:19
  43.2 6.8 %copy-start.3 = (bf16[64,1024]{1,0:T(8,128)(2,1)}, bf16[64,1024]{1,0:T(8,128)(2,1)S(1)}, u32[]{:S(2)}) copy-start(bf16[64,1024]{1,0:T(8,128)(2,1)S(1)} %collective-permute-done.refs_1_) | copy-start | bytes 393220
  43.2 5.6 %collective-permute-start.4 = (bf16[64,1024]{1,0:T(8,128)(2,1)S(1)}, bf16[64,1024]{1,0:T(8,128)(2,1)S(1)}, u32[]{:S(2)}, u32[]{:S(2)}) collective-permute-start(bf16[64,1024]{1,0:T(8,128)(2,1)S(1)} %collective-permute-done.refs_1_), channel_id=1, source_target_pairs={{0,1},{1,0},{2,3},{3,2},{4,5},{5,4},{6,7},{7,6},{8,9},{9,8},{10,11... | collective-permute-start | bytes 393224 | tf_op jit(solution)/shard_map/ppermute | solution.py:19
  48.1 1.9 %copy-start.4 = (bf16[64,1024]{1,0:T(8,128)(2,1)}, bf16[64,1024]{1,0:T(8,128)(2,1)S(1)}, u32[]{:S(2)}) copy-start(bf16[64,1024]{1,0:T(8,128)(2,1)S(1)} %collective-permute-done.1.refs_2_) | copy-start | bytes 393220
  48.1 1.5 %collective-permute-start.5 = (bf16[64,1024]{1,0:T(8,128)(2,1)S(1)}, bf16[64,1024]{1,0:T(8,128)(2,1)S(1)}, u32[]{:S(2)}, u32[]{:S(2)}) collective-permute-start(bf16[64,1024]{1,0:T(8,128)(2,1)S(1)} %collective-permute-done.1.refs_2_), channel_id=1, source_target_pairs={{0,1},{1,0},{2,3},{3,2},{4,5},{5,4},{6,7},{7,6},{8,9},{9,8},{10,11... | collective-permute-start | bytes 393224 | tf_op jit(solution)/shard_map/ppermute | solution.py:19
  48.7 1.4 copy-start.5
  48.7 1.3 collective-permute-start.6
  48.8 1.2 copy-start.6
  48.8 1.2 copy-start.7
  49.7 0.7 copy-start.8
  50.3 0.7 copy-start.9
  54.5 24.4 %all-to-all-start.1 = ((bf16[64,8,512]{2,1,0:T(8,128)(2,1)}), bf16[64,8,512]{2,1,0:T(8,128)(2,1)S(1)}, u32[]{:S(2)}, u32[]{:S(2)}) async-start(bf16[64,8,512]{2,1,0:T(8,128)(2,1)} %shard_map.136), calls=%async_computation.1 | async-start | bytes 1048576 | tf_op jit(solution)/shard_map/all_to_all | solution.py:44
  66.9 47.5 %collective-permute-start.10 = (bf16[384,2048]{1,0:T(8,128)(2,1)}, bf16[384,2048]{1,0:T(8,128)(2,1)}, u32[]{:S(2)}, u32[]{:S(2)}) collective-permute-start(bf16[384,2048]{1,0:T(8,128)(2,1)} %get-tuple-element.39), channel_id=1, source_target_pairs={{0,1},{1,0},{2,3},{3,2},{4,5},{5,4},{6,7},{7,6},{8,9},{9,8},{10,11... | collective-permute-start | bytes 4718600 | tf_op jit(solution)/shard_map/ppermute | solution.py:19
  79.1 3.4 %collective-permute-start.7 = (bf16[2,8,512]{2,1,0:T(8,128)(2,1)S(1)}, bf16[2,8,512]{2,1,0:T(8,128)(2,1)S(1)}, u32[]{:S(2)}, u32[]{:S(2)}) collective-permute-start(bf16[2,8,512]{2,1,0:T(8,128)(2,1)S(1)} %get-tuple-element.31), channel_id=1, source_target_pairs={{0,1},{1,0},{2,3},{3,2},{4,5},{5,4},{6,7},{7,6},{8,9},{9,8},{10,11... | collective-permute-start | bytes 49160 | tf_op jit(solution)/shard_map/ppermute | solution.py:19
  110.2 4.2 %collective-permute-start.9 = (bf16[128,1536]{1,0:T(8,128)(2,1)S(1)}, bf16[128,1536]{1,0:T(8,128)(2,1)S(1)}, u32[]{:S(2)}, u32[]{:S(2)}) collective-permute-start(bf16[128,1536]{1,0:T(8,128)(2,1)S(1)} %get-tuple-element.38), channel_id=1, source_target_pairs={{0,1},{1,0},{2,3},{3,2},{4,5},{5,4},{6,7},{7,6},{8,9},{9,8},{10,11... | collective-permute-start | bytes 1179656 | tf_op jit(solution)/shard_map/ppermute | solution.py:19
  141.0 3.4 %collective-permute-start.11 = (f32[2,8,512]{2,1,0:T(8,128)S(1)}, f32[2,8,512]{2,1,0:T(8,128)S(1)}, u32[]{:S(2)}, u32[]{:S(2)}) collective-permute-start(f32[2,8,512]{2,1,0:T(8,128)S(1)} %get-tuple-element.42), channel_id=1, source_target_pairs={{0,1},{1,0},{2,3},{3,2},{4,5},{5,4},{6,7},{7,6},{8,9},{9,8},{10,11... | collective-permute-start | bytes 98312 | tf_op jit(solution)/shard_map/ppermute | solution.py:19

commit v12 on v11

--- a/solution.py
+++ b/solution.py
@@ -599,12 +599,12 @@
         )
         return (gate / (1.0 + jnp.exp(-gate)) * up).astype(BF16)
 
-    hidden = act(0), act(2 * units)
+    hidden = jnp.concatenate([act(0), act(2 * units)], axis=1)
     quarters = []
     for p in range(4):
         lanes = slice(p * part, (p + 1) * part)
-        value = jnp.dot(hidden[0], first_ref[:, lanes], preferred_element_type=F32)
-        value = value + jnp.dot(hidden[1], rest_ref[:, lanes], preferred_element_type=F32)
+        weight = jnp.concatenate([first_ref[:, lanes], rest_ref[:, lanes]])
+        value = jnp.dot(hidden, weight, preferred_element_type=F32)
         quarters.append(value.astype(BF16))
     copies = []
     for g in range(groups):
@@ -679,14 +679,13 @@
     outgoing, *pieces = attend(
         queries, token_keys, token_values, kv_len, stored_keys, stored_values, out_weight
     )
-    own = pieces[:1] + [
-        lax.ppermute(piece, CHIPS, square_step(side, way))
-        for piece, way in zip(pieces[1:], (1, -1, 0), strict=True)
-    ]
+    own = list(pieces)
+    for j, way in ((1, 1), (3, 0), (2, -1)):
+        own[j] = lax.ppermute(pieces[j], CHIPS, square_step(side, way))
     tokens = lax.all_to_all(outgoing, CHIPS, 0, 0, tiled=True)
     other = [swapped(piece) for piece in own]
     weight = stack(own, other)
-    kept, gate_given, down_given = halves(w_gate, w_up, w_down, 0.75)
+    kept, gate_given, down_given = halves(w_gate, w_up, w_down, 0.875)
     gate_moved, down_moved = swapped(gate_given), swapped(down_given)
     pick, mix = route(expert_ids, route_weight, chips)
 

time: 146 us -> 144 us (0.986)
  Pallas kernels: 20.7 us -> 18.5 us
  local copies, waits for them, and re-layouts: 0.98 us -> 2.55 us
    unnamed x22 -> x26, local copies, waits for them, and re-layouts: 0.96 us -> 2.54 us
    pallas_call x1, Pallas kernels: 3.17 us -> 1.64 us  [down(): sending_call(down_body, dims, [IN_VMEM] * 4, 8, 2)]
  transfers between devices with their start and end apart: 14 -> 14, of which waited for: 7 -> 7; matrix products, arithmetic and copies ran while one was open for 0% -> 0% of each run, Pallas kernels for 9% -> 8%
where the time goes in v12:
time: 144 us
  starting transfers between devices  56.1 us (39%)
  blocking collectives  46.5 us (32%)
  waiting for transfers between devices  19.8 us (14%)
  Pallas kernels  18.5 us (13%)
  local copies, waits for them, and re-layouts  2.55 us (2%)
    all_to_all x2, blocking collectives, exchanged(): lax.all_to_all(x, CHIPS, 0, 0, tiled=True, axis_index_groups=[members])  46.5 us
    ppermute x9, starting transfers between devices, swapped(): return lax.ppermute(x, CORES, [(0, 1), (1, 0)])  34.6 us
    all_to_all x1, starting transfers between devices, exchanged(): lax.all_to_all(x, CHIPS, 0, 0, tiled=True, axis_index_groups=[members])  12.4 us
    all_to_all x1, waiting for transfers between devices, exchanged(): lax.all_to_all(x, CHIPS, 0, 0, tiled=True, axis_index_groups=[members])  11.1 us
    all_to_all x1, starting transfers between devices, on_device(): tokens = lax.all_to_all(outgoing, CHIPS, 0, 0, tiled=True)  6.62 us
    ppermute x3, waiting for transfers between devices, on_device(): own[j] = lax.ppermute(pieces[j], CHIPS, square_step(side, way))  5.92 us
    pallas_call x1, Pallas kernels, halves(): pl.pallas_call(halves_body, name='halves', out_shape=[pltpu.VMEM((int(wid...  4.08 us
    pallas_call x1, Pallas kernels, gate_up(): pl.pallas_call(gate_body, name='gate_up', out_shape=[pltpu.VMEM(dims, F32...  3.15 us
  transfers between devices with their start and end apart: 14, of which 7 were waited for; matrix products, arithmetic and copies ran while one was open for 0% of the time, Pallas kernels for 8%

profile of v12, /device:TPU:513, one launch (start us, length us, event | category | flops | bytes accessed | tf_op | source)
XLA Modules:
  0.0 143.6 jit_solution(7400719623972184775)
XLA Ops:
  0.0 4.1 %halves.1 = (bf16[1792,768]{1,0:T(8,128)(2,1)S(1)}, bf16[2048,768]{1,0:T(8,128)(2,1)}, bf16[384,2048]{1,0:T(8,128)(2,1)}) custom-call(bf16[1,4096,384]{2,1,0:T(8,128)(2,1)} %gate_hbm.3, bf16[1,4096,384]{2,1,0:T(8,128)(2,1)} %up_hbm.3, bf16[1,384,4096]{2,1,0:T(8,128)(2,1)} %down_hbm.3), custom_call_target="tpu_custom_call" | custom-call | tf_op jit(solution)/shard_map/halves/pallas_call | solution.py:312
  4.1 0.0 copy-start
  4.1 1.6 %copy-done = bf16[1792,768]{1,0:T(8,128)(2,1)} copy-done((bf16[1792,768]{1,0:T(8,128)(2,1)}, bf16[1792,768]{1,0:T(8,128)(2,1)S(1)}, u32[]{:S(2)}) %copy-start) | copy-done | bytes 2752536
  5.7 20.4 %collective-permute-start.8 = (bf16[2048,768]{1,0:T(8,128)(2,1)}, bf16[2048,768]{1,0:T(8,128)(2,1)}, u32[]{:S(2)}, u32[]{:S(2)}) collective-permute-start(bf16[2048,768]{1,0:T(8,128)(2,1)} %get-tuple-element.36), channel_id=1, source_target_pairs={{0,1},{1,0},{2,3},{3,2},{4,5},{5,4},{6,7},{7,6},{8,9},{9,8},{10,11... | collective-permute-start | bytes 9437192 | tf_op jit(solution)/shard_map/ppermute | solution.py:19
  26.1 3.0 %attend.1 = (bf16[64,8,256]{2,1,0:T(8,128)(2,1)}, bf16[64,1024]{1,0:T(8,128)(2,1)}, bf16[64,1024]{1,0:T(8,128)(2,1)}, bf16[64,1024]{1,0:T(8,128)(2,1)}, bf16[64,1024]{1,0:T(8,128)(2,1)}) custom-call(bf16[4,8192]{1,0:T(4,128)(2,1)} %q_hbm.1, bf16[4,512]{1,0:T(4,128)(2,1)} %tk_hbm.1, bf16[4,512]{1,0:T(4,128)(2,1)} %tv_hbm.1, s32[4]{0:T(128)} %len_hbm.1, ...), custom_call_target="tpu_custom_call" | custom-call | tf_op jit(solution)/shard_map/attend/pallas_call | solution.py:214
  29.1 0.0 copy-start.12
  29.1 0.0 copy-start.2
  29.2 0.0 copy-start.3
  29.2 0.0 copy-start.4
  29.2 6.6 %all-to-all-start = ((bf16[64,8,256]{2,1,0:T(8,128)(2,1)}), bf16[64,8,256]{2,1,0:T(8,128)(2,1)S(1)}, u32[]{:S(2)}, u32[]{:S(2)}) async-start(bf16[64,8,256]{2,1,0:T(8,128)(2,1)} %get-tuple-element.24), calls=%async_computation | async-start | bytes 524288 | tf_op jit(solution)/shard_map/all_to_all | solution.py:685
  35.8 0.1 collective-permute-start
  35.9 1.4 %collective-permute-start.1 = (bf16[64,1024]{1,0:T(8,128)(2,1)}, bf16[64,1024]{1,0:T(8,128)(2,1)S(1)}, u32[]{:S(2)}, u32[]{:S(2)}) collective-permute-start(bf16[64,1024]{1,0:T(8,128)(2,1)} %get-tuple-element.27), channel_id=1, source_target_pairs={{0,16},{2,0},{4,20},{6,4},{8,24},{10,8},{12,28},{14,12},{16,18},{1... | collective-permute-start | bytes 393224 | tf_op jit(solution)/shard_map/ppermute | solution.py:684
  37.4 0.9 collective-permute-start.2
  38.3 1.1 collective-permute-start.3
  39.4 4.7 %collective-permute-done.refs_1_ = bf16[64,1024]{1,0:T(8,128)(2,1)S(1)} collective-permute-done((bf16[64,1024]{1,0:T(8,128)(2,1)}, bf16[64,1024]{1,0:T(8,128)(2,1)S(1)}, u32[]{:S(2)}, u32[]{:S(2)}) %collective-permute-start) | collective-permute-done | bytes 131104 | tf_op jit(solution)/shard_map/ppermute | solution.py:684
  44.0 3.6 %collective-permute-start.4 = (bf16[64,1024]{1,0:T(8,128)(2,1)S(1)}, bf16[64,1024]{1,0:T(8,128)(2,1)S(1)}, u32[]{:S(2)}, u32[]{:S(2)}) collective-permute-start(bf16[64,1024]{1,0:T(8,128)(2,1)S(1)} %collective-permute-done.refs_1_), channel_id=1, source_target_pairs={{0,1},{1,0},{2,3},{3,2},{4,5},{5,4},{6,7},{7,6},{8,9},{9,8},{10,11... | collective-permute-start | bytes 393224 | tf_op jit(solution)/shard_map/ppermute | solution.py:19
  47.6 1.3 collective-permute-done.1.refs_2_
  48.9 0.0 copy-start.6
  48.9 0.7 collective-permute-start.5
  49.6 0.0 collective-permute-done.2.refs_3_
  49.6 0.0 copy-start.7
  49.6 0.1 collective-permute-start.6
  49.7 0.0 collective-permute-done.3.refs_4_
  49.7 0.0 copy-start.8
  49.7 0.0 collective-permute-done.4.refs_5_
  49.7 0.0 copy-start.9
  49.7 0.8 collective-permute-done.5.refs_6_
  50.5 0.4 collective-permute-done.6.refs_7_
  50.9 0.0 copy-done.5
  50.9 0.0 copy-done.6
  50.9 0.0 copy-done.7
  50.9 0.0 copy-done.8
  50.9 0.0 copy-done.9
  50.9 0.3 copy-done.10
  51.2 0.6 copy-done.11
  51.8 1.3 stack.1.weight_ref
  53.2 0.0 all-to-all-done.x_ref
  53.2 1.2 shard_map.136
  54.4 12.4 %all-to-all-start.1 = ((bf16[64,8,512]{2,1,0:T(8,128)(2,1)}), bf16[64,8,512]{2,1,0:T(8,128)(2,1)S(1)}, u32[]{:S(2)}, u32[]{:S(2)}) async-start(bf16[64,8,512]{2,1,0:T(8,128)(2,1)} %shard_map.136), calls=%async_computation.1 | async-start | bytes 1048576 | tf_op jit(solution)/shard_map/all_to_all | solution.py:44
  66.8 0.9 collective-permute-start.10
  67.7 0.0 copy-done.12
  67.7 11.1 %all-to-all-done.1.x_ref = bf16[64,8,512]{2,1,0:T(8,128)(2,1)S(1)} async-done(((bf16[64,8,512]{2,1,0:T(8,128)(2,1)}), bf16[64,8,512]{2,1,0:T(8,128)(2,1)S(1)}, u32[]{:S(2)}, u32[]{:S(2)}) %all-to-all-start.1) | async-done | bytes 524320 | tf_op jit(solution)/shard_map/all_to_all | solution.py:44
  78.8 0.0 copy-done.2
  78.8 0.2 shard_map.137
  79.1 2.6 %collective-permute-start.7 = (bf16[2,8,512]{2,1,0:T(8,128)(2,1)S(1)}, bf16[2,8,512]{2,1,0:T(8,128)(2,1)S(1)}, u32[]{:S(2)}, u32[]{:S(2)}) collective-permute-start(bf16[2,8,512]{2,1,0:T(8,128)(2,1)S(1)} %get-tuple-element.31), channel_id=1, source_target_pairs={{0,1},{1,0},{2,3},{3,2},{4,5},{5,4},{6,7},{7,6},{8,9},{9,8},{10,11... | collective-permute-start | bytes 49160 | tf_op jit(solution)/shard_map/ppermute | solution.py:19
  81.7 0.0 copy-done.3
  81.7 0.0 copy-done.4
  81.7 0.2 shard_map.138
  81.9 0.6 collective-permute-done.7.other_ref
  82.5 1.4 dispatch.1
  83.9 23.3 %all_to_all.20.x_ref = bf16[64,8,512]{2,1,0:T(8,128)(2,1)S(1)} all-to-all(bf16[64,8,512]{2,1,0:T(8,128)(2,1)} %get-tuple-element.33), channel_id=1, replica_groups={{124,126,0,2,4,6,8,10,12,14,16,18,20,22,24,26,28,30,32,34,36,38,40,42,4..., dimensions={0} | all-to-all | bytes 1048576 | tf_op jit(solution)/shard_map/all_to_all | solution.py:44
  107.2 0.0 collective-permute-done.8.moved_ref
  107.2 0.0 copy-done.1
  107.2 3.1 %gate_up.1 = (f32[128,1536]{1,0:T(8,128)S(1)}, bf16[128,1536]{1,0:T(8,128)(2,1)S(1)}) custom-call(bf16[64,8,512]{2,1,0:T(8,128)(2,1)S(1)} %all_to_all.20.x_ref, bf16[1792,768]{1,0:T(8,128)(2,1)S(1)} %copy-done.1, bf16[256,768]{1,0:T(8,128)(2,1)S(1)} %get-tuple-element.35.rest_ref, bf16[2048,768]{1,0:T(8,128)(2,1)} %collective-permute-done.8.moved_ref), custom_call_target="tpu_custom_call" | custom-call | tf_op jit(solution)/shard_map/gate_up/pallas_call | solution.py:555
  110.4 2.8 %collective-permute-start.9 = (bf16[128,1536]{1,0:T(8,128)(2,1)S(1)}, bf16[128,1536]{1,0:T(8,128)(2,1)S(1)}, u32[]{:S(2)}, u32[]{:S(2)}) collective-permute-start(bf16[128,1536]{1,0:T(8,128)(2,1)S(1)} %get-tuple-element.38), channel_id=1, source_target_pairs={{0,1},{1,0},{2,3},{3,2},{4,5},{5,4},{6,7},{7,6},{8,9},{9,8},{10,11... | collective-permute-start | bytes 1179656 | tf_op jit(solution)/shard_map/ppermute | solution.py:19
  113.2 1.4 fetch_down.1.first_ref
  114.6 0.0 collective-permute-done.10.rest_ref
  114.6 0.0 collective-permute-done.9.arrived_ref
  114.6 1.6 %shard_map.139 = bf16[64,8,512]{2,1,0:T(8,128)(2,1)} custom-call(f32[128,1536]{1,0:T(8,128)S(1)} %get-tuple-element.37.after_ref.part_ref, bf16[128,1536]{1,0:T(8,128)(2,1)S(1)} %collective-permute-done.9.arrived_ref, bf16[384,2048]{1,0:T(8,128)(2,1)S(1)} %fetch_down.1.first_ref, bf16[384,2048]{1,0:T(8,128)(2,1)S(1)} %collective-permute-done.10.rest_ref), custom_call_target="tpu_custom_call" | custom-call | tf_op jit(solution)/shard_map/pallas_call | solution.py:623
  116.3 23.2 %all_to_all.21.x_ref = bf16[64,8,512]{2,1,0:T(8,128)(2,1)S(1)} all-to-all(bf16[64,8,512]{2,1,0:T(8,128)(2,1)} %shard_map.139), channel_id=1, replica_groups={{124,126,0,2,4,6,8,10,12,14,16,18,20,22,24,26,28,30,32,34,36,38,40,42,4..., dimensions={0} | all-to-all | bytes 1048576 | tf_op jit(solution)/shard_map/all_to_all | solution.py:44
  139.4 0.2 shard_map.140
  139.6 2.5 %collective-permute-start.11 = (f32[2,8,512]{2,1,0:T(8,128)S(1)}, f32[2,8,512]{2,1,0:T(8,128)S(1)}, u32[]{:S(2)}, u32[]{:S(2)}) collective-permute-start(f32[2,8,512]{2,1,0:T(8,128)S(1)} %get-tuple-element.42), channel_id=1, source_target_pairs={{0,1},{1,0},{2,3},{3,2},{4,5},{5,4},{6,7},{7,6},{8,9},{9,8},{10,11... | collective-permute-start | bytes 98312 | tf_op jit(solution)/shard_map/ppermute | solution.py:19
  142.1 0.9 collective-permute-done.11.other_ref
  143.0 0.6 shard_map.141
  (5 shorter events, 0.0 us)
Async XLA Ops:
  4.1 1.6 %copy-start = (bf16[1792,768]{1,0:T(8,128)(2,1)}, bf16[1792,768]{1,0:T(8,128)(2,1)S(1)}, u32[]{:S(2)}) copy-start(bf16[1792,768]{1,0:T(8,128)(2,1)S(1)} %get-tuple-element.34.kept_ref) | copy-start | bytes 8257540
  5.7 101.6 %collective-permute-start.8 = (bf16[2048,768]{1,0:T(8,128)(2,1)}, bf16[2048,768]{1,0:T(8,128)(2,1)}, u32[]{:S(2)}, u32[]{:S(2)}) collective-permute-start(bf16[2048,768]{1,0:T(8,128)(2,1)} %get-tuple-element.36), channel_id=1, source_target_pairs={{0,1},{1,0},{2,3},{3,2},{4,5},{5,4},{6,7},{7,6},{8,9},{9,8},{10,11... | collective-permute-start | bytes 9437192 | tf_op jit(solution)/shard_map/ppermute | solution.py:19
  29.1 38.5 %copy-start.12 = (bf16[4096]{0:T(1024)(128)(2,1)S(1)}, bf16[4096]{0:T(1024)(128)(2,1)}, u32[]{:S(2)}) copy-start(bf16[4096]{0:T(1024)(128)(2,1)} %param.22) | copy-start | bytes 24580
  29.1 49.7 %copy-start.2 = (bf16[4,4096]{1,0:T(4,128)(2,1)S(1)}, bf16[4,4096]{1,0:T(4,128)(2,1)}, u32[]{:S(2)}) copy-start(bf16[4,4096]{1,0:T(4,128)(2,1)} %residual_ref.1) | copy-start | bytes 98308
  29.2 52.5 %copy-start.3 = (s32[8,8]{1,0:T(8,128)S(1)}, s32[8,8]{1,0:T(8,128)}, u32[]{:S(2)}) copy-start(s32[8,8]{1,0:T(8,128)} %ids_ref.1) | copy-start | bytes 772
  29.2 52.5 %copy-start.4 = (f32[8,8]{1,0:T(8,128)S(1)}, f32[8,8]{1,0:T(8,128)}, u32[]{:S(2)}) copy-start(f32[8,8]{1,0:T(8,128)} %weight_ref.1) | copy-start | bytes 772
  29.2 24.0 %all-to-all-start = ((bf16[64,8,256]{2,1,0:T(8,128)(2,1)}), bf16[64,8,256]{2,1,0:T(8,128)(2,1)S(1)}, u32[]{:S(2)}, u32[]{:S(2)}) async-start(bf16[64,8,256]{2,1,0:T(8,128)(2,1)} %get-tuple-element.24), calls=%async_computation | async-start | bytes 524288 | tf_op jit(solution)/shard_map/all_to_all | solution.py:685
  35.8 8.2 %collective-permute-start = (bf16[64,1024]{1,0:T(8,128)(2,1)}, bf16[64,1024]{1,0:T(8,128)(2,1)S(1)}, u32[]{:S(2)}, u32[]{:S(2)}) collective-permute-start(bf16[64,1024]{1,0:T(8,128)(2,1)} %get-tuple-element.26), channel_id=1, source_target_pairs={{0,2},{2,18},{4,6},{6,22},{8,10},{10,26},{12,14},{14,30},{16,0},{1... | collective-permute-start | bytes 393224 | tf_op jit(solution)/shard_map/ppermute | solution.py:684
  35.9 12.9 %collective-permute-start.1 = (bf16[64,1024]{1,0:T(8,128)(2,1)}, bf16[64,1024]{1,0:T(8,128)(2,1)S(1)}, u32[]{:S(2)}, u32[]{:S(2)}) collective-permute-start(bf16[64,1024]{1,0:T(8,128)(2,1)} %get-tuple-element.27), channel_id=1, source_target_pairs={{0,16},{2,0},{4,20},{6,4},{8,24},{10,8},{12,28},{14,12},{16,18},{1... | collective-permute-start | bytes 393224 | tf_op jit(solution)/shard_map/ppermute | solution.py:684
  37.4 12.2 %collective-permute-start.2 = (bf16[64,1024]{1,0:T(8,128)(2,1)}, bf16[64,1024]{1,0:T(8,128)(2,1)S(1)}, u32[]{:S(2)}, u32[]{:S(2)}) collective-permute-start(bf16[64,1024]{1,0:T(8,128)(2,1)} %get-tuple-element.28), channel_id=1, source_target_pairs={{0,18},{2,16},{4,22},{6,20},{8,26},{10,24},{12,30},{14,28},{16,2},... | collective-permute-start | bytes 393224 | tf_op jit(solution)/shard_map/ppermute | solution.py:684
  38.3 11.4 %collective-permute-start.3 = (bf16[64,1024]{1,0:T(8,128)(2,1)}, bf16[64,1024]{1,0:T(8,128)(2,1)S(1)}, u32[]{:S(2)}, u32[]{:S(2)}) collective-permute-start(bf16[64,1024]{1,0:T(8,128)(2,1)} %get-tuple-element.25.refs_0_), channel_id=1, source_target_pairs={{0,1},{1,0},{2,3},{3,2},{4,5},{5,4},{6,7},{7,6},{8,9},{9,8},{10,11... | collective-permute-start | bytes 393224 | tf_op jit(solution)/shard_map/ppermute | solution.py:19
  44.0 6.9 %copy-start.5 = (bf16[64,1024]{1,0:T(8,128)(2,1)}, bf16[64,1024]{1,0:T(8,128)(2,1)S(1)}, u32[]{:S(2)}) copy-start(bf16[64,1024]{1,0:T(8,128)(2,1)S(1)} %collective-permute-done.refs_1_) | copy-start | bytes 393220
  44.0 5.7 %collective-permute-start.4 = (bf16[64,1024]{1,0:T(8,128)(2,1)S(1)}, bf16[64,1024]{1,0:T(8,128)(2,1)S(1)}, u32[]{:S(2)}, u32[]{:S(2)}) collective-permute-start(bf16[64,1024]{1,0:T(8,128)(2,1)S(1)} %collective-permute-done.refs_1_), channel_id=1, source_target_pairs={{0,1},{1,0},{2,3},{3,2},{4,5},{5,4},{6,7},{7,6},{8,9},{9,8},{10,11... | collective-permute-start | bytes 393224 | tf_op jit(solution)/shard_map/ppermute | solution.py:19
  48.9 2.0 %copy-start.6 = (bf16[64,1024]{1,0:T(8,128)(2,1)}, bf16[64,1024]{1,0:T(8,128)(2,1)S(1)}, u32[]{:S(2)}) copy-start(bf16[64,1024]{1,0:T(8,128)(2,1)S(1)} %collective-permute-done.1.refs_2_) | copy-start | bytes 393220
  48.9 1.6 %collective-permute-start.5 = (bf16[64,1024]{1,0:T(8,128)(2,1)S(1)}, bf16[64,1024]{1,0:T(8,128)(2,1)S(1)}, u32[]{:S(2)}, u32[]{:S(2)}) collective-permute-start(bf16[64,1024]{1,0:T(8,128)(2,1)S(1)} %collective-permute-done.1.refs_2_), channel_id=1, source_target_pairs={{0,1},{1,0},{2,3},{3,2},{4,5},{5,4},{6,7},{7,6},{8,9},{9,8},{10,11... | collective-permute-start | bytes 393224 | tf_op jit(solution)/shard_map/ppermute | solution.py:19
  49.6 1.4 copy-start.7
  49.6 1.3 collective-permute-start.6
  49.7 1.2 copy-start.8
  49.7 1.2 copy-start.9
  50.5 0.7 copy-start.10
  51.2 0.7 copy-start.11
  54.4 24.4 %all-to-all-start.1 = ((bf16[64,8,512]{2,1,0:T(8,128)(2,1)}), bf16[64,8,512]{2,1,0:T(8,128)(2,1)S(1)}, u32[]{:S(2)}, u32[]{:S(2)}) async-start(bf16[64,8,512]{2,1,0:T(8,128)(2,1)} %shard_map.136), calls=%async_computation.1 | async-start | bytes 1048576 | tf_op jit(solution)/shard_map/all_to_all | solution.py:44
  66.8 47.8 %collective-permute-start.10 = (bf16[384,2048]{1,0:T(8,128)(2,1)}, bf16[384,2048]{1,0:T(8,128)(2,1)S(1)}, u32[]{:S(2)}, u32[]{:S(2)}) collective-permute-start(bf16[384,2048]{1,0:T(8,128)(2,1)} %get-tuple-element.39), channel_id=1, source_target_pairs={{0,1},{1,0},{2,3},{3,2},{4,5},{5,4},{6,7},{7,6},{8,9},{9,8},{10,11... | collective-permute-start | bytes 4718600 | tf_op jit(solution)/shard_map/ppermute | solution.py:19
  79.1 3.4 %collective-permute-start.7 = (bf16[2,8,512]{2,1,0:T(8,128)(2,1)S(1)}, bf16[2,8,512]{2,1,0:T(8,128)(2,1)S(1)}, u32[]{:S(2)}, u32[]{:S(2)}) collective-permute-start(bf16[2,8,512]{2,1,0:T(8,128)(2,1)S(1)} %get-tuple-element.31), channel_id=1, source_target_pairs={{0,1},{1,0},{2,3},{3,2},{4,5},{5,4},{6,7},{7,6},{8,9},{9,8},{10,11... | collective-permute-start | bytes 49160 | tf_op jit(solution)/shard_map/ppermute | solution.py:19
  82.5 24.7 %copy-start.1 = (bf16[1792,768]{1,0:T(8,128)(2,1)S(1)}, bf16[1792,768]{1,0:T(8,128)(2,1)}, u32[]{:S(2)}) copy-start(bf16[1792,768]{1,0:T(8,128)(2,1)} %copy-done) | copy-start | bytes 8257540
  110.4 4.2 %collective-permute-start.9 = (bf16[128,1536]{1,0:T(8,128)(2,1)S(1)}, bf16[128,1536]{1,0:T(8,128)(2,1)S(1)}, u32[]{:S(2)}, u32[]{:S(2)}) collective-permute-start(bf16[128,1536]{1,0:T(8,128)(2,1)S(1)} %get-tuple-element.38), channel_id=1, source_target_pairs={{0,1},{1,0},{2,3},{3,2},{4,5},{5,4},{6,7},{7,6},{8,9},{9,8},{10,11... | collective-permute-start | bytes 1179656 | tf_op jit(solution)/shard_map/ppermute | solution.py:19
  139.6 3.4 %collective-permute-start.11 = (f32[2,8,512]{2,1,0:T(8,128)S(1)}, f32[2,8,512]{2,1,0:T(8,128)S(1)}, u32[]{:S(2)}, u32[]{:S(2)}) collective-permute-start(f32[2,8,512]{2,1,0:T(8,128)S(1)} %get-tuple-element.42), channel_id=1, source_target_pairs={{0,1},{1,0},{2,3},{3,2},{4,5},{5,4},{6,7},{7,6},{8,9},{9,8},{10,11... | collective-permute-start | bytes 98312 | tf_op jit(solution)/shard_map/ppermute | solution.py:19

commit v13 on v11

--- a/solution.py
+++ b/solution.py
@@ -599,12 +599,12 @@
         )
         return (gate / (1.0 + jnp.exp(-gate)) * up).astype(BF16)
 
-    hidden = act(0), act(2 * units)
+    hidden = jnp.concatenate([act(0), act(2 * units)], axis=1)
     quarters = []
     for p in range(4):
         lanes = slice(p * part, (p + 1) * part)
-        value = jnp.dot(hidden[0], first_ref[:, lanes], preferred_element_type=F32)
-        value = value + jnp.dot(hidden[1], rest_ref[:, lanes], preferred_element_type=F32)
+        weight = jnp.concatenate([first_ref[:, lanes], rest_ref[:, lanes]])
+        value = jnp.dot(hidden, weight, preferred_element_type=F32)
         quarters.append(value.astype(BF16))
     copies = []
     for g in range(groups):

time: 146 us -> 146 us (level)
  no operation moved by 1% of the time
where the time goes in v13:
time: 146 us; the launch traced here: 145 us
  starting transfers between devices  56.6 us (39%)
  blocking collectives  46.5 us (32%)
  Pallas kernels  20.6 us (14%)
  waiting for transfers between devices  19.9 us (14%)
    all_to_all x2, blocking collectives, exchanged(): lax.all_to_all(x, CHIPS, 0, 0, tiled=True, axis_index_groups=[members])  46.5 us
    ppermute x9, starting transfers between devices, swapped(): return lax.ppermute(x, CORES, [(0, 1), (1, 0)])  34.6 us
    all_to_all x1, starting transfers between devices, exchanged(): lax.all_to_all(x, CHIPS, 0, 0, tiled=True, axis_index_groups=[members])  12.4 us
    all_to_all x1, waiting for transfers between devices, exchanged(): lax.all_to_all(x, CHIPS, 0, 0, tiled=True, axis_index_groups=[members])  11.1 us
    all_to_all x1, starting transfers between devices, on_device(): tokens = lax.all_to_all(outgoing, CHIPS, 0, 0, tiled=True)  7.24 us
    ppermute x3, waiting for transfers between devices, on_device(): lax.ppermute(piece, CHIPS, square_step(side, way))  6.09 us
    pallas_call x1, Pallas kernels, halves(): pl.pallas_call(halves_body, name='halves', out_shape=[pltpu.VMEM((int(wid...  4.05 us
    pallas_call x1, Pallas kernels, gate_up(): pl.pallas_call(gate_body, name='gate_up', out_shape=[pltpu.VMEM(dims, F32...  3.15 us
  transfers between devices with their start and end apart: 14, of which 7 were waited for; matrix products, arithmetic and copies ran while one was open for 0% of the time, Pallas kernels for 9%

profile of v13, /device:TPU:513, one launch (start us, length us, event | category | flops | bytes accessed | tf_op | source)
XLA Modules:
  0.0 144.8 jit_solution(11152303957297250096)
XLA Ops:
  0.0 4.1 %halves.1 = (bf16[1536,768]{1,0:T(8,128)(2,1)S(1)}, bf16[2048,768]{1,0:T(8,128)(2,1)}, bf16[384,2048]{1,0:T(8,128)(2,1)}) custom-call(bf16[1,4096,384]{2,1,0:T(8,128)(2,1)} %gate_hbm.3, bf16[1,4096,384]{2,1,0:T(8,128)(2,1)} %up_hbm.3, bf16[1,384,4096]{2,1,0:T(8,128)(2,1)} %down_hbm.3), custom_call_target="tpu_custom_call" | custom-call | tf_op jit(solution)/shard_map/halves/pallas_call | solution.py:312
  4.1 20.5 %collective-permute-start.8 = (bf16[2048,768]{1,0:T(8,128)(2,1)}, bf16[2048,768]{1,0:T(8,128)(2,1)}, u32[]{:S(2)}, u32[]{:S(2)}) collective-permute-start(bf16[2048,768]{1,0:T(8,128)(2,1)} %get-tuple-element.36), channel_id=1, source_target_pairs={{0,1},{1,0},{2,3},{3,2},{4,5},{5,4},{6,7},{7,6},{8,9},{9,8},{10,11... | collective-permute-start | bytes 9437192 | tf_op jit(solution)/shard_map/ppermute | solution.py:19
  24.6 3.0 %attend.1 = (bf16[64,8,256]{2,1,0:T(8,128)(2,1)}, bf16[64,1024]{1,0:T(8,128)(2,1)}, bf16[64,1024]{1,0:T(8,128)(2,1)}, bf16[64,1024]{1,0:T(8,128)(2,1)}, bf16[64,1024]{1,0:T(8,128)(2,1)}) custom-call(bf16[4,8192]{1,0:T(4,128)(2,1)} %q_hbm.1, bf16[4,512]{1,0:T(4,128)(2,1)} %tk_hbm.1, bf16[4,512]{1,0:T(4,128)(2,1)} %tv_hbm.1, s32[4]{0:T(128)} %len_hbm.1, ...), custom_call_target="tpu_custom_call" | custom-call | tf_op jit(solution)/shard_map/attend/pallas_call | solution.py:214
  27.6 0.0 copy-start.10
  27.6 0.0 copy-start
  27.6 0.0 copy-start.1
  27.7 0.0 copy-start.2
  27.7 7.2 %all-to-all-start = ((bf16[64,8,256]{2,1,0:T(8,128)(2,1)}), bf16[64,8,256]{2,1,0:T(8,128)(2,1)}, u32[]{:S(2)}, u32[]{:S(2)}) async-start(bf16[64,8,256]{2,1,0:T(8,128)(2,1)} %get-tuple-element.24), calls=%async_computation | async-start | bytes 524288 | tf_op jit(solution)/shard_map/all_to_all | solution.py:686
  34.9 0.1 collective-permute-start
  35.1 1.4 collective-permute-start.1
  36.5 0.9 collective-permute-start.2
  37.4 1.2 collective-permute-start.3
  38.5 4.7 %collective-permute-done.refs_1_ = bf16[64,1024]{1,0:T(8,128)(2,1)S(1)} collective-permute-done((bf16[64,1024]{1,0:T(8,128)(2,1)}, bf16[64,1024]{1,0:T(8,128)(2,1)S(1)}, u32[]{:S(2)}, u32[]{:S(2)}) %collective-permute-start) | collective-permute-done | bytes 131104 | tf_op jit(solution)/shard_map/ppermute | solution.py:683
  43.2 0.0 copy-start.3
  43.2 3.5 %collective-permute-start.4 = (bf16[64,1024]{1,0:T(8,128)(2,1)S(1)}, bf16[64,1024]{1,0:T(8,128)(2,1)S(1)}, u32[]{:S(2)}, u32[]{:S(2)}) collective-permute-start(bf16[64,1024]{1,0:T(8,128)(2,1)S(1)} %collective-permute-done.refs_1_), channel_id=1, source_target_pairs={{0,1},{1,0},{2,3},{3,2},{4,5},{5,4},{6,7},{7,6},{8,9},{9,8},{10,11... | collective-permute-start | bytes 393224 | tf_op jit(solution)/shard_map/ppermute | solution.py:19
  46.7 1.4 collective-permute-done.1.refs_2_
  48.1 0.0 copy-start.4
  48.1 0.5 collective-permute-start.5
  48.7 0.0 collective-permute-done.2.refs_3_
  48.7 0.0 copy-start.5
  48.7 0.1 collective-permute-start.6
  48.8 0.0 collective-permute-done.3.refs_4_
  48.8 0.0 copy-start.6
  48.8 0.0 collective-permute-done.4.refs_5_
  48.8 0.0 copy-start.7
  48.8 0.8 collective-permute-done.5.refs_6_
  49.7 0.0 copy-start.8
  49.7 0.4 collective-permute-done.6.refs_7_
  50.0 0.0 copy-done.3
  50.0 0.0 copy-done.4
  50.0 0.0 copy-done.5
  50.0 0.0 copy-done.6
  50.0 0.0 copy-done.7
  50.1 0.3 copy-done.8
  50.3 0.0 copy-start.9
  50.3 0.7 copy-done.9
  51.0 1.3 stack.1.weight_ref
  52.3 0.0 all-to-all-done.x_ref
  52.3 2.1 %shard_map.136 = bf16[64,8,512]{2,1,0:T(8,128)(2,1)} custom-call(bf16[64,8,256]{2,1,0:T(8,128)(2,1)} %all-to-all-done.x_ref, bf16[512,1024]{1,0:T(8,128)(2,1)S(1)} %stack.1.weight_ref), custom_call_target="tpu_custom_call" | custom-call | tf_op jit(solution)/shard_map/pallas_call | solution.py:381
  54.5 12.4 %all-to-all-start.1 = ((bf16[64,8,512]{2,1,0:T(8,128)(2,1)}), bf16[64,8,512]{2,1,0:T(8,128)(2,1)S(1)}, u32[]{:S(2)}, u32[]{:S(2)}) async-start(bf16[64,8,512]{2,1,0:T(8,128)(2,1)} %shard_map.136), calls=%async_computation.1 | async-start | bytes 1048576 | tf_op jit(solution)/shard_map/all_to_all | solution.py:44
  66.9 0.9 collective-permute-start.10
  67.7 0.0 copy-done.10
  67.7 11.1 %all-to-all-done.1.x_ref = bf16[64,8,512]{2,1,0:T(8,128)(2,1)S(1)} async-done(((bf16[64,8,512]{2,1,0:T(8,128)(2,1)}), bf16[64,8,512]{2,1,0:T(8,128)(2,1)S(1)}, u32[]{:S(2)}, u32[]{:S(2)}) %all-to-all-start.1) | async-done | bytes 524320 | tf_op jit(solution)/shard_map/all_to_all | solution.py:44
  78.9 0.0 copy-done
  78.9 0.2 shard_map.137
  79.1 2.6 %collective-permute-start.7 = (bf16[2,8,512]{2,1,0:T(8,128)(2,1)S(1)}, bf16[2,8,512]{2,1,0:T(8,128)(2,1)S(1)}, u32[]{:S(2)}, u32[]{:S(2)}) collective-permute-start(bf16[2,8,512]{2,1,0:T(8,128)(2,1)S(1)} %get-tuple-element.31), channel_id=1, source_target_pairs={{0,1},{1,0},{2,3},{3,2},{4,5},{5,4},{6,7},{7,6},{8,9},{9,8},{10,11... | collective-permute-start | bytes 49160 | tf_op jit(solution)/shard_map/ppermute | solution.py:19
  81.7 0.0 copy-done.1
  81.7 0.0 copy-done.2
  81.7 0.2 shard_map.138
  81.9 0.6 collective-permute-done.7.other_ref
  82.6 1.2 dispatch.1
  83.7 23.3 %all_to_all.20.x_ref = bf16[64,8,512]{2,1,0:T(8,128)(2,1)S(1)} all-to-all(bf16[64,8,512]{2,1,0:T(8,128)(2,1)} %get-tuple-element.33), channel_id=1, replica_groups={{124,126,0,2,4,6,8,10,12,14,16,18,20,22,24,26,28,30,32,34,36,38,40,42,4..., dimensions={0} | all-to-all | bytes 1048576 | tf_op jit(solution)/shard_map/all_to_all | solution.py:44
  107.1 0.0 collective-permute-done.8.moved_ref
  107.1 3.1 %gate_up.1 = (f32[128,1536]{1,0:T(8,128)S(1)}, bf16[128,1536]{1,0:T(8,128)(2,1)S(1)}) custom-call(bf16[64,8,512]{2,1,0:T(8,128)(2,1)S(1)} %all_to_all.20.x_ref, bf16[1536,768]{1,0:T(8,128)(2,1)S(1)} %get-tuple-element.34.kept_ref, bf16[512,768]{1,0:T(8,128)(2,1)S(1)} %get-tuple-element.35.rest_ref, bf16[2048,768]{1,0:T(8,128)(2,1)} %collective-permute-done.8.moved_ref), custom_call_target="tpu_custom_call" | custom-call | tf_op jit(solution)/shard_map/gate_up/pallas_call | solution.py:555
  110.2 2.8 %collective-permute-start.9 = (bf16[128,1536]{1,0:T(8,128)(2,1)S(1)}, bf16[128,1536]{1,0:T(8,128)(2,1)S(1)}, u32[]{:S(2)}, u32[]{:S(2)}) collective-permute-start(bf16[128,1536]{1,0:T(8,128)(2,1)S(1)} %get-tuple-element.38), channel_id=1, source_target_pairs={{0,1},{1,0},{2,3},{3,2},{4,5},{5,4},{6,7},{7,6},{8,9},{9,8},{10,11... | collective-permute-start | bytes 1179656 | tf_op jit(solution)/shard_map/ppermute | solution.py:19
  113.0 1.4 fetch_down.1.first_ref
  114.4 0.0 collective-permute-done.10.rest_ref
  114.4 0.0 collective-permute-done.9.arrived_ref
  114.4 3.1 %shard_map.139 = bf16[64,8,512]{2,1,0:T(8,128)(2,1)} custom-call(f32[128,1536]{1,0:T(8,128)S(1)} %get-tuple-element.37.after_ref.part_ref, bf16[128,1536]{1,0:T(8,128)(2,1)S(1)} %collective-permute-done.9.arrived_ref, bf16[384,2048]{1,0:T(8,128)(2,1)S(1)} %fetch_down.1.first_ref, bf16[384,2048]{1,0:T(8,128)(2,1)} %collective-permute-done.10.rest_ref), custom_call_target="tpu_custom_call" | custom-call | tf_op jit(solution)/shard_map/pallas_call | solution.py:623
  117.5 23.2 %all_to_all.21.x_ref = bf16[64,8,512]{2,1,0:T(8,128)(2,1)S(1)} all-to-all(bf16[64,8,512]{2,1,0:T(8,128)(2,1)} %shard_map.139), channel_id=1, replica_groups={{124,126,0,2,4,6,8,10,12,14,16,18,20,22,24,26,28,30,32,34,36,38,40,42,4..., dimensions={0} | all-to-all | bytes 1048576 | tf_op jit(solution)/shard_map/all_to_all | solution.py:44
  140.7 0.2 shard_map.140
  140.8 2.5 %collective-permute-start.11 = (f32[2,8,512]{2,1,0:T(8,128)S(1)}, f32[2,8,512]{2,1,0:T(8,128)S(1)}, u32[]{:S(2)}, u32[]{:S(2)}) collective-permute-start(f32[2,8,512]{2,1,0:T(8,128)S(1)} %get-tuple-element.42), channel_id=1, source_target_pairs={{0,1},{1,0},{2,3},{3,2},{4,5},{5,4},{6,7},{7,6},{8,9},{9,8},{10,11... | collective-permute-start | bytes 98312 | tf_op jit(solution)/shard_map/ppermute | solution.py:19
  143.4 0.9 collective-permute-done.11.other_ref
  144.2 0.6 shard_map.141
  (1 shorter events, 0.0 us)
Async XLA Ops:
  4.1 103.0 %collective-permute-start.8 = (bf16[2048,768]{1,0:T(8,128)(2,1)}, bf16[2048,768]{1,0:T(8,128)(2,1)}, u32[]{:S(2)}, u32[]{:S(2)}) collective-permute-start(bf16[2048,768]{1,0:T(8,128)(2,1)} %get-tuple-element.36), channel_id=1, source_target_pairs={{0,1},{1,0},{2,3},{3,2},{4,5},{5,4},{6,7},{7,6},{8,9},{9,8},{10,11... | collective-permute-start | bytes 9437192 | tf_op jit(solution)/shard_map/ppermute | solution.py:19
  27.6 40.1 %copy-start.10 = (bf16[4096]{0:T(1024)(128)(2,1)S(1)}, bf16[4096]{0:T(1024)(128)(2,1)}, u32[]{:S(2)}) copy-start(bf16[4096]{0:T(1024)(128)(2,1)} %param.22) | copy-start | bytes 24580
  27.6 51.2 %copy-start = (bf16[4,4096]{1,0:T(4,128)(2,1)S(1)}, bf16[4,4096]{1,0:T(4,128)(2,1)}, u32[]{:S(2)}) copy-start(bf16[4,4096]{1,0:T(4,128)(2,1)} %residual_ref.1) | copy-start | bytes 98308
  27.6 54.1 %copy-start.1 = (s32[8,8]{1,0:T(8,128)S(1)}, s32[8,8]{1,0:T(8,128)}, u32[]{:S(2)}) copy-start(s32[8,8]{1,0:T(8,128)} %ids_ref.1) | copy-start | bytes 772
  27.7 54.1 %copy-start.2 = (f32[8,8]{1,0:T(8,128)S(1)}, f32[8,8]{1,0:T(8,128)}, u32[]{:S(2)}) copy-start(f32[8,8]{1,0:T(8,128)} %weight_ref.1) | copy-start | bytes 772
  27.7 24.7 %all-to-all-start = ((bf16[64,8,256]{2,1,0:T(8,128)(2,1)}), bf16[64,8,256]{2,1,0:T(8,128)(2,1)}, u32[]{:S(2)}, u32[]{:S(2)}) async-start(bf16[64,8,256]{2,1,0:T(8,128)(2,1)} %get-tuple-element.24), calls=%async_computation | async-start | bytes 524288 | tf_op jit(solution)/shard_map/all_to_all | solution.py:686
  34.9 8.3 %collective-permute-start = (bf16[64,1024]{1,0:T(8,128)(2,1)}, bf16[64,1024]{1,0:T(8,128)(2,1)S(1)}, u32[]{:S(2)}, u32[]{:S(2)}) collective-permute-start(bf16[64,1024]{1,0:T(8,128)(2,1)} %get-tuple-element.26), channel_id=1, source_target_pairs={{0,2},{2,18},{4,6},{6,22},{8,10},{10,26},{12,14},{14,30},{16,0},{1... | collective-permute-start | bytes 393224 | tf_op jit(solution)/shard_map/ppermute | solution.py:683
  35.1 13.1 %collective-permute-start.1 = (bf16[64,1024]{1,0:T(8,128)(2,1)}, bf16[64,1024]{1,0:T(8,128)(2,1)S(1)}, u32[]{:S(2)}, u32[]{:S(2)}) collective-permute-start(bf16[64,1024]{1,0:T(8,128)(2,1)} %get-tuple-element.27), channel_id=1, source_target_pairs={{0,16},{2,0},{4,20},{6,4},{8,24},{10,8},{12,28},{14,12},{16,18},{1... | collective-permute-start | bytes 393224 | tf_op jit(solution)/shard_map/ppermute | solution.py:683
  36.5 12.2 %collective-permute-start.2 = (bf16[64,1024]{1,0:T(8,128)(2,1)}, bf16[64,1024]{1,0:T(8,128)(2,1)S(1)}, u32[]{:S(2)}, u32[]{:S(2)}) collective-permute-start(bf16[64,1024]{1,0:T(8,128)(2,1)} %get-tuple-element.28), channel_id=1, source_target_pairs={{0,18},{2,16},{4,22},{6,20},{8,26},{10,24},{12,30},{14,28},{16,2},... | collective-permute-start | bytes 393224 | tf_op jit(solution)/shard_map/ppermute | solution.py:683
  37.4 11.5 %collective-permute-start.3 = (bf16[64,1024]{1,0:T(8,128)(2,1)}, bf16[64,1024]{1,0:T(8,128)(2,1)S(1)}, u32[]{:S(2)}, u32[]{:S(2)}) collective-permute-start(bf16[64,1024]{1,0:T(8,128)(2,1)} %get-tuple-element.25.refs_0_), channel_id=1, source_target_pairs={{0,1},{1,0},{2,3},{3,2},{4,5},{5,4},{6,7},{7,6},{8,9},{9,8},{10,11... | collective-permute-start | bytes 393224 | tf_op jit(solution)/shard_map/ppermute | solution.py:19
  43.2 6.8 %copy-start.3 = (bf16[64,1024]{1,0:T(8,128)(2,1)}, bf16[64,1024]{1,0:T(8,128)(2,1)S(1)}, u32[]{:S(2)}) copy-start(bf16[64,1024]{1,0:T(8,128)(2,1)S(1)} %collective-permute-done.refs_1_) | copy-start | bytes 393220
  43.2 5.6 %collective-permute-start.4 = (bf16[64,1024]{1,0:T(8,128)(2,1)S(1)}, bf16[64,1024]{1,0:T(8,128)(2,1)S(1)}, u32[]{:S(2)}, u32[]{:S(2)}) collective-permute-start(bf16[64,1024]{1,0:T(8,128)(2,1)S(1)} %collective-permute-done.refs_1_), channel_id=1, source_target_pairs={{0,1},{1,0},{2,3},{3,2},{4,5},{5,4},{6,7},{7,6},{8,9},{9,8},{10,11... | collective-permute-start | bytes 393224 | tf_op jit(solution)/shard_map/ppermute | solution.py:19
  48.1 1.9 %copy-start.4 = (bf16[64,1024]{1,0:T(8,128)(2,1)}, bf16[64,1024]{1,0:T(8,128)(2,1)S(1)}, u32[]{:S(2)}) copy-start(bf16[64,1024]{1,0:T(8,128)(2,1)S(1)} %collective-permute-done.1.refs_2_) | copy-start | bytes 393220
  48.1 1.5 %collective-permute-start.5 = (bf16[64,1024]{1,0:T(8,128)(2,1)S(1)}, bf16[64,1024]{1,0:T(8,128)(2,1)S(1)}, u32[]{:S(2)}, u32[]{:S(2)}) collective-permute-start(bf16[64,1024]{1,0:T(8,128)(2,1)S(1)} %collective-permute-done.1.refs_2_), channel_id=1, source_target_pairs={{0,1},{1,0},{2,3},{3,2},{4,5},{5,4},{6,7},{7,6},{8,9},{9,8},{10,11... | collective-permute-start | bytes 393224 | tf_op jit(solution)/shard_map/ppermute | solution.py:19
  48.7 1.4 copy-start.5
  48.7 1.3 collective-permute-start.6
  48.8 1.2 copy-start.6
  48.8 1.2 copy-start.7
  49.7 0.7 copy-start.8
  50.3 0.7 copy-start.9
  54.5 24.4 %all-to-all-start.1 = ((bf16[64,8,512]{2,1,0:T(8,128)(2,1)}), bf16[64,8,512]{2,1,0:T(8,128)(2,1)S(1)}, u32[]{:S(2)}, u32[]{:S(2)}) async-start(bf16[64,8,512]{2,1,0:T(8,128)(2,1)} %shard_map.136), calls=%async_computation.1 | async-start | bytes 1048576 | tf_op jit(solution)/shard_map/all_to_all | solution.py:44
  66.9 47.5 %collective-permute-start.10 = (bf16[384,2048]{1,0:T(8,128)(2,1)}, bf16[384,2048]{1,0:T(8,128)(2,1)}, u32[]{:S(2)}, u32[]{:S(2)}) collective-permute-start(bf16[384,2048]{1,0:T(8,128)(2,1)} %get-tuple-element.39), channel_id=1, source_target_pairs={{0,1},{1,0},{2,3},{3,2},{4,5},{5,4},{6,7},{7,6},{8,9},{9,8},{10,11... | collective-permute-start | bytes 4718600 | tf_op jit(solution)/shard_map/ppermute | solution.py:19
  79.1 3.4 %collective-permute-start.7 = (bf16[2,8,512]{2,1,0:T(8,128)(2,1)S(1)}, bf16[2,8,512]{2,1,0:T(8,128)(2,1)S(1)}, u32[]{:S(2)}, u32[]{:S(2)}) collective-permute-start(bf16[2,8,512]{2,1,0:T(8,128)(2,1)S(1)} %get-tuple-element.31), channel_id=1, source_target_pairs={{0,1},{1,0},{2,3},{3,2},{4,5},{5,4},{6,7},{7,6},{8,9},{9,8},{10,11... | collective-permute-start | bytes 49160 | tf_op jit(solution)/shard_map/ppermute | solution.py:19
  110.2 4.2 %collective-permute-start.9 = (bf16[128,1536]{1,0:T(8,128)(2,1)S(1)}, bf16[128,1536]{1,0:T(8,128)(2,1)S(1)}, u32[]{:S(2)}, u32[]{:S(2)}) collective-permute-start(bf16[128,1536]{1,0:T(8,128)(2,1)S(1)} %get-tuple-element.38), channel_id=1, source_target_pairs={{0,1},{1,0},{2,3},{3,2},{4,5},{5,4},{6,7},{7,6},{8,9},{9,8},{10,11... | collective-permute-start | bytes 1179656 | tf_op jit(solution)/shard_map/ppermute | solution.py:19
  140.8 3.4 %collective-permute-start.11 = (f32[2,8,512]{2,1,0:T(8,128)S(1)}, f32[2,8,512]{2,1,0:T(8,128)S(1)}, u32[]{:S(2)}, u32[]{:S(2)}) collective-permute-start(f32[2,8,512]{2,1,0:T(8,128)S(1)} %get-tuple-element.42), channel_id=1, source_target_pairs={{0,1},{1,0},{2,3},{3,2},{4,5},{5,4},{6,7},{7,6},{8,9},{9,8},{10,11... | collective-permute-start | bytes 98312 | tf_op jit(solution)/shard_map/ppermute | solution.py:19
